TPU v7x, 32 devices: a whole 2x2x4 slice. The times are simulated.
32 devices in a mesh: section: 2 (over core), expert: 4 (over y, x), dp: 4 (over z).
Axes of the slice: x: 2, y: 2, z: 4, core: 2. Of those that a mesh axis runs over, the one named last changes fastest.
Arguments:
- inputs: bfloat16 [2, 4, 256, 1024], P(None, 'expert', 'dp'), may hold values from -36 to 36
- cotangent: bfloat16 [2, 4, 256, 1024], P(None, 'expert', 'dp'), may hold values from -6 to 6
- segment_ids: int32 [2, 4, 256], P(None, 'expert'), may hold values from 0 to 3, never falling along the last dimension, each value on 1 to 128 neighbouring positions
- routes: int32 [2, 2, 4, 256, 1], P('section', None, 'expert', 'dp'), may hold values from 0 to 7; in each aligned block of 64 rows (0 to 63, 64 to 127, ..., all dimensions but the last counted through in order) at most 10 rows name the same one
- norm_gains: bfloat16 [2, 2, 1024], P('section', None, ('expert', 'dp')), may hold values from 0.5 to 1.5
- norm_shifts: bfloat16 [2, 2, 1024], P('section', None, ('expert', 'dp')), may hold values from -3 to 3
- attn_qkv: bfloat16 [2, 1024, 3072], P('section', ('expert', 'dp')), may hold values from -0.1875 to 0.1875
- attn_proj: bfloat16 [2, 1024, 1024], P('section', ('expert', 'dp')), may hold values from -0.75 to 0.75
- dense_up: bfloat16 [2, 1024, 4096], P('section', ('expert', 'dp')), may hold values from -0.1875 to 0.1875
- dense_down: bfloat16 [2, 4096, 1024], P('section', ('expert', 'dp')), may hold values from -0.09375 to 0.09375
- router: bfloat16 [2, 1024, 8], P('section', ('expert', 'dp')), may hold values from -0.25 to 0.25
- mixer: bfloat16 [2, 1024, 2], P('section', ('expert', 'dp')), may hold values from -0.4375 to 0.4375
- expert_up: bfloat16 [2, 8, 1024, 4096], P('section', 'expert', None, 'dp'), may hold values from -0.1875 to 0.1875
- expert_down: bfloat16 [2, 8, 4096, 1024], P('section', 'expert', 'dp'), may hold values from -4 to 4
Outputs:
- activations: bfloat16 [2, 2, 4, 256, 1024], P('section', None, 'expert', 'dp')
- input_grads: float32 [2, 2, 4, 256, 1024], P('section', None, 'expert', 'dp')
- grad_norm_gains: float32 [2, 2, 1024], P('section', None, ('expert', 'dp'))
- grad_norm_shifts: float32 [2, 2, 1024], P('section', None, ('expert', 'dp'))
- grad_attn_qkv: float32 [2, 1024, 3072], P('section', ('expert', 'dp'))
- grad_attn_proj: float32 [2, 1024, 1024], P('section', ('expert', 'dp'))
- grad_dense_up: float32 [2, 1024, 4096], P('section', ('expert', 'dp'))
- grad_dense_down: float32 [2, 4096, 1024], P('section', ('expert', 'dp'))
- grad_router: float32 [2, 1024, 8], P('section', ('expert', 'dp'))
- grad_mixer: float32 [2, 1024, 2], P('section', ('expert', 'dp'))
- grad_expert_up: float32 [2, 8, 1024, 4096], P('section', 'expert', None, 'dp')
- grad_expert_down: float32 [2, 8, 4096, 1024], P('section', 'expert', 'dp')
- branch_rms: float32 [2, 3], P('section')
Inputs may be any that keep to these rules, and one draw needn't show every extreme that they name: `routes`: in each layer and micro-batch, at most 10 of the 64 tokens of one device's aligned block go to one expert, and some expert receives exactly 10.
All inputs are finite; a program needn't handle non-finite values.
Results may differ from a plain program's by a relative error of at most 0.022.
Values may be sent and summed in bfloat16 or wider, within the bound.
No kernel may reach another device: no remote copies, remote signals or barrier semaphores. Data moves between devices by JAX's collectives and lax.ppermute only.
A program may use at most 256 MiB of HBM per device.

v0:
```python
import jax
import jax.numpy as jnp
from jax import lax
from jax.sharding import PartitionSpec as P

HEADS = 16
HEAD_DIM = 64
EVERY = ("section", "expert", "dp")
HOMES = ("section", "expert")


def layer_norm(value_rows, gain_vec, shift_vec):
    centre = jnp.mean(value_rows, axis=-1, keepdims=True)
    centred = value_rows - centre
    variance = jnp.mean(centred * centred, axis=-1, keepdims=True)
    return centred * lax.rsqrt(variance + 1e-05) * gain_vec + shift_vec


def gelu_tanh(value_rows):
    return jax.nn.gelu(value_rows, approximate=True)


def gelu_grad(value_rows, grad_in):
    return jax.vjp(gelu_tanh, value_rows)[1](grad_in)[0]


def product(left_mat, right_mat):
    return jnp.dot(left_mat, right_mat, preferred_element_type=jnp.float32)


def product_tn(left_mat, right_mat):
    return lax.dot_general(
        left_mat, right_mat, (((0,), (0,)), ((), ())), preferred_element_type=jnp.float32
    )


def product_nt(left_mat, right_mat):
    return lax.dot_general(
        left_mat, right_mat, (((1,), (1,)), ((), ())), preferred_element_type=jnp.float32
    )


def low(values):
    return values.astype(jnp.bfloat16)


def exchange(blocks, axes):
    return lax.all_to_all(blocks, axes, split_axis=0, concat_axis=0, tiled=True)


def spread(block, axes):
    count = lax.axis_size(axes)
    return exchange(jnp.broadcast_to(block[None], (count,) + block.shape), axes)


def gather_rows(block):
    return lax.all_gather(block, "dp", axis=0, tiled=True)


def sum_blocks(blocks):
    return jnp.sum(blocks.astype(jnp.float32), axis=0)


def scatter_rows(partial_rows):
    count = lax.axis_size("dp")
    blocks = low(partial_rows).reshape(count, -1, partial_rows.shape[-1])
    return sum_blocks(exchange(blocks, "dp"))


def other_core(block):
    return lax.ppermute(block, "section", [(0, 1), (1, 0)])


def both_cores(block):
    return jnp.concatenate([block, other_core(block)], axis=0)


def halves_for_cores(block, section_id):
    half = block.shape[1] // 2
    kept = lax.dynamic_slice_in_dim(block, section_id * half, half, axis=1)
    sent = lax.dynamic_slice_in_dim(block, (1 - section_id) * half, half, axis=1)
    return jnp.concatenate([kept, other_core(sent)], axis=0)


def shards(
    inputs,
    cotangent,
    segment_ids,
    routes,
    norm_gains,
    norm_shifts,
    attn_qkv,
    attn_proj,
    dense_up,
    dense_down,
    router,
    mixer,
    expert_up,
    expert_down,
):
    sections = lax.axis_size("section")
    groups = lax.axis_size("expert")
    dp_size = lax.axis_size("dp")
    section_id = lax.axis_index("section")
    expert_id = lax.axis_index("expert")
    micro_count = inputs.shape[0]
    seq_rows = inputs.shape[2]
    width = inputs.shape[3]
    full_len = segment_ids.shape[2]
    experts_total = router.shape[2]
    hidden_rows = dense_down.shape[1]
    weight_rows = attn_qkv.shape[1]
    heads_here = HEADS // dp_size
    head_width = heads_here * HEAD_DIM
    capacity = max(2, 5 * seq_rows // (4 * experts_total))
    slots = dp_size * capacity
    devices = sections * groups * dp_size

    small_parts = jnp.concatenate([norm_gains[0], norm_shifts[0], router[0].T, mixer[0].T], axis=0)
    small_count = small_parts.shape[0]
    route_row = low(routes[0, :, 0, :, 0])
    message = jnp.concatenate([small_parts.reshape(-1), route_row.reshape(-1)])
    filled = message.shape[0]
    padded = -(-filled // 1024) * 1024
    message = jnp.pad(message, (0, padded - filled)).reshape(padded // 128, 128)
    small_all = spread(message, EVERY).reshape(sections, groups, dp_size, padded)
    params_all = small_all[..., : small_count * weight_rows].reshape(
        sections, groups * dp_size, small_count, weight_rows
    )
    params_all = params_all.transpose(0, 2, 1, 3).reshape(sections, small_count, width)
    routes_all = lax.dynamic_index_in_dim(
        small_all[..., small_count * weight_rows : filled], expert_id, 1, keepdims=False
    ).reshape(sections, dp_size, micro_count, seq_rows)
    routes_all = lax.dynamic_index_in_dim(routes_all, section_id, 2, keepdims=False)
    routes_all = routes_all.astype(jnp.int32)

    qkv_cols = attn_qkv[0].reshape(weight_rows, 3, dp_size, head_width).transpose(2, 0, 1, 3)
    qkv_cols = exchange(qkv_cols.reshape(dp_size, weight_rows, 3 * head_width), "dp")
    qkv_both = spread(spread(qkv_cols, "expert").reshape(width, 3 * head_width), "section")
    proj_rows = exchange(
        jnp.broadcast_to(attn_proj, (dp_size,) + attn_proj.shape[1:]), "dp"
    ).reshape(dp_size * weight_rows, width)
    proj_both = spread(spread(proj_rows, "expert").reshape(width, width), "section")
    up_cols = dense_up[0].reshape(weight_rows, groups, dp_size, hidden_rows).transpose(2, 0, 1, 3)
    hidden_here = groups * hidden_rows
    up_cols = exchange(up_cols.reshape(dp_size, weight_rows, hidden_here), "dp")
    up_both = spread(spread(up_cols, "expert").reshape(width, hidden_here), "section")
    down_both = spread(spread(dense_down[0], "expert").reshape(hidden_here, width), "section")
    exp_up_both = exchange(expert_up[0], "section")
    exp_down_both = exchange(expert_down[0], "section")

    segments = lax.dynamic_index_in_dim(segment_ids[:, 0], section_id, 0, keepdims=False)
    places = jnp.arange(full_len, dtype=jnp.int32)
    allowed = (segments[:, None] == segments[None, :]) & (places[None, :] <= places[:, None])
    earlier = (places[None, :] < places[:, None]) & (
        places[None, :] // seq_rows == places[:, None] // seq_rows
    )

    def slot_table(route_now):
        rank = jnp.sum(
            ((route_now[:, None] == route_now[None, :]) & earlier).astype(jnp.int32), axis=1
        )
        home = route_now % sections * groups + route_now // sections
        target = home * slots + places // seq_rows * capacity + rank
        slot_ids = jnp.arange(sections * groups * slots, dtype=jnp.int32)
        table = low(slot_ids[:, None] == target[None, :])
        hot = route_now[:, None] == jnp.arange(experts_total, dtype=jnp.int32)[None, :]
        return table, hot.astype(jnp.float32)

    def to_experts(token_rows, table):
        packed = low(product(table, token_rows)).reshape(sections * groups, slots, width)
        return exchange(packed, HOMES).reshape(-1, width)

    def from_experts(expert_rows, table):
        returned = exchange(low(expert_rows).reshape(sections * groups, slots, width), HOMES)
        return product_tn(table, returned.reshape(-1, width))

    def heads_of(columns):
        return columns.reshape(-1, heads_here, HEAD_DIM)

    def split_heads(packed):
        return [heads_of(packed[:, i * head_width : (i + 1) * head_width]) for i in range(3)]

    def forward_layer(layer, layer_in):
        params = params_all[layer].astype(jnp.float32)
        table, hot = slot_table(routes_all[layer].reshape(full_len))
        normed = low(layer_norm(layer_in, params[0:1], params[2:3]))
        normed_seq = gather_rows(normed)
        qkv = low(product(normed_seq, qkv_both[layer]))
        queries, keys, values = split_heads(qkv)
        scores = jnp.einsum("ihd,jhd->hij", queries, keys, preferred_element_type=jnp.float32)
        scores = jnp.where(allowed[None], scores * 0.125, -jnp.inf)
        exp_scores = jnp.exp(scores - jnp.max(scores, axis=-1, keepdims=True))
        probs = exp_scores / jnp.sum(exp_scores, axis=-1, keepdims=True)
        probs_low = low(probs)
        mixed = jnp.einsum("hij,jhd->ihd", probs_low, values, preferred_element_type=jnp.float32)
        mixed = exchange(low(mixed).reshape(dp_size, seq_rows, head_width), "dp")
        mixed = mixed.transpose(1, 0, 2).reshape(seq_rows, width)
        attn_branch = product(mixed, proj_both[layer])
        residual = layer_in + attn_branch
        mid_seq = gather_rows(low(layer_norm(residual, params[1:2], params[3:4])))
        expert_rows = to_experts(mid_seq, table)
        small_weights = params_all[layer, 4:]
        small_logits = product_nt(mid_seq, small_weights)
        gate_probs = jax.nn.softmax(small_logits[:, :experts_total], axis=-1)
        gate = jnp.sum(gate_probs * hot, axis=-1, keepdims=True)
        coef = jax.nn.softmax(small_logits[:, experts_total:], axis=-1)
        hidden = product(mid_seq, up_both[layer])
        hidden_low = low(gelu_tanh(hidden))
        dense_part = product(hidden_low, down_both[layer])
        exp_hidden = product(expert_rows, exp_up_both[layer])
        exp_hidden_low = low(gelu_tanh(exp_hidden))
        expert_part = from_experts(product(exp_hidden_low, exp_down_both[layer]), table)
        branch = scatter_rows(coef[:, 0:1] * dense_part + coef[:, 1:2] * gate * expert_part)
        layer_out = residual + branch
        squares = jnp.stack(
            [
                jnp.sum(attn_branch * attn_branch),
                jnp.sum(branch * branch),
                jnp.sum(layer_out * layer_out),
            ]
        )
        record = {
            "params": params,
            "small_weights": small_weights,
            "table": table,
            "hot": hot,
            "layer_in": layer_in,
            "normed_seq": normed_seq,
            "qkv": qkv,
            "probs": probs,
            "probs_low": probs_low,
            "mixed": mixed,
            "residual": residual,
            "mid_seq": mid_seq,
            "expert_rows": expert_rows,
            "gate_probs": gate_probs,
            "gate": gate,
            "coef": coef,
            "hidden": hidden,
            "hidden_low": hidden_low,
            "dense_part": dense_part,
            "exp_hidden": exp_hidden,
            "exp_hidden_low": exp_hidden_low,
            "expert_part": expert_part,
        }
        return layer_out, squares, record

    def backward_layer(layer, grad_low, record):
        grad_out = grad_low.astype(jnp.float32)
        params = record["params"]
        coef, gate, table = record["coef"], record["gate"], record["table"]
        grad_seq = gather_rows(grad_low).astype(jnp.float32)
        d_dense = low(coef[:, 0:1] * grad_seq)
        d_expert = low(coef[:, 1:2] * gate * grad_seq)
        expert_grad_rows = to_experts(d_expert, table)
        dense_dot = jnp.sum(grad_seq * record["dense_part"], axis=-1, keepdims=True)
        expert_dot = jnp.sum(grad_seq * record["expert_part"], axis=-1, keepdims=True)
        d_coef = jnp.concatenate([dense_dot, gate * expert_dot], axis=1)
        d_mix = coef * (d_coef - jnp.sum(coef * d_coef, axis=-1, keepdims=True))
        d_logits = record["gate_probs"] * (record["hot"] - gate) * (coef[:, 1:2] * expert_dot)
        d_small = low(jnp.concatenate([d_logits, d_mix], axis=1))
        d_up = low(gelu_grad(record["hidden"], product_nt(d_dense, down_both[layer])))
        d_mid_part = product_nt(d_up, up_both[layer]) + product(d_small, record["small_weights"])
        d_exp_hidden = gelu_grad(
            record["exp_hidden"], product_nt(expert_grad_rows, exp_down_both[layer])
        )
        d_exp_hidden = low(d_exp_hidden)
        d_mid_part = d_mid_part + from_experts(
            product_nt(d_exp_hidden, exp_up_both[layer]), table
        )
        d_mid = scatter_rows(d_mid_part)
        g_exp_up = product_tn(record["expert_rows"], d_exp_hidden)
        g_exp_down = product_tn(record["exp_hidden_low"], expert_grad_rows)
        mid_both = both_cores(record["mid_seq"])
        g_up = product_tn(mid_both, halves_for_cores(d_up, section_id))
        g_down = product_tn(
            both_cores(record["hidden_low"]), halves_for_cores(d_dense, section_id)
        )
        g_small = product_tn(d_small, record["mid_seq"])
        norm_back = jax.vjp(layer_norm, record["residual"], params[1:2], params[3:4])[1]
        d_resid_norm, d_gain_one, d_shift_one = norm_back(d_mid)
        d_resid = grad_out + d_resid_norm
        d_attn = low(d_resid)
        g_proj = product_tn(both_cores(record["mixed"]), halves_for_cores(d_attn, section_id))
        d_mixed = low(product_nt(d_attn, proj_both[layer]))
        d_mixed = d_mixed.reshape(seq_rows, dp_size, head_width).transpose(1, 0, 2)
        d_mixed = heads_of(exchange(d_mixed, "dp").reshape(full_len, head_width))
        queries, keys, values = split_heads(record["qkv"])
        probs = record["probs"]
        d_values = jnp.einsum(
            "hij,ihd->jhd", record["probs_low"], d_mixed, preferred_element_type=jnp.float32
        )
        d_probs = jnp.einsum("ihd,jhd->hij", d_mixed, values, preferred_element_type=jnp.float32)
        d_scores = low(probs * (d_probs - jnp.sum(probs * d_probs, axis=-1, keepdims=True)))
        d_queries = jnp.einsum(
            "hij,jhd->ihd", d_scores, keys, preferred_element_type=jnp.float32
        )
        d_keys = jnp.einsum(
            "hij,ihd->jhd", d_scores, queries, preferred_element_type=jnp.float32
        )
        d_qkv = low(
            jnp.concatenate(
                [
                    (d_queries * 0.125).reshape(full_len, head_width),
                    (d_keys * 0.125).reshape(full_len, head_width),
                    d_values.reshape(full_len, head_width),
                ],
                axis=1,
            )
        )
        d_normed = scatter_rows(product_nt(d_qkv, qkv_both[layer]))
        g_qkv = product_tn(
            both_cores(record["normed_seq"]), halves_for_cores(d_qkv, section_id)
        )
        first_back = jax.vjp(layer_norm, record["layer_in"], params[0:1], params[2:3])[1]
        d_input_norm, d_gain_zero, d_shift_zero = first_back(d_normed)
        small_grads = jnp.concatenate(
            [d_gain_zero, d_gain_one, d_shift_zero, d_shift_one, g_small], axis=0
        )

        def over_expert(grad_mat):
            blocks = low(grad_mat).reshape(groups, -1, grad_mat.shape[-1])
            return sum_blocks(exchange(blocks, "expert"))

        def over_dp(grad_mat):
            blocks = low(grad_mat).reshape(dp_size, weight_rows, grad_mat.shape[-1])
            return exchange(blocks, "dp")

        reduced = {
            "qkv": over_dp(over_expert(g_qkv)),
            "proj": sum_blocks(over_dp(over_expert(g_proj))),
            "up": over_dp(over_expert(g_up)),
            "down": over_expert(g_down),
        }
        return d_resid + d_input_norm, reduced, small_grads, g_exp_up, g_exp_down

    own_input = lax.dynamic_index_in_dim(inputs[:, 0], section_id, 0, keepdims=False)
    own_grad = lax.dynamic_index_in_dim(cotangent[:, 0], section_id, 0, keepdims=False)
    out_zero, squares_zero, record_zero = forward_layer(0, own_input.astype(jnp.float32))
    out_zero = low(out_zero)
    out_one, squares_one, record_one = forward_layer(1, out_zero.astype(jnp.float32))
    grad_one, reduced_one, small_one, exp_up_one, exp_down_one = backward_layer(
        1, own_grad, record_one
    )
    grad_zero, reduced_zero, small_zero, exp_up_zero, exp_down_zero = backward_layer(
        0, low(grad_one), record_zero
    )

    def to_owner(layer_zero, layer_one):
        return exchange(jnp.stack([layer_zero, layer_one]), "section")

    activations = to_owner(out_zero, low(out_one))
    input_grads = to_owner(grad_zero, grad_one)
    grad_exp_up = to_owner(exp_up_zero, exp_up_one)
    grad_exp_down = to_owner(exp_down_zero, exp_down_one)
    joined = {
        name: to_owner(reduced_zero[name].astype(jnp.float32), reduced_one[name].astype(jnp.float32))
        for name in reduced_zero
    }
    grad_qkv = joined["qkv"].transpose(2, 1, 0, 3).reshape(weight_rows, dp_size, 3, head_width)
    grad_qkv = grad_qkv.transpose(0, 2, 1, 3).reshape(weight_rows, 3 * width)
    grad_up = joined["up"].reshape(sections, dp_size, weight_rows, groups // sections, hidden_rows)
    grad_up = grad_up.transpose(2, 0, 3, 1, 4).reshape(weight_rows, -1)
    grad_proj = joined["proj"].transpose(1, 0, 2).reshape(weight_rows, width)
    grad_down = joined["down"].transpose(1, 0, 2).reshape(hidden_rows, width)

    small_grads = jnp.stack([small_zero, small_one]).reshape(
        sections, small_count, groups * dp_size, weight_rows
    )
    small_grads = small_grads.transpose(0, 2, 1, 3).reshape(
        sections, groups * dp_size, small_count * weight_rows
    )
    squares = jnp.stack([squares_zero, squares_one])
    squares = jnp.broadcast_to(squares[:, None], (sections, groups * dp_size, 3))
    small_message = jnp.concatenate([small_grads, squares], axis=-1)
    filled_back = small_message.shape[-1]
    padded_back = -(-filled_back // 1024) * 1024
    small_message = jnp.pad(small_message, ((0, 0), (0, 0), (0, padded_back - filled_back)))
    small_sum = sum_blocks(
        exchange(small_message.reshape(devices, padded_back // 128, 128), EVERY)
    ).reshape(-1)
    sums = small_sum[: small_count * weight_rows].reshape(small_count, weight_rows)
    totals = small_sum[small_count * weight_rows : filled_back]
    element_count = micro_count * seq_rows * width * groups * dp_size
    branch_rms = jnp.sqrt(totals / element_count)[None]
    return (
        activations[None, :, None],
        input_grads[None, :, None],
        sums[None, 0:2],
        sums[None, 2:4],
        grad_qkv[None],
        grad_proj[None],
        grad_up[None],
        grad_down[None],
        sums[4 : 4 + experts_total].T[None],
        sums[4 + experts_total :].T[None],
        grad_exp_up[None],
        grad_exp_down[None],
        branch_rms,
    )


def solution(mesh):
    placed = (
        P(None, "expert", "dp", None),
        P(None, "expert", "dp", None),
        P(None, "expert", None),
        P("section", None, "expert", "dp", None),
        P("section", None, ("expert", "dp")),
        P("section", None, ("expert", "dp")),
        P("section", ("expert", "dp"), None),
        P("section", ("expert", "dp"), None),
        P("section", ("expert", "dp"), None),
        P("section", ("expert", "dp"), None),
        P("section", ("expert", "dp"), None),
        P("section", ("expert", "dp"), None),
        P("section", "expert", None, "dp"),
        P("section", "expert", "dp", None),
    )
    return jax.shard_map(
        shards,
        mesh=mesh,
        in_specs=placed,
        out_specs=(
            P("section", None, "expert", "dp", None),
            P("section", None, "expert", "dp", None),
            P("section", None, ("expert", "dp")),
            P("section", None, ("expert", "dp")),
            P("section", ("expert", "dp"), None),
            P("section", ("expert", "dp"), None),
            P("section", ("expert", "dp"), None),
            P("section", ("expert", "dp"), None),
            P("section", ("expert", "dp"), None),
            P("section", ("expert", "dp"), None),
            P("section", "expert", None, "dp"),
            P("section", "expert", "dp", None),
            P("section", None),
        ),
        check_vma=False,
    )
```

profile of v0, /device:TPU:0, one launch (start us, length us, event | category | flops | bytes accessed | tf_op | source)
XLA Modules:
  0.0 920.5 jit_solution(6075323646682145550)
XLA Ops:
  0.7 5.8 all-to-all-start.15
  6.8 4.2 all-to-all-done.15
  11.0 12.0 %all_to_all.275 = bf16[2,1024,1024]{2,1,0:T(8,128)(2,1)} all-to-all(bf16[2,1024,1024]{2,1,0:T(8,128)(2,1)} %bitcast.414), channel_id=1, replica_groups=mesh['section'=2,'expert'=4,'dp'=4] {'section'}, dimensions={0} | all-to-all | bytes 8388608 | tf_op jit(solution)/shard_map/all_to_all | solution.py:48
  23.6 7.3 all-to-all-start
  31.9 6.3 all-to-all-done
  38.3 14.2 %all_to_all.276 = bf16[4,64,768]{2,1,0:T(8,128)(2,1)S(1)} all-to-all(bf16[4,64,768]{2,1,0:T(8,128)(2,1)S(1)} %reshape.704), channel_id=1, replica_groups=mesh['section'=2,'expert'=4,'dp'=4] {'dp'}, dimensions={0} | all-to-all | bytes 786432 | tf_op jit(solution)/shard_map/all_to_all | solution.py:48
  59.1 11.8 %all-to-all-done.5 = bf16[4,64,1024]{2,1,0:T(8,128)(2,1)S(1)} async-done(((bf16[4,64,1024]{2,1,0:T(8,128)(2,1)}), bf16[4,64,1024]{2,1,0:T(8,128)(2,1)S(1)}, u32[]{:S(2)}, u32[]{:S(2)}) %all-to-all-start.5) | async-done | bytes 524320 | tf_op jit(solution)/shard_map/all_to_all | solution.py:48
  77.9 16.7 %all_gather.18 = bf16[256,1024]{1,0:T(8,128)(2,1)} all-gather(bf16[64,1024]{1,0:T(8,128)(2,1)S(1)} %fusion.147), channel_id=1, replica_groups=mesh['section'=2,'expert'=4,'dp'=4] {'dp'}, dimensions={0}, use_global_device_ids=true | all-gather | bytes 655360 | tf_op jit(solution)/shard_map/all_gather | solution.py:57
  94.8 6.3 all_to_all.277
  115.1 5.2 all-to-all-done.8
  120.3 8.4 all_to_all.278
  130.3 4.3 all-to-all-start.6
  135.7 22.0 %all-to-all-done.6 = bf16[4,256,1024]{2,1,0:T(8,128)(2,1)S(1)} async-done(((bf16[4,256,1024]{2,1,0:T(8,128)(2,1)}), bf16[4,256,1024]{2,1,0:T(8,128)(2,1)S(1)}, u32[]{:S(2)}, u32[]{:S(2)}) %all-to-all-start.6) | async-done | bytes 2097184 | tf_op jit(solution)/shard_map/all_to_all | solution.py:48
  158.2 8.2 all_to_all.279
  177.3 15.9 %all_gather.19 = bf16[256,1024]{1,0:T(8,128)(2,1)S(1)} all-gather(bf16[64,1024]{1,0:T(8,128)(2,1)S(1)} %add_convert_fusion.3), channel_id=1, replica_groups=mesh['section'=2,'expert'=4,'dp'=4] {'dp'}, dimensions={0}, use_global_device_ids=true | all-gather | bytes 655360 | tf_op jit(solution)/shard_map/all_gather | solution.py:57
  198.7 8.1 all_to_all.280
  211.4 9.7 %all-to-all-done.13 = bf16[8,40,1024]{2,1,0:T(8,128)(2,1)S(1)} async-done(((bf16[8,40,1024]{2,1,0:T(8,128)(2,1)}), bf16[8,40,1024]{2,1,0:T(8,128)(2,1)S(1)}, u32[]{:S(2)}, u32[]{:S(2)}) %all-to-all-start.13) | async-done | bytes 655392 | tf_op jit(solution)/shard_map/all_to_all | solution.py:48
  232.5 19.4 %all-to-all-done.11 = bf16[4,256,1024]{2,1,0:T(8,128)(2,1)S(1)} async-done(((bf16[4,256,1024]{2,1,0:T(8,128)(2,1)}), bf16[4,256,1024]{2,1,0:T(8,128)(2,1)S(1)}, u32[]{:S(2)}, u32[]{:S(2)}) %all-to-all-start.11) | async-done | bytes 2097184 | tf_op jit(solution)/shard_map/all_to_all | solution.py:48
  254.6 6.0 all-to-all-start.12
  271.2 8.0 all-to-all-done.16
  284.7 14.9 %all-to-all-done.17 = bf16[4,64,1024]{2,1,0:T(8,128)(2,1)S(1)} async-done(((bf16[4,64,1024]{2,1,0:T(8,128)(2,1)}), bf16[4,64,1024]{2,1,0:T(8,128)(2,1)S(1)}, u32[]{:S(2)}, u32[]{:S(2)}) %all-to-all-start.17) | async-done | bytes 524320 | tf_op jit(solution)/shard_map/all_to_all | solution.py:48
  300.1 16.3 %all_gather.20 = bf16[256,1024]{1,0:T(8,128)(2,1)} all-gather(bf16[64,1024]{1,0:T(8,128)(2,1)S(1)} %fusion.144), channel_id=1, replica_groups=mesh['section'=2,'expert'=4,'dp'=4] {'dp'}, dimensions={0}, use_global_device_ids=true | all-gather | bytes 655360 | tf_op jit(solution)/shard_map/all_gather | solution.py:57
  325.6 5.8 all-to-all-done.18
  335.3 15.7 %all_gather.21 = bf16[256,1024]{1,0:T(8,128)(2,1)S(1)} all-gather(bf16[64,1024]{1,0:T(8,128)(2,1)S(1)} %add_convert_fusion.2), channel_id=1, replica_groups=mesh['section'=2,'expert'=4,'dp'=4] {'dp'}, dimensions={0}, use_global_device_ids=true | all-gather | bytes 655360 | tf_op jit(solution)/shard_map/all_gather | solution.py:57
  355.7 16.0 %all-gather = bf16[1,1,256,1024]{3,2,1,0:T(8,128)(2,1)S(1)} all-gather(bf16[1,1,64,1024]{3,2,1,0:T(8,128)(2,1)S(1)} %constant_dynamic-slice_fusion.16), channel_id=2, replica_groups=mesh['section'=2,'expert'=4,'dp'=4] {'dp'}, dimensions={2}, use_global_device_ids=true | all-gather | bytes 655360 | tf_op jit(solution)/shard_map/all_gather | solution.py:57
  386.5 6.9 all-to-all-done.20
  406.9 7.9 all-to-all-done.23
  429.0 5.5 all-to-all-done.24
  443.0 10.2 %all-to-all-done.21 = bf16[4,64,1024]{2,1,0:T(8,128)(2,1)S(1)} async-done(((bf16[4,64,1024]{2,1,0:T(8,128)(2,1)}), bf16[4,64,1024]{2,1,0:T(8,128)(2,1)S(1)}, u32[]{:S(2)}, u32[]{:S(2)}) %all-to-all-start.21) | async-done | bytes 524320 | tf_op jit(solution)/shard_map/all_to_all | solution.py:48
  463.8 7.2 all-to-all-done.25
  490.7 5.0 convolution_bitcast_fusion
  497.9 7.3 all-to-all-done.47
  505.1 4.4 all-to-all-start.51
  514.5 8.8 all-to-all-done.51
  523.3 5.0 all-to-all-start.27
  528.3 4.6 convolution_bitcast_fusion.2
  544.7 15.5 %all_gather.23 = bf16[256,1024]{1,0:T(8,128)(2,1)S(1)} all-gather(bf16[64,1024]{1,0:T(8,128)(2,1)S(1)} %get-tuple-element.132), channel_id=1, replica_groups=mesh['section'=2,'expert'=4,'dp'=4] {'dp'}, dimensions={0}, use_global_device_ids=true | all-gather | bytes 655360 | tf_op jit(solution)/shard_map/all_gather | solution.py:57
  571.1 4.6 all-to-all-done.28
  588.3 7.2 all-to-all-done.29
  602.4 10.9 %all-to-all-done.42 = bf16[4,256,512]{2,1,0:T(8,128)(2,1)S(1)} async-done(((bf16[4,256,512]{2,1,0:T(8,128)(2,1)}), bf16[4,256,512]{2,1,0:T(8,128)(2,1)S(1)}, u32[]{:S(2)}, u32[]{:S(2)}) %all-to-all-start.42) | async-done | bytes 1048608 | tf_op jit(solution)/shard_map/all_to_all | solution.py:48
  613.3 5.2 all-to-all-start.30
  639.9 5.2 all-to-all-start.48
  646.2 8.5 all-to-all-done.48
  654.7 4.6 all_to_all.281
  666.3 10.7 %all-to-all-done.45 = bf16[4,256,512]{2,1,0:T(8,128)(2,1)S(1)} async-done(((bf16[4,256,512]{2,1,0:T(8,128)(2,1)}), bf16[4,256,512]{2,1,0:T(8,128)(2,1)S(1)}, u32[]{:S(2)}, u32[]{:S(2)}) %all-to-all-start.45) | async-done | bytes 1048608 | tf_op jit(solution)/shard_map/all_to_all | solution.py:48
  680.4 8.5 pad_maximum_fusion
  695.5 4.2 pad_maximum_fusion.1
  709.6 9.9 %all-to-all-done.50 = bf16[4,256,512]{2,1,0:T(8,128)(2,1)S(1)} async-done(((bf16[4,256,512]{2,1,0:T(8,128)(2,1)}), bf16[4,256,512]{2,1,0:T(8,128)(2,1)S(1)}, u32[]{:S(2)}, u32[]{:S(2)}) %all-to-all-start.50) | async-done | bytes 1048608 | tf_op jit(solution)/shard_map/all_to_all | solution.py:48
  719.5 4.8 all-to-all-start.46
  742.4 6.4 all-to-all-done.32
  759.2 18.5 %all_to_all.282 = f32[2,1024,1024]{2,1,0:T(8,128)} all-to-all(f32[2,1024,1024]{2,1,0:T(8,128)} %pad_maximum_fusion), channel_id=1, replica_groups=mesh['section'=2,'expert'=4,'dp'=4] {'section'}, dimensions={0} | all-to-all | bytes 16777216 | tf_op jit(solution)/shard_map/all_to_all | solution.py:48
  777.6 18.5 %all_to_all.283 = f32[2,1024,1024]{2,1,0:T(8,128)} all-to-all(f32[2,1024,1024]{2,1,0:T(8,128)} %pad_maximum_fusion.1), channel_id=1, replica_groups=mesh['section'=2,'expert'=4,'dp'=4] {'section'}, dimensions={0} | all-to-all | bytes 16777216 | tf_op jit(solution)/shard_map/all_to_all | solution.py:48
  796.2 5.5 all_to_all.284
  801.7 4.6 all_to_all.285
  806.3 4.3 all-to-all-start.40
  813.4 11.4 %all-to-all-done.40 = bf16[4,256,512]{2,1,0:T(8,128)(2,1)} async-done(((bf16[4,256,512]{2,1,0:T(8,128)(2,1)}), bf16[4,256,512]{2,1,0:T(8,128)(2,1)}, u32[]{:S(2)}, u32[]{:S(2)}) %all-to-all-start.40) | async-done | bytes 1048608 | tf_op jit(solution)/shard_map/all_to_all | solution.py:48
  824.8 4.9 all_to_all.286
  829.7 4.2 all-to-all-start.35
  838.0 7.4 all-to-all-done.35
  851.5 5.8 all-to-all-done.34
  861.4 8.2 all-to-all-done.41
  885.0 5.0 all-to-all-start.36
  898.8 4.4 all_to_all.288
  907.6 9.0 copy.271
  (719 shorter events, 357.4 us)
Async XLA Ops:
  0.6 58.2 %copy-start = (s32[2,1,256]{2,1,0:T(1,128)S(1)}, s32[2,1,256]{2,1,0:T(1,128)}, u32[]{:S(2)}) copy-start(s32[2,1,256]{2,1,0:T(1,128)} %param.16) | copy-start | bytes 6148
  0.7 10.3 %all-to-all-start.15 = ((bf16[2,1024,1024]{2,1,0:T(8,128)(2,1)}), bf16[2,1024,1024]{2,1,0:T(8,128)(2,1)}, u32[]{:S(2)}, u32[]{:S(2)}) async-start(bf16[2,1024,1024]{2,1,0:T(8,128)(2,1)} %bitcast.413), calls=%async_computation.15 | async-start | bytes 8388608 | tf_op jit(solution)/shard_map/all_to_all | solution.py:48
  23.6 14.6 %all-to-all-start = ((bf16[32,8,128]{2,1,0:T(8,128)(2,1)}), bf16[32,8,128]{2,1,0:T(8,128)(2,1)S(1)}, u32[]{:S(2)}, u32[]{:S(2)}) async-start(bf16[32,8,128]{2,1,0:T(8,128)(2,1)} %broadcast_in_dim.101), calls=%async_computation | async-start | bytes 131072 | tf_op jit(solution)/shard_map/all_to_all | solution.py:48
  53.3 17.6 %all-to-all-start.5 = ((bf16[4,64,1024]{2,1,0:T(8,128)(2,1)}), bf16[4,64,1024]{2,1,0:T(8,128)(2,1)S(1)}, u32[]{:S(2)}, u32[]{:S(2)}) async-start(bf16[4,64,1024]{2,1,0:T(8,128)(2,1)} %broadcast_in_dim.108), calls=%async_computation.5 | async-start | bytes 1048576 | tf_op jit(solution)/shard_map/all_to_all | solution.py:48
  72.2 22.3 %all-to-all-start.2 = ((bf16[4,4,64,768]{3,2,1,0:T(8,128)(2,1)}), bf16[4,4,64,768]{3,2,1,0:T(8,128)(2,1)S(1)}, u32[]{:S(2)}, u32[]{:S(2)}) async-start(bf16[4,4,64,768]{3,2,1,0:T(8,128)(2,1)} %broadcast_in_dim.102), calls=%async_computation.2 | async-start | bytes 3145728 | tf_op jit(solution)/shard_map/all_to_all | solution.py:48
  101.0 19.3 %all-to-all-start.8 = ((bf16[4,64,1024]{2,1,0:T(8,128)(2,1)}), bf16[4,64,1024]{2,1,0:T(8,128)(2,1)}, u32[]{:S(2)}, u32[]{:S(2)}) async-start(bf16[4,64,1024]{2,1,0:T(8,128)(2,1)} %reshape.711), calls=%async_computation.8 | async-start | bytes 1048576 | tf_op jit(solution)/shard_map/all_to_all | solution.py:48
  130.3 27.4 %all-to-all-start.6 = ((bf16[4,256,1024]{2,1,0:T(8,128)(2,1)}), bf16[4,256,1024]{2,1,0:T(8,128)(2,1)S(1)}, u32[]{:S(2)}, u32[]{:S(2)}) async-start(bf16[4,256,1024]{2,1,0:T(8,128)(2,1)} %broadcast_in_dim.110), calls=%async_computation.6 | async-start | bytes 4194304 | tf_op jit(solution)/shard_map/all_to_all | solution.py:48
  134.8 133.7 %copy-start.85 = (s32[256]{0:T(256)}, s32[256]{0:T(256)S(1)}, u32[]{:S(2)}) copy-start(s32[256]{0:T(256)S(1)} %eq.127) | copy-start | bytes 3076
  169.0 29.2 %all-to-all-start.9 = ((bf16[4,4,64,1024]{3,2,1,0:T(8,128)(2,1)}), bf16[4,4,64,1024]{3,2,1,0:T(8,128)(2,1)S(1)}, u32[]{:S(2)}, u32[]{:S(2)}) async-start(bf16[4,4,64,1024]{3,2,1,0:T(8,128)(2,1)} %broadcast_in_dim.113), calls=%async_computation.9 | async-start | bytes 4194304 | tf_op jit(solution)/shard_map/all_to_all | solution.py:48
  206.9 14.3 %all-to-all-start.13 = ((bf16[8,40,1024]{2,1,0:T(8,128)(2,1)}), bf16[8,40,1024]{2,1,0:T(8,128)(2,1)S(1)}, u32[]{:S(2)}, u32[]{:S(2)}) async-start(bf16[8,40,1024]{2,1,0:T(8,128)(2,1)} %bitcast.31), calls=%async_computation.13 | async-start | bytes 1310720 | tf_op jit(solution)/shard_map/all_to_all | solution.py:48
  222.7 29.2 %all-to-all-start.11 = ((bf16[4,256,1024]{2,1,0:T(8,128)(2,1)}), bf16[4,256,1024]{2,1,0:T(8,128)(2,1)S(1)}, u32[]{:S(2)}, u32[]{:S(2)}) async-start(bf16[4,256,1024]{2,1,0:T(8,128)(2,1)} %broadcast_in_dim.224), calls=%async_computation.11 | async-start | bytes 4194304 | tf_op jit(solution)/shard_map/all_to_all | solution.py:48
  226.6 42.0 %copy-start.70 = (f32[256,10]{0,1:T(8,128)}, f32[256,10]{0,1:T(8,128)S(1)}, u32[]{:S(2)}) copy-start(f32[256,10]{0,1:T(8,128)S(1)} %fusion.185) | copy-start | bytes 30724
  226.7 41.9 %copy-start.110 = (f32[256]{0:T(256)}, f32[256]{0:T(256)S(1)}, u32[]{:S(2)}) copy-start(f32[256]{0:T(256)S(1)} %slice_reduce_fusion.9) | copy-start | bytes 3076
  226.7 41.9 %copy-start.134 = (f32[256]{0:T(256)}, f32[256]{0:T(256)S(1)}, u32[]{:S(2)}) copy-start(f32[256]{0:T(256)S(1)} %fusion.194) | copy-start | bytes 3076
  226.8 41.9 %copy-start.124 = (f32[256,2]{0,1:T(2,128)}, f32[256,2]{0,1:T(2,128)S(1)}, u32[]{:S(2)}) copy-start(f32[256,2]{0,1:T(2,128)S(1)} %broadcast_divide_fusion.3) | copy-start | bytes 6148
  254.6 10.4 %all-to-all-start.12 = ((bf16[2,1024,1024]{2,1,0:T(8,128)(2,1)}), bf16[2,1024,1024]{2,1,0:T(8,128)(2,1)}, u32[]{:S(2)}, u32[]{:S(2)}) async-start(bf16[2,1024,1024]{2,1,0:T(8,128)(2,1)} %broadcast_in_dim.226), calls=%async_computation.12 | async-start | bytes 8388608 | tf_op jit(solution)/shard_map/all_to_all | solution.py:48
  265.0 14.1 %all-to-all-start.16 = ((bf16[8,40,1024]{2,1,0:T(8,128)(2,1)}), bf16[8,40,1024]{2,1,0:T(8,128)(2,1)S(1)}, u32[]{:S(2)}, u32[]{:S(2)}) async-start(bf16[8,40,1024]{2,1,0:T(8,128)(2,1)} %bitcast.37), calls=%async_computation.16 | async-start | bytes 1310720 | tf_op jit(solution)/shard_map/all_to_all | solution.py:48
  280.9 18.7 %all-to-all-start.17 = ((bf16[4,64,1024]{2,1,0:T(8,128)(2,1)}), bf16[4,64,1024]{2,1,0:T(8,128)(2,1)S(1)}, u32[]{:S(2)}, u32[]{:S(2)}) async-start(bf16[4,64,1024]{2,1,0:T(8,128)(2,1)} %bitcast.39), calls=%async_computation.17 | async-start | bytes 1048576 | tf_op jit(solution)/shard_map/all_to_all | solution.py:48
  322.2 9.2 %all-to-all-start.18 = ((bf16[4,64,256]{2,1,0:T(8,128)(2,1)}), bf16[4,64,256]{2,1,0:T(8,128)(2,1)S(1)}, u32[]{:S(2)}, u32[]{:S(2)}) async-start(bf16[4,64,256]{2,1,0:T(8,128)(2,1)} %copy.233), calls=%async_computation.18 | async-start | bytes 262144 | tf_op jit(solution)/shard_map/all_to_all | solution.py:48
  325.6 73.4 %copy-start.103 = (s32[256]{0:T(256)}, s32[256]{0:T(256)S(1)}, u32[]{:S(2)}) copy-start(s32[256]{0:T(256)S(1)} %add_add_fusion.6) | copy-start | bytes 3076
  352.2 19.9 %all-to-all-start.19 = ((bf16[8,40,1024]{2,1,0:T(8,128)(2,1)}), bf16[8,40,1024]{2,1,0:T(8,128)(2,1)S(1)}, u32[]{:S(2)}, u32[]{:S(2)}) async-start(bf16[8,40,1024]{2,1,0:T(8,128)(2,1)} %bitcast.53), calls=%async_computation.19 | async-start | bytes 1310720 | tf_op jit(solution)/shard_map/all_to_all | solution.py:48
  378.7 14.7 %all-to-all-start.20 = ((bf16[8,40,1024]{2,1,0:T(8,128)(2,1)}), bf16[8,40,1024]{2,1,0:T(8,128)(2,1)S(1)}, u32[]{:S(2)}, u32[]{:S(2)}) async-start(bf16[8,40,1024]{2,1,0:T(8,128)(2,1)} %bitcast.57), calls=%async_computation.20 | async-start | bytes 1310720 | tf_op jit(solution)/shard_map/all_to_all | solution.py:48
  400.3 14.5 %all-to-all-start.23 = ((bf16[8,40,1024]{2,1,0:T(8,128)(2,1)}), bf16[8,40,1024]{2,1,0:T(8,128)(2,1)S(1)}, u32[]{:S(2)}, u32[]{:S(2)}) async-start(bf16[8,40,1024]{2,1,0:T(8,128)(2,1)} %bitcast.69), calls=%async_computation.23 | async-start | bytes 1310720 | tf_op jit(solution)/shard_map/all_to_all | solution.py:48
  420.4 14.1 %all-to-all-start.24 = ((bf16[8,40,1024]{2,1,0:T(8,128)(2,1)}), bf16[8,40,1024]{2,1,0:T(8,128)(2,1)S(1)}, u32[]{:S(2)}, u32[]{:S(2)}) async-start(bf16[8,40,1024]{2,1,0:T(8,128)(2,1)} %bitcast.454), calls=%async_computation.24 | async-start | bytes 1310720 | tf_op jit(solution)/shard_map/all_to_all | solution.py:48
  434.5 18.7 %all-to-all-start.21 = ((bf16[4,64,1024]{2,1,0:T(8,128)(2,1)}), bf16[4,64,1024]{2,1,0:T(8,128)(2,1)S(1)}, u32[]{:S(2)}, u32[]{:S(2)}) async-start(bf16[4,64,1024]{2,1,0:T(8,128)(2,1)} %bitcast.59), calls=%async_computation.21 | async-start | bytes 1048576 | tf_op jit(solution)/shard_map/all_to_all | solution.py:48
  453.2 17.7 %all-to-all-start.25 = ((bf16[4,64,1024]{2,1,0:T(8,128)(2,1)}), bf16[4,64,1024]{2,1,0:T(8,128)(2,1)S(1)}, u32[]{:S(2)}, u32[]{:S(2)}) async-start(bf16[4,64,1024]{2,1,0:T(8,128)(2,1)} %bitcast.430), calls=%async_computation.25 | async-start | bytes 1048576 | tf_op jit(solution)/shard_map/all_to_all | solution.py:48
  456.7 173.9 %collective-permute-start.8 = (bf16[256,1024]{1,0:T(8,128)(2,1)S(1)}, bf16[256,1024]{1,0:T(8,128)(2,1)}, u32[]{:S(2)}, u32[]{:S(2)}) collective-permute-start(bf16[256,1024]{1,0:T(8,128)(2,1)S(1)} %all_gather.19), channel_id=1, source_target_pairs={{0,16},{16,0},{1,17},{17,1},{2,18},{18,2},{3,19},{19,3},{4,20},{20... | collective-permute-start | bytes 1572872 | tf_op jit(solution)/shard_map/ppermute | solution.py:71
  456.8 23.9 %collective-permute-start.10 = (bf16[256,1024]{1,0:T(8,128)(2,1)S(1)}, bf16[256,1024]{1,0:T(8,128)(2,1)}, u32[]{:S(2)}, u32[]{:S(2)}) collective-permute-start(bf16[256,1024]{1,0:T(8,128)(2,1)S(1)} %all_gather.21), channel_id=1, source_target_pairs={{0,16},{16,0},{1,17},{17,1},{2,18},{18,2},{3,19},{19,3},{4,20},{20... | collective-permute-start | bytes 1572872 | tf_op jit(solution)/shard_map/ppermute | solution.py:71
  457.3 26.9 %collective-permute-start.14 = (bf16[256,1024]{1,0:T(8,128)(2,1)}, bf16[256,1024]{1,0:T(8,128)(2,1)}, u32[]{:S(2)}, u32[]{:S(2)}) collective-permute-start(bf16[256,1024]{1,0:T(8,128)(2,1)} %get-tuple-element.191), channel_id=1, source_target_pairs={{0,16},{16,0},{1,17},{17,1},{2,18},{18,2},{3,19},{19,3},{4,20},{20... | collective-permute-start | bytes 1572872 | tf_op jit(solution)/shard_map/ppermute | solution.py:71
  462.3 18.4 %collective-permute-start.11 = (bf16[256,512]{1,0:T(8,128)(2,1)}, bf16[256,512]{1,0:T(8,128)(2,1)}, u32[]{:S(2)}, u32[]{:S(2)}) collective-permute-start(bf16[256,512]{1,0:T(8,128)(2,1)} %get-tuple-element.151), channel_id=1, source_target_pairs={{0,16},{16,0},{1,17},{17,1},{2,18},{18,2},{3,19},{19,3},{4,20},{20... | collective-permute-start | bytes 786440 | tf_op jit(solution)/shard_map/ppermute | solution.py:71
  463.6 20.7 %collective-permute-start.15 = (bf16[256,512]{1,0:T(8,128)(2,1)}, bf16[256,512]{1,0:T(8,128)(2,1)}, u32[]{:S(2)}, u32[]{:S(2)}) collective-permute-start(bf16[256,512]{1,0:T(8,128)(2,1)} %get-tuple-element.147), channel_id=1, source_target_pairs={{0,16},{16,0},{1,17},{17,1},{2,18},{18,2},{3,19},{19,3},{4,20},{20... | collective-permute-start | bytes 786440 | tf_op jit(solution)/shard_map/ppermute | solution.py:71
  477.3 9.8 %all-to-all-start.26 = ((bf16[4,64,256]{2,1,0:T(8,128)(2,1)}), bf16[4,64,256]{2,1,0:T(8,128)(2,1)S(1)}, u32[]{:S(2)}, u32[]{:S(2)}) async-start(bf16[4,64,256]{2,1,0:T(8,128)(2,1)} %bitcast.402), calls=%async_computation.26 | async-start | bytes 262144 | tf_op jit(solution)/shard_map/all_to_all | solution.py:48
  480.7 152.8 %collective-permute-start.12 = (bf16[256,1024]{1,0:T(8,128)(2,1)}, bf16[256,1024]{1,0:T(8,128)(2,1)}, u32[]{:S(2)}, u32[]{:S(2)}) collective-permute-start(bf16[256,1024]{1,0:T(8,128)(2,1)} %get-tuple-element.185), channel_id=1, source_target_pairs={{0,16},{16,0},{1,17},{17,1},{2,18},{18,2},{3,19},{19,3},{4,20},{20... | collective-permute-start | bytes 1572872 | tf_op jit(solution)/shard_map/ppermute | solution.py:71
  480.8 144.0 %collective-permute-start.2 = (bf16[256,1024]{1,0:T(8,128)(2,1)}, bf16[256,1024]{1,0:T(8,128)(2,1)}, u32[]{:S(2)}, u32[]{:S(2)}) collective-permute-start(bf16[256,1024]{1,0:T(8,128)(2,1)} %all_gather.20), channel_id=1, source_target_pairs={{0,16},{16,0},{1,17},{17,1},{2,18},{18,2},{3,19},{19,3},{4,20},{20... | collective-permute-start | bytes 1572872 | tf_op jit(solution)/shard_map/ppermute | solution.py:71
  484.2 52.7 %collective-permute-start.6 = (bf16[64,1024]{1,0:T(8,128)(2,1)}, bf16[64,1024]{1,0:T(8,128)(2,1)}, u32[]{:S(2)}, u32[]{:S(2)}) collective-permute-start(bf16[64,1024]{1,0:T(8,128)(2,1)} %bitcast.174), channel_id=1, source_target_pairs={{0,16},{16,0},{1,17},{17,1},{2,18},{18,2},{3,19},{19,3},{4,20},{20... | collective-permute-start | bytes 393224 | tf_op jit(solution)/shard_map/ppermute | solution.py:71
  487.1 18.0 %all-to-all-start.47 = ((bf16[4,256,512]{2,1,0:T(8,128)(2,1)}), bf16[4,256,512]{2,1,0:T(8,128)(2,1)S(1)}, u32[]{:S(2)}, u32[]{:S(2)}) async-start(bf16[4,256,512]{2,1,0:T(8,128)(2,1)} %bitcast.436), calls=%async_computation.47 | async-start | bytes 2097152 | tf_op jit(solution)/shard_map/all_to_all | solution.py:48
  505.1 18.2 %all-to-all-start.51 = ((bf16[4,256,512]{2,1,0:T(8,128)(2,1)}), bf16[4,256,512]{2,1,0:T(8,128)(2,1)}, u32[]{:S(2)}, u32[]{:S(2)}) async-start(bf16[4,256,512]{2,1,0:T(8,128)(2,1)} %bitcast.435), calls=%async_computation.51 | async-start | bytes 2097152 | tf_op jit(solution)/shard_map/all_to_all | solution.py:48
  523.3 18.7 %all-to-all-start.27 = ((bf16[4,64,1024]{2,1,0:T(8,128)(2,1)}), bf16[4,64,1024]{2,1,0:T(8,128)(2,1)S(1)}, u32[]{:S(2)}, u32[]{:S(2)}) async-start(bf16[4,64,1024]{2,1,0:T(8,128)(2,1)} %bitcast.457), calls=%async_computation.27 | async-start | bytes 1048576 | tf_op jit(solution)/shard_map/all_to_all | solution.py:48
  536.1 1.3 collective-permute-start.7
  540.7 84.1 %collective-permute-start.3 = (bf16[256,384]{0,1:T(8,128)(2,1)}, bf16[256,384]{0,1:T(8,128)(2,1)}, u32[]{:S(2)}, u32[]{:S(2)}) collective-permute-start(bf16[256,384]{0,1:T(8,128)(2,1)} %get-tuple-element.157), channel_id=1, source_target_pairs={{0,16},{16,0},{1,17},{17,1},{2,18},{18,2},{3,19},{19,3},{4,20},{20... | collective-permute-start | bytes 589832 | tf_op jit(solution)/shard_map/ppermute | solution.py:71
  561.5 14.1 %all-to-all-start.28 = ((bf16[8,40,1024]{2,1,0:T(8,128)(2,1)}), bf16[8,40,1024]{2,1,0:T(8,128)(2,1)S(1)}, u32[]{:S(2)}, u32[]{:S(2)}) async-start(bf16[8,40,1024]{2,1,0:T(8,128)(2,1)} %bitcast.85), calls=%async_computation.28 | async-start | bytes 1310720 | tf_op jit(solution)/shard_map/all_to_all | solution.py:48
  570.7 60.0 %collective-permute-start.9 = (bf16[256,512]{1,0:T(8,128)(2,1)}, bf16[256,512]{1,0:T(8,128)(2,1)}, u32[]{:S(2)}, u32[]{:S(2)}) collective-permute-start(bf16[256,512]{1,0:T(8,128)(2,1)} %get-tuple-element.149), channel_id=1, source_target_pairs={{0,16},{16,0},{1,17},{17,1},{2,18},{18,2},{3,19},{19,3},{4,20},{20... | collective-permute-start | bytes 786440 | tf_op jit(solution)/shard_map/ppermute | solution.py:71
  581.3 14.1 %all-to-all-start.29 = ((bf16[8,40,1024]{2,1,0:T(8,128)(2,1)}), bf16[8,40,1024]{2,1,0:T(8,128)(2,1)S(1)}, u32[]{:S(2)}, u32[]{:S(2)}) async-start(bf16[8,40,1024]{2,1,0:T(8,128)(2,1)} %bitcast.87), calls=%async_computation.29 | async-start | bytes 1310720 | tf_op jit(solution)/shard_map/all_to_all | solution.py:48
  595.4 17.9 %all-to-all-start.42 = ((bf16[4,256,512]{2,1,0:T(8,128)(2,1)}), bf16[4,256,512]{2,1,0:T(8,128)(2,1)S(1)}, u32[]{:S(2)}, u32[]{:S(2)}) async-start(bf16[4,256,512]{2,1,0:T(8,128)(2,1)} %bitcast.122), calls=%async_computation.42 | async-start | bytes 2097152 | tf_op jit(solution)/shard_map/all_to_all | solution.py:48
  613.3 26.6 %all-to-all-start.30 = ((bf16[4,64,1024]{2,1,0:T(8,128)(2,1)}), bf16[4,64,1024]{2,1,0:T(8,128)(2,1)S(1)}, u32[]{:S(2)}, u32[]{:S(2)}) async-start(bf16[4,64,1024]{2,1,0:T(8,128)(2,1)} %bitcast.429), calls=%async_computation.30 | async-start | bytes 1048576 | tf_op jit(solution)/shard_map/all_to_all | solution.py:48
  624.8 127.6 %collective-permute-start = (bf16[256,1024]{1,0:T(8,128)(2,1)}, bf16[256,1024]{1,0:T(8,128)(2,1)}, u32[]{:S(2)}, u32[]{:S(2)}) collective-permute-start(bf16[256,1024]{1,0:T(8,128)(2,1)} %all_gather.18), channel_id=1, source_target_pairs={{0,16},{16,0},{1,17},{17,1},{2,18},{18,2},{3,19},{19,3},{4,20},{20... | collective-permute-start | bytes 1572872 | tf_op jit(solution)/shard_map/ppermute | solution.py:71
  624.9 8.6 collective-permute-start.13
  630.6 109.4 %collective-permute-start.4 = (bf16[64,1024]{1,0:T(8,128)(2,1)}, bf16[64,1024]{1,0:T(8,128)(2,1)}, u32[]{:S(2)}, u32[]{:S(2)}) collective-permute-start(bf16[64,1024]{1,0:T(8,128)(2,1)} %bitcast.172), channel_id=1, source_target_pairs={{0,16},{16,0},{1,17},{17,1},{2,18},{18,2},{3,19},{19,3},{4,20},{20... | collective-permute-start | bytes 393224 | tf_op jit(solution)/shard_map/ppermute | solution.py:71
  639.9 14.7 %all-to-all-start.48 = ((bf16[4,64,512]{2,1,0:T(8,128)(2,1)}), bf16[4,64,512]{2,1,0:T(8,128)(2,1)S(1)}, u32[]{:S(2)}, u32[]{:S(2)}) async-start(bf16[4,64,512]{2,1,0:T(8,128)(2,1)} %bitcast.130), calls=%async_computation.48 | async-start | bytes 524288 | tf_op jit(solution)/shard_map/all_to_all | solution.py:48
  659.3 17.7 %all-to-all-start.45 = ((bf16[4,256,512]{2,1,0:T(8,128)(2,1)}), bf16[4,256,512]{2,1,0:T(8,128)(2,1)S(1)}, u32[]{:S(2)}, u32[]{:S(2)}) async-start(bf16[4,256,512]{2,1,0:T(8,128)(2,1)} %bitcast.434), calls=%async_computation.45 | async-start | bytes 2097152 | tf_op jit(solution)/shard_map/all_to_all | solution.py:48
  677.0 11.9 %all-to-all-start.31 = ((bf16[4,64,256]{2,1,0:T(8,128)(2,1)}), bf16[4,64,256]{2,1,0:T(8,128)(2,1)S(1)}, u32[]{:S(2)}, u32[]{:S(2)}) async-start(bf16[4,64,256]{2,1,0:T(8,128)(2,1)} %bitcast.400), calls=%async_computation.31 | async-start | bytes 262144 | tf_op jit(solution)/shard_map/all_to_all | solution.py:48
  688.9 14.1 %all-to-all-start.37 = ((bf16[4,256,384]{2,1,0:T(8,128)(2,1)}), bf16[4,256,384]{2,1,0:T(8,128)(2,1)S(1)}, u32[]{:S(2)}, u32[]{:S(2)}) async-start(bf16[4,256,384]{2,1,0:T(8,128)(2,1)} %bitcast.444), calls=%async_computation.37 | async-start | bytes 1572864 | tf_op jit(solution)/shard_map/all_to_all | solution.py:48
  703.0 16.6 %all-to-all-start.50 = ((bf16[4,256,512]{2,1,0:T(8,128)(2,1)}), bf16[4,256,512]{2,1,0:T(8,128)(2,1)S(1)}, u32[]{:S(2)}, u32[]{:S(2)}) async-start(bf16[4,256,512]{2,1,0:T(8,128)(2,1)} %bitcast.433), calls=%async_computation.50 | async-start | bytes 2097152 | tf_op jit(solution)/shard_map/all_to_all | solution.py:48
  719.5 13.0 %all-to-all-start.46 = ((bf16[4,64,512]{2,1,0:T(8,128)(2,1)}), bf16[4,64,512]{2,1,0:T(8,128)(2,1)S(1)}, u32[]{:S(2)}, u32[]{:S(2)}) async-start(bf16[4,64,512]{2,1,0:T(8,128)(2,1)} %bitcast.127), calls=%async_computation.46 | async-start | bytes 524288 | tf_op jit(solution)/shard_map/all_to_all | solution.py:48
  732.5 16.3 %all-to-all-start.32 = ((bf16[4,64,1024]{2,1,0:T(8,128)(2,1)}), bf16[4,64,1024]{2,1,0:T(8,128)(2,1)}, u32[]{:S(2)}, u32[]{:S(2)}) async-start(bf16[4,64,1024]{2,1,0:T(8,128)(2,1)} %bitcast.456), calls=%async_computation.32 | async-start | bytes 1048576 | tf_op jit(solution)/shard_map/all_to_all | solution.py:48
  737.6 2.4 collective-permute-start.5
  738.5 13.9 %collective-permute-start.1 = (bf16[256,384]{0,1:T(8,128)(2,1)}, bf16[256,384]{0,1:T(8,128)(2,1)S(1)}, u32[]{:S(2)}, u32[]{:S(2)}) collective-permute-start(bf16[256,384]{0,1:T(8,128)(2,1)} %get-tuple-element.155), channel_id=1, source_target_pairs={{0,16},{16,0},{1,17},{17,1},{2,18},{18,2},{3,19},{19,3},{4,20},{20... | collective-permute-start | bytes 589832 | tf_op jit(solution)/shard_map/ppermute | solution.py:71
  748.8 10.4 %all-to-all-start.43 = ((bf16[4,64,512]{2,1,0:T(8,128)(2,1)}), bf16[4,64,512]{2,1,0:T(8,128)(2,1)S(1)}, u32[]{:S(2)}, u32[]{:S(2)}) async-start(bf16[4,64,512]{2,1,0:T(8,128)(2,1)} %bitcast.123), calls=%async_computation.43 | async-start | bytes 524288 | tf_op jit(solution)/shard_map/all_to_all | solution.py:48
  806.3 18.5 %all-to-all-start.40 = ((bf16[4,256,512]{2,1,0:T(8,128)(2,1)}), bf16[4,256,512]{2,1,0:T(8,128)(2,1)}, u32[]{:S(2)}, u32[]{:S(2)}) async-start(bf16[4,256,512]{2,1,0:T(8,128)(2,1)} %bitcast.415), calls=%async_computation.40 | async-start | bytes 2097152 | tf_op jit(solution)/shard_map/all_to_all | solution.py:48
  829.7 15.7 %all-to-all-start.35 = ((bf16[4,256,384]{2,1,0:T(8,128)(2,1)}), bf16[4,256,384]{2,1,0:T(8,128)(2,1)}, u32[]{:S(2)}, u32[]{:S(2)}) async-start(bf16[4,256,384]{2,1,0:T(8,128)(2,1)} %bitcast.445), calls=%async_computation.35 | async-start | bytes 1572864 | tf_op jit(solution)/shard_map/all_to_all | solution.py:48
  845.4 11.8 %all-to-all-start.34 = ((f32[32,8,128]{2,1,0:T(8,128)}), f32[32,8,128]{2,1,0:T(8,128)S(1)}, u32[]{:S(2)}, u32[]{:S(2)}) async-start(f32[32,8,128]{2,1,0:T(8,128)} %bitcast.181), calls=%async_computation.34 | async-start | bytes 262144 | tf_op jit(solution)/shard_map/all_to_all | solution.py:48
  857.2 12.4 %all-to-all-start.41 = ((bf16[4,64,512]{2,1,0:T(8,128)(2,1)}), bf16[4,64,512]{2,1,0:T(8,128)(2,1)S(1)}, u32[]{:S(2)}, u32[]{:S(2)}) async-start(bf16[4,64,512]{2,1,0:T(8,128)(2,1)} %bitcast.120), calls=%async_computation.41 | async-start | bytes 524288 | tf_op jit(solution)/shard_map/all_to_all | solution.py:48
  869.6 11.4 %all-to-all-start.38 = ((bf16[4,64,384]{2,1,0:T(8,128)(2,1)}), bf16[4,64,384]{2,1,0:T(8,128)(2,1)}, u32[]{:S(2)}, u32[]{:S(2)}) async-start(bf16[4,64,384]{2,1,0:T(8,128)(2,1)} %bitcast.442), calls=%async_computation.38 | async-start | bytes 393216 | tf_op jit(solution)/shard_map/all_to_all | solution.py:48
  885.0 12.9 %all-to-all-start.36 = ((bf16[4,64,384]{2,1,0:T(8,128)(2,1)}), bf16[4,64,384]{2,1,0:T(8,128)(2,1)S(1)}, u32[]{:S(2)}, u32[]{:S(2)}) async-start(bf16[4,64,384]{2,1,0:T(8,128)(2,1)} %bitcast.112), calls=%async_computation.36 | async-start | bytes 393216 | tf_op jit(solution)/shard_map/all_to_all | solution.py:48
  (180 other events, 1782.0 us)
where the time goes:
time: 935 us; the launch traced here: 920 us
  waiting for transfers between devices  268 us (29%)
  blocking collectives  218 us (23%)
  starting transfers between devices  170 us (18%)
  matrix products  136 us (15%)
  local copies, waits for them, and re-layouts  70.2 us (8%)
  other arithmetic  53.8 us (6%)
    all_to_all x41, waiting for transfers between devices, exchange(): return lax.all_to_all(blocks, axes, split_axis=0, concat_axis=0, tiled=True)  268 us
    all_to_all x41, starting transfers between devices, exchange(): return lax.all_to_all(blocks, axes, split_axis=0, concat_axis=0, tiled=True)  167 us
    all_to_all x14, blocking collectives, exchange(): return lax.all_to_all(blocks, axes, split_axis=0, concat_axis=0, tiled=True)  122 us
    all_gather x6, blocking collectives, gather_rows(): return lax.all_gather(block, 'dp', axis=0, tiled=True)  96.1 us
    dot_general x18, matrix products, product_tn(): lax.dot_general(left_mat, right_mat, (((0,), (0,)), ((), ())), preferred_...  44.7 us
    dot_general x18, matrix products, product(): return jnp.dot(left_mat, right_mat, preferred_element_type=jnp.float32)  43.2 us
    dot_general x14, matrix products, product_nt(): lax.dot_general(left_mat, right_mat, (((1,), (1,)), ((), ())), preferred_...  33.4 us
    unnamed x378, local copies, waits for them, and re-layouts  20.9 us
  transfers between devices with their start and end apart: 57, of which 36 were waited for; matrix products, arithmetic and copies ran while one was open for 21% of the time, Pallas kernels for 0%

commit v1 on v0

--- a/solution.py
+++ b/solution.py
@@ -69,6 +69,44 @@
 
 def other_core(block):
     return lax.ppermute(block, "section", [(0, 1), (1, 0)])
+
+
+def place_blocks(blocks, index_of):
+    placed = jnp.zeros((len(blocks),) + blocks[0].shape, blocks[0].dtype)
+    for step, block in enumerate(blocks):
+        placed = lax.dynamic_update_index_in_dim(placed, block, index_of(step), 0)
+    return placed
+
+
+def permute_spread(block, axis):
+    count = lax.axis_size(axis)
+    place = lax.axis_index(axis)
+    blocks = [block]
+    for step in range(1, count):
+        route = [((i - step) % count, i) for i in range(count)]
+        blocks.append(lax.ppermute(block, axis, route))
+    return place_blocks(blocks, lambda step: (place - step) % count)
+
+
+def permute_parts(blocks, axis):
+    count = lax.axis_size(axis)
+    place = lax.axis_index(axis)
+    parts = [lax.dynamic_index_in_dim(blocks, place, 0, keepdims=False)]
+    for step in range(1, count):
+        route = [((i - step) % count, i) for i in range(count)]
+        part = lax.dynamic_index_in_dim(blocks, (place + step) % count, 0, keepdims=False)
+        parts.append(lax.ppermute(part, axis, route))
+    return parts
+
+
+def permute_exchange(blocks, axis):
+    count = lax.axis_size(axis)
+    place = lax.axis_index(axis)
+    return place_blocks(permute_parts(blocks, axis), lambda step: (place - step) % count)
+
+
+def permute_sum(blocks, axis):
+    return sum(part.astype(jnp.float32) for part in permute_parts(blocks, axis))
 
 
 def both_cores(block):
@@ -134,20 +172,36 @@
     routes_all = lax.dynamic_index_in_dim(routes_all, section_id, 2, keepdims=False)
     routes_all = routes_all.astype(jnp.int32)
 
+    on_first = section_id == 0
+
+    def by_layer(of_own_layer, of_other_layer):
+        return (
+            jnp.where(on_first, of_own_layer, of_other_layer),
+            jnp.where(on_first, of_other_layer, of_own_layer),
+        )
+
     qkv_cols = attn_qkv[0].reshape(weight_rows, 3, dp_size, head_width).transpose(2, 0, 1, 3)
     qkv_cols = exchange(qkv_cols.reshape(dp_size, weight_rows, 3 * head_width), "dp")
-    qkv_both = spread(spread(qkv_cols, "expert").reshape(width, 3 * head_width), "section")
-    proj_rows = exchange(
-        jnp.broadcast_to(attn_proj, (dp_size,) + attn_proj.shape[1:]), "dp"
-    ).reshape(dp_size * weight_rows, width)
-    proj_both = spread(spread(proj_rows, "expert").reshape(width, width), "section")
+    qkv_own = spread(qkv_cols, "expert").reshape(width, 3 * head_width)
+    qkv_both = by_layer(qkv_own, other_core(qkv_own))
+    proj_own = spread(permute_spread(attn_proj[0], "dp"), "expert").reshape(width, width)
+    proj_both = by_layer(proj_own, other_core(proj_own))
+    hidden_here = groups * hidden_rows
+    down_both = lax.all_gather(dense_down[0], HOMES, axis=0, tiled=True)
+    down_both = down_both.reshape(sections, hidden_here, width)
     up_cols = dense_up[0].reshape(weight_rows, groups, dp_size, hidden_rows).transpose(2, 0, 1, 3)
-    hidden_here = groups * hidden_rows
-    up_cols = exchange(up_cols.reshape(dp_size, weight_rows, hidden_here), "dp")
-    up_both = spread(spread(up_cols, "expert").reshape(width, hidden_here), "section")
-    down_both = spread(spread(dense_down[0], "expert").reshape(hidden_here, width), "section")
-    exp_up_both = exchange(expert_up[0], "section")
-    exp_down_both = exchange(expert_down[0], "section")
+    up_cols = permute_exchange(up_cols.reshape(dp_size, weight_rows, hidden_here), "dp")
+    up_cols = up_cols.reshape(dp_size * weight_rows, hidden_here)
+    up_both = lax.all_gather(up_cols, HOMES, axis=0, tiled=True)
+    up_both = up_both.reshape(sections, width, hidden_here)
+
+    def expert_of_layers(own_layer):
+        kept = lax.dynamic_index_in_dim(own_layer, section_id, 0, keepdims=False)
+        sent = lax.dynamic_index_in_dim(own_layer, 1 - section_id, 0, keepdims=False)
+        return by_layer(kept, other_core(sent))
+
+    exp_up_both = expert_of_layers(expert_up[0])
+    exp_down_both = expert_of_layers(expert_down[0])
 
     segments = lax.dynamic_index_in_dim(segment_ids[:, 0], section_id, 0, keepdims=False)
     places = jnp.arange(full_len, dtype=jnp.int32)
@@ -246,11 +300,11 @@
         }
         return layer_out, squares, record
 
-    def backward_layer(layer, grad_low, record):
+    def backward_layer(layer, grad_low, grad_seq, record):
         grad_out = grad_low.astype(jnp.float32)
         params = record["params"]
         coef, gate, table = record["coef"], record["gate"], record["table"]
-        grad_seq = gather_rows(grad_low).astype(jnp.float32)
+        grad_seq = grad_seq.astype(jnp.float32)
         d_dense = low(coef[:, 0:1] * grad_seq)
         d_expert = low(coef[:, 1:2] * gate * grad_seq)
         expert_grad_rows = to_experts(d_expert, table)
@@ -270,8 +324,12 @@
             product_nt(d_exp_hidden, exp_up_both[layer]), table
         )
         d_mid = scatter_rows(d_mid_part)
-        g_exp_up = product_tn(record["expert_rows"], d_exp_hidden)
-        g_exp_down = product_tn(record["exp_hidden_low"], expert_grad_rows)
+        expert_operands = (
+            record["expert_rows"],
+            d_exp_hidden,
+            record["exp_hidden_low"],
+            expert_grad_rows,
+        )
         mid_both = both_cores(record["mid_seq"])
         g_up = product_tn(mid_both, halves_for_cores(d_up, section_id))
         g_down = product_tn(
@@ -320,42 +378,62 @@
         )
 
         def over_expert(grad_mat):
-            blocks = low(grad_mat).reshape(groups, -1, grad_mat.shape[-1])
-            return sum_blocks(exchange(blocks, "expert"))
-
-        def over_dp(grad_mat):
-            blocks = low(grad_mat).reshape(dp_size, weight_rows, grad_mat.shape[-1])
-            return exchange(blocks, "dp")
-
+            return lax.psum_scatter(low(grad_mat), "expert", scatter_dimension=0, tiled=True)
+
+        def by_rows(grad_mat, count):
+            return low(grad_mat).reshape(count, -1, grad_mat.shape[-1])
+
+        if layer == 0:
+            qkv_sum = exchange(by_rows(sum_blocks(exchange(by_rows(g_qkv, groups), "expert")), dp_size), "dp")
+        else:
+            qkv_sum = permute_exchange(by_rows(over_expert(g_qkv), dp_size), "dp")
+        proj_sum = permute_sum(by_rows(g_proj, groups), "expert")
         reduced = {
-            "qkv": over_dp(over_expert(g_qkv)),
-            "proj": sum_blocks(over_dp(over_expert(g_proj))),
-            "up": over_dp(over_expert(g_up)),
+            "qkv": qkv_sum,
+            "proj": permute_sum(by_rows(proj_sum, dp_size), "dp"),
+            "up": permute_exchange(by_rows(over_expert(g_up), dp_size), "dp"),
             "down": over_expert(g_down),
         }
-        return d_resid + d_input_norm, reduced, small_grads, g_exp_up, g_exp_down
+        return d_resid + d_input_norm, reduced, small_grads, expert_operands
 
     own_input = lax.dynamic_index_in_dim(inputs[:, 0], section_id, 0, keepdims=False)
     own_grad = lax.dynamic_index_in_dim(cotangent[:, 0], section_id, 0, keepdims=False)
+    grad_seqs = lax.all_gather(cotangent[:, 0], "dp", axis=1, tiled=True)
+    own_grad_seq = lax.dynamic_index_in_dim(grad_seqs, section_id, 0, keepdims=False)
     out_zero, squares_zero, record_zero = forward_layer(0, own_input.astype(jnp.float32))
     out_zero = low(out_zero)
     out_one, squares_one, record_one = forward_layer(1, out_zero.astype(jnp.float32))
-    grad_one, reduced_one, small_one, exp_up_one, exp_down_one = backward_layer(
-        1, own_grad, record_one
-    )
-    grad_zero, reduced_zero, small_zero, exp_up_zero, exp_down_zero = backward_layer(
-        0, low(grad_one), record_zero
+    out_one = low(out_one)
+    grad_one, reduced_one, small_one, operands_one = backward_layer(
+        1, own_grad, own_grad_seq, record_one
+    )
+    grad_one_low = low(grad_one)
+    grad_zero, reduced_zero, small_zero, operands_zero = backward_layer(
+        0, grad_one_low, gather_rows(grad_one_low), record_zero
     )
 
     def to_owner(layer_zero, layer_one):
-        return exchange(jnp.stack([layer_zero, layer_one]), "section")
-
-    activations = to_owner(out_zero, low(out_one))
+        from_other_zero, from_other_one = other_core(layer_zero), other_core(layer_one)
+        return jnp.stack(
+            [
+                jnp.where(on_first, layer_zero, from_other_one),
+                jnp.where(on_first, from_other_zero, layer_one),
+            ]
+        )
+
+    activations = to_owner(out_zero, out_one)
     input_grads = to_owner(grad_zero, grad_one)
-    grad_exp_up = to_owner(exp_up_zero, exp_up_one)
-    grad_exp_down = to_owner(exp_down_zero, exp_down_one)
+    rows_in, d_hidden_in, hidden_in, d_rows_in = [
+        to_owner(of_zero, of_one) for of_zero, of_one in zip(operands_zero, operands_one)
+    ]
+    grad_exp_up = jnp.einsum(
+        "erd,erh->edh", rows_in, d_hidden_in, preferred_element_type=jnp.float32
+    )
+    grad_exp_down = jnp.einsum(
+        "erh,erd->ehd", hidden_in, d_rows_in, preferred_element_type=jnp.float32
+    )
     joined = {
-        name: to_owner(reduced_zero[name].astype(jnp.float32), reduced_one[name].astype(jnp.float32))
+        name: to_owner(reduced_zero[name], reduced_one[name]).astype(jnp.float32)
         for name in reduced_zero
     }
     grad_qkv = joined["qkv"].transpose(2, 1, 0, 3).reshape(weight_rows, dp_size, 3, head_width)

time: 935 us -> 729 us (0.78)
  blocking collectives: 218 us -> 91.1 us
  waiting for transfers between devices: 268 us -> 217 us
  starting transfers between devices: 170 us -> 141 us
  between operations: 4.01 us -> 18.9 us
    all_to_all x14 -> x1, blocking collectives: 122 us -> 14.2 us  [exchange(): return lax.all_to_all(blocks, axes, split_axis=0, concat_axis=0, tiled=True)]
    all_to_all x41 -> x24, waiting for transfers between devices: 268 us -> 160 us  [exchange(): return lax.all_to_all(blocks, axes, split_axis=0, concat_axis=0, tiled=True)]
    all_to_all x41 -> x24, starting transfers between devices: 167 us -> 95.1 us  [exchange(): return lax.all_to_all(blocks, axes, split_axis=0, concat_axis=0, tiled=True)]
    ppermute x0 -> x27, waiting for transfers between devices: none -> 51.4 us  [the longest x24 48.7 us: permute_parts(): parts.append(lax.ppermute(part, axis, route))]
    ppermute x0 -> x27, starting transfers between devices: none -> 30.8 us  [the longest x24 26.9 us: permute_parts(): parts.append(lax.ppermute(part, axis, route))]
    dot_general x18 -> x14, matrix products: 44.7 us -> 24.7 us  [product_tn(): lax.dot_general(left_mat, right_mat, (((0,), (0,)), ((), ())), preferred_...]
    all_gather x6 -> x5, blocking collectives: 96.1 us -> 76.8 us  [gather_rows(): return lax.all_gather(block, 'dp', axis=0, tiled=True)]
    squeeze x0 -> x10, local copies, waits for them, and re-layouts: none -> 12 us  [the longest x8 7.24 us: permute_parts(): lax.dynamic_index_in_dim(blocks, (place + step) % count, 0, keepdims=False)]
  transfers between devices with their start and end apart: 57 -> 99, of which waited for: 36 -> 38; matrix products, arithmetic and copies ran while one was open for 21% -> 30% of each run, Pallas kernels for 0% -> 0%
where the time goes in v1:
time: 729 us; the launch traced here: 717 us
  waiting for transfers between devices  217 us (30%)
  starting transfers between devices  141 us (19%)
  matrix products  127 us (17%)
  blocking collectives  91.1 us (12%)
  local copies, waits for them, and re-layouts  66.6 us (9%)
  other arithmetic  55.9 us (8%)
  between operations  18.9 us (3%)
    all_to_all x24, waiting for transfers between devices, exchange(): return lax.all_to_all(blocks, axes, split_axis=0, concat_axis=0, tiled=True)  160 us
    all_to_all x24, starting transfers between devices, exchange(): return lax.all_to_all(blocks, axes, split_axis=0, concat_axis=0, tiled=True)  95.1 us
    all_gather x5, blocking collectives, gather_rows(): return lax.all_gather(block, 'dp', axis=0, tiled=True)  76.8 us
    ppermute x24, waiting for transfers between devices, permute_parts(): parts.append(lax.ppermute(part, axis, route))  48.7 us
    dot_general x18, matrix products, product(): return jnp.dot(left_mat, right_mat, preferred_element_type=jnp.float32)  41.1 us
    dot_general x14, matrix products, product_nt(): lax.dot_general(left_mat, right_mat, (((1,), (1,)), ((), ())), preferred_...  36.5 us
    ppermute x24, starting transfers between devices, permute_parts(): parts.append(lax.ppermute(part, axis, route))  26.9 us
    dot_general x14, matrix products, product_tn(): lax.dot_general(left_mat, right_mat, (((0,), (0,)), ((), ())), preferred_...  24.7 us
  transfers between devices with their start and end apart: 99, of which 38 were waited for; matrix products, arithmetic and copies ran while one was open for 30% of the time, Pallas kernels for 0%

profile of v1, /device:TPU:0, one launch (start us, length us, event | category | flops | bytes accessed | tf_op | source)
XLA Modules:
  0.0 716.6 jit_solution(7024446216499199050)
XLA Ops:
  19.9 4.8 collective-permute-done.6
  26.4 6.6 all-to-all-start
  34.0 6.4 all-to-all-done
  40.4 14.2 %all_to_all.125 = bf16[4,64,768]{2,1,0:T(8,128)(2,1)S(1)} all-to-all(bf16[4,64,768]{2,1,0:T(8,128)(2,1)S(1)} %reshape.748), channel_id=1, replica_groups=mesh['section'=2,'expert'=4,'dp'=4] {'dp'}, dimensions={0} | all-to-all | bytes 786432 | tf_op jit(solution)/shard_map/all_to_all | solution.py:48
  55.9 3.6 all-to-all-start.2
  71.7 7.9 %all-to-all-done.2 = bf16[4,4,64,768]{3,2,1,0:T(8,128)(2,1)S(1)} async-done(((bf16[4,4,64,768]{3,2,1,0:T(8,128)(2,1)}), bf16[4,4,64,768]{3,2,1,0:T(8,128)(2,1)S(1)}, u32[]{:S(2)}, u32[]{:S(2)}) %all-to-all-start.2) | async-done | bytes 1572896 | tf_op jit(solution)/shard_map/all_to_all | solution.py:48
  81.4 3.6 all-to-all-start.4
  86.4 29.1 %all-to-all-done.4 = bf16[4,4,64,1024]{3,2,1,0:T(8,128)(2,1)S(1)} async-done(((bf16[4,4,64,1024]{3,2,1,0:T(8,128)(2,1)}), bf16[4,4,64,1024]{3,2,1,0:T(8,128)(2,1)S(1)}, u32[]{:S(2)}, u32[]{:S(2)}) %all-to-all-start.4) | async-done | bytes 2097184 | tf_op jit(solution)/shard_map/all_to_all | solution.py:48
  116.5 16.3 %all_gather.24 = bf16[256,1024]{1,0:T(8,128)(2,1)S(1)} all-gather(bf16[64,1024]{1,0:T(8,128)(2,1)S(1)} %fusion.156), channel_id=1, replica_groups=mesh['section'=2,'expert'=4,'dp'=4] {'dp'}, dimensions={0}, use_global_device_ids=true | all-gather | bytes 655360 | tf_op jit(solution)/shard_map/all_gather | solution.py:57
  138.6 4.7 all-to-all-start.3
  143.3 5.9 all-to-all-done.3
  152.3 15.3 %all_gather.25 = bf16[256,1024]{1,0:T(8,128)(2,1)S(1)} all-gather(bf16[64,1024]{1,0:T(8,128)(2,1)S(1)} %add_convert_fusion.3), channel_id=1, replica_groups=mesh['section'=2,'expert'=4,'dp'=4] {'dp'}, dimensions={0}, use_global_device_ids=true | all-gather | bytes 655360 | tf_op jit(solution)/shard_map/all_gather | solution.py:57
  168.8 3.5 all-to-all-start.5
  173.4 9.6 %all-to-all-done.5 = bf16[8,40,1024]{2,1,0:T(8,128)(2,1)S(1)} async-done(((bf16[8,40,1024]{2,1,0:T(8,128)(2,1)}), bf16[8,40,1024]{2,1,0:T(8,128)(2,1)S(1)}, u32[]{:S(2)}, u32[]{:S(2)}) %all-to-all-start.5) | async-done | bytes 655392 | tf_op jit(solution)/shard_map/all_to_all | solution.py:48
  182.9 4.0 multiply_convert_fusion.1
  188.8 4.6 all-to-all-start.6
  193.4 3.6 multiply_convert_fusion.5
  199.5 4.5 all-to-all-done.6
  205.7 3.5 all-to-all-start.7
  209.5 14.9 %all-to-all-done.7 = bf16[4,64,1024]{2,1,0:T(8,128)(2,1)S(1)} async-done(((bf16[4,64,1024]{2,1,0:T(8,128)(2,1)}), bf16[4,64,1024]{2,1,0:T(8,128)(2,1)S(1)}, u32[]{:S(2)}, u32[]{:S(2)}) %all-to-all-start.7) | async-done | bytes 524320 | tf_op jit(solution)/shard_map/all_to_all | solution.py:48
  225.6 15.5 %all_gather.28 = bf16[256,1024]{1,0:T(8,128)(2,1)S(1)} all-gather(bf16[64,1024]{1,0:T(8,128)(2,1)S(1)} %fusion.153), channel_id=1, replica_groups=mesh['section'=2,'expert'=4,'dp'=4] {'dp'}, dimensions={0}, use_global_device_ids=true | all-gather | bytes 655360 | tf_op jit(solution)/shard_map/all_gather | solution.py:57
  250.4 5.9 all-to-all-done.8
  259.4 14.7 %all_gather.29 = bf16[256,1024]{1,0:T(8,128)(2,1)S(1)} all-gather(bf16[64,1024]{1,0:T(8,128)(2,1)S(1)} %add_convert_fusion.2), channel_id=1, replica_groups=mesh['section'=2,'expert'=4,'dp'=4] {'dp'}, dimensions={0}, use_global_device_ids=true | all-gather | bytes 655360 | tf_op jit(solution)/shard_map/all_gather | solution.py:57
  275.3 3.5 all-to-all-start.9
  280.2 9.2 %all-to-all-done.9 = bf16[8,40,1024]{2,1,0:T(8,128)(2,1)S(1)} async-done(((bf16[8,40,1024]{2,1,0:T(8,128)(2,1)}), bf16[8,40,1024]{2,1,0:T(8,128)(2,1)S(1)}, u32[]{:S(2)}, u32[]{:S(2)}) %all-to-all-start.9) | async-done | bytes 655392 | tf_op jit(solution)/shard_map/all_to_all | solution.py:48
  295.8 3.5 convolution_convert_fusion.12
  299.3 3.5 all-to-all-start.10
  303.0 3.7 multiply_convert_fusion.4
  306.7 6.8 all-to-all-done.10
  315.0 4.0 fusion.80
  320.4 3.9 all-to-all-start.12
  327.8 7.1 all-to-all-done.12
  334.9 5.3 fusion.39
  340.2 3.5 convolution_convert_fusion.10
  343.8 3.5 all-to-all-start.13
  347.4 4.1 fusion.73
  351.4 6.5 all-to-all-done.13
  357.9 4.1 all-to-all-start.11
  366.2 11.1 %all-to-all-done.11 = bf16[4,64,1024]{2,1,0:T(8,128)(2,1)} async-done(((bf16[4,64,1024]{2,1,0:T(8,128)(2,1)}), bf16[4,64,1024]{2,1,0:T(8,128)(2,1)}, u32[]{:S(2)}, u32[]{:S(2)}) %all-to-all-start.11) | async-done | bytes 524320 | tf_op jit(solution)/shard_map/all_to_all | solution.py:48
  387.5 7.7 %all-to-all-done.14 = bf16[4,64,1024]{2,1,0:T(8,128)(2,1)S(1)} async-done(((bf16[4,64,1024]{2,1,0:T(8,128)(2,1)}), bf16[4,64,1024]{2,1,0:T(8,128)(2,1)S(1)}, u32[]{:S(2)}, u32[]{:S(2)}) %all-to-all-start.14) | async-done | bytes 524320 | tf_op jit(solution)/shard_map/all_to_all | solution.py:48
  406.9 5.2 all-to-all-done.15
  453.2 4.1 all-to-all-start.16
  457.5 4.9 collective-permute-done.34
  470.3 7.0 collective-permute-done.37
  480.9 3.7 collective-permute-done.48
  491.5 15.0 %all_gather.31 = bf16[256,1024]{1,0:T(8,128)(2,1)S(1)} all-gather(bf16[64,1024]{1,0:T(8,128)(2,1)S(1)} %get-tuple-element.112), channel_id=1, replica_groups=mesh['section'=2,'expert'=4,'dp'=4] {'dp'}, dimensions={0}, use_global_device_ids=true | all-gather | bytes 655360 | tf_op jit(solution)/shard_map/all_gather | solution.py:57
  518.1 4.2 all-to-all-start.17
  533.1 4.6 all-to-all-done.17
  537.7 4.8 fusion.32
  545.3 3.5 all-to-all-start.18
  561.3 4.8 collective-permute-done.19
  572.1 4.3 all-to-all-start.19
  577.6 5.8 convolution_bitcast_fusion.1
  585.0 5.8 convolution_bitcast_fusion
  595.8 4.6 all-to-all-start.20
  617.4 5.2 collective-permute-done.26
  623.9 3.6 collective-permute-start.30
  646.2 5.2 collective-permute-done.44
  658.8 4.1 all-to-all-start.21
  670.7 7.1 all-to-all-done.21
  680.9 4.1 all-to-all-start.22
  686.5 6.4 all-to-all-done.22
  692.9 3.7 all-to-all-start.24
  700.6 3.5 all-to-all-done.24
  (755 shorter events, 278.4 us)
Async XLA Ops:
  8.0 185.4 %all-gather.6.cloned.1.call-start = ((), (), s32[]{:S(2)}) async-start(), calls=%async_computation.30 | async-start | bytes 4718592 | tf_op jit(solution)/shard_map/all_gather | solution.py:195
  13.4 11.2 %collective-permute-start.6 = (bf16[64,1024]{1,0:T(8,128)(2,1)S(1)}, bf16[64,1024]{1,0:T(8,128)(2,1)S(1)}, u32[]{:S(2)}, u32[]{:S(2)}) collective-permute-start(bf16[64,1024]{1,0:T(8,128)(2,1)S(1)} %get-tuple-element.142), channel_id=1, source_target_pairs={{2,0},{3,1},{0,2},{1,3},{6,4},{7,5},{4,6},{5,7},{10,8},{11,9},{8,1... | collective-permute-start | bytes 393224 | tf_op jit(solution)/shard_map/ppermute | solution.py:98
  26.4 13.9 %all-to-all-start = ((bf16[32,8,128]{2,1,0:T(8,128)(2,1)}), bf16[32,8,128]{2,1,0:T(8,128)(2,1)S(1)}, u32[]{:S(2)}, u32[]{:S(2)}) async-start(bf16[32,8,128]{2,1,0:T(8,128)(2,1)} %broadcast_in_dim.217), calls=%async_computation | async-start | bytes 131072 | tf_op jit(solution)/shard_map/all_to_all | solution.py:48
  55.9 23.7 %all-to-all-start.2 = ((bf16[4,4,64,768]{3,2,1,0:T(8,128)(2,1)}), bf16[4,4,64,768]{3,2,1,0:T(8,128)(2,1)S(1)}, u32[]{:S(2)}, u32[]{:S(2)}) async-start(bf16[4,4,64,768]{3,2,1,0:T(8,128)(2,1)} %broadcast_in_dim.218), calls=%async_computation.2 | async-start | bytes 3145728 | tf_op jit(solution)/shard_map/all_to_all | solution.py:48
  59.5 137.6 %all-gather.8.cloned.1.call-start = ((), (), s32[]{:S(2)}) async-start(), calls=%async_computation.36 | async-start | bytes 4718592 | tf_op jit(solution)/shard_map/all_gather | solution.py:190
  59.8 11.8 %collective-permute-start.2 = (bf16[64,1024]{1,0:T(8,128)(2,1)S(1)}, bf16[64,1024]{1,0:T(8,128)(2,1)S(1)}, u32[]{:S(2)}, u32[]{:S(2)}) collective-permute-start(bf16[64,1024]{1,0:T(8,128)(2,1)S(1)} %bitcast.531), channel_id=1, source_target_pairs={{2,0},{3,1},{0,2},{1,3},{6,4},{7,5},{4,6},{5,7},{10,8},{11,9},{8,1... | collective-permute-start | bytes 393224 | tf_op jit(solution)/shard_map/ppermute | solution.py:87
  61.6 10.1 %collective-permute-start.3 = (bf16[64,1024]{1,0:T(8,128)(2,1)S(1)}, bf16[64,1024]{1,0:T(8,128)(2,1)S(1)}, u32[]{:S(2)}, u32[]{:S(2)}) collective-permute-start(bf16[64,1024]{1,0:T(8,128)(2,1)S(1)} %bitcast.532), channel_id=1, source_target_pairs={{1,0},{2,1},{3,2},{0,3},{5,4},{6,5},{7,6},{4,7},{9,8},{10,9},{11,1... | collective-permute-start | bytes 393224 | tf_op jit(solution)/shard_map/ppermute | solution.py:87
  66.6 106.7 %collective-permute-start.8 = (bf16[1024,1024]{1,0:T(8,128)(2,1)}, bf16[1024,1024]{1,0:T(8,128)(2,1)}, u32[]{:S(2)}, u32[]{:S(2)}) collective-permute-start(bf16[1024,1024]{1,0:T(8,128)(2,1)} %dynamic-slice_bitcast_fusion.1), channel_id=1, source_target_pairs={{0,16},{16,0},{1,17},{17,1},{2,18},{18,2},{3,19},{19,3},{4,20},{20... | collective-permute-start | bytes 6291464 | tf_op jit(solution)/shard_map/ppermute | solution.py:71
  68.1 118.9 %collective-permute-start.9 = (bf16[1024,1024]{1,0:T(8,128)(2,1)}, bf16[1024,1024]{1,0:T(8,128)(2,1)}, u32[]{:S(2)}, u32[]{:S(2)}) collective-permute-start(bf16[1024,1024]{1,0:T(8,128)(2,1)} %dynamic-slice_bitcast_fusion), channel_id=1, source_target_pairs={{0,16},{16,0},{1,17},{17,1},{2,18},{18,2},{3,19},{19,3},{4,20},{20... | collective-permute-start | bytes 6291464 | tf_op jit(solution)/shard_map/ppermute | solution.py:71
  81.4 34.1 %all-to-all-start.4 = ((bf16[4,4,64,1024]{3,2,1,0:T(8,128)(2,1)}), bf16[4,4,64,1024]{3,2,1,0:T(8,128)(2,1)S(1)}, u32[]{:S(2)}, u32[]{:S(2)}) async-start(bf16[4,4,64,1024]{3,2,1,0:T(8,128)(2,1)} %broadcast_in_dim.225), calls=%async_computation.4 | async-start | bytes 4194304 | tf_op jit(solution)/shard_map/all_to_all | solution.py:48
  85.4 47.4 %collective-permute-start = (bf16[1024,768]{1,0:T(8,128)(2,1)}, bf16[1024,768]{1,0:T(8,128)(2,1)}, u32[]{:S(2)}, u32[]{:S(2)}) collective-permute-start(bf16[1024,768]{1,0:T(8,128)(2,1)} %bitcast.483), channel_id=1, source_target_pairs={{0,16},{16,0},{1,17},{17,1},{2,18},{18,2},{3,19},{19,3},{4,20},{20... | collective-permute-start | bytes 4718600 | tf_op jit(solution)/shard_map/ppermute | solution.py:71
  115.5 34.4 %collective-permute-start.4 = (bf16[1024,1024]{1,0:T(8,128)(2,1)S(1)}, bf16[1024,1024]{1,0:T(8,128)(2,1)}, u32[]{:S(2)}, u32[]{:S(2)}) collective-permute-start(bf16[1024,1024]{1,0:T(8,128)(2,1)S(1)} %bitcast.474), channel_id=1, source_target_pairs={{0,16},{16,0},{1,17},{17,1},{2,18},{18,2},{3,19},{19,3},{4,20},{20... | collective-permute-start | bytes 6291464 | tf_op jit(solution)/shard_map/ppermute | solution.py:71
  138.6 10.6 %all-to-all-start.3 = ((bf16[4,64,256]{2,1,0:T(8,128)(2,1)}), bf16[4,64,256]{2,1,0:T(8,128)(2,1)S(1)}, u32[]{:S(2)}, u32[]{:S(2)}) async-start(bf16[4,64,256]{2,1,0:T(8,128)(2,1)} %copy.170), calls=%async_computation.3 | async-start | bytes 262144 | tf_op jit(solution)/shard_map/all_to_all | solution.py:48
  168.8 14.1 %all-to-all-start.5 = ((bf16[8,40,1024]{2,1,0:T(8,128)(2,1)}), bf16[8,40,1024]{2,1,0:T(8,128)(2,1)S(1)}, u32[]{:S(2)}, u32[]{:S(2)}) async-start(bf16[8,40,1024]{2,1,0:T(8,128)(2,1)} %bitcast.34), calls=%async_computation.5 | async-start | bytes 1310720 | tf_op jit(solution)/shard_map/all_to_all | solution.py:48
  188.8 15.3 %all-to-all-start.6 = ((bf16[8,40,1024]{2,1,0:T(8,128)(2,1)}), bf16[8,40,1024]{2,1,0:T(8,128)(2,1)S(1)}, u32[]{:S(2)}, u32[]{:S(2)}) async-start(bf16[8,40,1024]{2,1,0:T(8,128)(2,1)} %bitcast.40), calls=%async_computation.6 | async-start | bytes 1310720 | tf_op jit(solution)/shard_map/all_to_all | solution.py:48
  205.7 18.7 %all-to-all-start.7 = ((bf16[4,64,1024]{2,1,0:T(8,128)(2,1)}), bf16[4,64,1024]{2,1,0:T(8,128)(2,1)S(1)}, u32[]{:S(2)}, u32[]{:S(2)}) async-start(bf16[4,64,1024]{2,1,0:T(8,128)(2,1)} %bitcast.42), calls=%async_computation.7 | async-start | bytes 1048576 | tf_op jit(solution)/shard_map/all_to_all | solution.py:48
  275.3 14.1 %all-to-all-start.9 = ((bf16[8,40,1024]{2,1,0:T(8,128)(2,1)}), bf16[8,40,1024]{2,1,0:T(8,128)(2,1)S(1)}, u32[]{:S(2)}, u32[]{:S(2)}) async-start(bf16[8,40,1024]{2,1,0:T(8,128)(2,1)} %bitcast.467), calls=%async_computation.9 | async-start | bytes 1310720 | tf_op jit(solution)/shard_map/all_to_all | solution.py:48
  278.8 36.2 %all-gather.10.cloned.1.call-start = ((), (), s32[]{:S(2)}) async-start(), calls=%async_computation.37 | async-start | bytes 1310720 | tf_op jit(solution)/shard_map/all_gather | solution.py:401
  279.4 13.5 %collective-permute-start.64 = (bf16[320,1024]{1,0:T(8,128)(2,1)}, bf16[320,1024]{1,0:T(8,128)(2,1)}, u32[]{:S(2)}, u32[]{:S(2)}) collective-permute-start(bf16[320,1024]{1,0:T(8,128)(2,1)} %copy-done.45), channel_id=1, source_target_pairs={{0,16},{16,0},{1,17},{17,1},{2,18},{18,2},{3,19},{19,3},{4,20},{20... | collective-permute-start | bytes 1966088 | tf_op jit(solution)/shard_map/ppermute | solution.py:71
  299.3 14.1 %all-to-all-start.10 = ((bf16[8,40,1024]{2,1,0:T(8,128)(2,1)}), bf16[8,40,1024]{2,1,0:T(8,128)(2,1)S(1)}, u32[]{:S(2)}, u32[]{:S(2)}) async-start(bf16[8,40,1024]{2,1,0:T(8,128)(2,1)} %bitcast.495), calls=%async_computation.10 | async-start | bytes 1310720 | tf_op jit(solution)/shard_map/all_to_all | solution.py:48
  320.4 14.5 %all-to-all-start.12 = ((bf16[8,40,1024]{2,1,0:T(8,128)(2,1)}), bf16[8,40,1024]{2,1,0:T(8,128)(2,1)S(1)}, u32[]{:S(2)}, u32[]{:S(2)}) async-start(bf16[8,40,1024]{2,1,0:T(8,128)(2,1)} %bitcast.466), calls=%async_computation.12 | async-start | bytes 1310720 | tf_op jit(solution)/shard_map/all_to_all | solution.py:48
  324.3 57.7 %collective-permute-start.46 = (bf16[256,1024]{1,0:T(8,128)(2,1)S(1)}, bf16[256,1024]{1,0:T(8,128)(2,1)}, u32[]{:S(2)}, u32[]{:S(2)}) collective-permute-start(bf16[256,1024]{1,0:T(8,128)(2,1)S(1)} %all_gather.29), channel_id=1, source_target_pairs={{0,16},{16,0},{1,17},{17,1},{2,18},{18,2},{3,19},{19,3},{4,20},{20... | collective-permute-start | bytes 1572872 | tf_op jit(solution)/shard_map/ppermute | solution.py:71
  343.8 14.1 %all-to-all-start.13 = ((bf16[8,40,1024]{2,1,0:T(8,128)(2,1)}), bf16[8,40,1024]{2,1,0:T(8,128)(2,1)S(1)}, u32[]{:S(2)}, u32[]{:S(2)}) async-start(bf16[8,40,1024]{2,1,0:T(8,128)(2,1)} %bitcast.494), calls=%async_computation.13 | async-start | bytes 1310720 | tf_op jit(solution)/shard_map/all_to_all | solution.py:48
  357.9 19.4 %all-to-all-start.11 = ((bf16[4,64,1024]{2,1,0:T(8,128)(2,1)}), bf16[4,64,1024]{2,1,0:T(8,128)(2,1)}, u32[]{:S(2)}, u32[]{:S(2)}) async-start(bf16[4,64,1024]{2,1,0:T(8,128)(2,1)} %bitcast.472), calls=%async_computation.11 | async-start | bytes 1048576 | tf_op jit(solution)/shard_map/all_to_all | solution.py:48
  377.4 17.9 %all-to-all-start.14 = ((bf16[4,64,1024]{2,1,0:T(8,128)(2,1)}), bf16[4,64,1024]{2,1,0:T(8,128)(2,1)S(1)}, u32[]{:S(2)}, u32[]{:S(2)}) async-start(bf16[4,64,1024]{2,1,0:T(8,128)(2,1)} %bitcast.481), calls=%async_computation.14 | async-start | bytes 1048576 | tf_op jit(solution)/shard_map/all_to_all | solution.py:48
  380.8 87.7 %reduce-scatter.10.cloned.1.call-start = ((), (), s32[]{:S(2)}) async-start(), calls=%async_computation.33 | async-start | bytes 1310720 | tf_op jit(solution)/shard_map/reduce_scatter | solution.py:381
  406.2 146.3 %reduce-scatter.6.cloned.1.call-start = ((), (), s32[]{:S(2)}) async-start(), calls=%async_computation.31 | async-start | bytes 983040 | tf_op jit(solution)/shard_map/reduce_scatter | solution.py:381
  406.3 21.7 %collective-permute-start.60 = (bf16[320,1024]{1,0:T(8,128)(2,1)S(1)}, bf16[320,1024]{1,0:T(8,128)(2,1)}, u32[]{:S(2)}, u32[]{:S(2)}) collective-permute-start(bf16[320,1024]{1,0:T(8,128)(2,1)S(1)} %bitcast.463), channel_id=1, source_target_pairs={{0,16},{16,0},{1,17},{17,1},{2,18},{18,2},{3,19},{19,3},{4,20},{20... | collective-permute-start | bytes 1966088 | tf_op jit(solution)/shard_map/ppermute | solution.py:71
  406.4 16.8 %collective-permute-start.16 = (bf16[256,1024]{1,0:T(8,128)(2,1)}, bf16[256,1024]{1,0:T(8,128)(2,1)}, u32[]{:S(2)}, u32[]{:S(2)}) collective-permute-start(bf16[256,1024]{1,0:T(8,128)(2,1)} %copy-done.49), channel_id=1, source_target_pairs={{0,16},{16,0},{1,17},{17,1},{2,18},{18,2},{3,19},{19,3},{4,20},{20... | collective-permute-start | bytes 1572872 | tf_op jit(solution)/shard_map/ppermute | solution.py:71
  427.0 190.3 %reduce-scatter.14.cloned.1.call-start = ((), (), s32[]{:S(2)}) async-start(), calls=%async_computation.35 | async-start | bytes 1310720 | tf_op jit(solution)/shard_map/reduce_scatter | solution.py:381
  427.2 200.3 %collective-permute-start.14 = (bf16[256,1024]{1,0:T(8,128)(2,1)}, bf16[256,1024]{1,0:T(8,128)(2,1)}, u32[]{:S(2)}, u32[]{:S(2)}) collective-permute-start(bf16[256,1024]{1,0:T(8,128)(2,1)} %copy-done.47), channel_id=1, source_target_pairs={{0,16},{16,0},{1,17},{17,1},{2,18},{18,2},{3,19},{19,3},{4,20},{20... | collective-permute-start | bytes 1572872 | tf_op jit(solution)/shard_map/ppermute | solution.py:71
  427.4 177.6 %collective-permute-start.23 = (bf16[64,1024]{1,0:T(8,128)(2,1)}, bf16[64,1024]{1,0:T(8,128)(2,1)}, u32[]{:S(2)}, u32[]{:S(2)}) collective-permute-start(bf16[64,1024]{1,0:T(8,128)(2,1)} %bitcast.203), channel_id=1, source_target_pairs={{0,16},{16,0},{1,17},{17,1},{2,18},{18,2},{3,19},{19,3},{4,20},{20... | collective-permute-start | bytes 393224 | tf_op jit(solution)/shard_map/ppermute | solution.py:71
  448.3 14.1 %collective-permute-start.34 = (bf16[256,512]{1,0:T(8,128)(2,1)}, bf16[256,512]{1,0:T(8,128)(2,1)}, u32[]{:S(2)}, u32[]{:S(2)}) collective-permute-start(bf16[256,512]{1,0:T(8,128)(2,1)} %get-tuple-element.131), channel_id=1, source_target_pairs={{8,0},{12,4},{0,8},{4,12},{9,1},{13,5},{1,9},{5,13},{10,2},{14,6},... | collective-permute-start | bytes 786440 | tf_op jit(solution)/shard_map/ppermute | solution.py:98
  450.2 12.2 %collective-permute-start.33 = (bf16[256,512]{1,0:T(8,128)(2,1)}, bf16[256,512]{1,0:T(8,128)(2,1)}, u32[]{:S(2)}, u32[]{:S(2)}) collective-permute-start(bf16[256,512]{1,0:T(8,128)(2,1)} %get-tuple-element.129), channel_id=1, source_target_pairs={{12,0},{0,4},{4,8},{8,12},{13,1},{1,5},{5,9},{9,13},{14,2},{2,6},{... | collective-permute-start | bytes 786440 | tf_op jit(solution)/shard_map/ppermute | solution.py:98
  453.2 32.1 %all-to-all-start.16 = ((bf16[4,64,1024]{2,1,0:T(8,128)(2,1)}), bf16[4,64,1024]{2,1,0:T(8,128)(2,1)}, u32[]{:S(2)}, u32[]{:S(2)}) async-start(bf16[4,64,1024]{2,1,0:T(8,128)(2,1)} %bitcast.79), calls=%async_computation.16 | async-start | bytes 1048576 | tf_op jit(solution)/shard_map/all_to_all | solution.py:48
  457.3 179.9 %reduce-scatter.8.cloned.1.call-start = ((), (), s32[]{:S(2)}) async-start(), calls=%async_computation.32 | async-start | bytes 1310720 | tf_op jit(solution)/shard_map/reduce_scatter | solution.py:381
  467.7 10.2 %collective-permute-start.36 = (bf16[64,512]{1,0:T(8,128)(2,1)S(1)}, bf16[64,512]{1,0:T(8,128)(2,1)}, u32[]{:S(2)}, u32[]{:S(2)}) collective-permute-start(bf16[64,512]{1,0:T(8,128)(2,1)S(1)} %get-tuple-element.166), channel_id=1, source_target_pairs={{3,0},{0,1},{1,2},{2,3},{7,4},{4,5},{5,6},{6,7},{11,8},{8,9},{9,10... | collective-permute-start | bytes 196616 | tf_op jit(solution)/shard_map/ppermute | solution.py:98
  470.3 42.8 %collective-permute-start.41 = (bf16[256,1024]{1,0:T(8,128)(2,1)S(1)}, bf16[256,1024]{1,0:T(8,128)(2,1)}, u32[]{:S(2)}, u32[]{:S(2)}) collective-permute-start(bf16[256,1024]{1,0:T(8,128)(2,1)S(1)} %all_gather.25), channel_id=1, source_target_pairs={{0,16},{16,0},{1,17},{17,1},{2,18},{18,2},{3,19},{19,3},{4,20},{20... | collective-permute-start | bytes 1572872 | tf_op jit(solution)/shard_map/ppermute | solution.py:71
  479.5 30.0 %collective-permute-start.49 = (bf16[64,512]{1,0:T(8,128)(2,1)}, bf16[64,512]{1,0:T(8,128)(2,1)}, u32[]{:S(2)}, u32[]{:S(2)}) collective-permute-start(bf16[64,512]{1,0:T(8,128)(2,1)} %get-tuple-element.156), channel_id=1, source_target_pairs={{2,0},{3,1},{0,2},{1,3},{6,4},{7,5},{4,6},{5,7},{10,8},{11,9},{8,1... | collective-permute-start | bytes 196616 | tf_op jit(solution)/shard_map/ppermute | solution.py:98
  484.6 26.5 %collective-permute-start.50 = (bf16[64,512]{1,0:T(8,128)(2,1)}, bf16[64,512]{1,0:T(8,128)(2,1)}, u32[]{:S(2)}, u32[]{:S(2)}) collective-permute-start(bf16[64,512]{1,0:T(8,128)(2,1)} %get-tuple-element.155), channel_id=1, source_target_pairs={{1,0},{2,1},{3,2},{0,3},{5,4},{6,5},{7,6},{4,7},{9,8},{10,9},{11,1... | collective-permute-start | bytes 196616 | tf_op jit(solution)/shard_map/ppermute | solution.py:98
  511.1 18.3 %collective-permute-start.53 = (bf16[256,1024]{1,0:T(8,128)(2,1)}, bf16[256,1024]{1,0:T(8,128)(2,1)}, u32[]{:S(2)}, u32[]{:S(2)}) collective-permute-start(bf16[256,1024]{1,0:T(8,128)(2,1)} %get-tuple-element.194), channel_id=1, source_target_pairs={{0,16},{16,0},{1,17},{17,1},{2,18},{18,2},{3,19},{19,3},{4,20},{20... | collective-permute-start | bytes 1572872 | tf_op jit(solution)/shard_map/ppermute | solution.py:71
  513.0 35.9 %collective-permute-start.61 = (bf16[320,1024]{1,0:T(8,128)(2,1)}, bf16[320,1024]{1,0:T(8,128)(2,1)}, u32[]{:S(2)}, u32[]{:S(2)}) collective-permute-start(bf16[320,1024]{1,0:T(8,128)(2,1)} %fusion.39), channel_id=1, source_target_pairs={{0,16},{16,0},{1,17},{17,1},{2,18},{18,2},{3,19},{19,3},{4,20},{20... | collective-permute-start | bytes 1966088 | tf_op jit(solution)/shard_map/ppermute | solution.py:71
  518.1 19.7 %all-to-all-start.17 = ((bf16[8,40,1024]{2,1,0:T(8,128)(2,1)}), bf16[8,40,1024]{2,1,0:T(8,128)(2,1)}, u32[]{:S(2)}, u32[]{:S(2)}) async-start(bf16[8,40,1024]{2,1,0:T(8,128)(2,1)} %bitcast.83), calls=%async_computation.17 | async-start | bytes 1310720 | tf_op jit(solution)/shard_map/all_to_all | solution.py:48
  522.3 119.6 %reduce-scatter.12.cloned.1.call-start = ((), (), s32[]{:S(2)}) async-start(), calls=%async_computation.34 | async-start | bytes 1310720 | tf_op jit(solution)/shard_map/reduce_scatter | solution.py:381
  529.5 25.2 %collective-permute-start.65 = (bf16[320,1024]{1,0:T(8,128)(2,1)S(1)}, bf16[320,1024]{1,0:T(8,128)(2,1)S(1)}, u32[]{:S(2)}, u32[]{:S(2)}) collective-permute-start(bf16[320,1024]{1,0:T(8,128)(2,1)S(1)} %bitcast.461), channel_id=1, source_target_pairs={{0,16},{16,0},{1,17},{17,1},{2,18},{18,2},{3,19},{19,3},{4,20},{20... | collective-permute-start | bytes 1966088 | tf_op jit(solution)/shard_map/ppermute | solution.py:71
  529.6 105.2 %collective-permute-start.39 = (f32[64,512]{1,0:T(8,128)}, f32[64,512]{1,0:T(8,128)}, u32[]{:S(2)}, u32[]{:S(2)}) collective-permute-start(f32[64,512]{1,0:T(8,128)} %fusion.191), channel_id=1, source_target_pairs={{0,16},{16,0},{1,17},{17,1},{2,18},{18,2},{3,19},{19,3},{4,20},{20... | collective-permute-start | bytes 393224 | tf_op jit(solution)/shard_map/ppermute | solution.py:71
  545.3 25.4 %all-to-all-start.18 = ((bf16[8,40,1024]{2,1,0:T(8,128)(2,1)}), bf16[8,40,1024]{2,1,0:T(8,128)(2,1)S(1)}, u32[]{:S(2)}, u32[]{:S(2)}) async-start(bf16[8,40,1024]{2,1,0:T(8,128)(2,1)} %bitcast.85), calls=%async_computation.18 | async-start | bytes 1310720 | tf_op jit(solution)/shard_map/all_to_all | solution.py:48
  548.9 27.4 %collective-permute-start.62 = (bf16[320,1024]{1,0:T(8,128)(2,1)}, bf16[320,1024]{1,0:T(8,128)(2,1)}, u32[]{:S(2)}, u32[]{:S(2)}) collective-permute-start(bf16[320,1024]{1,0:T(8,128)(2,1)} %fusion.32), channel_id=1, source_target_pairs={{0,16},{16,0},{1,17},{17,1},{2,18},{18,2},{3,19},{19,3},{4,20},{20... | collective-permute-start | bytes 1966088 | tf_op jit(solution)/shard_map/ppermute | solution.py:71
  570.1 13.2 %collective-permute-start.66 = (bf16[320,1024]{1,0:T(8,128)(2,1)}, bf16[320,1024]{1,0:T(8,128)(2,1)}, u32[]{:S(2)}, u32[]{:S(2)}) collective-permute-start(bf16[320,1024]{1,0:T(8,128)(2,1)} %bitcast.84), channel_id=1, source_target_pairs={{0,16},{16,0},{1,17},{17,1},{2,18},{18,2},{3,19},{19,3},{4,20},{20... | collective-permute-start | bytes 1966088 | tf_op jit(solution)/shard_map/ppermute | solution.py:71
  572.1 19.8 %all-to-all-start.19 = ((bf16[4,64,1024]{2,1,0:T(8,128)(2,1)}), bf16[4,64,1024]{2,1,0:T(8,128)(2,1)}, u32[]{:S(2)}, u32[]{:S(2)}) async-start(bf16[4,64,1024]{2,1,0:T(8,128)(2,1)} %bitcast.482), calls=%async_computation.19 | async-start | bytes 1048576 | tf_op jit(solution)/shard_map/all_to_all | solution.py:48
  595.8 14.0 %all-to-all-start.20 = ((bf16[4,64,256]{2,1,0:T(8,128)(2,1)}), bf16[4,64,256]{2,1,0:T(8,128)(2,1)S(1)}, u32[]{:S(2)}, u32[]{:S(2)}) async-start(bf16[4,64,256]{2,1,0:T(8,128)(2,1)} %bitcast.451), calls=%async_computation.20 | async-start | bytes 262144 | tf_op jit(solution)/shard_map/all_to_all | solution.py:48
  608.7 13.9 %collective-permute-start.26 = (bf16[256,512]{1,0:T(8,128)(2,1)}, bf16[256,512]{1,0:T(8,128)(2,1)}, u32[]{:S(2)}, u32[]{:S(2)}) collective-permute-start(bf16[256,512]{1,0:T(8,128)(2,1)} %get-tuple-element.128), channel_id=1, source_target_pairs={{8,0},{12,4},{0,8},{4,12},{9,1},{13,5},{1,9},{5,13},{10,2},{14,6},... | collective-permute-start | bytes 786440 | tf_op jit(solution)/shard_map/ppermute | solution.py:98
  609.3 13.3 %collective-permute-start.25 = (bf16[256,512]{1,0:T(8,128)(2,1)}, bf16[256,512]{1,0:T(8,128)(2,1)}, u32[]{:S(2)}, u32[]{:S(2)}) collective-permute-start(bf16[256,512]{1,0:T(8,128)(2,1)} %get-tuple-element.126), channel_id=1, source_target_pairs={{12,0},{0,4},{4,8},{8,12},{13,1},{1,5},{5,9},{9,13},{14,2},{2,6},{... | collective-permute-start | bytes 786440 | tf_op jit(solution)/shard_map/ppermute | solution.py:98
  617.3 22.2 %collective-permute-start.57 = (bf16[256,512]{1,0:T(8,128)(2,1)}, bf16[256,512]{1,0:T(8,128)(2,1)S(1)}, u32[]{:S(2)}, u32[]{:S(2)}) collective-permute-start(bf16[256,512]{1,0:T(8,128)(2,1)} %reduce-scatter.14.cloned.1.call-done), channel_id=1, source_target_pairs={{0,16},{16,0},{1,17},{17,1},{2,18},{18,2},{3,19},{19,3},{4,20},{20... | collective-permute-start | bytes 786440 | tf_op jit(solution)/shard_map/ppermute | solution.py:71
  623.9 11.1 %collective-permute-start.30 = (bf16[64,512]{1,0:T(8,128)(2,1)S(1)}, bf16[64,512]{1,0:T(8,128)(2,1)S(1)}, u32[]{:S(2)}, u32[]{:S(2)}) collective-permute-start(bf16[64,512]{1,0:T(8,128)(2,1)S(1)} %get-tuple-element.164), channel_id=1, source_target_pairs={{1,0},{2,1},{3,2},{0,3},{5,4},{6,5},{7,6},{4,7},{9,8},{10,9},{11,1... | collective-permute-start | bytes 196616 | tf_op jit(solution)/shard_map/ppermute | solution.py:98
  631.4 27.4 %all-to-all-start.23 = ((bf16[4,256,384]{2,1,0:T(8,128)(2,1)}), bf16[4,256,384]{2,1,0:T(8,128)(2,1)S(1)}, u32[]{:S(2)}, u32[]{:S(2)}) async-start(bf16[4,256,384]{2,1,0:T(8,128)(2,1)} %bitcast.109), calls=%async_computation.23 | async-start | bytes 1572864 | tf_op jit(solution)/shard_map/all_to_all | solution.py:48
  634.9 21.4 %collective-permute-start.51 = (bf16[4,64,512]{2,1,0:T(8,128)(2,1)S(1)}, bf16[4,64,512]{2,1,0:T(8,128)(2,1)S(1)}, u32[]{:S(2)}, u32[]{:S(2)}) collective-permute-start(bf16[4,64,512]{2,1,0:T(8,128)(2,1)S(1)} %copy-done.42), channel_id=1, source_target_pairs={{0,16},{16,0},{1,17},{17,1},{2,18},{18,2},{3,19},{19,3},{4,20},{20... | collective-permute-start | bytes 786440 | tf_op jit(solution)/shard_map/ppermute | solution.py:71
  635.0 50.0 %collective-permute-start.12 = (f32[64,1024]{1,0:T(8,128)}, f32[64,1024]{1,0:T(8,128)}, u32[]{:S(2)}, u32[]{:S(2)}) collective-permute-start(f32[64,1024]{1,0:T(8,128)} %get-tuple-element.113), channel_id=1, source_target_pairs={{0,16},{16,0},{1,17},{17,1},{2,18},{18,2},{3,19},{19,3},{4,20},{20... | collective-permute-start | bytes 786440 | tf_op jit(solution)/shard_map/ppermute | solution.py:71
  635.5 68.7 %collective-permute-start.21 = (bf16[4,64,384]{2,1,0:T(8,128)(2,1)}, bf16[4,64,384]{2,1,0:T(8,128)(2,1)}, u32[]{:S(2)}, u32[]{:S(2)}) collective-permute-start(bf16[4,64,384]{2,1,0:T(8,128)(2,1)} %bitcast_dynamic-update-slice_fusion.12), channel_id=1, source_target_pairs={{0,16},{16,0},{1,17},{17,1},{2,18},{18,2},{3,19},{19,3},{4,20},{20... | collective-permute-start | bytes 589832 | tf_op jit(solution)/shard_map/ppermute | solution.py:71
  635.6 23.0 %collective-permute-start.40 = (f32[64,512]{1,0:T(8,128)S(1)}, f32[64,512]{1,0:T(8,128)S(1)}, u32[]{:S(2)}, u32[]{:S(2)}) collective-permute-start(f32[64,512]{1,0:T(8,128)S(1)} %get-tuple-element.107), channel_id=1, source_target_pairs={{0,16},{16,0},{1,17},{17,1},{2,18},{18,2},{3,19},{19,3},{4,20},{20... | collective-permute-start | bytes 393224 | tf_op jit(solution)/shard_map/ppermute | solution.py:71
  658.8 19.1 %all-to-all-start.21 = ((bf16[4,64,1024]{2,1,0:T(8,128)(2,1)}), bf16[4,64,1024]{2,1,0:T(8,128)(2,1)}, u32[]{:S(2)}, u32[]{:S(2)}) async-start(bf16[4,64,1024]{2,1,0:T(8,128)(2,1)} %bitcast.95), calls=%async_computation.21 | async-start | bytes 1048576 | tf_op jit(solution)/shard_map/all_to_all | solution.py:48
  680.9 12.0 %all-to-all-start.22 = ((f32[32,8,128]{2,1,0:T(8,128)}), f32[32,8,128]{2,1,0:T(8,128)S(1)}, u32[]{:S(2)}, u32[]{:S(2)}) async-start(f32[32,8,128]{2,1,0:T(8,128)} %bitcast.212), calls=%async_computation.22 | async-start | bytes 262144 | tf_op jit(solution)/shard_map/all_to_all | solution.py:48
  685.2 14.5 %collective-permute-start.13 = (f32[64,1024]{1,0:T(8,128)S(1)}, f32[64,1024]{1,0:T(8,128)S(1)}, u32[]{:S(2)}, u32[]{:S(2)}) collective-permute-start(f32[64,1024]{1,0:T(8,128)S(1)} %get-tuple-element.109), channel_id=1, source_target_pairs={{0,16},{16,0},{1,17},{17,1},{2,18},{18,2},{3,19},{19,3},{4,20},{20... | collective-permute-start | bytes 786440 | tf_op jit(solution)/shard_map/ppermute | solution.py:71
  692.9 11.3 %all-to-all-start.24 = ((bf16[4,64,384]{2,1,0:T(8,128)(2,1)}), bf16[4,64,384]{2,1,0:T(8,128)(2,1)S(1)}, u32[]{:S(2)}, u32[]{:S(2)}) async-start(bf16[4,64,384]{2,1,0:T(8,128)(2,1)} %bitcast.110), calls=%async_computation.24 | async-start | bytes 393216 | tf_op jit(solution)/shard_map/all_to_all | solution.py:48
  (186 other events, 1892.1 us)
Sparse Core Ops, SparseCore 0:
  25.7 48.2 all-gather.5
  75.8 53.5 all-gather.7
Sparse Core Ops, SparseCore 1:
  280.9 27.6 all-gather.9
  386.4 27.4 reduce-scatter.9
  427.1 23.2 reduce-scatter.5
  453.5 33.8 reduce-scatter.13
  516.1 33.2 reduce-scatter.7
  552.5 27.7 reduce-scatter.11

commit v2 on v0

v2 whole, which is shorter than its diff:
```python
from types import SimpleNamespace

import jax
import jax.numpy as jnp
from jax import lax
from jax.experimental import pallas as pl
from jax.experimental.pallas import tpu as pltpu
from jax.sharding import PartitionSpec as P

HEADS = 16
HEAD_DIM = 64
SEC, EX, DP = "section", "expert", "dp"
EVERY = (SEC, EX, DP)
HOMES = (SEC, EX)


def layer_norm(value_rows, gain_vec, shift_vec):
    centre = jnp.mean(value_rows, axis=-1, keepdims=True)
    centred = value_rows - centre
    variance = jnp.mean(centred * centred, axis=-1, keepdims=True)
    return centred * lax.rsqrt(variance + 1e-05) * gain_vec + shift_vec


def gelu_tanh(value_rows):
    return jax.nn.gelu(value_rows, approximate=True)


def gelu_grad(value_rows, grad_in):
    return jax.vjp(gelu_tanh, value_rows)[1](grad_in)[0]


def product(left_mat, right_mat):
    return jnp.dot(left_mat, right_mat, preferred_element_type=jnp.float32)


def product_tn(left_mat, right_mat):
    return lax.dot_general(
        left_mat, right_mat, (((0,), (0,)), ((), ())), preferred_element_type=jnp.float32
    )


def product_nt(left_mat, right_mat):
    return lax.dot_general(
        left_mat, right_mat, (((1,), (1,)), ((), ())), preferred_element_type=jnp.float32
    )


def low(values):
    return values.astype(jnp.bfloat16)


def exchange(blocks, axes):
    return lax.all_to_all(blocks, axes, split_axis=0, concat_axis=0, tiled=True)


def spread(block, axes):
    count = lax.axis_size(axes)
    return exchange(jnp.broadcast_to(block[None], (count,) + block.shape), axes)


def gather_rows(block):
    return lax.all_gather(block, DP, axis=0, tiled=True)


def sum_blocks(blocks):
    return jnp.sum(blocks.astype(jnp.float32), axis=0)


def row_blocks(partial_rows):
    return low(partial_rows).reshape(lax.axis_size(DP), -1, partial_rows.shape[-1])


def beside(move, blocks, work, operands, late=()):
    blocks, operands = lax.optimization_barrier((blocks, operands))
    return lax.optimization_barrier((move(blocks), work(*operands, *late)))


def over_dp(blocks):
    return exchange(blocks, DP)


def over_homes(blocks):
    return exchange(blocks, HOMES)


def after(values, event):
    return lax.optimization_barrier((values, event))[0]


def permute_copies(block, axis):
    count = lax.axis_size(axis)
    blocks = [block]
    for step in range(1, count):
        route = [((i - step) % count, i) for i in range(count)]
        blocks.append(lax.ppermute(block, axis, route))
    return blocks


def own_parts(blocks, axis):
    count = lax.axis_size(axis)
    place = lax.axis_index(axis)
    return [
        lax.dynamic_index_in_dim(blocks, (place + step) % count, 0, keepdims=False)
        for step in range(count)
    ]


def sent_parts(parts, axis):
    count = len(parts)
    return [parts[0]] + [
        lax.ppermute(parts[step], axis, [((i - step) % count, i) for i in range(count)])
        for step in range(1, count)
    ]


def permute_parts(blocks, axis):
    return sent_parts(own_parts(blocks, axis), axis)


SCALAR = pl.BlockSpec(memory_space=pltpu.SMEM)
WHOLE = pl.BlockSpec(memory_space=pltpu.VMEM)


def in_order(blocks, axis):
    count = lax.axis_size(axis)

    def kernel(place, *refs):
        for step in range(count):
            refs[-1][(place[0] + count - step) % count] = refs[step][...]

    return pl.pallas_call(
        kernel,
        out_shape=jax.ShapeDtypeStruct((count,) + blocks[0].shape, blocks[0].dtype),
        in_specs=[SCALAR] + [WHOLE] * count,
        compiler_params=pltpu.CompilerParams(vmem_limit_bytes=32 << 20),
        name="in_order",
    )(lax.axis_index(axis).reshape(1), *blocks)


def finish_weights(section_id, ups, attns, down_sums, hidden_rows):
    dp_size, rows, half_hidden = ups[0].shape
    down_rows, half_width = down_sums[0].shape
    width = 2 * half_width
    head_width = width // dp_size
    qkv_half = 3 * head_width // 2

    def kernel(place, *refs):
        qkv_ref, proj_ref, up_ref, down_ref = refs[12:]

        def write(up_halves, attn_halves, down_halves):
            for half in range(2):
                up, attn = up_halves[half], attn_halves[half]
                here = slice(half * half_width, (half + 1) * half_width)
                proj_sum = attn[0, :, :half_width].astype(jnp.float32)
                for z in range(1, dp_size):
                    proj_sum = proj_sum + attn[z, :, :half_width].astype(jnp.float32)
                proj_ref[:, here] = proj_sum
                down_ref[:, here] = down_halves[half][...].astype(jnp.float32)
                for z in range(dp_size):
                    for piece in range(half_hidden // hidden_rows):
                        group = half * (half_hidden // hidden_rows) + piece
                        start = (group * dp_size + z) * hidden_rows
                        up_ref[:, start : start + hidden_rows] = up[
                            z, :, piece * hidden_rows : (piece + 1) * hidden_rows
                        ].astype(jnp.float32)
                    at = 0
                    while at < qkv_half:
                        column = half * qkv_half + at
                        part, inner = column // head_width, column % head_width
                        size = min(head_width - inner, qkv_half - at)
                        first = half_width + at
                        start = part * width + z * head_width + inner
                        qkv_ref[:, start : start + size] = attn[
                            z, :, first : first + size
                        ].astype(jnp.float32)
                        at = at + size

        @pl.when(place[0] == 0)
        def _():
            write(refs[0:2], refs[4:6], refs[8:10])

        @pl.when(place[0] != 0)
        def _():
            write(refs[3:1:-1], refs[7:5:-1], refs[11:9:-1])

    shapes = ((rows, 3 * width), (rows, width), (rows, 2 * half_hidden * dp_size), (down_rows, width))
    return pl.pallas_call(
        kernel,
        out_shape=[jax.ShapeDtypeStruct(shape, jnp.float32) for shape in shapes],
        in_specs=[SCALAR] + [WHOLE] * 12,
        compiler_params=pltpu.CompilerParams(vmem_limit_bytes=32 << 20),
        name="finish_weights",
    )(section_id.reshape(1), *ups, *attns, *down_sums)


def finish_rows(section_id, *arrays):
    count = len(arrays)

    def kernel(place, *refs):
        outs = refs[4 * count :]
        for index in range(count):
            own_zero, other_zero, own_one, other_one = refs[4 * index : 4 * index + 4]

            @pl.when(place[0] == 0)
            def _():
                outs[index][0] = own_zero[...]
                outs[index][1] = other_zero[...]

            @pl.when(place[0] != 0)
            def _():
                outs[index][0] = other_one[...]
                outs[index][1] = own_one[...]

    return pl.pallas_call(
        kernel,
        out_shape=[
            jax.ShapeDtypeStruct((2,) + array[0].shape, array[0].dtype) for array in arrays
        ],
        in_specs=[SCALAR] + [WHOLE] * (4 * count),
        compiler_params=pltpu.CompilerParams(vmem_limit_bytes=32 << 20),
        name="finish_rows",
    )(section_id.reshape(1), *[rows for array in arrays for rows in array])


def sum_parts(parts):
    return sum(part.astype(jnp.float32) for part in parts)


def softmax_rows(queries, keys, allowed):
    scores = product_nt(queries, keys) * 0.125
    scores = jnp.where(allowed, scores, -jnp.inf)
    exp_scores = jnp.exp(scores - jnp.max(scores, axis=-1, keepdims=True))
    return exp_scores / jnp.sum(exp_scores, axis=-1, keepdims=True)


def allowed_keys(seg_column, seg_row):
    rows, columns = seg_column.shape[0], seg_row.shape[1]
    query_at = lax.broadcasted_iota(jnp.int32, (rows, columns), 0)
    key_at = lax.broadcasted_iota(jnp.int32, (rows, columns), 1)
    return (seg_column == seg_row) & (key_at <= query_at)


def head_slices(packed, head, head_width):
    start = head * HEAD_DIM
    return [
        packed[:, part * head_width + start : part * head_width + start + HEAD_DIM]
        for part in range(3)
    ]


def attention_kernel(seg_column, seg_row, qkv_ref, mixed_ref):
    head_width = mixed_ref.shape[1]
    allowed = allowed_keys(seg_column[...], seg_row[...])
    packed = qkv_ref[...]
    mixed = []
    for head in range(head_width // HEAD_DIM):
        queries, keys, values = head_slices(packed, head, head_width)
        probs = softmax_rows(queries, keys, allowed)
        mixed.append(low(product(low(probs), values)))
    mixed_ref[...] = jnp.concatenate(mixed, axis=1)


def attention_back_kernel(seg_column, seg_row, qkv_ref, d_mixed_ref, d_qkv_ref):
    head_width = d_mixed_ref.shape[1]
    allowed = allowed_keys(seg_column[...], seg_row[...])
    packed = qkv_ref[...]
    d_mixed_all = d_mixed_ref[...]
    grads = [[], [], []]
    for head in range(head_width // HEAD_DIM):
        queries, keys, values = head_slices(packed, head, head_width)
        d_mixed = d_mixed_all[:, head * HEAD_DIM : (head + 1) * HEAD_DIM]
        probs = softmax_rows(queries, keys, allowed)
        d_probs = product_nt(d_mixed, values)
        d_scores = low(probs * (d_probs - jnp.sum(probs * d_probs, axis=-1, keepdims=True)))
        grads[0].append(low(product(d_scores, keys) * 0.125))
        grads[1].append(low(product_tn(d_scores, queries) * 0.125))
        grads[2].append(low(product_tn(low(probs), d_mixed)))
    d_qkv_ref[...] = jnp.concatenate(grads[0] + grads[1] + grads[2], axis=1)


def attention(segments, qkv):
    head_width = qkv.shape[1] // 3
    return pl.pallas_call(
        attention_kernel,
        out_shape=jax.ShapeDtypeStruct((qkv.shape[0], head_width), jnp.bfloat16),
        compiler_params=pltpu.CompilerParams(vmem_limit_bytes=32 << 20),
        name="attention",
    )(segments[:, None], segments[None, :], qkv)


def attention_back(segments, qkv, d_mixed):
    return pl.pallas_call(
        attention_back_kernel,
        out_shape=jax.ShapeDtypeStruct(qkv.shape, jnp.bfloat16),
        compiler_params=pltpu.CompilerParams(vmem_limit_bytes=32 << 20),
        name="attention_back",
    )(segments[:, None], segments[None, :], qkv, d_mixed)


OWNER_TILE = 256


def owner_grads(section_id, left_mats, right_mats):
    rows, left_width = left_mats[0].shape
    right_width = right_mats[0].shape[1]
    tiles = left_width // OWNER_TILE

    def kernel(place, *refs):
        out_ref = refs[8]
        expert, tile = pl.program_id(0), pl.program_id(1)
        first = place[0] == 0
        for source, here in enumerate(
            (
                first & (expert == 0),
                first & (expert == 1),
                ~first & (expert == 1),
                ~first & (expert == 0),
            )
        ):

            @pl.when(here)
            def _():
                left = refs[source][:, pl.ds(tile * OWNER_TILE, OWNER_TILE)]
                out_ref[0] = product_tn(left, refs[4 + source][...])

    whole = [
        pl.BlockSpec(mat.shape, lambda expert, tile: (0, 0))
        for mat in (*left_mats, *right_mats)
    ]
    return pl.pallas_call(
        kernel,
        out_shape=jax.ShapeDtypeStruct((2, left_width, right_width), jnp.float32),
        grid=(2, tiles),
        in_specs=[pl.BlockSpec(memory_space=pltpu.SMEM)] + whole,
        out_specs=pl.BlockSpec((1, OWNER_TILE, right_width), lambda expert, tile: (expert, tile, 0)),
        compiler_params=pltpu.CompilerParams(vmem_limit_bytes=40 << 20),
        name="owner_grads",
    )(section_id.reshape(1), *left_mats, *right_mats)


def statistics(value_rows):
    centre = jnp.mean(value_rows, axis=-1, keepdims=True)
    centred = value_rows - centre
    variance = jnp.mean(centred * centred, axis=-1, keepdims=True)
    spread_inverse = lax.rsqrt(variance + 1e-05)
    return centred * spread_inverse, spread_inverse


def column_sums(value_rows):
    return jnp.sum(value_rows, axis=0, keepdims=True)


def block_sum(blocks_ref):
    total = blocks_ref[0].astype(jnp.float32)
    for place in range(1, blocks_ref.shape[0]):
        total = total + blocks_ref[place].astype(jnp.float32)
    return total


def call(kernel, name, outs, *operands):
    return pl.pallas_call(
        kernel,
        out_shape=[jax.ShapeDtypeStruct(shape, dtype) for shape, dtype in outs],
        compiler_params=pltpu.CompilerParams(vmem_limit_bytes=32 << 20),
        name=name,
    )(*operands)


def project(mixed_blocks, proj_mat, layer_in, gain, shift):
    def kernel(mixed_ref, proj_ref, in_ref, gain_ref, shift_ref, rows_ref, res_ref, mid_ref, sq_ref):
        places = mixed_ref.shape[0]
        mixed = jnp.concatenate([mixed_ref[place] for place in range(places)], axis=1)
        rows_ref[...] = mixed
        branch = product(mixed, proj_ref[...])
        residual = in_ref[...].astype(jnp.float32) + branch
        res_ref[...] = residual
        mid_ref[...] = low(statistics(residual)[0] * gain_ref[...] + shift_ref[...])
        sq_ref[...] = column_sums(branch * branch)

    rows, width = layer_in.shape
    outs = [((rows, width), jnp.bfloat16), ((rows, width), jnp.float32)]
    outs += [((rows, width), jnp.bfloat16), ((1, width), jnp.float32)]
    return call(kernel, "project", outs, mixed_blocks, proj_mat, layer_in, gain, shift)


def layer_end(branch_blocks, residual, gain, shift):
    def kernel(blocks_ref, res_ref, gain_ref, shift_ref, out_ref, normed_ref, sq_ref):
        branch = block_sum(blocks_ref)
        layer_out = res_ref[...] + branch
        rounded = low(layer_out)
        out_ref[...] = rounded
        normed = statistics(rounded.astype(jnp.float32))[0]
        normed_ref[...] = low(normed * gain_ref[...] + shift_ref[...])
        sq_ref[0:1] = column_sums(branch * branch)
        sq_ref[1:2] = column_sums(layer_out * layer_out)

    shape = residual.shape
    outs = [(shape, jnp.bfloat16), (shape, jnp.bfloat16), ((2, shape[1]), jnp.float32)]
    return call(kernel, "layer_end", outs, branch_blocks, residual, gain, shift)


def norm_back(blocks_ref, value_ref, gain_ref, grad_ref, gain_grad_ref, shift_grad_ref):
    d_normed = block_sum(blocks_ref)
    normed, spread_inverse = statistics(value_ref[...].astype(jnp.float32))
    gain_grad_ref[...] = column_sums(d_normed * normed)
    shift_grad_ref[...] = column_sums(d_normed)
    d_centred = d_normed * gain_ref[...]
    along = jnp.mean(d_centred * normed, axis=-1, keepdims=True)
    d_value = d_centred - jnp.mean(d_centred, axis=-1, keepdims=True) - normed * along
    return grad_ref[...].astype(jnp.float32) + d_value * spread_inverse


def mid_back(mid_blocks, residual, gain, grad_out, proj_mat, dp_size):
    def kernel(blocks_ref, res_ref, gain_ref, grad_ref, proj_ref, *outs):
        sum_ref, low_ref, mixed_ref, gain_grad_ref, shift_grad_ref = outs
        grad = norm_back(blocks_ref, res_ref, gain_ref, grad_ref, gain_grad_ref, shift_grad_ref)
        sum_ref[...] = grad
        low_ref[...] = low(grad)
        d_mixed = low(product_nt(low(grad), proj_ref[...]))
        part = d_mixed.shape[1] // dp_size
        for place in range(dp_size):
            mixed_ref[place] = d_mixed[:, place * part : (place + 1) * part]

    rows, width = residual.shape
    row = ((1, width), jnp.float32)
    outs = [((rows, width), jnp.float32), ((rows, width), jnp.bfloat16)]
    outs += [((dp_size, rows, width // dp_size), jnp.bfloat16), row, row]
    return call(kernel, "mid_back", outs, mid_blocks, residual, gain, grad_out, proj_mat)


def input_back(in_blocks, layer_in, gain, grad_resid):
    def kernel(blocks_ref, in_ref, gain_ref, grad_ref, sum_ref, low_ref, gain_grad_ref, shift_grad_ref):
        grad = norm_back(blocks_ref, in_ref, gain_ref, grad_ref, gain_grad_ref, shift_grad_ref)
        sum_ref[...] = grad
        low_ref[...] = low(grad)

    shape = layer_in.shape
    row = ((1, shape[1]), jnp.float32)
    outs = [(shape, jnp.float32), (shape, jnp.bfloat16), row, row]
    return call(kernel, "input_back", outs, in_blocks, layer_in, gain, grad_resid)


LANES = 128


def pack_small(parts_of_layers, squares_of_layers, weight_rows):
    layers = len(parts_of_layers)
    flat = [part for parts in parts_of_layers for part in parts] + list(squares_of_layers)
    width = flat[0].shape[1]
    used = sum(part.shape[0] for part in parts_of_layers[0])
    height = -(-(used + 1) // 8) * 8
    places = width // weight_rows

    def kernel(*refs):
        out_ref, rows_ref = refs[-2], refs[-1]
        per_layer = len(parts_of_layers[0])
        for layer in range(layers):
            rows_ref[...] = jnp.zeros(rows_ref.shape, jnp.float32)
            start = 0
            for part in refs[layer * per_layer : (layer + 1) * per_layer]:
                rows_ref[start : start + part.shape[0]] = part[...]
                start = start + part.shape[0]
            lane = lax.broadcasted_iota(jnp.int32, (1, width), 1) % LANES
            marked = jnp.zeros((1, width), jnp.float32)
            sums = jnp.sum(refs[layers * per_layer + layer][...], axis=1, keepdims=True)
            for kind in range(3):
                marked = jnp.where(lane == kind, sums[kind : kind + 1], marked)
            rows_ref[start : start + 1] = marked
            for place in range(places):
                column = place * weight_rows // LANES * LANES
                out_ref[layer * places + place] = rows_ref[:, column : column + LANES]

    return pl.pallas_call(
        kernel,
        out_shape=jax.ShapeDtypeStruct((layers * places, height, LANES), jnp.float32),
        scratch_shapes=[pltpu.VMEM((height, width), jnp.float32)],
        name="pack_small",
    )(*flat)


def other_core(block):
    return lax.ppermute(block, SEC, [(0, 1), (1, 0)])


def both_cores(block):
    return jnp.concatenate([block, other_core(block)], axis=0)


def halves_for_cores(block, section_id):
    half = block.shape[1] // 2
    kept = lax.dynamic_slice_in_dim(block, section_id * half, half, axis=1)
    sent = lax.dynamic_slice_in_dim(block, (1 - section_id) * half, half, axis=1)
    return jnp.concatenate([kept, other_core(sent)], axis=0)


def shards(
    inputs,
    cotangent,
    segment_ids,
    routes,
    norm_gains,
    norm_shifts,
    attn_qkv,
    attn_proj,
    dense_up,
    dense_down,
    router,
    mixer,
    expert_up,
    expert_down,
):
    sections = lax.axis_size(SEC)
    groups = lax.axis_size(EX)
    dp_size = lax.axis_size(DP)
    section_id = lax.axis_index(SEC)
    expert_id = lax.axis_index(EX)
    micro_count = inputs.shape[0]
    seq_rows = inputs.shape[2]
    width = inputs.shape[3]
    full_len = segment_ids.shape[2]
    experts_total = router.shape[2]
    hidden_rows = dense_down.shape[1]
    weight_rows = attn_qkv.shape[1]
    heads_here = HEADS // dp_size
    head_width = heads_here * HEAD_DIM
    capacity = max(2, 5 * seq_rows // (4 * experts_total))
    slots = dp_size * capacity
    devices = sections * groups * dp_size

    small_parts = jnp.concatenate([norm_gains[0], norm_shifts[0], router[0].T, mixer[0].T], axis=0)
    small_count = small_parts.shape[0]
    route_row = low(routes[0, :, 0, :, 0])
    message = jnp.concatenate([small_parts.reshape(-1), route_row.reshape(-1)])
    filled = message.shape[0]
    padded = -(-filled // 1024) * 1024
    message = jnp.pad(message, (0, padded - filled)).reshape(padded // 128, 128)

    def expert_parts(*own_layers):
        return [
            (
                lax.dynamic_index_in_dim(own_layer, section_id, 0, keepdims=False),
                lax.dynamic_index_in_dim(own_layer, 1 - section_id, 0, keepdims=False),
            )
            for own_layer in own_layers
        ]

    hidden_here = groups * hidden_rows
    small_all, (proj_rows, up_parts) = beside(
        lambda blocks: exchange(blocks, EVERY),
        jnp.broadcast_to(message[None], (devices,) + message.shape),
        lambda proj_shard, up_cols: (
            in_order(permute_copies(proj_shard, DP), DP),
            own_parts(
                up_cols.reshape(weight_rows, groups, dp_size, hidden_rows)
                .transpose(2, 0, 1, 3)
                .reshape(dp_size, weight_rows, hidden_here),
                DP,
            ),
        ),
        (attn_proj[0], dense_up[0]),
    )
    small_all = small_all.reshape(sections, groups, dp_size, padded)

    def params_of(small_all):
        params_all = small_all[..., : small_count * weight_rows].reshape(
            sections, groups * dp_size, small_count, weight_rows
        )
        return params_all.transpose(0, 2, 1, 3).reshape(sections, small_count, width)

    def routes_of(small_all):
        routes_all = lax.dynamic_index_in_dim(
            small_all[..., small_count * weight_rows : filled], expert_id, 1, keepdims=False
        ).reshape(sections, dp_size, micro_count, seq_rows)
        routes_all = lax.dynamic_index_in_dim(routes_all, section_id, 2, keepdims=False)
        return routes_all.astype(jnp.int32)

    on_first = section_id == 0

    def by_layer(pair):
        of_own_layer, of_other_layer = pair
        return (
            jnp.where(on_first, of_own_layer, of_other_layer),
            jnp.where(on_first, of_other_layer, of_own_layer),
        )

    proj_both = lax.all_gather(proj_rows.reshape(-1, width), HOMES, axis=0, tiled=True)
    proj_both = proj_both.reshape(sections, width, width)
    qkv_cols = attn_qkv[0].reshape(weight_rows, 3, dp_size, head_width).transpose(2, 0, 1, 3)
    qkv_cols, small_all = lax.optimization_barrier(
        (qkv_cols.reshape(dp_size, weight_rows, 3 * head_width), small_all)
    )
    qkv_cols, expert_weights = beside(
        over_dp, qkv_cols, expert_parts, (expert_up[0], expert_down[0])
    )
    params_all = params_of(small_all)
    routes_all = routes_of(small_all)
    own_input = lax.dynamic_index_in_dim(inputs[:, 0], section_id, 0, keepdims=False)
    first_params = params_all[0].astype(jnp.float32)
    first_normed = low(
        layer_norm(own_input.astype(jnp.float32), first_params[0:1], first_params[2:3])
    )
    qkv_own, (first_seq, up_rows) = beside(
        lambda blocks: exchange(blocks, EX),
        jnp.broadcast_to(qkv_cols[None], (groups,) + qkv_cols.shape),
        lambda rows, *parts: (
            in_order(permute_copies(rows, DP), DP),
            in_order(sent_parts(parts, DP), DP),
        ),
        (first_normed, *up_parts),
    )
    first_seq = first_seq.reshape(full_len, width)
    qkv_own = qkv_own.reshape(width, 3 * head_width)
    qkv_pair = (qkv_own, other_core(qkv_own))
    exp_up_pair, exp_down_pair = [(kept, other_core(sent)) for kept, sent in expert_weights]
    first_qkv = low(product(first_seq, by_layer(qkv_pair)[0]))
    up_both = lax.all_gather(up_rows.reshape(-1, hidden_here), HOMES, axis=0, tiled=True)
    up_both = up_both.reshape(sections, width, hidden_here)
    down_both = lax.all_gather(dense_down[0], HOMES, axis=0, tiled=True)
    down_both = down_both.reshape(sections, hidden_here, width)

    segments = lax.dynamic_index_in_dim(segment_ids[:, 0], section_id, 0, keepdims=False)
    places = jnp.arange(full_len, dtype=jnp.int32)
    earlier = (places[None, :] < places[:, None]) & (
        places[None, :] // seq_rows == places[:, None] // seq_rows
    )

    def slot_table(route_now):
        rank = jnp.sum(
            ((route_now[:, None] == route_now[None, :]) & earlier).astype(jnp.int32), axis=1
        )
        home = route_now % sections * groups + route_now // sections
        target = home * slots + places // seq_rows * capacity + rank
        slot_ids = jnp.arange(sections * groups * slots, dtype=jnp.int32)
        table = low(slot_ids[:, None] == target[None, :])
        hot = route_now[:, None] == jnp.arange(experts_total, dtype=jnp.int32)[None, :]
        return table, hot.astype(jnp.float32)

    def packed_rows(token_rows, table):
        return low(product(table, token_rows)).reshape(sections * groups, slots, width)

    def coefficients(mid_seq, small_weights, hot):
        small_logits = product_nt(mid_seq, small_weights)
        gate_probs = jax.nn.softmax(small_logits[:, :experts_total], axis=-1)
        gate = jnp.sum(gate_probs * hot, axis=-1, keepdims=True)
        coef = jax.nn.softmax(small_logits[:, experts_total:], axis=-1)
        return gate_probs, gate, coef

    def dense_in(mid_seq, up_mat):
        hidden = product(mid_seq, up_mat)
        return hidden, low(gelu_tanh(hidden))

    def attended(qkv):
        return attention(segments, qkv).reshape(dp_size, seq_rows, head_width)

    def forward_zero():
        params = first_params
        table, hot = slot_table(routes_all[0].reshape(full_len))
        mixed, residual, mid, attn_squares = project(
            over_dp(attended(first_qkv)), proj_both[0], own_input, params[1:2], params[3:4]
        )
        mid_seq = gather_rows(mid)
        small_weights = params_all[0, 4:]
        exp_up_mat, exp_down_mat = by_layer(exp_up_pair)[0], by_layer(exp_down_pair)[0]

        expert_rows, (gate_probs, gate, coef) = beside(
            over_homes,
            packed_rows(mid_seq, table),
            lambda mid_seq, small_weights: coefficients(mid_seq, small_weights, hot),
            (mid_seq, small_weights),
        )
        expert_rows = expert_rows.reshape(-1, width)
        exp_hidden = product(expert_rows, exp_up_mat)
        exp_hidden_low = low(gelu_tanh(exp_hidden))

        def return_work(mid_seq, up_mat, down_mat):
            hidden, hidden_low = dense_in(mid_seq, up_mat)
            return hidden, hidden_low, product(hidden_low, down_mat)

        returned, (hidden, hidden_low, dense_part) = beside(
            over_homes,
            low(product(exp_hidden_low, exp_down_mat)).reshape(-1, slots, width),
            return_work,
            (mid_seq,),
            (up_both[0], down_both[0]),
        )
        expert_part = product_tn(table, returned.reshape(-1, width))
        branch_part = coef[:, 0:1] * dense_part + coef[:, 1:2] * gate * expert_part
        branch, settled = beside(
            over_dp,
            row_blocks(branch_part),
            lambda *pairs: [by_layer(pair) for pair in pairs],
            (qkv_pair, exp_up_pair, exp_down_pair),
        )
        next_params = params_all[1].astype(jnp.float32)
        out_low, next_normed, squares = layer_end(
            branch, residual, next_params[0:1], next_params[2:3]
        )
        record = SimpleNamespace(
            params=params,
            small_weights=small_weights,
            table=table,
            hot=hot,
            layer_in=own_input,
            normed_seq=first_seq,
            qkv=first_qkv,
            mixed=mixed,
            residual=residual,
            mid_seq=mid_seq,
            expert_rows=expert_rows,
            gate_probs=gate_probs,
            gate=gate,
            coef=coef,
            hidden=hidden,
            hidden_low=hidden_low,
            dense_part=dense_part,
            exp_hidden=exp_hidden,
            exp_hidden_low=exp_hidden_low,
            expert_part=expert_part,
        )
        squares = jnp.concatenate([attn_squares, squares], axis=0)
        return out_low, next_normed, squares, record, settled

    def forward_one(layer_in, normed):
        params = params_all[1].astype(jnp.float32)
        table, hot = slot_table(routes_all[1].reshape(full_len))
        normed_seq = gather_rows(normed)
        qkv = low(product(normed_seq, qkv_both[1]))
        mixed, residual, mid, attn_squares = project(
            over_dp(attended(qkv)), proj_both[1], layer_in, params[1:2], params[3:4]
        )
        mid_seq = gather_rows(mid)
        grad_seqs = lax.all_gather(after(cotangent[:, 0], mid_seq), DP, axis=1, tiled=True)
        own_grad_seq = lax.dynamic_index_in_dim(grad_seqs, section_id, 0, keepdims=False)
        small_weights = params_all[1, 4:]

        def dispatch_work(mid_seq, small_weights, up_mat):
            return coefficients(mid_seq, small_weights, hot), dense_in(mid_seq, up_mat)

        expert_rows, ((gate_probs, gate, coef), (hidden, hidden_low)) = beside(
            over_homes,
            packed_rows(mid_seq, table),
            dispatch_work,
            (mid_seq, small_weights, up_both[1]),
        )
        expert_rows = expert_rows.reshape(-1, width)
        exp_hidden = product(expert_rows, exp_up_both[1])
        exp_hidden_low = low(gelu_tanh(exp_hidden))
        returned, dense_part = beside(
            over_homes,
            low(product(exp_hidden_low, exp_down_both[1])).reshape(-1, slots, width),
            product,
            (hidden_low, down_both[1]),
        )
        expert_part = product_tn(table, returned.reshape(-1, width))
        branch_part = coef[:, 0:1] * dense_part + coef[:, 1:2] * gate * expert_part
        branch = lax.psum_scatter(low(branch_part), DP, scatter_dimension=0, tiled=True)
        record = SimpleNamespace(
            params=params,
            small_weights=small_weights,
            table=table,
            hot=hot,
            layer_in=layer_in,
            normed_seq=normed_seq,
            qkv=qkv,
            mixed=mixed,
            residual=residual,
            mid_seq=mid_seq,
            expert_rows=expert_rows,
            gate_probs=gate_probs,
            gate=gate,
            coef=coef,
            hidden=hidden,
            hidden_low=hidden_low,
            dense_part=dense_part,
            exp_hidden=exp_hidden,
            exp_hidden_low=exp_hidden_low,
            expert_part=expert_part,
        )
        return branch, attn_squares, record, own_grad_seq

    def over_expert(grad_mat):
        return lax.psum_scatter(grad_mat, EX, scatter_dimension=0, tiled=True)

    def by_rows(grad_mat, count):
        return low(grad_mat).reshape(count, -1, grad_mat.shape[-1])

    def shared_product(left_mat, right_mat):
        return low(
            product_tn(both_cores(left_mat), halves_for_cores(right_mat, section_id))
        )

    def dp_blocks(*grad_mats):
        blocks = [by_rows(grad_mat, dp_size) for grad_mat in grad_mats]
        return own_parts(jnp.concatenate(blocks, axis=2), DP)

    half_hidden, half_width = hidden_here // 2, width // 2

    def backward_layer(layer, grad_low, grad_seq, record, sums_one=(), operands_one=None, settle=()):
        params = record.params
        coef, gate, table = record.coef, record.gate, record.table
        grad_seq = grad_seq.astype(jnp.float32)
        d_expert = low(coef[:, 1:2] * gate * grad_seq)

        def dense_back(grad_seq, coef, down_mat, up_mat, *sums_one):
            early = dp_blocks(*sums_one) if sums_one else ()
            d_dense = low(coef[:, 0:1] * grad_seq)
            dense_dot = jnp.sum(grad_seq * record.dense_part, axis=-1, keepdims=True)
            expert_dot = jnp.sum(grad_seq * record.expert_part, axis=-1, keepdims=True)
            d_coef = jnp.concatenate([dense_dot, gate * expert_dot], axis=1)
            d_mix = coef * (d_coef - jnp.sum(coef * d_coef, axis=-1, keepdims=True))
            d_logits = record.gate_probs * (record.hot - gate) * (coef[:, 1:2] * expert_dot)
            d_small = low(jnp.concatenate([d_logits, d_mix], axis=1))
            d_up = low(gelu_grad(record.hidden, product_nt(d_dense, down_mat)))
            d_mid_part = product_nt(d_up, up_mat) + product(d_small, record.small_weights)
            return d_dense, d_small, d_up, d_mid_part, early

        expert_grad_rows, (d_dense, d_small, d_up, d_mid_part, early) = beside(
            over_homes,
            packed_rows(d_expert, table),
            dense_back,
            (grad_seq, coef, down_both[layer], up_both[layer]),
            tuple(sums_one),
        )
        expert_grad_rows = expert_grad_rows.reshape(-1, width)
        d_exp_hidden = low(
            gelu_grad(record.exp_hidden, product_nt(expert_grad_rows, exp_down_both[layer]))
        )
        expert_operands = (
            record.expert_rows,
            d_exp_hidden,
            record.exp_hidden_low,
            expert_grad_rows,
        )

        swapped = tuple(other_core(operand) for operand in expert_operands)

        def owner_mats(index):
            return (
                expert_operands[index],
                swapped[index],
                operands_one[0][index],
                operands_one[1][index],
            )

        def dense_grads(hidden_low, d_dense, mid_seq, d_up, d_small):
            g_dense = [shared_product(mid_seq, d_up), shared_product(hidden_low, d_dense)]
            g_small = product_tn(d_small, mid_seq)
            return jnp.concatenate(g_dense, axis=1), g_small

        expert_back = low(product_nt(d_exp_hidden, exp_up_both[layer])).reshape(-1, slots, width)
        if layer == 0:
            returned, (parts_one, g_exp_down) = beside(
                over_homes,
                expert_back,
                lambda early, *mats: (sent_parts(early, DP), owner_grads(section_id, *mats)),
                (early, owner_mats(2), owner_mats(3)),
            )
        else:
            returned = over_homes(expert_back)
        d_mid_part = d_mid_part + product_tn(table, returned.reshape(-1, width))
        mid_blocks, operands = lax.optimization_barrier(
            (
                row_blocks(d_mid_part),
                (record.hidden_low, d_dense, record.mid_seq, d_up, d_small),
            )
        )
        g_dense, g_small = dense_grads(*operands)
        dense_sum = over_expert(g_dense)
        d_mid, g_dense, g_small = lax.optimization_barrier(
            (over_dp(mid_blocks), g_dense, g_small)
        )
        d_resid, d_attn, d_mixed, d_gain_one, d_shift_one = mid_back(
            d_mid, record.residual, params[1:2], grad_low, proj_both[layer], dp_size
        )
        d_mixed, g_proj = beside(over_dp, d_mixed, shared_product, (record.mixed, d_attn))
        d_qkv = attention_back(segments, record.qkv, d_mixed.reshape(full_len, head_width))

        in_blocks, normed_seq, d_qkv = lax.optimization_barrier(
            (row_blocks(product_nt(d_qkv, qkv_both[layer])), record.normed_seq, d_qkv)
        )
        g_attn = jnp.concatenate([g_proj, shared_product(normed_seq, d_qkv)], axis=1)
        attn_sum = over_expert(g_attn)
        beside_it = (g_attn, settle)
        d_normed, beside_it = lax.optimization_barrier((over_dp(in_blocks), beside_it))
        def finish(in_blocks):
            return input_back(in_blocks, record.layer_in, params[0:1], d_resid)

        up_moved = None
        if layer == 0:
            up_moved, finished = beside(
                over_dp, by_rows(dense_sum[:, :half_hidden], dp_size), finish, (), (d_normed,)
            )
        else:
            finished = finish(d_normed)
        d_input, d_input_low, d_gain_zero, d_shift_zero = finished
        small_grads = (d_gain_zero, d_gain_one, d_shift_zero, d_shift_one, g_small)
        if layer == 0:
            extra = (parts_one, owner_mats, g_exp_down, up_moved)
        else:
            extra = (expert_operands, swapped, beside_it[1])
        return d_input, d_input_low, (dense_sum, attn_sum), small_grads, extra

    own_grad = lax.dynamic_index_in_dim(cotangent[:, 0], section_id, 0, keepdims=False)
    out_zero, next_normed, squares_zero, record_zero, settled = forward_zero()
    qkv_both, exp_up_both, exp_down_both = settled
    branch_one, attn_squares_one, record_one, own_grad_seq = forward_one(out_zero, next_normed)
    grad_one, grad_one_low, sums_one, small_one, operands_one = backward_layer(
        1, own_grad, own_grad_seq, record_one, settle=branch_one
    )
    dense_one, attn_one = sums_one
    branch_one = operands_one[2].astype(jnp.float32)
    out_one = record_one.residual + branch_one
    squares_one = jnp.concatenate(
        [attn_squares_one, column_sums(branch_one * branch_one), column_sums(out_one * out_one)]
    )
    out_one = low(out_one)
    grad_zero, _, (dense_zero, attn_zero), small_zero, extra = backward_layer(
        0,
        grad_one_low,
        gather_rows(grad_one_low),
        record_zero,
        (dense_one[:, :half_hidden], attn_one),
        operands_one,
    )
    parts_one, owner_mats, grad_exp_down, up_zero = extra

    moved_one = in_order(after(parts_one, grad_zero), DP)
    small_message = pack_small(
        (small_zero, small_one), (squares_zero, squares_one), weight_rows
    )
    small_moved, grad_exp_up = beside(
        lambda blocks: exchange(blocks, EVERY),
        small_message,
        lambda *mats: owner_grads(section_id, *mats),
        (owner_mats(0), owner_mats(1)),
    )
    attn_zero = over_dp(by_rows(attn_zero, dp_size))
    up_one, attn_one = moved_one[..., :half_hidden], moved_one[..., half_hidden:]
    down_zero, down_one = dense_zero[:, half_hidden:], dense_one[:, half_hidden:]

    def of_both(of_zero, of_one):
        return of_zero, other_core(of_zero), of_one, other_core(of_one)

    grad_qkv, grad_proj, grad_up, grad_down = finish_weights(
        section_id,
        of_both(up_zero, up_one),
        of_both(attn_zero, attn_one),
        of_both(down_zero, down_one),
        hidden_rows,
    )
    activations, input_grads = finish_rows(
        section_id, of_both(out_zero, out_one), of_both(grad_zero, grad_one)
    )
    small_sum = jnp.sum(small_moved, axis=0)
    place = expert_id * dp_size + lax.axis_index(DP)
    sums = lax.dynamic_slice_in_dim(
        small_sum[:small_count], place * weight_rows % LANES, weight_rows, axis=1
    )
    totals = small_sum[small_count, :3]
    element_count = micro_count * seq_rows * width * groups * dp_size
    branch_rms = jnp.sqrt(totals / element_count)[None]
    return (
        activations[None, :, None],
        input_grads[None, :, None],
        sums[None, 0:2],
        sums[None, 2:4],
        grad_qkv[None],
        grad_proj[None],
        grad_up[None],
        grad_down[None],
        sums[4 : 4 + experts_total].T[None],
        sums[4 + experts_total :].T[None],
        grad_exp_up[None],
        grad_exp_down[None],
        branch_rms,
    )


def solution(mesh):
    placed = (
        P(None, EX, DP, None),
        P(None, EX, DP, None),
        P(None, EX, None),
        P(SEC, None, EX, DP, None),
        P(SEC, None, (EX, DP)),
        P(SEC, None, (EX, DP)),
        P(SEC, (EX, DP), None),
        P(SEC, (EX, DP), None),
        P(SEC, (EX, DP), None),
        P(SEC, (EX, DP), None),
        P(SEC, (EX, DP), None),
        P(SEC, (EX, DP), None),
        P(SEC, EX, None, DP),
        P(SEC, EX, DP, None),
    )
    return jax.shard_map(
        shards,
        mesh=mesh,
        in_specs=placed,
        out_specs=(
            P(SEC, None, EX, DP, None),
            P(SEC, None, EX, DP, None),
            P(SEC, None, (EX, DP)),
            P(SEC, None, (EX, DP)),
            P(SEC, (EX, DP), None),
            P(SEC, (EX, DP), None),
            P(SEC, (EX, DP), None),
            P(SEC, (EX, DP), None),
            P(SEC, (EX, DP), None),
            P(SEC, (EX, DP), None),
            P(SEC, EX, None, DP),
            P(SEC, EX, DP, None),
            P(SEC, None),
        ),
        check_vma=False,
    )
```

time: 935 us -> 602 us (0.64)
  blocking collectives: 218 us -> 76.5 us
  waiting for transfers between devices: 268 us -> 149 us
  starting transfers between devices: 170 us -> 115 us
  matrix products: 136 us -> 84 us
  Pallas kernels: 0 us -> 45.2 us
  other arithmetic: 53.8 us -> 33.6 us
  between operations: 4.01 us -> 15.9 us
    all_to_all x41 -> x22, waiting for transfers between devices: 268 us -> 122 us  [exchange(): return lax.all_to_all(blocks, axes, split_axis=0, concat_axis=0, tiled=True)]
    all_to_all x14 -> x1, blocking collectives: 122 us -> 11 us  [exchange(): return lax.all_to_all(blocks, axes, split_axis=0, concat_axis=0, tiled=True)]
    all_to_all x41 -> x22, starting transfers between devices: 167 us -> 87.7 us  [exchange(): return lax.all_to_all(blocks, axes, split_axis=0, concat_axis=0, tiled=True)]
    pallas_call x0 -> x20, Pallas kernels: none -> 45.2 us  [the longest x2 16.4 us: owner_grads(): pl.pallas_call(kernel, out_shape=jax.ShapeDtypeStruct((2, left_width, rig...]
    all_gather x6 -> x4, blocking collectives: 96.1 us -> 65.5 us  [gather_rows(): return lax.all_gather(block, DP, axis=0, tiled=True)]
    another operation x16 -> x4, other arithmetic: 23.6 us -> 0.05 us  [the longest x9 17.6 us: to_owner(): return exchange(jnp.stack([layer_zero, layer_one]), 'section')]
    ppermute x16 -> x49, starting transfers between devices: 3.56 us -> 26.7 us  [the longest x6 10.8 us: permute_copies(): blocks.append(lax.ppermute(block, axis, route))]
    ppermute x16 -> x49, waiting for transfers between devices: 0.54 us -> 22 us  [the longest x6 11.1 us: permute_copies(): blocks.append(lax.ppermute(block, axis, route))]
  transfers between devices with their start and end apart: 57 -> 80, of which waited for: 36 -> 28; matrix products, arithmetic and copies ran while one was open for 21% -> 24% of each run, Pallas kernels for 0% -> 6%
where the time goes in v2:
time: 602 us; the launch traced here: 591 us
  waiting for transfers between devices  149 us (25%)
  starting transfers between devices  115 us (19%)
  matrix products  84 us (14%)
  blocking collectives  76.5 us (13%)
  local copies, waits for them, and re-layouts  71.8 us (12%)
  Pallas kernels  45.2 us (8%)
  other arithmetic  33.6 us (6%)
  between operations  15.9 us (3%)
    all_to_all x22, waiting for transfers between devices, exchange(): return lax.all_to_all(blocks, axes, split_axis=0, concat_axis=0, tiled=True)  122 us
    all_to_all x22, starting transfers between devices, exchange(): return lax.all_to_all(blocks, axes, split_axis=0, concat_axis=0, tiled=True)  87.7 us
    all_gather x4, blocking collectives, gather_rows(): return lax.all_gather(block, DP, axis=0, tiled=True)  65.5 us
    dot_general x16, matrix products, product(): return jnp.dot(left_mat, right_mat, preferred_element_type=jnp.float32)  35.4 us
    unnamed x238, local copies, waits for them, and re-layouts  28.9 us
    dot_general x14, matrix products, product_tn(): lax.dot_general(left_mat, right_mat, (((0,), (0,)), ((), ())), preferred_...  26.4 us
    dot_general x12, matrix products, product_nt(): lax.dot_general(left_mat, right_mat, (((1,), (1,)), ((), ())), preferred_...  22.3 us
    pallas_call x2, Pallas kernels, owner_grads(): pl.pallas_call(kernel, out_shape=jax.ShapeDtypeStruct((2, left_width, rig...  16.4 us
  transfers between devices with their start and end apart: 80, of which 28 were waited for; matrix products, arithmetic and copies ran while one was open for 24% of the time, Pallas kernels for 6%

profile of v2, /device:TPU:0, one launch (start us, length us, event | category | flops | bytes accessed | tf_op | source)
XLA Modules:
  0.0 590.6 jit_solution(6039035152698873985)
XLA Ops:
  10.2 3.0 collective-permute-start
  25.5 5.1 all-to-all-done
  32.7 3.5 all-to-all-start.1
  37.9 7.1 %dynamic-slice_bitcast_fusion = (bf16[1024,1024]{1,0:T(8,128)(2,1)}, bf16[1024,1024]{1,0:T(8,128)(2,1)}, bf16[1024,1024]{1,0:T(8,128)(2,1)}, bf16[1024,1024]{1,0:T(8,128)(2,1)}) fusion(bf16[2,1024,1024]{2,1,0:T(8,128)(2,1)} %bitcast.221, s32[]{:T(128)S(6)} %select_n.221, s32[]{:T(128)S(6)} %select_n.217, bf16[2,1024,1024]{2,1,0:T(8,128)(2,1)} %bitcast.222), kind=kLoop, calls=%fused_computation.8 | loop fusion | bytes 16777224 | tf_op jit(solution)/shard_map/jit(dynamic_index_in_dim)/squeeze | solution.py:542
  45.0 3.0 all-to-all-done.1
  49.3 3.6 all-to-all-start.2
  61.8 7.1 %collective-permute-done.4.refs_2_ = bf16[64,1024]{1,0:T(8,128)(2,1)S(1)} collective-permute-done((bf16[64,1024]{1,0:T(8,128)(2,1)S(1)}, bf16[64,1024]{1,0:T(8,128)(2,1)S(1)}, u32[]{:S(2)}, u32[]{:S(2)}) %collective-permute-start.4) | collective-permute-done | bytes 131104 | tf_op jit(solution)/shard_map/ppermute | solution.py:95
  69.7 6.6 %collective-permute-done.7.refs_2_ = bf16[64,1024]{1,0:T(8,128)(2,1)S(1)} collective-permute-done((bf16[64,1024]{1,0:T(8,128)(2,1)}, bf16[64,1024]{1,0:T(8,128)(2,1)S(1)}, u32[]{:S(2)}, u32[]{:S(2)}) %collective-permute-start.7) | collective-permute-done | bytes 131104 | tf_op jit(solution)/shard_map/ppermute | solution.py:111
  87.7 3.5 all-to-all-start.3
  91.2 4.8 slice_bitcast_fusion.1
  96.0 4.0 fusion.169
  101.2 17.0 %all_gather.25 = bf16[256,1024]{1,0:T(8,128)(2,1)S(1)} all-gather(bf16[64,1024]{1,0:T(8,128)(2,1)S(1)} %get-tuple-element.238), channel_id=1, replica_groups=mesh['section'=2,'expert'=4,'dp'=4] {'dp'}, dimensions={0}, use_global_device_ids=true | all-gather | bytes 655360 | tf_op jit(solution)/shard_map/all_gather | solution.py:62
  119.3 4.4 all-to-all-start.4
  125.8 15.1 %all-to-all-done.4 = bf16[8,40,1024]{2,1,0:T(8,128)(2,1)S(1)} async-done(((bf16[8,40,1024]{2,1,0:T(8,128)(2,1)}), bf16[8,40,1024]{2,1,0:T(8,128)(2,1)S(1)}, u32[]{:S(2)}, u32[]{:S(2)}) %all-to-all-start.4) | async-done | bytes 655392 | tf_op jit(solution)/shard_map/all_to_all | solution.py:53
  140.9 3.8 multiply_convert_fusion.1
  146.5 4.2 all-to-all-start.5
  150.8 3.7 fusion.52
  157.0 4.4 all-to-all-done.5
  161.4 3.1 add_convert_fusion.1
  164.5 4.6 all-to-all-start.6
  169.1 4.6 broadcast_select_fusion.2
  173.7 3.5 broadcast_select_fusion.4
  177.2 3.8 broadcast_select_fusion
  181.1 3.1 all-to-all-done.6.blocks_ref
  185.5 16.5 %all_gather.28 = bf16[256,1024]{1,0:T(8,128)(2,1)} all-gather(bf16[64,1024]{1,0:T(8,128)(2,1)S(1)} %get-tuple-element.264), channel_id=1, replica_groups=mesh['section'=2,'expert'=4,'dp'=4] {'dp'}, dimensions={0}, use_global_device_ids=true | all-gather | bytes 655360 | tf_op jit(solution)/shard_map/all_gather | solution.py:62
  207.2 3.3 all-to-all-start.7
  210.5 4.7 fusion.168
  219.9 15.9 %all_gather.29 = bf16[256,1024]{1,0:T(8,128)(2,1)S(1)} all-gather(bf16[64,1024]{1,0:T(8,128)(2,1)S(1)} %get-tuple-element.267), channel_id=1, replica_groups=mesh['section'=2,'expert'=4,'dp'=4] {'dp'}, dimensions={0}, use_global_device_ids=true | all-gather | bytes 655360 | tf_op jit(solution)/shard_map/all_gather | solution.py:62
  237.4 4.2 all-to-all-start.8
  242.2 3.8 fusion.60
  246.0 6.3 %all-to-all-done.8 = bf16[8,40,1024]{2,1,0:T(8,128)(2,1)} async-done(((bf16[8,40,1024]{2,1,0:T(8,128)(2,1)}), bf16[8,40,1024]{2,1,0:T(8,128)(2,1)}, u32[]{:S(2)}, u32[]{:S(2)}) %all-to-all-start.8) | async-done | bytes 655392 | tf_op jit(solution)/shard_map/all_to_all | solution.py:53
  252.3 4.0 multiply_convert_fusion
  258.0 4.4 all-to-all-start.10
  262.4 3.5 fusion.177
  265.9 7.2 %all-to-all-done.10 = bf16[8,40,1024]{2,1,0:T(8,128)(2,1)} async-done(((bf16[8,40,1024]{2,1,0:T(8,128)(2,1)}), bf16[8,40,1024]{2,1,0:T(8,128)(2,1)}, u32[]{:S(2)}, u32[]{:S(2)}) %all-to-all-start.10) | async-done | bytes 655392 | tf_op jit(solution)/shard_map/all_to_all | solution.py:53
  277.5 4.2 all-to-all-start.9
  281.7 3.3 multiply_reduce_fusion.2
  292.3 3.8 fusion.25.refs_6_
  297.9 4.2 all-to-all-start.11
  302.8 10.0 %all-to-all-done.11 = bf16[8,40,1024]{2,1,0:T(8,128)(2,1)} async-done(((bf16[8,40,1024]{2,1,0:T(8,128)(2,1)}), bf16[8,40,1024]{2,1,0:T(8,128)(2,1)}, u32[]{:S(2)}, u32[]{:S(2)}) %all-to-all-start.11) | async-done | bytes 655392 | tf_op jit(solution)/shard_map/all_to_all | solution.py:53
  323.2 4.2 all-to-all-start.12
  330.2 12.5 %all-to-all-done.12.blocks_ref = bf16[4,64,1024]{2,1,0:T(8,128)(2,1)} async-done(((bf16[4,64,1024]{2,1,0:T(8,128)(2,1)}), bf16[4,64,1024]{2,1,0:T(8,128)(2,1)}, u32[]{:S(2)}, u32[]{:S(2)}) %all-to-all-start.12) | async-done | bytes 524320 | tf_op jit(solution)/shard_map/all_to_all | solution.py:53
  348.3 3.5 all-to-all-start.13
  354.2 4.0 all-to-all-done.13
  367.4 4.1 all-to-all-start.14
  375.8 10.8 %all-to-all-done.14.blocks_ref = bf16[4,64,1024]{2,1,0:T(8,128)(2,1)} async-done(((bf16[4,64,1024]{2,1,0:T(8,128)(2,1)}), bf16[4,64,1024]{2,1,0:T(8,128)(2,1)}, u32[]{:S(2)}, u32[]{:S(2)}) %all-to-all-start.14) | async-done | bytes 524320 | tf_op jit(solution)/shard_map/all_to_all | solution.py:53
  388.0 16.0 %all_gather.31 = bf16[256,1024]{1,0:T(8,128)(2,1)S(1)} all-gather(bf16[64,1024]{1,0:T(8,128)(2,1)S(1)} %get-tuple-element.317.grad_ref), channel_id=1, replica_groups=mesh['section'=2,'expert'=4,'dp'=4] {'dp'}, dimensions={0}, use_global_device_ids=true | all-gather | bytes 655360 | tf_op jit(solution)/shard_map/all_gather | solution.py:62
  407.1 4.2 all-to-all-start.15
  422.2 3.8 fusion.18.refs_4_
  428.7 4.2 all-to-all-start.16
  440.4 8.2 %owner_grads.2 = f32[2,1024,1024]{2,1,0:T(8,128)} custom-call(s32[1]{0:T(128)} %bitcast.place, bf16[320,1024]{1,0:T(8,128)(2,1)S(1)} %copy-done.16, bf16[320,1024]{1,0:T(8,128)(2,1)} %collective-permute-done.22.refs_1_, bf16[320,1024]{1,0:T(8,128)(2,1)S(1)} %copy-done.18, bf16[320,1024]{1,0:T(8,128)(2,1)} %collective-permute-done.23.refs_3_, ...), custom_call_target="tpu_custom_call" | custom-call | tf_op jit(solution)/shard_map/owner_grads/pallas_call | solution.py:330
  459.7 5.2 all-to-all-start.18
  466.8 13.0 %all-to-all-done.18.blocks_ref = bf16[4,64,1024]{2,1,0:T(8,128)(2,1)} async-done(((bf16[4,64,1024]{2,1,0:T(8,128)(2,1)}), bf16[4,64,1024]{2,1,0:T(8,128)(2,1)}, u32[]{:S(2)}, u32[]{:S(2)}) %all-to-all-start.18) | async-done | bytes 524320 | tf_op jit(solution)/shard_map/all_to_all | solution.py:53
  485.1 3.3 all-to-all-start.19
  489.9 5.0 all-to-all-done.19
  504.6 3.6 all-to-all-start.20
  510.0 13.2 %all-to-all-done.20.blocks_ref = bf16[4,64,1024]{2,1,0:T(8,128)(2,1)S(1)} async-done(((bf16[4,64,1024]{2,1,0:T(8,128)(2,1)}), bf16[4,64,1024]{2,1,0:T(8,128)(2,1)S(1)}, u32[]{:S(2)}, u32[]{:S(2)}) %all-to-all-start.20) | async-done | bytes 524320 | tf_op jit(solution)/shard_map/all_to_all | solution.py:53
  523.3 11.0 %all_to_all.115.refs_0_ = bf16[4,64,512]{2,1,0:T(8,128)(2,1)S(1)} all-to-all(bf16[4,64,512]{2,1,0:T(8,128)(2,1)S(1)} %bitcast.235), channel_id=1, replica_groups=mesh['section'=2,'expert'=4,'dp'=4] {'dp'}, dimensions={0} | all-to-all | bytes 524288 | tf_op jit(solution)/shard_map/all_to_all | solution.py:53
  534.3 3.2 reduce-scatter.14.cloned.1.call-done
  537.5 4.6 all-to-all-start.22
  550.5 4.7 all-to-all-done.22.refs_4_
  555.2 3.6 all-to-all-start.21
  566.1 8.3 %owner_grads.3 = f32[2,1024,1024]{2,1,0:T(8,128)} custom-call(s32[1]{0:T(128)} %bitcast.place, bf16[320,1024]{1,0:T(8,128)(2,1)S(1)} %bitcast.206, bf16[320,1024]{1,0:T(8,128)(2,1)} %collective-permute-done.39.refs_1_, bf16[320,1024]{1,0:T(8,128)(2,1)} %bitcast.51.refs_2_, bf16[320,1024]{1,0:T(8,128)(2,1)} %collective-permute-done.40.refs_3_, ...), custom_call_target="tpu_custom_call" | custom-call | tf_op jit(solution)/shard_map/owner_grads/pallas_call | solution.py:330
  580.3 3.3 finish_weights.1
  (521 shorter events, 191.0 us)
Async XLA Ops:
  7.2 84.0 %all-gather.12.cloned.1.call-start = ((), (), s32[]{:S(2)}) async-start(), calls=%async_computation.36 | async-start | bytes 4718592 | tf_op jit(solution)/shard_map/all_gather | solution.py:618
  10.2 12.9 %collective-permute-start = (bf16[64,1024]{1,0:T(8,128)(2,1)}, bf16[64,1024]{1,0:T(8,128)(2,1)S(1)}, u32[]{:S(2)}, u32[]{:S(2)}) collective-permute-start(bf16[64,1024]{1,0:T(8,128)(2,1)} %bitcast.212), channel_id=1, source_target_pairs={{3,0},{0,1},{1,2},{2,3},{7,4},{4,5},{5,6},{6,7},{11,8},{8,9},{9,10... | collective-permute-start | bytes 393224 | tf_op jit(solution)/shard_map/ppermute | solution.py:95
  13.2 11.4 %collective-permute-start.1 = (bf16[64,1024]{1,0:T(8,128)(2,1)}, bf16[64,1024]{1,0:T(8,128)(2,1)S(1)}, u32[]{:S(2)}, u32[]{:S(2)}) collective-permute-start(bf16[64,1024]{1,0:T(8,128)(2,1)} %bitcast.213), channel_id=1, source_target_pairs={{2,0},{3,1},{0,2},{1,3},{6,4},{7,5},{4,6},{5,7},{10,8},{11,9},{8,1... | collective-permute-start | bytes 393224 | tf_op jit(solution)/shard_map/ppermute | solution.py:95
  15.8 8.9 %collective-permute-start.2 = (bf16[64,1024]{1,0:T(8,128)(2,1)}, bf16[64,1024]{1,0:T(8,128)(2,1)S(1)}, u32[]{:S(2)}, u32[]{:S(2)}) collective-permute-start(bf16[64,1024]{1,0:T(8,128)(2,1)} %bitcast.214), channel_id=1, source_target_pairs={{1,0},{2,1},{3,2},{0,3},{5,4},{6,5},{7,6},{4,7},{9,8},{10,9},{11,1... | collective-permute-start | bytes 393224 | tf_op jit(solution)/shard_map/ppermute | solution.py:95
  17.1 13.4 %all-to-all-start = ((bf16[32,8,128]{2,1,0:T(8,128)(2,1)}), bf16[32,8,128]{2,1,0:T(8,128)(2,1)S(1)}, u32[]{:S(2)}, u32[]{:S(2)}) async-start(bf16[32,8,128]{2,1,0:T(8,128)(2,1)} %broadcast_in_dim.49), calls=%async_computation | async-start | bytes 131072 | tf_op jit(solution)/shard_map/all_to_all | solution.py:53
  20.0 75.9 %all-gather.6.cloned.1.call-start = ((), (), s32[]{:S(2)}) async-start(), calls=%async_computation.28 | async-start | bytes 4718592 | tf_op jit(solution)/shard_map/all_gather | solution.py:586
  32.7 15.4 %all-to-all-start.1 = ((bf16[4,64,768]{2,1,0:T(8,128)(2,1)}), bf16[4,64,768]{2,1,0:T(8,128)(2,1)S(1)}, u32[]{:S(2)}, u32[]{:S(2)}) async-start(bf16[4,64,768]{2,1,0:T(8,128)(2,1)} %reshape.428), calls=%async_computation.1 | async-start | bytes 786432 | tf_op jit(solution)/shard_map/all_to_all | solution.py:53
  49.3 27.9 %all-to-all-start.2 = ((bf16[4,4,64,768]{3,2,1,0:T(8,128)(2,1)}), bf16[4,4,64,768]{3,2,1,0:T(8,128)(2,1)S(1)}, u32[]{:S(2)}, u32[]{:S(2)}) async-start(bf16[4,4,64,768]{3,2,1,0:T(8,128)(2,1)} %broadcast_in_dim.51), calls=%async_computation.2 | async-start | bytes 3145728 | tf_op jit(solution)/shard_map/all_to_all | solution.py:53
  52.9 97.9 %all-gather.8.cloned.1.call-start = ((), (), s32[]{:S(2)}) async-start(), calls=%async_computation.29 | async-start | bytes 4718592 | tf_op jit(solution)/shard_map/all_gather | solution.py:616
  53.0 8.3 %collective-permute-start.3 = (bf16[64,1024]{1,0:T(8,128)(2,1)S(1)}, bf16[64,1024]{1,0:T(8,128)(2,1)S(1)}, u32[]{:S(2)}, u32[]{:S(2)}) collective-permute-start(bf16[64,1024]{1,0:T(8,128)(2,1)S(1)} %fusion.106.refs_0_), channel_id=1, source_target_pairs={{3,0},{0,1},{1,2},{2,3},{7,4},{4,5},{5,6},{6,7},{11,8},{8,9},{9,10... | collective-permute-start | bytes 393224 | tf_op jit(solution)/shard_map/ppermute | solution.py:95
  53.0 15.9 %collective-permute-start.4 = (bf16[64,1024]{1,0:T(8,128)(2,1)S(1)}, bf16[64,1024]{1,0:T(8,128)(2,1)S(1)}, u32[]{:S(2)}, u32[]{:S(2)}) collective-permute-start(bf16[64,1024]{1,0:T(8,128)(2,1)S(1)} %fusion.106.refs_0_), channel_id=1, source_target_pairs={{2,0},{3,1},{0,2},{1,3},{6,4},{7,5},{4,6},{5,7},{10,8},{11,9},{8,1... | collective-permute-start | bytes 393224 | tf_op jit(solution)/shard_map/ppermute | solution.py:95
  55.0 13.9 %collective-permute-start.5 = (bf16[64,1024]{1,0:T(8,128)(2,1)S(1)}, bf16[64,1024]{1,0:T(8,128)(2,1)S(1)}, u32[]{:S(2)}, u32[]{:S(2)}) collective-permute-start(bf16[64,1024]{1,0:T(8,128)(2,1)S(1)} %fusion.106.refs_0_), channel_id=1, source_target_pairs={{1,0},{2,1},{3,2},{0,3},{5,4},{6,5},{7,6},{4,7},{9,8},{10,9},{11,1... | collective-permute-start | bytes 393224 | tf_op jit(solution)/shard_map/ppermute | solution.py:95
  56.8 12.8 %collective-permute-start.6 = (bf16[64,1024]{1,0:T(8,128)(2,1)}, bf16[64,1024]{1,0:T(8,128)(2,1)S(1)}, u32[]{:S(2)}, u32[]{:S(2)}) collective-permute-start(bf16[64,1024]{1,0:T(8,128)(2,1)} %get-tuple-element.232), channel_id=1, source_target_pairs={{3,0},{0,1},{1,2},{2,3},{7,4},{4,5},{5,6},{6,7},{11,8},{8,9},{9,10... | collective-permute-start | bytes 393224 | tf_op jit(solution)/shard_map/ppermute | solution.py:111
  57.4 18.9 %collective-permute-start.7 = (bf16[64,1024]{1,0:T(8,128)(2,1)}, bf16[64,1024]{1,0:T(8,128)(2,1)S(1)}, u32[]{:S(2)}, u32[]{:S(2)}) collective-permute-start(bf16[64,1024]{1,0:T(8,128)(2,1)} %get-tuple-element.233), channel_id=1, source_target_pairs={{2,0},{3,1},{0,2},{1,3},{6,4},{7,5},{4,6},{5,7},{10,8},{11,9},{8,1... | collective-permute-start | bytes 393224 | tf_op jit(solution)/shard_map/ppermute | solution.py:111
  61.3 15.0 %collective-permute-start.8 = (bf16[64,1024]{1,0:T(8,128)(2,1)S(1)}, bf16[64,1024]{1,0:T(8,128)(2,1)S(1)}, u32[]{:S(2)}, u32[]{:S(2)}) collective-permute-start(bf16[64,1024]{1,0:T(8,128)(2,1)S(1)} %copy-done.95), channel_id=1, source_target_pairs={{1,0},{2,1},{3,2},{0,3},{5,4},{6,5},{7,6},{4,7},{9,8},{10,9},{11,1... | collective-permute-start | bytes 393224 | tf_op jit(solution)/shard_map/ppermute | solution.py:111
  77.3 6.7 %collective-permute-start.9 = (bf16[1024,768]{1,0:T(8,128)(2,1)S(1)}, bf16[1024,768]{1,0:T(8,128)(2,1)}, u32[]{:S(2)}, u32[]{:S(2)}) collective-permute-start(bf16[1024,768]{1,0:T(8,128)(2,1)S(1)} %bitcast.218), channel_id=1, source_target_pairs={{0,16},{16,0},{1,17},{17,1},{2,18},{18,2},{3,19},{19,3},{4,20},{20... | collective-permute-start | bytes 4718600 | tf_op jit(solution)/shard_map/ppermute | solution.py:482
  83.5 57.4 %collective-permute-start.10 = (bf16[1024,1024]{1,0:T(8,128)(2,1)}, bf16[1024,1024]{1,0:T(8,128)(2,1)}, u32[]{:S(2)}, u32[]{:S(2)}) collective-permute-start(bf16[1024,1024]{1,0:T(8,128)(2,1)} %get-tuple-element.245), channel_id=1, source_target_pairs={{0,16},{16,0},{1,17},{17,1},{2,18},{18,2},{3,19},{19,3},{4,20},{20... | collective-permute-start | bytes 6291464 | tf_op jit(solution)/shard_map/ppermute | solution.py:482
  84.0 60.8 %collective-permute-start.11 = (bf16[1024,1024]{1,0:T(8,128)(2,1)}, bf16[1024,1024]{1,0:T(8,128)(2,1)}, u32[]{:S(2)}, u32[]{:S(2)}) collective-permute-start(bf16[1024,1024]{1,0:T(8,128)(2,1)} %get-tuple-element.247), channel_id=1, source_target_pairs={{0,16},{16,0},{1,17},{17,1},{2,18},{18,2},{3,19},{19,3},{4,20},{20... | collective-permute-start | bytes 6291464 | tf_op jit(solution)/shard_map/ppermute | solution.py:482
  87.7 12.3 %all-to-all-start.3 = ((bf16[4,64,256]{2,1,0:T(8,128)(2,1)}), bf16[4,64,256]{2,1,0:T(8,128)(2,1)S(1)}, u32[]{:S(2)}, u32[]{:S(2)}) async-start(bf16[4,64,256]{2,1,0:T(8,128)(2,1)} %bitcast.29), calls=%async_computation.3 | async-start | bytes 262144 | tf_op jit(solution)/shard_map/all_to_all | solution.py:53
  119.3 21.6 %all-to-all-start.4 = ((bf16[8,40,1024]{2,1,0:T(8,128)(2,1)}), bf16[8,40,1024]{2,1,0:T(8,128)(2,1)S(1)}, u32[]{:S(2)}, u32[]{:S(2)}) async-start(bf16[8,40,1024]{2,1,0:T(8,128)(2,1)} %bitcast.226), calls=%async_computation.4 | async-start | bytes 1310720 | tf_op jit(solution)/shard_map/all_to_all | solution.py:53
  146.5 14.9 %all-to-all-start.5 = ((bf16[8,40,1024]{2,1,0:T(8,128)(2,1)}), bf16[8,40,1024]{2,1,0:T(8,128)(2,1)}, u32[]{:S(2)}, u32[]{:S(2)}) async-start(bf16[8,40,1024]{2,1,0:T(8,128)(2,1)} %bitcast.239), calls=%async_computation.5 | async-start | bytes 1310720 | tf_op jit(solution)/shard_map/all_to_all | solution.py:53
  164.5 19.6 %all-to-all-start.6 = ((bf16[4,64,1024]{2,1,0:T(8,128)(2,1)}), bf16[4,64,1024]{2,1,0:T(8,128)(2,1)}, u32[]{:S(2)}, u32[]{:S(2)}) async-start(bf16[4,64,1024]{2,1,0:T(8,128)(2,1)} %bitcast.232), calls=%async_computation.6 | async-start | bytes 1048576 | tf_op jit(solution)/shard_map/all_to_all | solution.py:53
  207.2 9.2 %all-to-all-start.7 = ((bf16[4,64,256]{2,1,0:T(8,128)(2,1)}), bf16[4,64,256]{2,1,0:T(8,128)(2,1)S(1)}, u32[]{:S(2)}, u32[]{:S(2)}) async-start(bf16[4,64,256]{2,1,0:T(8,128)(2,1)} %bitcast.41), calls=%async_computation.7 | async-start | bytes 262144 | tf_op jit(solution)/shard_map/all_to_all | solution.py:53
  237.4 14.9 %all-to-all-start.8 = ((bf16[8,40,1024]{2,1,0:T(8,128)(2,1)}), bf16[8,40,1024]{2,1,0:T(8,128)(2,1)}, u32[]{:S(2)}, u32[]{:S(2)}) async-start(bf16[8,40,1024]{2,1,0:T(8,128)(2,1)} %bitcast.225), calls=%async_computation.8 | async-start | bytes 1310720 | tf_op jit(solution)/shard_map/all_to_all | solution.py:53
  241.6 31.4 %all-gather.10.cloned.1.call-start = ((), (), s32[]{:S(2)}) async-start(), calls=%async_computation.30 | async-start | bytes 1310720 | tf_op jit(solution)/shard_map/all_gather | solution.py:732
  258.0 15.0 %all-to-all-start.10 = ((bf16[8,40,1024]{2,1,0:T(8,128)(2,1)}), bf16[8,40,1024]{2,1,0:T(8,128)(2,1)}, u32[]{:S(2)}, u32[]{:S(2)}) async-start(bf16[8,40,1024]{2,1,0:T(8,128)(2,1)} %bitcast.240), calls=%async_computation.10 | async-start | bytes 1310720 | tf_op jit(solution)/shard_map/all_to_all | solution.py:53
  277.5 14.9 %all-to-all-start.9 = ((bf16[8,40,1024]{2,1,0:T(8,128)(2,1)}), bf16[8,40,1024]{2,1,0:T(8,128)(2,1)}, u32[]{:S(2)}, u32[]{:S(2)}) async-start(bf16[8,40,1024]{2,1,0:T(8,128)(2,1)} %bitcast.224), calls=%async_computation.9 | async-start | bytes 1310720 | tf_op jit(solution)/shard_map/all_to_all | solution.py:53
  297.9 14.9 %all-to-all-start.11 = ((bf16[8,40,1024]{2,1,0:T(8,128)(2,1)}), bf16[8,40,1024]{2,1,0:T(8,128)(2,1)}, u32[]{:S(2)}, u32[]{:S(2)}) async-start(bf16[8,40,1024]{2,1,0:T(8,128)(2,1)} %bitcast.238), calls=%async_computation.11 | async-start | bytes 1310720 | tf_op jit(solution)/shard_map/all_to_all | solution.py:53
  302.1 73.6 %reduce-scatter.6.cloned.1.call-start = ((), (), s32[]{:S(2)}) async-start(), calls=%async_computation.31 | async-start | bytes 655360 | tf_op jit(solution)/shard_map/reduce_scatter | solution.py:756
  302.7 115.1 %reduce-scatter.8.cloned.1.call-start = ((), (), s32[]{:S(2)}) async-start(), calls=%async_computation.32 | async-start | bytes 2621440 | tf_op jit(solution)/shard_map/reduce_scatter | solution.py:782
  315.8 5.0 collective-permute-start.13
  323.2 19.4 %all-to-all-start.12 = ((bf16[4,64,1024]{2,1,0:T(8,128)(2,1)}), bf16[4,64,1024]{2,1,0:T(8,128)(2,1)}, u32[]{:S(2)}, u32[]{:S(2)}) async-start(bf16[4,64,1024]{2,1,0:T(8,128)(2,1)} %bitcast.230), calls=%async_computation.12 | async-start | bytes 1048576 | tf_op jit(solution)/shard_map/all_to_all | solution.py:53
  347.1 4.8 collective-permute-start.17
  348.3 9.9 %all-to-all-start.13 = ((bf16[4,64,256]{2,1,0:T(8,128)(2,1)}), bf16[4,64,256]{2,1,0:T(8,128)(2,1)S(1)}, u32[]{:S(2)}, u32[]{:S(2)}) async-start(bf16[4,64,256]{2,1,0:T(8,128)(2,1)} %copy-done.48), calls=%async_computation.13 | async-start | bytes 262144 | tf_op jit(solution)/shard_map/all_to_all | solution.py:53
  366.1 5.5 collective-permute-start.19
  367.4 19.1 %all-to-all-start.14 = ((bf16[4,64,1024]{2,1,0:T(8,128)(2,1)}), bf16[4,64,1024]{2,1,0:T(8,128)(2,1)}, u32[]{:S(2)}, u32[]{:S(2)}) async-start(bf16[4,64,1024]{2,1,0:T(8,128)(2,1)} %bitcast.227), calls=%async_computation.14 | async-start | bytes 1048576 | tf_op jit(solution)/shard_map/all_to_all | solution.py:53
  371.5 48.1 %reduce-scatter.10.cloned.1.call-start = ((), (), s32[]{:S(2)}) async-start(), calls=%async_computation.33 | async-start | bytes 2293760 | tf_op jit(solution)/shard_map/reduce_scatter | solution.py:782
  375.1 52.7 %collective-permute-start.22 = (bf16[320,1024]{1,0:T(8,128)(2,1)}, bf16[320,1024]{1,0:T(8,128)(2,1)}, u32[]{:S(2)}, u32[]{:S(2)}) collective-permute-start(bf16[320,1024]{1,0:T(8,128)(2,1)} %copy-done.15), channel_id=1, source_target_pairs={{0,16},{16,0},{1,17},{17,1},{2,18},{18,2},{3,19},{19,3},{4,20},{20... | collective-permute-start | bytes 1966088 | tf_op jit(solution)/shard_map/ppermute | solution.py:482
  375.2 52.6 %collective-permute-start.23 = (bf16[320,1024]{1,0:T(8,128)(2,1)}, bf16[320,1024]{1,0:T(8,128)(2,1)}, u32[]{:S(2)}, u32[]{:S(2)}) collective-permute-start(bf16[320,1024]{1,0:T(8,128)(2,1)} %copy-done.17), channel_id=1, source_target_pairs={{0,16},{16,0},{1,17},{17,1},{2,18},{18,2},{3,19},{19,3},{4,20},{20... | collective-permute-start | bytes 1966088 | tf_op jit(solution)/shard_map/ppermute | solution.py:482
  375.7 52.2 %collective-permute-start.25 = (bf16[320,1024]{1,0:T(8,128)(2,1)}, bf16[320,1024]{1,0:T(8,128)(2,1)}, u32[]{:S(2)}, u32[]{:S(2)}) collective-permute-start(bf16[320,1024]{1,0:T(8,128)(2,1)} %bitcast.57.refs_6_), channel_id=1, source_target_pairs={{0,16},{16,0},{1,17},{17,1},{2,18},{18,2},{3,19},{19,3},{4,20},{20... | collective-permute-start | bytes 1966088 | tf_op jit(solution)/shard_map/ppermute | solution.py:482
  407.1 14.9 %all-to-all-start.15 = ((bf16[8,40,1024]{2,1,0:T(8,128)(2,1)}), bf16[8,40,1024]{2,1,0:T(8,128)(2,1)}, u32[]{:S(2)}, u32[]{:S(2)}) async-start(bf16[8,40,1024]{2,1,0:T(8,128)(2,1)} %bitcast.223), calls=%async_computation.16 | async-start | bytes 1310720 | tf_op jit(solution)/shard_map/all_to_all | solution.py:53
  421.9 5.9 %collective-permute-start.24 = (bf16[320,1024]{1,0:T(8,128)(2,1)}, bf16[320,1024]{1,0:T(8,128)(2,1)S(1)}, u32[]{:S(2)}, u32[]{:S(2)}) collective-permute-start(bf16[320,1024]{1,0:T(8,128)(2,1)} %bitcast.77.refs_4_), channel_id=1, source_target_pairs={{0,16},{16,0},{1,17},{17,1},{2,18},{18,2},{3,19},{19,3},{4,20},{20... | collective-permute-start | bytes 1966088 | tf_op jit(solution)/shard_map/ppermute | solution.py:482
  428.7 21.9 %all-to-all-start.16 = ((bf16[8,40,1024]{2,1,0:T(8,128)(2,1)}), bf16[8,40,1024]{2,1,0:T(8,128)(2,1)}, u32[]{:S(2)}, u32[]{:S(2)}) async-start(bf16[8,40,1024]{2,1,0:T(8,128)(2,1)} %bitcast.237), calls=%async_computation.19 | async-start | bytes 1310720 | tf_op jit(solution)/shard_map/all_to_all | solution.py:53
  432.9 75.3 %reduce-scatter.12.cloned.1.call-start = ((), (), s32[]{:S(2)}) async-start(), calls=%async_computation.34 | async-start | bytes 2621440 | tf_op jit(solution)/shard_map/reduce_scatter | solution.py:782
  433.0 15.6 %collective-permute-start.26 = (bf16[64,1408]{1,0:T(8,128)(2,1)}, bf16[64,1408]{1,0:T(8,128)(2,1)S(1)}, u32[]{:S(2)}, u32[]{:S(2)}) collective-permute-start(bf16[64,1408]{1,0:T(8,128)(2,1)} %get-tuple-element.335), channel_id=1, source_target_pairs={{3,0},{0,1},{1,2},{2,3},{7,4},{4,5},{5,6},{6,7},{11,8},{8,9},{9,10... | collective-permute-start | bytes 540680 | tf_op jit(solution)/shard_map/ppermute | solution.py:111
  433.0 16.2 %collective-permute-start.27 = (bf16[64,1408]{1,0:T(8,128)(2,1)S(1)}, bf16[64,1408]{1,0:T(8,128)(2,1)S(1)}, u32[]{:S(2)}, u32[]{:S(2)}) collective-permute-start(bf16[64,1408]{1,0:T(8,128)(2,1)S(1)} %copy-done.94), channel_id=1, source_target_pairs={{2,0},{3,1},{0,2},{1,3},{6,4},{7,5},{4,6},{5,7},{10,8},{11,9},{8,1... | collective-permute-start | bytes 540680 | tf_op jit(solution)/shard_map/ppermute | solution.py:111
  435.0 15.0 %collective-permute-start.28 = (bf16[64,1408]{1,0:T(8,128)(2,1)S(1)}, bf16[64,1408]{1,0:T(8,128)(2,1)S(1)}, u32[]{:S(2)}, u32[]{:S(2)}) collective-permute-start(bf16[64,1408]{1,0:T(8,128)(2,1)S(1)} %copy-done.93), channel_id=1, source_target_pairs={{1,0},{2,1},{3,2},{0,3},{5,4},{6,5},{7,6},{4,7},{9,8},{10,9},{11,1... | collective-permute-start | bytes 540680 | tf_op jit(solution)/shard_map/ppermute | solution.py:111
  459.7 20.1 %all-to-all-start.18 = ((bf16[4,64,1024]{2,1,0:T(8,128)(2,1)}), bf16[4,64,1024]{2,1,0:T(8,128)(2,1)}, u32[]{:S(2)}, u32[]{:S(2)}) async-start(bf16[4,64,1024]{2,1,0:T(8,128)(2,1)} %bitcast.231), calls=%async_computation.22 | async-start | bytes 1048576 | tf_op jit(solution)/shard_map/all_to_all | solution.py:53
  485.1 9.8 %all-to-all-start.19 = ((bf16[4,64,256]{2,1,0:T(8,128)(2,1)}), bf16[4,64,256]{2,1,0:T(8,128)(2,1)S(1)}, u32[]{:S(2)}, u32[]{:S(2)}) async-start(bf16[4,64,256]{2,1,0:T(8,128)(2,1)} %copy-done.47), calls=%async_computation.23 | async-start | bytes 262144 | tf_op jit(solution)/shard_map/all_to_all | solution.py:53
  488.5 49.0 %reduce-scatter.14.cloned.1.call-start = ((), (), s32[]{:S(2)}) async-start(), calls=%async_computation.35 | async-start | bytes 2293760 | tf_op jit(solution)/shard_map/reduce_scatter | solution.py:782
  504.6 18.7 %all-to-all-start.20 = ((bf16[4,64,1024]{2,1,0:T(8,128)(2,1)}), bf16[4,64,1024]{2,1,0:T(8,128)(2,1)S(1)}, u32[]{:S(2)}, u32[]{:S(2)}) async-start(bf16[4,64,1024]{2,1,0:T(8,128)(2,1)} %bitcast.83), calls=%async_computation.24 | async-start | bytes 1048576 | tf_op jit(solution)/shard_map/all_to_all | solution.py:53
  537.5 17.7 %all-to-all-start.22 = ((bf16[4,64,896]{2,1,0:T(8,128)(2,1)}), bf16[4,64,896]{2,1,0:T(8,128)(2,1)S(1)}, u32[]{:S(2)}, u32[]{:S(2)}) async-start(bf16[4,64,896]{2,1,0:T(8,128)(2,1)} %bitcast.243), calls=%async_computation.27 | async-start | bytes 917504 | tf_op jit(solution)/shard_map/all_to_all | solution.py:53
  542.1 8.3 %collective-permute-start.39 = (bf16[320,1024]{1,0:T(8,128)(2,1)S(1)}, bf16[320,1024]{1,0:T(8,128)(2,1)}, u32[]{:S(2)}, u32[]{:S(2)}) collective-permute-start(bf16[320,1024]{1,0:T(8,128)(2,1)S(1)} %bitcast.205), channel_id=1, source_target_pairs={{0,16},{16,0},{1,17},{17,1},{2,18},{18,2},{3,19},{19,3},{4,20},{20... | collective-permute-start | bytes 1966088 | tf_op jit(solution)/shard_map/ppermute | solution.py:482
  542.1 8.3 %collective-permute-start.40 = (bf16[320,1024]{1,0:T(8,128)(2,1)}, bf16[320,1024]{1,0:T(8,128)(2,1)}, u32[]{:S(2)}, u32[]{:S(2)}) collective-permute-start(bf16[320,1024]{1,0:T(8,128)(2,1)} %bitcast.51.refs_2_), channel_id=1, source_target_pairs={{0,16},{16,0},{1,17},{17,1},{2,18},{18,2},{3,19},{19,3},{4,20},{20... | collective-permute-start | bytes 1966088 | tf_op jit(solution)/shard_map/ppermute | solution.py:482
  542.6 7.8 %collective-permute-start.42 = (bf16[320,1024]{1,0:T(8,128)(2,1)}, bf16[320,1024]{1,0:T(8,128)(2,1)}, u32[]{:S(2)}, u32[]{:S(2)}) collective-permute-start(bf16[320,1024]{1,0:T(8,128)(2,1)} %copy-done.13), channel_id=1, source_target_pairs={{0,16},{16,0},{1,17},{17,1},{2,18},{18,2},{3,19},{19,3},{4,20},{20... | collective-permute-start | bytes 1966088 | tf_op jit(solution)/shard_map/ppermute | solution.py:482
  542.6 7.8 %collective-permute-start.41 = (bf16[320,1024]{1,0:T(8,128)(2,1)}, bf16[320,1024]{1,0:T(8,128)(2,1)}, u32[]{:S(2)}, u32[]{:S(2)}) collective-permute-start(bf16[320,1024]{1,0:T(8,128)(2,1)} %copy-done.19), channel_id=1, source_target_pairs={{0,16},{16,0},{1,17},{17,1},{2,18},{18,2},{3,19},{19,3},{4,20},{20... | collective-permute-start | bytes 1966088 | tf_op jit(solution)/shard_map/ppermute | solution.py:482
  555.2 21.9 %all-to-all-start.21 = ((f32[32,16,128]{2,1,0:T(8,128)}), f32[32,16,128]{2,1,0:T(8,128)}, u32[]{:S(2)}, u32[]{:S(2)}) async-start(f32[32,16,128]{2,1,0:T(8,128)} %pack_small.1), calls=%async_computation.25 | async-start | bytes 524288 | tf_op jit(solution)/shard_map/all_to_all | solution.py:53
  558.8 15.6 %collective-permute-start.38 = (f32[64,1024]{1,0:T(8,128)}, f32[64,1024]{1,0:T(8,128)}, u32[]{:S(2)}, u32[]{:S(2)}) collective-permute-start(f32[64,1024]{1,0:T(8,128)} %copy-done.35), channel_id=1, source_target_pairs={{0,16},{16,0},{1,17},{17,1},{2,18},{18,2},{3,19},{19,3},{4,20},{20... | collective-permute-start | bytes 786440 | tf_op jit(solution)/shard_map/ppermute | solution.py:482
  559.1 15.7 %collective-permute-start.37 = (f32[64,1024]{1,0:T(8,128)}, f32[64,1024]{1,0:T(8,128)}, u32[]{:S(2)}, u32[]{:S(2)}) collective-permute-start(f32[64,1024]{1,0:T(8,128)} %get-tuple-element.375.refs_4_), channel_id=1, source_target_pairs={{0,16},{16,0},{1,17},{17,1},{2,18},{18,2},{3,19},{19,3},{4,20},{20... | collective-permute-start | bytes 786440 | tf_op jit(solution)/shard_map/ppermute | solution.py:482
  559.4 19.4 %collective-permute-start.48 = (bf16[256,512]{1,0:T(8,128)(2,1)S(1)}, bf16[256,512]{1,0:T(8,128)(2,1)}, u32[]{:S(2)}, u32[]{:S(2)}) collective-permute-start(bf16[256,512]{1,0:T(8,128)(2,1)S(1)} %copy-done.10), channel_id=1, source_target_pairs={{0,16},{16,0},{1,17},{17,1},{2,18},{18,2},{3,19},{19,3},{4,20},{20... | collective-permute-start | bytes 786440 | tf_op jit(solution)/shard_map/ppermute | solution.py:482
  562.7 17.5 %collective-permute-start.46 = (bf16[4,64,896]{2,1,0:T(8,128)(2,1)S(1)}, bf16[4,64,896]{2,1,0:T(8,128)(2,1)}, u32[]{:S(2)}, u32[]{:S(2)}) collective-permute-start(bf16[4,64,896]{2,1,0:T(8,128)(2,1)S(1)} %slice.266.refs_6_), channel_id=1, source_target_pairs={{0,16},{16,0},{1,17},{17,1},{2,18},{18,2},{3,19},{19,3},{4,20},{20... | collective-permute-start | bytes 1376264 | tf_op jit(solution)/shard_map/ppermute | solution.py:482
  563.7 16.6 %collective-permute-start.45 = (bf16[4,64,896]{2,1,0:T(8,128)(2,1)S(1)}, bf16[4,64,896]{2,1,0:T(8,128)(2,1)}, u32[]{:S(2)}, u32[]{:S(2)}) collective-permute-start(bf16[4,64,896]{2,1,0:T(8,128)(2,1)S(1)} %all-to-all-done.22.refs_4_), channel_id=1, source_target_pairs={{0,16},{16,0},{1,17},{17,1},{2,18},{18,2},{3,19},{19,3},{4,20},{20... | collective-permute-start | bytes 1376264 | tf_op jit(solution)/shard_map/ppermute | solution.py:482
  574.4 5.8 collective-permute-start.47
  574.8 5.4 collective-permute-start.43
  (135 other events, 1457.0 us)
Sparse Core Ops, SparseCore 0:
  9.9 39.9 all-gather.11
  52.4 43.2 all-gather.5
  98.1 42.8 all-gather.7
  243.7 28.5 all-gather.9
  304.9 22.3 reduce-scatter.5
  330.2 33.5 reduce-scatter.7
  376.3 32.9 reduce-scatter.9
  459.8 36.9 reduce-scatter.11
  504.7 32.7 reduce-scatter.13

commit v3 on v2

--- a/solution.py
+++ b/solution.py
@@ -12,6 +12,7 @@
 SEC, EX, DP = "section", "expert", "dp"
 EVERY = (SEC, EX, DP)
 HOMES = (SEC, EX)
+LANES = 128
 
 
 def layer_norm(value_rows, gain_vec, shift_vec):
@@ -73,6 +74,11 @@
 def beside(move, blocks, work, operands, late=()):
     blocks, operands = lax.optimization_barrier((blocks, operands))
     return lax.optimization_barrier((move(blocks), work(*operands, *late)))
+
+
+def started(operands, blocks):
+    tile = blocks[0, :16, :128]
+    return after(operands, other_core(tile))
 
 
 def over_dp(blocks):
@@ -297,6 +303,30 @@
     )(segments[:, None], segments[None, :], qkv, d_mixed)
 
 
+def pair_grads(section_id, *pairs):
+    mats = [side for left, right in pairs for side in (left, other_core(left), right, other_core(right))]
+    left_width = pairs[0][0].shape[1]
+    halves = [right.shape[1] // 2 for _, right in pairs]
+
+    def kernel(place, *refs):
+        start = 0
+        for index, half in enumerate(halves):
+            left_own, left_other, right_own, right_other = refs[4 * index : 4 * index + 4]
+            here = pl.ds(pl.multiple_of(place[0] * half, LANES), half)
+            total = product_tn(left_own[...], right_own[:, here])
+            total = total + product_tn(left_other[...], right_other[:, here])
+            refs[-1][:, start : start + half] = low(total)
+            start = start + half
+
+    return pl.pallas_call(
+        kernel,
+        out_shape=jax.ShapeDtypeStruct((left_width, sum(halves)), jnp.bfloat16),
+        in_specs=[SCALAR] + [WHOLE] * len(mats),
+        compiler_params=pltpu.CompilerParams(vmem_limit_bytes=40 << 20),
+        name="pair_grads",
+    )(section_id.reshape(1), *mats)
+
+
 OWNER_TILE = 256
 
 
@@ -358,20 +388,33 @@
 
 
 def call(kernel, name, outs, *operands):
+    specs = [
+        pl.BlockSpec(memory_space=pl.ANY) if operand.shape[1:] == (operand.shape[-1],) * 2 else WHOLE
+        for operand in operands
+    ]
+    mats = [operand.shape[1:] for operand, spec in zip(operands, specs) if spec is not WHOLE]
+    scratch = [pltpu.VMEM(shape, jnp.bfloat16) for shape in mats]
+    scratch += [pltpu.SemaphoreType.DMA for _ in mats]
     return pl.pallas_call(
         kernel,
+        in_specs=specs,
         out_shape=[jax.ShapeDtypeStruct(shape, dtype) for shape, dtype in outs],
+        scratch_shapes=scratch,
         compiler_params=pltpu.CompilerParams(vmem_limit_bytes=32 << 20),
         name=name,
     )(*operands)
 
 
-def project(mixed_blocks, proj_mat, layer_in, gain, shift):
-    def kernel(mixed_ref, proj_ref, in_ref, gain_ref, shift_ref, rows_ref, res_ref, mid_ref, sq_ref):
+def project(layer, mixed_blocks, proj_mat, layer_in, gain, shift):
+    def kernel(mixed_ref, proj_ref, in_ref, gain_ref, shift_ref, *outs):
+        rows_ref, res_ref, mid_ref, sq_ref, proj_here, arrived = outs
+        fetch = pltpu.make_async_copy(proj_ref.at[layer], proj_here, arrived)
+        fetch.start()
         places = mixed_ref.shape[0]
         mixed = jnp.concatenate([mixed_ref[place] for place in range(places)], axis=1)
         rows_ref[...] = mixed
-        branch = product(mixed, proj_ref[...])
+        fetch.wait()
+        branch = product(mixed, proj_here[...])
         residual = in_ref[...].astype(jnp.float32) + branch
         res_ref[...] = residual
         mid_ref[...] = low(statistics(residual)[0] * gain_ref[...] + shift_ref[...])
@@ -410,13 +453,16 @@
     return grad_ref[...].astype(jnp.float32) + d_value * spread_inverse
 
 
-def mid_back(mid_blocks, residual, gain, grad_out, proj_mat, dp_size):
+def mid_back(layer, mid_blocks, residual, gain, grad_out, proj_mat, dp_size):
     def kernel(blocks_ref, res_ref, gain_ref, grad_ref, proj_ref, *outs):
-        sum_ref, low_ref, mixed_ref, gain_grad_ref, shift_grad_ref = outs
+        sum_ref, low_ref, mixed_ref, gain_grad_ref, shift_grad_ref, proj_here, arrived = outs
+        fetch = pltpu.make_async_copy(proj_ref.at[layer], proj_here, arrived)
+        fetch.start()
         grad = norm_back(blocks_ref, res_ref, gain_ref, grad_ref, gain_grad_ref, shift_grad_ref)
         sum_ref[...] = grad
         low_ref[...] = low(grad)
-        d_mixed = low(product_nt(low(grad), proj_ref[...]))
+        fetch.wait()
+        d_mixed = low(product_nt(low(grad), proj_here[...]))
         part = d_mixed.shape[1] // dp_size
         for place in range(dp_size):
             mixed_ref[place] = d_mixed[:, place * part : (place + 1) * part]
@@ -438,9 +484,6 @@
     row = ((1, shape[1]), jnp.float32)
     outs = [(shape, jnp.float32), (shape, jnp.bfloat16), row, row]
     return call(kernel, "input_back", outs, in_blocks, layer_in, gain, grad_resid)
-
-
-LANES = 128
 
 
 def pack_small(parts_of_layers, squares_of_layers, weight_rows):
@@ -480,17 +523,6 @@
 
 def other_core(block):
     return lax.ppermute(block, SEC, [(0, 1), (1, 0)])
-
-
-def both_cores(block):
-    return jnp.concatenate([block, other_core(block)], axis=0)
-
-
-def halves_for_cores(block, section_id):
-    half = block.shape[1] // 2
-    kept = lax.dynamic_slice_in_dim(block, section_id * half, half, axis=1)
-    sent = lax.dynamic_slice_in_dim(block, (1 - section_id) * half, half, axis=1)
-    return jnp.concatenate([kept, other_core(sent)], axis=0)
 
 
 def shards(
@@ -599,14 +631,17 @@
     first_normed = low(
         layer_norm(own_input.astype(jnp.float32), first_params[0:1], first_params[2:3])
     )
-    qkv_own, (first_seq, up_rows) = beside(
+    down_both = lax.all_gather(dense_down[0], HOMES, axis=0, tiled=True)
+    qkv_own, (first_seq, up_rows, down_both) = beside(
         lambda blocks: exchange(blocks, EX),
         jnp.broadcast_to(qkv_cols[None], (groups,) + qkv_cols.shape),
-        lambda rows, *parts: (
+        lambda rows, parts, down_both: (
             in_order(permute_copies(rows, DP), DP),
             in_order(sent_parts(parts, DP), DP),
+            down_both,
         ),
-        (first_normed, *up_parts),
+        (first_normed, up_parts),
+        (down_both,),
     )
     first_seq = first_seq.reshape(full_len, width)
     qkv_own = qkv_own.reshape(width, 3 * head_width)
@@ -615,7 +650,6 @@
     first_qkv = low(product(first_seq, by_layer(qkv_pair)[0]))
     up_both = lax.all_gather(up_rows.reshape(-1, hidden_here), HOMES, axis=0, tiled=True)
     up_both = up_both.reshape(sections, width, hidden_here)
-    down_both = lax.all_gather(dense_down[0], HOMES, axis=0, tiled=True)
     down_both = down_both.reshape(sections, hidden_here, width)
 
     segments = lax.dynamic_index_in_dim(segment_ids[:, 0], section_id, 0, keepdims=False)
@@ -645,6 +679,14 @@
         coef = jax.nn.softmax(small_logits[:, experts_total:], axis=-1)
         return gate_probs, gate, coef
 
+    own_expert = (
+        jnp.arange(experts_total, dtype=jnp.int32)[None, :] == expert_id * sections + section_id
+    ).astype(jnp.float32)
+
+    def row_scale(expert_rows, small_weights):
+        _, gate, coef = coefficients(expert_rows, small_weights, own_expert)
+        return coef[:, 1:2] * gate
+
     def dense_in(mid_seq, up_mat):
         hidden = product(mid_seq, up_mat)
         return hidden, low(gelu_tanh(hidden))
@@ -656,31 +698,35 @@
         params = first_params
         table, hot = slot_table(routes_all[0].reshape(full_len))
         mixed, residual, mid, attn_squares = project(
-            over_dp(attended(first_qkv)), proj_both[0], own_input, params[1:2], params[3:4]
+            0, over_dp(attended(first_qkv)), proj_both, own_input, params[1:2], params[3:4]
         )
         mid_seq = gather_rows(mid)
         small_weights = params_all[0, 4:]
         exp_up_mat, exp_down_mat = by_layer(exp_up_pair)[0], by_layer(exp_down_pair)[0]
 
-        expert_rows, (gate_probs, gate, coef) = beside(
+        expert_rows, ((gate_probs, gate, coef), own_grad_seq) = beside(
             over_homes,
             packed_rows(mid_seq, table),
-            lambda mid_seq, small_weights: coefficients(mid_seq, small_weights, hot),
-            (mid_seq, small_weights),
+            lambda mid_seq, small_weights, grad: (
+                coefficients(mid_seq, small_weights, hot),
+                in_order(permute_copies(grad, DP), DP).reshape(full_len, width),
+            ),
+            (mid_seq, small_weights, own_grad),
         )
         expert_rows = expert_rows.reshape(-1, width)
         exp_hidden = product(expert_rows, exp_up_mat)
         exp_hidden_low = low(gelu_tanh(exp_hidden))
 
-        def return_work(mid_seq, up_mat, down_mat):
+        def return_work(mid_seq, expert_rows, up_mat, down_mat):
             hidden, hidden_low = dense_in(mid_seq, up_mat)
-            return hidden, hidden_low, product(hidden_low, down_mat)
-
-        returned, (hidden, hidden_low, dense_part) = beside(
+            scale = row_scale(expert_rows, small_weights)
+            return scale, hidden, hidden_low, product(hidden_low, down_mat)
+
+        returned, (scale, hidden, hidden_low, dense_part) = beside(
             over_homes,
             low(product(exp_hidden_low, exp_down_mat)).reshape(-1, slots, width),
             return_work,
-            (mid_seq,),
+            (mid_seq, expert_rows),
             (up_both[0], down_both[0]),
         )
         expert_part = product_tn(table, returned.reshape(-1, width))
@@ -707,6 +753,7 @@
             residual=residual,
             mid_seq=mid_seq,
             expert_rows=expert_rows,
+            scale=scale,
             gate_probs=gate_probs,
             gate=gate,
             coef=coef,
@@ -718,38 +765,48 @@
             expert_part=expert_part,
         )
         squares = jnp.concatenate([attn_squares, squares], axis=0)
-        return out_low, next_normed, squares, record, settled
-
-    def forward_one(layer_in, normed):
+        return out_low, next_normed, squares, record, (*settled, own_grad_seq)
+
+    def forward_one(layer_in, normed, own_grad_seq):
         params = params_all[1].astype(jnp.float32)
         table, hot = slot_table(routes_all[1].reshape(full_len))
         normed_seq = gather_rows(normed)
         qkv = low(product(normed_seq, qkv_both[1]))
+        mixed, up_apart = beside(
+            over_dp, attended(qkv), lambda mats: (mats[0], mats[1]), (up_both,)
+        )
         mixed, residual, mid, attn_squares = project(
-            over_dp(attended(qkv)), proj_both[1], layer_in, params[1:2], params[3:4]
-        )
-        mid_seq = gather_rows(mid)
-        grad_seqs = lax.all_gather(after(cotangent[:, 0], mid_seq), DP, axis=1, tiled=True)
-        own_grad_seq = lax.dynamic_index_in_dim(grad_seqs, section_id, 0, keepdims=False)
+            1, mixed, proj_both, layer_in, params[1:2], params[3:4]
+        )
+        grad_rows, mid_seq = beside(
+            over_homes, packed_rows(own_grad_seq, table), gather_rows, (mid,)
+        )
         small_weights = params_all[1, 4:]
 
-        def dispatch_work(mid_seq, small_weights, up_mat):
-            return coefficients(mid_seq, small_weights, hot), dense_in(mid_seq, up_mat)
-
-        expert_rows, ((gate_probs, gate, coef), (hidden, hidden_low)) = beside(
+        def dispatch_work(mid_seq, small_weights, up_mat, down_both):
+            return (
+                coefficients(mid_seq, small_weights, hot),
+                dense_in(mid_seq, up_mat),
+                (down_both[0], down_both[1]),
+            )
+
+        expert_rows, ((gate_probs, gate, coef), (hidden, hidden_low), down_apart) = beside(
             over_homes,
             packed_rows(mid_seq, table),
             dispatch_work,
-            (mid_seq, small_weights, up_both[1]),
+            (mid_seq, small_weights, up_apart[1], down_both),
         )
         expert_rows = expert_rows.reshape(-1, width)
         exp_hidden = product(expert_rows, exp_up_both[1])
         exp_hidden_low = low(gelu_tanh(exp_hidden))
-        returned, dense_part = beside(
+        returned, (dense_part, scale) = beside(
             over_homes,
             low(product(exp_hidden_low, exp_down_both[1])).reshape(-1, slots, width),
-            product,
-            (hidden_low, down_both[1]),
+            lambda hidden_low, down_mat, expert_rows: (
+                product(hidden_low, down_mat),
+                row_scale(expert_rows, small_weights),
+            ),
+            (hidden_low, down_apart[1], expert_rows),
         )
         expert_part = product_tn(table, returned.reshape(-1, width))
         branch_part = coef[:, 0:1] * dense_part + coef[:, 1:2] * gate * expert_part
@@ -766,6 +823,7 @@
             residual=residual,
             mid_seq=mid_seq,
             expert_rows=expert_rows,
+            scale=scale,
             gate_probs=gate_probs,
             gate=gate,
             coef=coef,
@@ -776,18 +834,13 @@
             exp_hidden_low=exp_hidden_low,
             expert_part=expert_part,
         )
-        return branch, attn_squares, record, own_grad_seq
+        return branch, attn_squares, record, grad_rows, up_apart, down_apart
 
     def over_expert(grad_mat):
         return lax.psum_scatter(grad_mat, EX, scatter_dimension=0, tiled=True)
 
     def by_rows(grad_mat, count):
         return low(grad_mat).reshape(count, -1, grad_mat.shape[-1])
-
-    def shared_product(left_mat, right_mat):
-        return low(
-            product_tn(both_cores(left_mat), halves_for_cores(right_mat, section_id))
-        )
 
     def dp_blocks(*grad_mats):
         blocks = [by_rows(grad_mat, dp_size) for grad_mat in grad_mats]
@@ -795,13 +848,11 @@
 
     half_hidden, half_width = hidden_here // 2, width // 2
 
-    def backward_layer(layer, grad_low, grad_seq, record, sums_one=(), operands_one=None, settle=()):
+    def backward_layer(layer, grad_low, grad_seq, record, sums_one=(), operands_one=None, settle=(), grad_rows=None):
         params = record.params
         coef, gate, table = record.coef, record.gate, record.table
-        grad_seq = grad_seq.astype(jnp.float32)
-        d_expert = low(coef[:, 1:2] * gate * grad_seq)
-
         def dense_back(grad_seq, coef, down_mat, up_mat, *sums_one):
+            grad_seq = grad_seq.astype(jnp.float32)
             early = dp_blocks(*sums_one) if sums_one else ()
             d_dense = low(coef[:, 0:1] * grad_seq)
             dense_dot = jnp.sum(grad_seq * record.dense_part, axis=-1, keepdims=True)
@@ -814,14 +865,18 @@
             d_mid_part = product_nt(d_up, up_mat) + product(d_small, record.small_weights)
             return d_dense, d_small, d_up, d_mid_part, early
 
-        expert_grad_rows, (d_dense, d_small, d_up, d_mid_part, early) = beside(
-            over_homes,
-            packed_rows(d_expert, table),
-            dense_back,
-            (grad_seq, coef, down_both[layer], up_both[layer]),
-            tuple(sums_one),
-        )
-        expert_grad_rows = expert_grad_rows.reshape(-1, width)
+        dense_operands = (grad_seq, coef, down_apart[layer], up_apart[layer])
+        if layer == 0:
+            grad_rows, dense_grad = beside(
+                over_homes,
+                packed_rows(grad_seq, table),
+                dense_back,
+                dense_operands,
+                tuple(sums_one),
+            )
+        expert_grad_rows = low(
+            record.scale * grad_rows.reshape(-1, width).astype(jnp.float32)
+        )
         d_exp_hidden = low(
             gelu_grad(record.exp_hidden, product_nt(expert_grad_rows, exp_down_both[layer]))
         )
@@ -843,9 +898,8 @@
             )
 
         def dense_grads(hidden_low, d_dense, mid_seq, d_up, d_small):
-            g_dense = [shared_product(mid_seq, d_up), shared_product(hidden_low, d_dense)]
-            g_small = product_tn(d_small, mid_seq)
-            return jnp.concatenate(g_dense, axis=1), g_small
+            g_dense = pair_grads(section_id, (mid_seq, d_up), (hidden_low, d_dense))
+            return g_dense, product_tn(d_small, mid_seq)
 
         expert_back = low(product_nt(d_exp_hidden, exp_up_both[layer])).reshape(-1, slots, width)
         if layer == 0:
@@ -853,10 +907,16 @@
                 over_homes,
                 expert_back,
                 lambda early, *mats: (sent_parts(early, DP), owner_grads(section_id, *mats)),
-                (early, owner_mats(2), owner_mats(3)),
+                (dense_grad[4], owner_mats(2), owner_mats(3)),
             )
         else:
-            returned = over_homes(expert_back)
+            returned, dense_grad = beside(
+                over_homes,
+                expert_back,
+                lambda blocks, *operands: dense_back(*started(operands, blocks)),
+                (expert_back, *dense_operands),
+            )
+        d_dense, d_small, d_up, d_mid_part, _ = dense_grad
         d_mid_part = d_mid_part + product_tn(table, returned.reshape(-1, width))
         mid_blocks, operands = lax.optimization_barrier(
             (
@@ -865,47 +925,45 @@
             )
         )
         g_dense, g_small = dense_grads(*operands)
-        dense_sum = over_expert(g_dense)
         d_mid, g_dense, g_small = lax.optimization_barrier(
             (over_dp(mid_blocks), g_dense, g_small)
         )
+        dense_sum = over_expert(g_dense)
         d_resid, d_attn, d_mixed, d_gain_one, d_shift_one = mid_back(
-            d_mid, record.residual, params[1:2], grad_low, proj_both[layer], dp_size
-        )
-        d_mixed, g_proj = beside(over_dp, d_mixed, shared_product, (record.mixed, d_attn))
-        d_qkv = attention_back(segments, record.qkv, d_mixed.reshape(full_len, head_width))
-
+            layer, d_mid, record.residual, params[1:2], grad_low, proj_both, dp_size
+        )
+        d_mixed = over_dp(d_mixed)
+
+        def attention_grads(d_mixed):
+            d_qkv = attention_back(segments, record.qkv, d_mixed.reshape(full_len, head_width))
+            return d_qkv, row_blocks(product_nt(d_qkv, qkv_both[layer]))
+
+        d_qkv, in_blocks = attention_grads(d_mixed)
         in_blocks, normed_seq, d_qkv = lax.optimization_barrier(
-            (row_blocks(product_nt(d_qkv, qkv_both[layer])), record.normed_seq, d_qkv)
-        )
-        g_attn = jnp.concatenate([g_proj, shared_product(normed_seq, d_qkv)], axis=1)
+            (in_blocks, record.normed_seq, d_qkv)
+        )
+        g_attn = pair_grads(section_id, (record.mixed, d_attn), (normed_seq, d_qkv))
         attn_sum = over_expert(g_attn)
         beside_it = (g_attn, settle)
         d_normed, beside_it = lax.optimization_barrier((over_dp(in_blocks), beside_it))
-        def finish(in_blocks):
-            return input_back(in_blocks, record.layer_in, params[0:1], d_resid)
-
-        up_moved = None
-        if layer == 0:
-            up_moved, finished = beside(
-                over_dp, by_rows(dense_sum[:, :half_hidden], dp_size), finish, (), (d_normed,)
-            )
-        else:
-            finished = finish(d_normed)
-        d_input, d_input_low, d_gain_zero, d_shift_zero = finished
+        d_input, d_input_low, d_gain_zero, d_shift_zero = input_back(
+            d_normed, record.layer_in, params[0:1], d_resid
+        )
         small_grads = (d_gain_zero, d_gain_one, d_shift_zero, d_shift_one, g_small)
         if layer == 0:
-            extra = (parts_one, owner_mats, g_exp_down, up_moved)
+            extra = (parts_one, owner_mats, g_exp_down)
         else:
             extra = (expert_operands, swapped, beside_it[1])
         return d_input, d_input_low, (dense_sum, attn_sum), small_grads, extra
 
     own_grad = lax.dynamic_index_in_dim(cotangent[:, 0], section_id, 0, keepdims=False)
     out_zero, next_normed, squares_zero, record_zero, settled = forward_zero()
-    qkv_both, exp_up_both, exp_down_both = settled
-    branch_one, attn_squares_one, record_one, own_grad_seq = forward_one(out_zero, next_normed)
+    qkv_both, exp_up_both, exp_down_both, own_grad_seq = settled
+    branch_one, attn_squares_one, record_one, grad_rows, up_apart, down_apart = forward_one(
+        out_zero, next_normed, own_grad_seq
+    )
     grad_one, grad_one_low, sums_one, small_one, operands_one = backward_layer(
-        1, own_grad, own_grad_seq, record_one, settle=branch_one
+        1, own_grad, own_grad_seq, record_one, settle=branch_one, grad_rows=grad_rows
     )
     dense_one, attn_one = sums_one
     branch_one = operands_one[2].astype(jnp.float32)
@@ -922,7 +980,7 @@
         (dense_one[:, :half_hidden], attn_one),
         operands_one,
     )
-    parts_one, owner_mats, grad_exp_down, up_zero = extra
+    parts_one, owner_mats, grad_exp_down = extra
 
     moved_one = in_order(after(parts_one, grad_zero), DP)
     small_message = pack_small(
@@ -934,7 +992,8 @@
         lambda *mats: owner_grads(section_id, *mats),
         (owner_mats(0), owner_mats(1)),
     )
-    attn_zero = over_dp(by_rows(attn_zero, dp_size))
+    up_zero = over_dp(by_rows(after(dense_zero[:, :half_hidden], small_moved), dp_size))
+    attn_zero = over_dp(by_rows(after(attn_zero, up_zero), dp_size))
     up_one, attn_one = moved_one[..., :half_hidden], moved_one[..., half_hidden:]
     down_zero, down_one = dense_zero[:, half_hidden:], dense_one[:, half_hidden:]
 

time: 602 us -> 580 us (0.963)
  matrix products: 84 us -> 65 us
  Pallas kernels: 45.2 us -> 55.9 us
  local copies, waits for them, and re-layouts: 71.8 us -> 62.8 us
  waiting for transfers between devices: 149 us -> 140 us
    all_to_all x22 -> x21, waiting for transfers between devices: 122 us -> 92.5 us  [exchange(): return lax.all_to_all(blocks, axes, split_axis=0, concat_axis=0, tiled=True)]
    dot_general x14 -> x6, matrix products: 26.4 us -> 11.4 us  [product_tn(): lax.dot_general(left_mat, right_mat, (((0,), (0,)), ((), ())), preferred_...]
    slice x3 -> x0, local copies, waits for them, and re-layouts: 13.4 us -> none  [the longest x1 4.77 us: forward_zero(): down_both[0]]
    pallas_call x7 -> x11, Pallas kernels: 10.4 us -> 21.7 us  [the longest x4 11.6 us: pair_grads(): pl.pallas_call(kernel, out_shape=jax.ShapeDtypeStruct((left_width, sum(ha...]
    squeeze x0 -> x2, local copies, waits for them, and re-layouts: none -> 9.28 us  [the longest x1 4.67 us: forward_one(): mats[1]]
    all_gather x1, waiting for transfers between devices: 0.01 us -> 7.17 us  [shards(): lax.all_gather(proj_rows.reshape(-1, width), HOMES, axis=0, tiled=True)]
    all_to_all x1 -> x2, blocking collectives: 11 us -> 18.1 us  [exchange(): return lax.all_to_all(blocks, axes, split_axis=0, concat_axis=0, tiled=True)]
    all_to_all x22 -> x21, starting transfers between devices: 87.7 us -> 82.8 us  [exchange(): return lax.all_to_all(blocks, axes, split_axis=0, concat_axis=0, tiled=True)]
  transfers between devices with their start and end apart: 80 -> 81, of which waited for: 28 -> 40; matrix products, arithmetic and copies ran while one was open for 24% -> 17% of each run, Pallas kernels for 6% -> 9%
where the time goes in v3:
time: 580 us; the launch traced here: 568 us
  waiting for transfers between devices  140 us (24%)
  starting transfers between devices  116 us (20%)
  blocking collectives  82.4 us (14%)
  matrix products  65 us (11%)
  local copies, waits for them, and re-layouts  62.8 us (11%)
  Pallas kernels  55.9 us (10%)
  other arithmetic  29.3 us (5%)
  between operations  16.2 us (3%)
    all_to_all x21, waiting for transfers between devices, exchange(): return lax.all_to_all(blocks, axes, split_axis=0, concat_axis=0, tiled=True)  92.5 us
    all_to_all x21, starting transfers between devices, exchange(): return lax.all_to_all(blocks, axes, split_axis=0, concat_axis=0, tiled=True)  82.8 us
    all_gather x4, blocking collectives, gather_rows(): return lax.all_gather(block, DP, axis=0, tiled=True)  64.3 us
    dot_general x16, matrix products, product(): return jnp.dot(left_mat, right_mat, preferred_element_type=jnp.float32)  32.8 us
    unnamed x274, local copies, waits for them, and re-layouts  31.9 us
    dot_general x14, matrix products, product_nt(): lax.dot_general(left_mat, right_mat, (((1,), (1,)), ((), ())), preferred_...  20.8 us
    all_to_all x2, blocking collectives, exchange(): return lax.all_to_all(blocks, axes, split_axis=0, concat_axis=0, tiled=True)  18.1 us
    pallas_call x2, Pallas kernels, owner_grads(): pl.pallas_call(kernel, out_shape=jax.ShapeDtypeStruct((2, left_width, rig...  15.8 us
  transfers between devices with their start and end apart: 81, of which 40 were waited for; matrix products, arithmetic and copies ran while one was open for 17% of the time, Pallas kernels for 9%

profile of v3, /device:TPU:0, one launch (start us, length us, event | category | flops | bytes accessed | tf_op | source)
XLA Modules:
  0.0 568.1 jit_solution(15088011340093401866)
XLA Ops:
  10.2 3.0 collective-permute-start
  17.1 2.9 all-to-all-start
  25.5 5.1 all-to-all-done
  33.3 3.5 all-to-all-start.1
  38.4 7.2 %dynamic-slice_bitcast_fusion = (bf16[1024,1024]{1,0:T(8,128)(2,1)}, bf16[1024,1024]{1,0:T(8,128)(2,1)}, bf16[1024,1024]{1,0:T(8,128)(2,1)}, bf16[1024,1024]{1,0:T(8,128)(2,1)}) fusion(bf16[2,1024,1024]{2,1,0:T(8,128)(2,1)} %bitcast.246, s32[]{:T(128)S(6)} %select_n.195, s32[]{:T(128)S(6)} %select_n.191, bf16[2,1024,1024]{2,1,0:T(8,128)(2,1)} %bitcast.247), kind=kLoop, calls=%fused_computation.12 | loop fusion | bytes 16777224 | tf_op jit(solution)/shard_map/jit(dynamic_index_in_dim)/squeeze | solution.py:574
  45.5 3.2 all-to-all-done.1
  50.0 3.7 all-to-all-start.2
  62.7 7.1 %collective-permute-done.4.refs_2_ = bf16[64,1024]{1,0:T(8,128)(2,1)S(1)} collective-permute-done((bf16[64,1024]{1,0:T(8,128)(2,1)S(1)}, bf16[64,1024]{1,0:T(8,128)(2,1)S(1)}, u32[]{:S(2)}, u32[]{:S(2)}) %collective-permute-start.4) | collective-permute-done | bytes 131104 | tf_op jit(solution)/shard_map/ppermute | solution.py:101
  70.5 6.6 %collective-permute-done.7.refs_2_ = bf16[64,1024]{1,0:T(8,128)(2,1)S(1)} collective-permute-done((bf16[64,1024]{1,0:T(8,128)(2,1)}, bf16[64,1024]{1,0:T(8,128)(2,1)S(1)}, u32[]{:S(2)}, u32[]{:S(2)}) %collective-permute-start.7) | collective-permute-done | bytes 131104 | tf_op jit(solution)/shard_map/ppermute | solution.py:117
  84.7 3.6 all-to-all-start.3
  89.3 7.2 %all-gather.5.cloned.1.call-done = bf16[2048,1024]{1,0:T(8,128)(2,1)} async-done(((bf16[256,1024]{1,0:T(8,128)(2,1)}), bf16[2048,1024]{1,0:T(8,128)(2,1)}) %all-gather.5.cloned.1.call-update) | async-done | bytes 4194320 | tf_op jit(solution)/shard_map/all_gather | solution.py:618
  99.6 16.1 %all_gather.23.refs_0_ = bf16[256,1024]{1,0:T(8,128)(2,1)S(1)} all-gather(bf16[64,1024]{1,0:T(8,128)(2,1)S(1)} %get-tuple-element.250), channel_id=1, replica_groups=mesh['section'=2,'expert'=4,'dp'=4] {'dp'}, dimensions={0}, use_global_device_ids=true | all-gather | bytes 655360 | tf_op jit(solution)/shard_map/all_gather | solution.py:63
  121.1 3.6 all-to-all-start.4
  125.7 2.9 collective-permute-done.11.refs_2_
  128.7 13.1 %all-to-all-done.4 = bf16[8,40,1024]{2,1,0:T(8,128)(2,1)S(1)} async-done(((bf16[8,40,1024]{2,1,0:T(8,128)(2,1)}), bf16[8,40,1024]{2,1,0:T(8,128)(2,1)S(1)}, u32[]{:S(2)}, u32[]{:S(2)}) %all-to-all-start.4) | async-done | bytes 655392 | tf_op jit(solution)/shard_map/all_to_all | solution.py:54
  141.7 3.8 multiply_convert_fusion.1
  147.4 4.2 all-to-all-start.5
  153.9 3.5 fusion.58
  159.0 3.2 all-to-all-done.5
  163.8 3.9 all-to-all-start.6
  167.7 4.6 broadcast_select_fusion
  172.3 3.6 broadcast_select_fusion.4
  176.0 3.9 broadcast_select_fusion.2
  179.8 2.8 all-to-all-done.6.blocks_ref
  183.0 16.3 %all_gather.25.refs_4_ = bf16[256,1024]{1,0:T(8,128)(2,1)} all-gather(bf16[64,1024]{1,0:T(8,128)(2,1)S(1)} %get-tuple-element.279), channel_id=1, replica_groups=mesh['section'=2,'expert'=4,'dp'=4] {'dp'}, dimensions={0}, use_global_device_ids=true | all-gather | bytes 655360 | tf_op jit(solution)/shard_map/all_gather | solution.py:63
  204.4 3.3 all-to-all-start.7
  207.7 4.7 slice_bitcast_fusion.2
  217.3 3.7 all-to-all-start.8
  221.0 15.7 %all_gather.26.refs_0_ = bf16[256,1024]{1,0:T(8,128)(2,1)S(1)} all-gather(bf16[64,1024]{1,0:T(8,128)(2,1)S(1)} %get-tuple-element.288), channel_id=1, replica_groups=mesh['section'=2,'expert'=4,'dp'=4] {'dp'}, dimensions={0}, use_global_device_ids=true | all-gather | bytes 655360 | tf_op jit(solution)/shard_map/all_gather | solution.py:63
  238.2 3.4 fusion.66
  241.7 3.8 all-to-all-start.9
  245.5 4.6 slice_bitcast_fusion
  250.1 6.0 %all-to-all-done.9 = bf16[8,40,1024]{2,1,0:T(8,128)(2,1)S(1)} async-done(((bf16[8,40,1024]{2,1,0:T(8,128)(2,1)}), bf16[8,40,1024]{2,1,0:T(8,128)(2,1)S(1)}, u32[]{:S(2)}, u32[]{:S(2)}) %all-to-all-start.9) | async-done | bytes 655392 | tf_op jit(solution)/shard_map/all_to_all | solution.py:54
  256.1 3.8 multiply_convert_fusion
  262.1 4.4 all-to-all-start.10
  266.6 3.3 fusion.129
  269.9 7.2 %all-to-all-done.10 = bf16[8,40,1024]{2,1,0:T(8,128)(2,1)} async-done(((bf16[8,40,1024]{2,1,0:T(8,128)(2,1)}), bf16[8,40,1024]{2,1,0:T(8,128)(2,1)}, u32[]{:S(2)}, u32[]{:S(2)}) %all-to-all-start.10) | async-done | bytes 655392 | tf_op jit(solution)/shard_map/all_to_all | solution.py:54
  278.4 3.7 fusion.29.refs_6_
  286.6 4.2 all-to-all-start.11
  291.5 3.4 fusion.43.refs_2_
  297.0 4.5 all-to-all-done.11
  304.3 5.0 all-to-all-start.12
  319.4 6.4 %all-to-all-done.12.blocks_ref = bf16[4,64,1024]{2,1,0:T(8,128)(2,1)} async-done(((bf16[4,64,1024]{2,1,0:T(8,128)(2,1)}), bf16[4,64,1024]{2,1,0:T(8,128)(2,1)}, u32[]{:S(2)}, u32[]{:S(2)}) %all-to-all-start.12) | async-done | bytes 524320 | tf_op jit(solution)/shard_map/all_to_all | solution.py:54
  331.0 9.4 %all_to_all.115 = bf16[4,64,256]{2,1,0:T(8,128)(2,1)S(1)} all-to-all(bf16[4,64,256]{2,1,0:T(8,128)(2,1)S(1)} %get-tuple-element.334), channel_id=1, replica_groups=mesh['section'=2,'expert'=4,'dp'=4] {'dp'}, dimensions={0} | all-to-all | bytes 262144 | tf_op jit(solution)/shard_map/all_to_all | solution.py:54
  345.4 4.1 all-to-all-start.14
  351.4 3.9 pair_grads.5
  357.1 7.6 %all-to-all-done.14.blocks_ref = bf16[4,64,1024]{2,1,0:T(8,128)(2,1)} async-done(((bf16[4,64,1024]{2,1,0:T(8,128)(2,1)}), bf16[4,64,1024]{2,1,0:T(8,128)(2,1)}, u32[]{:S(2)}, u32[]{:S(2)}) %all-to-all-start.14) | async-done | bytes 524320 | tf_op jit(solution)/shard_map/all_to_all | solution.py:54
  367.3 16.3 %all_gather.27 = bf16[256,1024]{1,0:T(8,128)(2,1)S(1)} all-gather(bf16[64,1024]{1,0:T(8,128)(2,1)S(1)} %get-tuple-element.343.grad_ref), channel_id=1, replica_groups=mesh['section'=2,'expert'=4,'dp'=4] {'dp'}, dimensions={0}, use_global_device_ids=true | all-gather | bytes 655360 | tf_op jit(solution)/shard_map/all_gather | solution.py:63
  385.5 4.2 all-to-all-start.15
  404.8 3.6 fusion.22.refs_4_
  411.1 4.5 all-to-all-start.16
  425.9 7.8 %owner_grads.2 = f32[2,1024,1024]{2,1,0:T(8,128)} custom-call(s32[1]{0:T(128)} %bitcast.place, bf16[320,1024]{1,0:T(8,128)(2,1)S(1)} %copy-done.37, bf16[320,1024]{1,0:T(8,128)(2,1)} %collective-permute-done.25.refs_1_, bf16[320,1024]{1,0:T(8,128)(2,1)S(1)} %copy-done.39, bf16[320,1024]{1,0:T(8,128)(2,1)} %collective-permute-done.26.refs_3_, ...), custom_call_target="tpu_custom_call" | custom-call | tf_op jit(solution)/shard_map/owner_grads/pallas_call | solution.py:360
  437.9 5.8 %all-to-all-start.17 = ((bf16[4,64,1024]{2,1,0:T(8,128)(2,1)}), bf16[4,64,1024]{2,1,0:T(8,128)(2,1)}, u32[]{:S(2)}, u32[]{:S(2)}) async-start(bf16[4,64,1024]{2,1,0:T(8,128)(2,1)} %bitcast.256), calls=%async_computation.20 | async-start | bytes 1048576 | tf_op jit(solution)/shard_map/all_to_all | solution.py:54
  451.5 6.7 %all-to-all-done.17.blocks_ref = bf16[4,64,1024]{2,1,0:T(8,128)(2,1)} async-done(((bf16[4,64,1024]{2,1,0:T(8,128)(2,1)}), bf16[4,64,1024]{2,1,0:T(8,128)(2,1)}, u32[]{:S(2)}, u32[]{:S(2)}) %all-to-all-start.17) | async-done | bytes 524320 | tf_op jit(solution)/shard_map/all_to_all | solution.py:54
  462.9 8.7 %all_to_all.116 = bf16[4,64,256]{2,1,0:T(8,128)(2,1)S(1)} all-to-all(bf16[4,64,256]{2,1,0:T(8,128)(2,1)S(1)} %get-tuple-element.388), channel_id=1, replica_groups=mesh['section'=2,'expert'=4,'dp'=4] {'dp'}, dimensions={0} | all-to-all | bytes 262144 | tf_op jit(solution)/shard_map/all_to_all | solution.py:54
  481.1 3.6 all-to-all-start.19
  488.1 11.6 %all-to-all-done.19.blocks_ref = bf16[4,64,1024]{2,1,0:T(8,128)(2,1)S(1)} async-done(((bf16[4,64,1024]{2,1,0:T(8,128)(2,1)}), bf16[4,64,1024]{2,1,0:T(8,128)(2,1)S(1)}, u32[]{:S(2)}, u32[]{:S(2)}) %all-to-all-start.19) | async-done | bytes 524320 | tf_op jit(solution)/shard_map/all_to_all | solution.py:54
  503.9 3.9 all-to-all-start.20
  509.0 8.1 %owner_grads.3 = f32[2,1024,1024]{2,1,0:T(8,128)} custom-call(s32[1]{0:T(128)} %bitcast.place, bf16[320,1024]{1,0:T(8,128)(2,1)S(1)} %bitcast.222, bf16[320,1024]{1,0:T(8,128)(2,1)} %collective-permute-done.42.refs_1_, bf16[320,1024]{1,0:T(8,128)(2,1)S(1)} %bitcast.226, bf16[320,1024]{1,0:T(8,128)(2,1)} %collective-permute-done.43.refs_3_, ...), custom_call_target="tpu_custom_call" | custom-call | tf_op jit(solution)/shard_map/owner_grads/pallas_call | solution.py:360
  520.6 3.4 all-to-all-start.21
  524.1 7.8 %reduce-scatter.14.cloned.1.call-done = bf16[256,896]{1,0:T(8,128)(2,1)} async-done(((bf16[1024,896]{1,0:T(8,128)(2,1)}), bf16[256,896]{1,0:T(8,128)(2,1)}) %reduce-scatter.14.cloned.1.call-update) | async-done | bytes 458768 | tf_op jit(solution)/shard_map/reduce_scatter | solution.py:840
  533.1 3.5 all-to-all-start.22
  540.6 9.0 %all-to-all-done.22.refs_4_ = bf16[4,64,896]{2,1,0:T(8,128)(2,1)S(1)} async-done(((bf16[4,64,896]{2,1,0:T(8,128)(2,1)}), bf16[4,64,896]{2,1,0:T(8,128)(2,1)S(1)}, u32[]{:S(2)}, u32[]{:S(2)}) %all-to-all-start.22) | async-done | bytes 458784 | tf_op jit(solution)/shard_map/all_to_all | solution.py:54
  557.7 3.2 finish_weights.1
  (561 shorter events, 185.6 us)
Async XLA Ops:
  7.2 70.9 %all-gather.9.cloned.1.call-start = ((), (), s32[]{:S(2)}) async-start(), calls=%async_computation.35 | async-start | bytes 4718592 | tf_op jit(solution)/shard_map/all_gather | solution.py:634
  10.2 12.8 %collective-permute-start = (bf16[64,1024]{1,0:T(8,128)(2,1)}, bf16[64,1024]{1,0:T(8,128)(2,1)S(1)}, u32[]{:S(2)}, u32[]{:S(2)}) collective-permute-start(bf16[64,1024]{1,0:T(8,128)(2,1)} %bitcast.234), channel_id=1, source_target_pairs={{3,0},{0,1},{1,2},{2,3},{7,4},{4,5},{5,6},{6,7},{11,8},{8,9},{9,10... | collective-permute-start | bytes 393224 | tf_op jit(solution)/shard_map/ppermute | solution.py:101
  13.2 11.4 %collective-permute-start.1 = (bf16[64,1024]{1,0:T(8,128)(2,1)}, bf16[64,1024]{1,0:T(8,128)(2,1)S(1)}, u32[]{:S(2)}, u32[]{:S(2)}) collective-permute-start(bf16[64,1024]{1,0:T(8,128)(2,1)} %bitcast.235), channel_id=1, source_target_pairs={{2,0},{3,1},{0,2},{1,3},{6,4},{7,5},{4,6},{5,7},{10,8},{11,9},{8,1... | collective-permute-start | bytes 393224 | tf_op jit(solution)/shard_map/ppermute | solution.py:101
  15.8 8.9 %collective-permute-start.2 = (bf16[64,1024]{1,0:T(8,128)(2,1)}, bf16[64,1024]{1,0:T(8,128)(2,1)S(1)}, u32[]{:S(2)}, u32[]{:S(2)}) collective-permute-start(bf16[64,1024]{1,0:T(8,128)(2,1)} %bitcast.236), channel_id=1, source_target_pairs={{1,0},{2,1},{3,2},{0,3},{5,4},{6,5},{7,6},{4,7},{9,8},{10,9},{11,1... | collective-permute-start | bytes 393224 | tf_op jit(solution)/shard_map/ppermute | solution.py:101
  17.1 13.4 %all-to-all-start = ((bf16[32,8,128]{2,1,0:T(8,128)(2,1)}), bf16[32,8,128]{2,1,0:T(8,128)(2,1)S(1)}, u32[]{:S(2)}, u32[]{:S(2)}) async-start(bf16[32,8,128]{2,1,0:T(8,128)(2,1)} %broadcast_in_dim.53), calls=%async_computation | async-start | bytes 131072 | tf_op jit(solution)/shard_map/all_to_all | solution.py:54
  20.1 76.4 %all-gather.5.cloned.1.call-start = ((), (), s32[]{:S(2)}) async-start(), calls=%async_computation.28 | async-start | bytes 4718592 | tf_op jit(solution)/shard_map/all_gather | solution.py:618
  33.3 15.4 %all-to-all-start.1 = ((bf16[4,64,768]{2,1,0:T(8,128)(2,1)}), bf16[4,64,768]{2,1,0:T(8,128)(2,1)S(1)}, u32[]{:S(2)}, u32[]{:S(2)}) async-start(bf16[4,64,768]{2,1,0:T(8,128)(2,1)} %reshape.447), calls=%async_computation.1 | async-start | bytes 786432 | tf_op jit(solution)/shard_map/all_to_all | solution.py:54
  50.0 28.1 %all-to-all-start.2 = ((bf16[4,4,64,768]{3,2,1,0:T(8,128)(2,1)}), bf16[4,4,64,768]{3,2,1,0:T(8,128)(2,1)S(1)}, u32[]{:S(2)}, u32[]{:S(2)}) async-start(bf16[4,4,64,768]{3,2,1,0:T(8,128)(2,1)} %broadcast_in_dim.55), calls=%async_computation.2 | async-start | bytes 3145728 | tf_op jit(solution)/shard_map/all_to_all | solution.py:54
  53.8 100.1 %all-gather.7.cloned.1.call-start = ((), (), s32[]{:S(2)}) async-start(), calls=%async_computation.29 | async-start | bytes 4718592 | tf_op jit(solution)/shard_map/all_gather | solution.py:651
  53.8 8.3 %collective-permute-start.3 = (bf16[64,1024]{1,0:T(8,128)(2,1)S(1)}, bf16[64,1024]{1,0:T(8,128)(2,1)S(1)}, u32[]{:S(2)}, u32[]{:S(2)}) collective-permute-start(bf16[64,1024]{1,0:T(8,128)(2,1)S(1)} %fusion.80.refs_0_), channel_id=1, source_target_pairs={{3,0},{0,1},{1,2},{2,3},{7,4},{4,5},{5,6},{6,7},{11,8},{8,9},{9,10... | collective-permute-start | bytes 393224 | tf_op jit(solution)/shard_map/ppermute | solution.py:101
  53.9 15.9 %collective-permute-start.4 = (bf16[64,1024]{1,0:T(8,128)(2,1)S(1)}, bf16[64,1024]{1,0:T(8,128)(2,1)S(1)}, u32[]{:S(2)}, u32[]{:S(2)}) collective-permute-start(bf16[64,1024]{1,0:T(8,128)(2,1)S(1)} %fusion.80.refs_0_), channel_id=1, source_target_pairs={{2,0},{3,1},{0,2},{1,3},{6,4},{7,5},{4,6},{5,7},{10,8},{11,9},{8,1... | collective-permute-start | bytes 393224 | tf_op jit(solution)/shard_map/ppermute | solution.py:101
  55.9 13.9 %collective-permute-start.5 = (bf16[64,1024]{1,0:T(8,128)(2,1)S(1)}, bf16[64,1024]{1,0:T(8,128)(2,1)S(1)}, u32[]{:S(2)}, u32[]{:S(2)}) collective-permute-start(bf16[64,1024]{1,0:T(8,128)(2,1)S(1)} %fusion.80.refs_0_), channel_id=1, source_target_pairs={{1,0},{2,1},{3,2},{0,3},{5,4},{6,5},{7,6},{4,7},{9,8},{10,9},{11,1... | collective-permute-start | bytes 393224 | tf_op jit(solution)/shard_map/ppermute | solution.py:101
  57.7 12.8 %collective-permute-start.6 = (bf16[64,1024]{1,0:T(8,128)(2,1)}, bf16[64,1024]{1,0:T(8,128)(2,1)S(1)}, u32[]{:S(2)}, u32[]{:S(2)}) collective-permute-start(bf16[64,1024]{1,0:T(8,128)(2,1)} %get-tuple-element.244), channel_id=1, source_target_pairs={{3,0},{0,1},{1,2},{2,3},{7,4},{4,5},{5,6},{6,7},{11,8},{8,9},{9,10... | collective-permute-start | bytes 393224 | tf_op jit(solution)/shard_map/ppermute | solution.py:117
  58.3 18.9 %collective-permute-start.7 = (bf16[64,1024]{1,0:T(8,128)(2,1)}, bf16[64,1024]{1,0:T(8,128)(2,1)S(1)}, u32[]{:S(2)}, u32[]{:S(2)}) collective-permute-start(bf16[64,1024]{1,0:T(8,128)(2,1)} %get-tuple-element.245), channel_id=1, source_target_pairs={{2,0},{3,1},{0,2},{1,3},{6,4},{7,5},{4,6},{5,7},{10,8},{11,9},{8,1... | collective-permute-start | bytes 393224 | tf_op jit(solution)/shard_map/ppermute | solution.py:117
  62.2 15.0 %collective-permute-start.8 = (bf16[64,1024]{1,0:T(8,128)(2,1)S(1)}, bf16[64,1024]{1,0:T(8,128)(2,1)S(1)}, u32[]{:S(2)}, u32[]{:S(2)}) collective-permute-start(bf16[64,1024]{1,0:T(8,128)(2,1)S(1)} %copy-done.106), channel_id=1, source_target_pairs={{1,0},{2,1},{3,2},{0,3},{5,4},{6,5},{7,6},{4,7},{9,8},{10,9},{11,1... | collective-permute-start | bytes 393224 | tf_op jit(solution)/shard_map/ppermute | solution.py:117
  80.1 61.6 %collective-permute-start.13 = (bf16[1024,1024]{1,0:T(8,128)(2,1)}, bf16[1024,1024]{1,0:T(8,128)(2,1)}, u32[]{:S(2)}, u32[]{:S(2)}) collective-permute-start(bf16[1024,1024]{1,0:T(8,128)(2,1)} %get-tuple-element.258), channel_id=1, source_target_pairs={{0,16},{16,0},{1,17},{17,1},{2,18},{18,2},{3,19},{19,3},{4,20},{20... | collective-permute-start | bytes 6291464 | tf_op jit(solution)/shard_map/ppermute | solution.py:525
  80.4 65.1 %collective-permute-start.14 = (bf16[1024,1024]{1,0:T(8,128)(2,1)}, bf16[1024,1024]{1,0:T(8,128)(2,1)}, u32[]{:S(2)}, u32[]{:S(2)}) collective-permute-start(bf16[1024,1024]{1,0:T(8,128)(2,1)} %get-tuple-element.260), channel_id=1, source_target_pairs={{0,16},{16,0},{1,17},{17,1},{2,18},{18,2},{3,19},{19,3},{4,20},{20... | collective-permute-start | bytes 6291464 | tf_op jit(solution)/shard_map/ppermute | solution.py:525
  84.7 11.8 %all-to-all-start.3 = ((bf16[4,64,256]{2,1,0:T(8,128)(2,1)}), bf16[4,64,256]{2,1,0:T(8,128)(2,1)S(1)}, u32[]{:S(2)}, u32[]{:S(2)}) async-start(bf16[4,64,256]{2,1,0:T(8,128)(2,1)} %bitcast.30), calls=%async_computation.3 | async-start | bytes 262144 | tf_op jit(solution)/shard_map/all_to_all | solution.py:54
  116.8 8.9 %collective-permute-start.10 = (bf16[64,1024]{1,0:T(8,128)(2,1)S(1)}, bf16[64,1024]{1,0:T(8,128)(2,1)S(1)}, u32[]{:S(2)}, u32[]{:S(2)}) collective-permute-start(bf16[64,1024]{1,0:T(8,128)(2,1)S(1)} %dynamic-slice_bitcast_fusion.4.refs_0_.grad_ref), channel_id=1, source_target_pairs={{3,0},{0,1},{1,2},{2,3},{7,4},{4,5},{5,6},{6,7},{11,8},{8,9},{9,10... | collective-permute-start | bytes 393224 | tf_op jit(solution)/shard_map/ppermute | solution.py:101
  118.6 10.0 %collective-permute-start.11 = (bf16[64,1024]{1,0:T(8,128)(2,1)S(1)}, bf16[64,1024]{1,0:T(8,128)(2,1)S(1)}, u32[]{:S(2)}, u32[]{:S(2)}) collective-permute-start(bf16[64,1024]{1,0:T(8,128)(2,1)S(1)} %dynamic-slice_bitcast_fusion.4.refs_0_.grad_ref), channel_id=1, source_target_pairs={{2,0},{3,1},{0,2},{1,3},{6,4},{7,5},{4,6},{5,7},{10,8},{11,9},{8,1... | collective-permute-start | bytes 393224 | tf_op jit(solution)/shard_map/ppermute | solution.py:101
  121.1 7.5 %collective-permute-start.12 = (bf16[64,1024]{1,0:T(8,128)(2,1)S(1)}, bf16[64,1024]{1,0:T(8,128)(2,1)S(1)}, u32[]{:S(2)}, u32[]{:S(2)}) collective-permute-start(bf16[64,1024]{1,0:T(8,128)(2,1)S(1)} %dynamic-slice_bitcast_fusion.4.refs_0_.grad_ref), channel_id=1, source_target_pairs={{1,0},{2,1},{3,2},{0,3},{5,4},{6,5},{7,6},{4,7},{9,8},{10,9},{11,1... | collective-permute-start | bytes 393224 | tf_op jit(solution)/shard_map/ppermute | solution.py:101
  121.1 20.6 %all-to-all-start.4 = ((bf16[8,40,1024]{2,1,0:T(8,128)(2,1)}), bf16[8,40,1024]{2,1,0:T(8,128)(2,1)S(1)}, u32[]{:S(2)}, u32[]{:S(2)}) async-start(bf16[8,40,1024]{2,1,0:T(8,128)(2,1)} %bitcast.33), calls=%async_computation.4 | async-start | bytes 1310720 | tf_op jit(solution)/shard_map/all_to_all | solution.py:54
  147.4 14.8 %all-to-all-start.5 = ((bf16[8,40,1024]{2,1,0:T(8,128)(2,1)}), bf16[8,40,1024]{2,1,0:T(8,128)(2,1)S(1)}, u32[]{:S(2)}, u32[]{:S(2)}) async-start(bf16[8,40,1024]{2,1,0:T(8,128)(2,1)} %bitcast.263), calls=%async_computation.5 | async-start | bytes 1310720 | tf_op jit(solution)/shard_map/all_to_all | solution.py:54
  163.8 18.8 %all-to-all-start.6 = ((bf16[4,64,1024]{2,1,0:T(8,128)(2,1)}), bf16[4,64,1024]{2,1,0:T(8,128)(2,1)S(1)}, u32[]{:S(2)}, u32[]{:S(2)}) async-start(bf16[4,64,1024]{2,1,0:T(8,128)(2,1)} %bitcast.257), calls=%async_computation.6 | async-start | bytes 1048576 | tf_op jit(solution)/shard_map/all_to_all | solution.py:54
  204.4 9.2 %all-to-all-start.7 = ((bf16[4,64,256]{2,1,0:T(8,128)(2,1)}), bf16[4,64,256]{2,1,0:T(8,128)(2,1)S(1)}, u32[]{:S(2)}, u32[]{:S(2)}) async-start(bf16[4,64,256]{2,1,0:T(8,128)(2,1)} %bitcast.44), calls=%async_computation.7 | async-start | bytes 262144 | tf_op jit(solution)/shard_map/all_to_all | solution.py:54
  217.3 19.4 %all-to-all-start.8 = ((bf16[8,40,1024]{2,1,0:T(8,128)(2,1)}), bf16[8,40,1024]{2,1,0:T(8,128)(2,1)S(1)}, u32[]{:S(2)}, u32[]{:S(2)}) async-start(bf16[8,40,1024]{2,1,0:T(8,128)(2,1)} %bitcast.48), calls=%async_computation.8 | async-start | bytes 1310720 | tf_op jit(solution)/shard_map/all_to_all | solution.py:54
  241.7 14.4 %all-to-all-start.9 = ((bf16[8,40,1024]{2,1,0:T(8,128)(2,1)}), bf16[8,40,1024]{2,1,0:T(8,128)(2,1)S(1)}, u32[]{:S(2)}, u32[]{:S(2)}) async-start(bf16[8,40,1024]{2,1,0:T(8,128)(2,1)} %bitcast.249), calls=%async_computation.9 | async-start | bytes 1310720 | tf_op jit(solution)/shard_map/all_to_all | solution.py:54
  262.1 15.1 %all-to-all-start.10 = ((bf16[8,40,1024]{2,1,0:T(8,128)(2,1)}), bf16[8,40,1024]{2,1,0:T(8,128)(2,1)}, u32[]{:S(2)}, u32[]{:S(2)}) async-start(bf16[8,40,1024]{2,1,0:T(8,128)(2,1)} %bitcast.264), calls=%async_computation.10 | async-start | bytes 1310720 | tf_op jit(solution)/shard_map/all_to_all | solution.py:54
  286.6 14.9 %all-to-all-start.11 = ((bf16[8,40,1024]{2,1,0:T(8,128)(2,1)}), bf16[8,40,1024]{2,1,0:T(8,128)(2,1)}, u32[]{:S(2)}, u32[]{:S(2)}) async-start(bf16[8,40,1024]{2,1,0:T(8,128)(2,1)} %bitcast.261), calls=%async_computation.11 | async-start | bytes 1310720 | tf_op jit(solution)/shard_map/all_to_all | solution.py:54
  290.9 66.2 %reduce-scatter.6.cloned.1.call-start = ((), (), s32[]{:S(2)}) async-start(), calls=%async_computation.30 | async-start | bytes 655360 | tf_op jit(solution)/shard_map/reduce_scatter | solution.py:813
  304.3 21.5 %all-to-all-start.12 = ((bf16[4,64,1024]{2,1,0:T(8,128)(2,1)}), bf16[4,64,1024]{2,1,0:T(8,128)(2,1)}, u32[]{:S(2)}, u32[]{:S(2)}) async-start(bf16[4,64,1024]{2,1,0:T(8,128)(2,1)} %bitcast.255), calls=%async_computation.12 | async-start | bytes 1048576 | tf_op jit(solution)/shard_map/all_to_all | solution.py:54
  309.2 87.5 %reduce-scatter.8.cloned.1.call-start = ((), (), s32[]{:S(2)}) async-start(), calls=%async_computation.31 | async-start | bytes 2621440 | tf_op jit(solution)/shard_map/reduce_scatter | solution.py:840
  344.4 6.1 %collective-permute-start.22 = (bf16[256,1024]{1,0:T(8,128)(2,1)}, bf16[256,1024]{1,0:T(8,128)(2,1)}, u32[]{:S(2)}, u32[]{:S(2)}) collective-permute-start(bf16[256,1024]{1,0:T(8,128)(2,1)} %all_gather.25.refs_4_), channel_id=1, source_target_pairs={{0,16},{16,0},{1,17},{17,1},{2,18},{18,2},{3,19},{19,3},{4,20},{20... | collective-permute-start | bytes 1572872 | tf_op jit(solution)/shard_map/ppermute | solution.py:525
  344.4 6.1 %collective-permute-start.23 = (bf16[256,768]{1,0:T(8,128)(2,1)S(1)}, bf16[256,768]{1,0:T(8,128)(2,1)}, u32[]{:S(2)}, u32[]{:S(2)}) collective-permute-start(bf16[256,768]{1,0:T(8,128)(2,1)S(1)} %attention_back.2.refs_6_), channel_id=1, source_target_pairs={{0,16},{16,0},{1,17},{17,1},{2,18},{18,2},{3,19},{19,3},{4,20},{20... | collective-permute-start | bytes 1179656 | tf_op jit(solution)/shard_map/ppermute | solution.py:525
  344.9 4.9 collective-permute-start.20
  345.0 4.9 collective-permute-start.21
  345.4 19.2 %all-to-all-start.14 = ((bf16[4,64,1024]{2,1,0:T(8,128)(2,1)}), bf16[4,64,1024]{2,1,0:T(8,128)(2,1)}, u32[]{:S(2)}, u32[]{:S(2)}) async-start(bf16[4,64,1024]{2,1,0:T(8,128)(2,1)} %bitcast.252), calls=%async_computation.14 | async-start | bytes 1048576 | tf_op jit(solution)/shard_map/all_to_all | solution.py:54
  349.6 49.9 %reduce-scatter.10.cloned.1.call-start = ((), (), s32[]{:S(2)}) async-start(), calls=%async_computation.32 | async-start | bytes 2293760 | tf_op jit(solution)/shard_map/reduce_scatter | solution.py:840
  355.3 54.9 %collective-permute-start.25 = (bf16[320,1024]{1,0:T(8,128)(2,1)}, bf16[320,1024]{1,0:T(8,128)(2,1)}, u32[]{:S(2)}, u32[]{:S(2)}) collective-permute-start(bf16[320,1024]{1,0:T(8,128)(2,1)} %copy-done.36), channel_id=1, source_target_pairs={{0,16},{16,0},{1,17},{17,1},{2,18},{18,2},{3,19},{19,3},{4,20},{20... | collective-permute-start | bytes 1966088 | tf_op jit(solution)/shard_map/ppermute | solution.py:525
  356.6 53.7 %collective-permute-start.26 = (bf16[320,1024]{1,0:T(8,128)(2,1)}, bf16[320,1024]{1,0:T(8,128)(2,1)}, u32[]{:S(2)}, u32[]{:S(2)}) collective-permute-start(bf16[320,1024]{1,0:T(8,128)(2,1)} %copy-done.38), channel_id=1, source_target_pairs={{0,16},{16,0},{1,17},{17,1},{2,18},{18,2},{3,19},{19,3},{4,20},{20... | collective-permute-start | bytes 1966088 | tf_op jit(solution)/shard_map/ppermute | solution.py:525
  356.7 53.6 %collective-permute-start.28 = (bf16[320,1024]{1,0:T(8,128)(2,1)S(1)}, bf16[320,1024]{1,0:T(8,128)(2,1)}, u32[]{:S(2)}, u32[]{:S(2)}) collective-permute-start(bf16[320,1024]{1,0:T(8,128)(2,1)S(1)} %fusion.31.refs_6_), channel_id=1, source_target_pairs={{0,16},{16,0},{1,17},{17,1},{2,18},{18,2},{3,19},{19,3},{4,20},{20... | collective-permute-start | bytes 1966088 | tf_op jit(solution)/shard_map/ppermute | solution.py:525
  385.5 17.9 %all-to-all-start.15 = ((bf16[8,40,1024]{2,1,0:T(8,128)(2,1)}), bf16[8,40,1024]{2,1,0:T(8,128)(2,1)}, u32[]{:S(2)}, u32[]{:S(2)}) async-start(bf16[8,40,1024]{2,1,0:T(8,128)(2,1)} %bitcast.248), calls=%async_computation.16 | async-start | bytes 1310720 | tf_op jit(solution)/shard_map/all_to_all | solution.py:54
  404.6 5.6 collective-permute-start.27
  411.1 24.0 %all-to-all-start.16 = ((bf16[8,40,1024]{2,1,0:T(8,128)(2,1)}), bf16[8,40,1024]{2,1,0:T(8,128)(2,1)}, u32[]{:S(2)}, u32[]{:S(2)}) async-start(bf16[8,40,1024]{2,1,0:T(8,128)(2,1)} %bitcast.262), calls=%async_computation.19 | async-start | bytes 1310720 | tf_op jit(solution)/shard_map/all_to_all | solution.py:54
  415.7 18.0 %collective-permute-start.29 = (bf16[64,1408]{1,0:T(8,128)(2,1)}, bf16[64,1408]{1,0:T(8,128)(2,1)S(1)}, u32[]{:S(2)}, u32[]{:S(2)}) collective-permute-start(bf16[64,1408]{1,0:T(8,128)(2,1)} %get-tuple-element.365), channel_id=1, source_target_pairs={{3,0},{0,1},{1,2},{2,3},{7,4},{4,5},{5,6},{6,7},{11,8},{8,9},{9,10... | collective-permute-start | bytes 540680 | tf_op jit(solution)/shard_map/ppermute | solution.py:117
  417.5 16.1 %collective-permute-start.30 = (bf16[64,1408]{1,0:T(8,128)(2,1)}, bf16[64,1408]{1,0:T(8,128)(2,1)S(1)}, u32[]{:S(2)}, u32[]{:S(2)}) collective-permute-start(bf16[64,1408]{1,0:T(8,128)(2,1)} %get-tuple-element.366), channel_id=1, source_target_pairs={{2,0},{3,1},{0,2},{1,3},{6,4},{7,5},{4,6},{5,7},{10,8},{11,9},{8,1... | collective-permute-start | bytes 540680 | tf_op jit(solution)/shard_map/ppermute | solution.py:117
  420.1 14.3 %collective-permute-start.31 = (bf16[64,1408]{1,0:T(8,128)(2,1)}, bf16[64,1408]{1,0:T(8,128)(2,1)S(1)}, u32[]{:S(2)}, u32[]{:S(2)}) collective-permute-start(bf16[64,1408]{1,0:T(8,128)(2,1)} %get-tuple-element.367), channel_id=1, source_target_pairs={{1,0},{2,1},{3,2},{0,3},{5,4},{6,5},{7,6},{4,7},{9,8},{10,9},{11,1... | collective-permute-start | bytes 540680 | tf_op jit(solution)/shard_map/ppermute | solution.py:117
  437.9 20.3 %all-to-all-start.17 = ((bf16[4,64,1024]{2,1,0:T(8,128)(2,1)}), bf16[4,64,1024]{2,1,0:T(8,128)(2,1)}, u32[]{:S(2)}, u32[]{:S(2)}) async-start(bf16[4,64,1024]{2,1,0:T(8,128)(2,1)} %bitcast.256), calls=%async_computation.20 | async-start | bytes 1048576 | tf_op jit(solution)/shard_map/all_to_all | solution.py:54
  443.7 75.1 %reduce-scatter.12.cloned.1.call-start = ((), (), s32[]{:S(2)}) async-start(), calls=%async_computation.33 | async-start | bytes 2621440 | tf_op jit(solution)/shard_map/reduce_scatter | solution.py:840
  458.2 73.7 %reduce-scatter.14.cloned.1.call-start = ((), (), s32[]{:S(2)}) async-start(), calls=%async_computation.34 | async-start | bytes 2293760 | tf_op jit(solution)/shard_map/reduce_scatter | solution.py:840
  481.1 18.7 %all-to-all-start.19 = ((bf16[4,64,1024]{2,1,0:T(8,128)(2,1)}), bf16[4,64,1024]{2,1,0:T(8,128)(2,1)S(1)}, u32[]{:S(2)}, u32[]{:S(2)}) async-start(bf16[4,64,1024]{2,1,0:T(8,128)(2,1)} %bitcast.251), calls=%async_computation.22 | async-start | bytes 1048576 | tf_op jit(solution)/shard_map/all_to_all | solution.py:54
  484.7 19.1 %collective-permute-start.42 = (bf16[320,1024]{1,0:T(8,128)(2,1)S(1)}, bf16[320,1024]{1,0:T(8,128)(2,1)}, u32[]{:S(2)}, u32[]{:S(2)}) collective-permute-start(bf16[320,1024]{1,0:T(8,128)(2,1)S(1)} %bitcast.221), channel_id=1, source_target_pairs={{0,16},{16,0},{1,17},{17,1},{2,18},{18,2},{3,19},{19,3},{4,20},{20... | collective-permute-start | bytes 1966088 | tf_op jit(solution)/shard_map/ppermute | solution.py:525
  484.9 19.0 %collective-permute-start.43 = (bf16[320,1024]{1,0:T(8,128)(2,1)S(1)}, bf16[320,1024]{1,0:T(8,128)(2,1)}, u32[]{:S(2)}, u32[]{:S(2)}) collective-permute-start(bf16[320,1024]{1,0:T(8,128)(2,1)S(1)} %bitcast.225), channel_id=1, source_target_pairs={{0,16},{16,0},{1,17},{17,1},{2,18},{18,2},{3,19},{19,3},{4,20},{20... | collective-permute-start | bytes 1966088 | tf_op jit(solution)/shard_map/ppermute | solution.py:525
  485.3 18.6 %collective-permute-start.45 = (bf16[320,1024]{1,0:T(8,128)(2,1)S(1)}, bf16[320,1024]{1,0:T(8,128)(2,1)}, u32[]{:S(2)}, u32[]{:S(2)}) collective-permute-start(bf16[320,1024]{1,0:T(8,128)(2,1)S(1)} %copy-done.35), channel_id=1, source_target_pairs={{0,16},{16,0},{1,17},{17,1},{2,18},{18,2},{3,19},{19,3},{4,20},{20... | collective-permute-start | bytes 1966088 | tf_op jit(solution)/shard_map/ppermute | solution.py:525
  485.4 18.5 %collective-permute-start.44 = (bf16[320,1024]{1,0:T(8,128)(2,1)}, bf16[320,1024]{1,0:T(8,128)(2,1)}, u32[]{:S(2)}, u32[]{:S(2)}) collective-permute-start(bf16[320,1024]{1,0:T(8,128)(2,1)} %copy-done.40), channel_id=1, source_target_pairs={{0,16},{16,0},{1,17},{17,1},{2,18},{18,2},{3,19},{19,3},{4,20},{20... | collective-permute-start | bytes 1966088 | tf_op jit(solution)/shard_map/ppermute | solution.py:525
  503.9 14.9 %all-to-all-start.20 = ((f32[32,16,128]{2,1,0:T(8,128)}), f32[32,16,128]{2,1,0:T(8,128)S(1)}, u32[]{:S(2)}, u32[]{:S(2)}) async-start(f32[32,16,128]{2,1,0:T(8,128)} %pack_small.1), calls=%async_computation.23 | async-start | bytes 524288 | tf_op jit(solution)/shard_map/all_to_all | solution.py:54
  520.6 12.5 %all-to-all-start.21 = ((bf16[4,64,512]{2,1,0:T(8,128)(2,1)}), bf16[4,64,512]{2,1,0:T(8,128)(2,1)S(1)}, u32[]{:S(2)}, u32[]{:S(2)}) async-start(bf16[4,64,512]{2,1,0:T(8,128)(2,1)} %bitcast.96), calls=%async_computation.25 | async-start | bytes 524288 | tf_op jit(solution)/shard_map/all_to_all | solution.py:54
  533.1 16.4 %all-to-all-start.22 = ((bf16[4,64,896]{2,1,0:T(8,128)(2,1)}), bf16[4,64,896]{2,1,0:T(8,128)(2,1)S(1)}, u32[]{:S(2)}, u32[]{:S(2)}) async-start(bf16[4,64,896]{2,1,0:T(8,128)(2,1)} %bitcast.272), calls=%async_computation.27 | async-start | bytes 917504 | tf_op jit(solution)/shard_map/all_to_all | solution.py:54
  536.6 13.0 %collective-permute-start.41 = (f32[64,1024]{1,0:T(8,128)}, f32[64,1024]{1,0:T(8,128)}, u32[]{:S(2)}, u32[]{:S(2)}) collective-permute-start(f32[64,1024]{1,0:T(8,128)} %get-tuple-element.398.refs_6_), channel_id=1, source_target_pairs={{0,16},{16,0},{1,17},{17,1},{2,18},{18,2},{3,19},{19,3},{4,20},{20... | collective-permute-start | bytes 786440 | tf_op jit(solution)/shard_map/ppermute | solution.py:525
  536.7 13.5 %collective-permute-start.40 = (f32[64,1024]{1,0:T(8,128)}, f32[64,1024]{1,0:T(8,128)}, u32[]{:S(2)}, u32[]{:S(2)}) collective-permute-start(f32[64,1024]{1,0:T(8,128)} %get-tuple-element.397.refs_4_), channel_id=1, source_target_pairs={{0,16},{16,0},{1,17},{17,1},{2,18},{18,2},{3,19},{19,3},{4,20},{20... | collective-permute-start | bytes 786440 | tf_op jit(solution)/shard_map/ppermute | solution.py:525
  537.2 18.6 %collective-permute-start.51 = (bf16[256,512]{1,0:T(8,128)(2,1)S(1)}, bf16[256,512]{1,0:T(8,128)(2,1)S(1)}, u32[]{:S(2)}, u32[]{:S(2)}) collective-permute-start(bf16[256,512]{1,0:T(8,128)(2,1)S(1)} %copy-done.32), channel_id=1, source_target_pairs={{0,16},{16,0},{1,17},{17,1},{2,18},{18,2},{3,19},{19,3},{4,20},{20... | collective-permute-start | bytes 786440 | tf_op jit(solution)/shard_map/ppermute | solution.py:525
  539.8 17.7 %collective-permute-start.49 = (bf16[4,64,896]{2,1,0:T(8,128)(2,1)S(1)}, bf16[4,64,896]{2,1,0:T(8,128)(2,1)}, u32[]{:S(2)}, u32[]{:S(2)}) collective-permute-start(bf16[4,64,896]{2,1,0:T(8,128)(2,1)S(1)} %slice.278.refs_6_), channel_id=1, source_target_pairs={{0,16},{16,0},{1,17},{17,1},{2,18},{18,2},{3,19},{19,3},{4,20},{20... | collective-permute-start | bytes 1376264 | tf_op jit(solution)/shard_map/ppermute | solution.py:525
  549.6 8.1 %collective-permute-start.48 = (bf16[4,64,896]{2,1,0:T(8,128)(2,1)S(1)}, bf16[4,64,896]{2,1,0:T(8,128)(2,1)}, u32[]{:S(2)}, u32[]{:S(2)}) collective-permute-start(bf16[4,64,896]{2,1,0:T(8,128)(2,1)S(1)} %all-to-all-done.22.refs_4_), channel_id=1, source_target_pairs={{0,16},{16,0},{1,17},{17,1},{2,18},{18,2},{3,19},{19,3},{4,20},{20... | collective-permute-start | bytes 1376264 | tf_op jit(solution)/shard_map/ppermute | solution.py:525
  549.6 7.9 %collective-permute-start.47 = (bf16[4,64,512]{2,1,0:T(8,128)(2,1)S(1)}, bf16[4,64,512]{2,1,0:T(8,128)(2,1)}, u32[]{:S(2)}, u32[]{:S(2)}) collective-permute-start(bf16[4,64,512]{2,1,0:T(8,128)(2,1)S(1)} %slice.277.refs_2_), channel_id=1, source_target_pairs={{0,16},{16,0},{1,17},{17,1},{2,18},{18,2},{3,19},{19,3},{4,20},{20... | collective-permute-start | bytes 786440 | tf_op jit(solution)/shard_map/ppermute | solution.py:525
  (155 other events, 1468.0 us)
Sparse Core Ops, SparseCore 0:
  9.9 39.9 all-gather.8
  52.4 44.0 all-gather.4
  99.0 42.7 all-gather.6
  294.2 24.9 reduce-scatter.5
  325.9 34.5 reduce-scatter.7
  363.6 35.8 reduce-scatter.9
  458.3 34.5 reduce-scatter.11
  496.0 35.8 reduce-scatter.13

commit v4 on v3

--- a/solution.py
+++ b/solution.py
@@ -303,6 +303,148 @@
     )(segments[:, None], segments[None, :], qkv, d_mixed)
 
 
+IN_HBM = pl.BlockSpec(memory_space=pltpu.HBM)
+
+
+def in_hbm(mat):
+    return pltpu.with_memory_space_constraint(mat, pltpu.HBM)
+
+
+def expert_call(kernel, name, outs, section_id, operands, up_pair, down_pair, extra=()):
+    width, hidden = up_pair[0].shape
+    half = hidden // 2
+    return pl.pallas_call(
+        kernel,
+        out_shape=[pltpu.HBM(shape, dtype) for shape, dtype in outs],
+        out_specs=[WHOLE for _ in outs],
+        in_specs=[SCALAR] + [WHOLE] * len(operands) + [IN_HBM] * (4 + len(extra)),
+        scratch_shapes=[
+            pltpu.VMEM((2, width, half), jnp.bfloat16),
+            pltpu.VMEM((2, half, width), jnp.bfloat16),
+            pltpu.SemaphoreType.DMA((2, 2)),
+        ]
+        + [pltpu.VMEM((2, mat.shape[0], half), mat.dtype) for mat in extra]
+        + [pltpu.SemaphoreType.DMA((2,)) for _ in extra],
+        compiler_params=pltpu.CompilerParams(vmem_limit_bytes=40 << 20),
+        name=name,
+    )(section_id.reshape(1), *operands, *[in_hbm(mat) for mat in (*up_pair, *down_pair, *extra)])
+
+
+def expert_weights_in(layer, place, sources, up_here, down_here, arrived):
+    half = up_here.shape[2]
+
+    def copies(which, part):
+        columns = pl.ds(part * half, half)
+        return (
+            pltpu.make_async_copy(
+                sources[which].at[:, columns], up_here.at[part], arrived.at[0, part]
+            ),
+            pltpu.make_async_copy(
+                sources[2 + which].at[columns], down_here.at[part], arrived.at[1, part]
+            ),
+        )
+
+    for which in range(2):
+
+        @pl.when((place[0] == layer) if which == 0 else (place[0] != layer))
+        def _():
+            for part in range(2):
+                for copy in copies(which, part):
+                    copy.start()
+
+    return [copies(0, part) for part in range(2)]
+
+
+def row_scales(logits, expert):
+    lane = lax.broadcasted_iota(jnp.int32, logits.shape, 1)
+    experts = logits.shape[1] - 2
+
+    def share(among, one):
+        chosen = jnp.where(among, logits, -jnp.inf)
+        weights = jnp.exp(chosen - jnp.max(chosen, axis=1, keepdims=True))
+        part = jnp.sum(jnp.where(one, weights, 0.0), axis=1, keepdims=True)
+        return part / jnp.sum(weights, axis=1, keepdims=True)
+
+    return share(lane >= experts, lane == experts + 1) * share(lane < experts, lane == expert)
+
+
+def expert_forward(layer, section_id, expert, rows, small_weights, up_pair, down_pair):
+    def kernel(place, expert_ref, rows_ref, small_ref, *refs):
+        scale_ref, hidden_ref, low_ref, part_ref, up_here, down_here, arrived = refs[4:]
+        waits = expert_weights_in(layer, place, refs[:4], up_here, down_here, arrived)
+        scale_ref[...] = row_scales(product_nt(rows_ref[...], small_ref[...]), expert_ref[0, 0])
+        half = up_here.shape[2]
+        total = None
+        for part in range(2):
+            here = slice(part * half, (part + 1) * half)
+            waits[part][0].wait()
+            hidden = product(rows_ref[...], up_here[part])
+            hidden_ref[:, here] = hidden
+            hidden_low = low(gelu_tanh(hidden))
+            low_ref[:, here] = hidden_low
+            waits[part][1].wait()
+            added = product(hidden_low, down_here[part])
+            total = added if total is None else total + added
+        part_ref[...] = low(total)
+
+    count, width = rows.shape
+    hidden = up_pair[0].shape[1]
+    outs = [((count, 1), jnp.float32), ((count, hidden), jnp.float32)]
+    outs += [((count, hidden), jnp.bfloat16), ((count, width), jnp.bfloat16)]
+    return expert_call(
+        kernel,
+        "expert_forward",
+        outs,
+        section_id,
+        (expert.reshape(1, 1), rows, small_weights),
+        up_pair,
+        down_pair,
+    )
+
+
+def expert_backward(layer, section_id, grad_rows, scale, hidden, up_pair, down_pair):
+    def kernel(place, rows_ref, scale_ref, *refs):
+        scaled_ref, d_hidden_ref, back_ref, up_here, down_here, arrived = refs[5:11]
+        hidden_here, hidden_arrived = refs[11:]
+        waits = expert_weights_in(layer, place, refs[:4], up_here, down_here, arrived)
+        half = up_here.shape[2]
+        fetches = [
+            pltpu.make_async_copy(
+                refs[4].at[:, pl.ds(part * half, half)], hidden_here.at[part], hidden_arrived.at[part]
+            )
+            for part in range(2)
+        ]
+        for fetch in fetches:
+            fetch.start()
+        scaled = low(scale_ref[...] * rows_ref[...].astype(jnp.float32))
+        scaled_ref[...] = scaled
+        total = None
+        for part in range(2):
+            here = slice(part * half, (part + 1) * half)
+            waits[part][1].wait()
+            d_low = product_nt(scaled, down_here[part])
+            fetches[part].wait()
+            d_hidden = low(gelu_grad(hidden_here[part], d_low))
+            d_hidden_ref[:, here] = d_hidden
+            waits[part][0].wait()
+            added = product_nt(d_hidden, up_here[part])
+            total = added if total is None else total + added
+        back_ref[...] = low(total)
+
+    shape = ((grad_rows.shape), jnp.bfloat16)
+    outs = [shape, (hidden.shape, jnp.bfloat16), shape]
+    return expert_call(
+        kernel,
+        "expert_backward",
+        outs,
+        section_id,
+        (grad_rows, scale),
+        up_pair,
+        down_pair,
+        (hidden,),
+    )
+
+
 def pair_grads(section_id, *pairs):
     mats = [side for left, right in pairs for side in (left, other_core(left), right, other_core(right))]
     left_width = pairs[0][0].shape[1]
@@ -327,7 +469,7 @@
     )(section_id.reshape(1), *mats)
 
 
-OWNER_TILE = 256
+OWNER_TILE = 512
 
 
 def owner_grads(section_id, left_mats, right_mats):
@@ -336,36 +478,46 @@
     tiles = left_width // OWNER_TILE
 
     def kernel(place, *refs):
-        out_ref = refs[8]
+        out_ref, left_here, right_here, arrived = refs[8:]
         expert, tile = pl.program_id(0), pl.program_id(1)
-        first = place[0] == 0
-        for source, here in enumerate(
-            (
-                first & (expert == 0),
-                first & (expert == 1),
-                ~first & (expert == 1),
-                ~first & (expert == 0),
+
+        def copies(source, slot):
+            return (
+                pltpu.make_async_copy(refs[source], left_here.at[slot], arrived.at[0, slot]),
+                pltpu.make_async_copy(refs[4 + source], right_here.at[slot], arrived.at[1, slot]),
             )
-        ):
-
-            @pl.when(here)
+
+        for first, sources in ((True, (0, 1)), (False, (3, 2))):
+            here = (place[0] == 0) if first else (place[0] != 0)
+
+            @pl.when(here & (expert == 0) & (tile == 0))
             def _():
-                left = refs[source][:, pl.ds(tile * OWNER_TILE, OWNER_TILE)]
-                out_ref[0] = product_tn(left, refs[4 + source][...])
-
-    whole = [
-        pl.BlockSpec(mat.shape, lambda expert, tile: (0, 0))
-        for mat in (*left_mats, *right_mats)
-    ]
+                for slot, source in enumerate(sources):
+                    for copy in copies(source, slot):
+                        copy.start()
+
+        @pl.when(tile == 0)
+        def _():
+            for copy in copies(0, expert):
+                copy.wait()
+
+        left = left_here[expert, :, pl.ds(tile * OWNER_TILE, OWNER_TILE)]
+        out_ref[0] = product_tn(left, right_here[expert])
+
     return pl.pallas_call(
         kernel,
         out_shape=jax.ShapeDtypeStruct((2, left_width, right_width), jnp.float32),
         grid=(2, tiles),
-        in_specs=[pl.BlockSpec(memory_space=pltpu.SMEM)] + whole,
+        in_specs=[SCALAR] + [IN_HBM] * 8,
         out_specs=pl.BlockSpec((1, OWNER_TILE, right_width), lambda expert, tile: (expert, tile, 0)),
+        scratch_shapes=[
+            pltpu.VMEM((2, rows, left_width), jnp.bfloat16),
+            pltpu.VMEM((2, rows, right_width), jnp.bfloat16),
+            pltpu.SemaphoreType.DMA((2, 2)),
+        ],
         compiler_params=pltpu.CompilerParams(vmem_limit_bytes=40 << 20),
         name="owner_grads",
-    )(section_id.reshape(1), *left_mats, *right_mats)
+    )(section_id.reshape(1), *[in_hbm(mat) for mat in (*left_mats, *right_mats)])
 
 
 def statistics(value_rows):
@@ -389,8 +541,14 @@
 
 def call(kernel, name, outs, *operands):
     specs = [
-        pl.BlockSpec(memory_space=pl.ANY) if operand.shape[1:] == (operand.shape[-1],) * 2 else WHOLE
+        pl.BlockSpec(memory_space=pltpu.HBM)
+        if operand.shape[1:] == (operand.shape[-1],) * 2
+        else WHOLE
         for operand in operands
+    ]
+    operands = [
+        operand if spec is WHOLE else pltpu.with_memory_space_constraint(operand, pltpu.HBM)
+        for operand, spec in zip(operands, specs)
     ]
     mats = [operand.shape[1:] for operand, spec in zip(operands, specs) if spec is not WHOLE]
     scratch = [pltpu.VMEM(shape, jnp.bfloat16) for shape in mats]
@@ -679,13 +837,7 @@
         coef = jax.nn.softmax(small_logits[:, experts_total:], axis=-1)
         return gate_probs, gate, coef
 
-    own_expert = (
-        jnp.arange(experts_total, dtype=jnp.int32)[None, :] == expert_id * sections + section_id
-    ).astype(jnp.float32)
-
-    def row_scale(expert_rows, small_weights):
-        _, gate, coef = coefficients(expert_rows, small_weights, own_expert)
-        return coef[:, 1:2] * gate
+    own_expert = expert_id * sections + section_id
 
     def dense_in(mid_seq, up_mat):
         hidden = product(mid_seq, up_mat)
@@ -702,7 +854,6 @@
         )
         mid_seq = gather_rows(mid)
         small_weights = params_all[0, 4:]
-        exp_up_mat, exp_down_mat = by_layer(exp_up_pair)[0], by_layer(exp_down_pair)[0]
 
         expert_rows, ((gate_probs, gate, coef), own_grad_seq) = beside(
             over_homes,
@@ -714,19 +865,19 @@
             (mid_seq, small_weights, own_grad),
         )
         expert_rows = expert_rows.reshape(-1, width)
-        exp_hidden = product(expert_rows, exp_up_mat)
-        exp_hidden_low = low(gelu_tanh(exp_hidden))
-
-        def return_work(mid_seq, expert_rows, up_mat, down_mat):
+        scale, exp_hidden, exp_hidden_low, exp_out = expert_forward(
+            0, section_id, own_expert, expert_rows, small_weights, exp_up_pair, exp_down_pair
+        )
+
+        def return_work(mid_seq, up_mat, down_mat):
             hidden, hidden_low = dense_in(mid_seq, up_mat)
-            scale = row_scale(expert_rows, small_weights)
-            return scale, hidden, hidden_low, product(hidden_low, down_mat)
-
-        returned, (scale, hidden, hidden_low, dense_part) = beside(
+            return hidden, hidden_low, product(hidden_low, down_mat)
+
+        returned, (hidden, hidden_low, dense_part) = beside(
             over_homes,
-            low(product(exp_hidden_low, exp_down_mat)).reshape(-1, slots, width),
+            exp_out.reshape(-1, slots, width),
             return_work,
-            (mid_seq, expert_rows),
+            (mid_seq,),
             (up_both[0], down_both[0]),
         )
         expert_part = product_tn(table, returned.reshape(-1, width))
@@ -734,8 +885,8 @@
         branch, settled = beside(
             over_dp,
             row_blocks(branch_part),
-            lambda *pairs: [by_layer(pair) for pair in pairs],
-            (qkv_pair, exp_up_pair, exp_down_pair),
+            lambda qkv_pair, down_both: (by_layer(qkv_pair), (down_both[0], down_both[1])),
+            (qkv_pair, down_both),
         )
         next_params = params_all[1].astype(jnp.float32)
         out_low, next_normed, squares = layer_end(
@@ -783,30 +934,21 @@
         )
         small_weights = params_all[1, 4:]
 
-        def dispatch_work(mid_seq, small_weights, up_mat, down_both):
-            return (
-                coefficients(mid_seq, small_weights, hot),
-                dense_in(mid_seq, up_mat),
-                (down_both[0], down_both[1]),
-            )
-
-        expert_rows, ((gate_probs, gate, coef), (hidden, hidden_low), down_apart) = beside(
+        def dispatch_work(mid_seq, small_weights, up_mat):
+            return coefficients(mid_seq, small_weights, hot), dense_in(mid_seq, up_mat)
+
+        expert_rows, ((gate_probs, gate, coef), (hidden, hidden_low)) = beside(
             over_homes,
             packed_rows(mid_seq, table),
             dispatch_work,
-            (mid_seq, small_weights, up_apart[1], down_both),
+            (mid_seq, small_weights, up_apart[1]),
         )
         expert_rows = expert_rows.reshape(-1, width)
-        exp_hidden = product(expert_rows, exp_up_both[1])
-        exp_hidden_low = low(gelu_tanh(exp_hidden))
-        returned, (dense_part, scale) = beside(
-            over_homes,
-            low(product(exp_hidden_low, exp_down_both[1])).reshape(-1, slots, width),
-            lambda hidden_low, down_mat, expert_rows: (
-                product(hidden_low, down_mat),
-                row_scale(expert_rows, small_weights),
-            ),
-            (hidden_low, down_apart[1], expert_rows),
+        scale, exp_hidden, exp_hidden_low, exp_out = expert_forward(
+            1, section_id, own_expert, expert_rows, small_weights, exp_up_pair, exp_down_pair
+        )
+        returned, dense_part = beside(
+            over_homes, exp_out.reshape(-1, slots, width), product, (hidden_low, down_apart[1])
         )
         expert_part = product_tn(table, returned.reshape(-1, width))
         branch_part = coef[:, 0:1] * dense_part + coef[:, 1:2] * gate * expert_part
@@ -834,7 +976,7 @@
             exp_hidden_low=exp_hidden_low,
             expert_part=expert_part,
         )
-        return branch, attn_squares, record, grad_rows, up_apart, down_apart
+        return branch, attn_squares, record, grad_rows, up_apart
 
     def over_expert(grad_mat):
         return lax.psum_scatter(grad_mat, EX, scatter_dimension=0, tiled=True)
@@ -874,11 +1016,14 @@
                 dense_operands,
                 tuple(sums_one),
             )
-        expert_grad_rows = low(
-            record.scale * grad_rows.reshape(-1, width).astype(jnp.float32)
-        )
-        d_exp_hidden = low(
-            gelu_grad(record.exp_hidden, product_nt(expert_grad_rows, exp_down_both[layer]))
+        expert_grad_rows, d_exp_hidden, expert_back = expert_backward(
+            layer,
+            section_id,
+            grad_rows.reshape(-1, width),
+            record.scale,
+            record.exp_hidden,
+            exp_up_pair,
+            exp_down_pair,
         )
         expert_operands = (
             record.expert_rows,
@@ -901,7 +1046,7 @@
             g_dense = pair_grads(section_id, (mid_seq, d_up), (hidden_low, d_dense))
             return g_dense, product_tn(d_small, mid_seq)
 
-        expert_back = low(product_nt(d_exp_hidden, exp_up_both[layer])).reshape(-1, slots, width)
+        expert_back = expert_back.reshape(-1, slots, width)
         if layer == 0:
             returned, (parts_one, g_exp_down) = beside(
                 over_homes,
@@ -925,10 +1070,13 @@
             )
         )
         g_dense, g_small = dense_grads(*operands)
+        if layer == 1:
+            dense_sum = over_expert(g_dense)
         d_mid, g_dense, g_small = lax.optimization_barrier(
             (over_dp(mid_blocks), g_dense, g_small)
         )
-        dense_sum = over_expert(g_dense)
+        if layer == 0:
+            dense_sum = over_expert(g_dense)
         d_resid, d_attn, d_mixed, d_gain_one, d_shift_one = mid_back(
             layer, d_mid, record.residual, params[1:2], grad_low, proj_both, dp_size
         )
@@ -958,8 +1106,8 @@
 
     own_grad = lax.dynamic_index_in_dim(cotangent[:, 0], section_id, 0, keepdims=False)
     out_zero, next_normed, squares_zero, record_zero, settled = forward_zero()
-    qkv_both, exp_up_both, exp_down_both, own_grad_seq = settled
-    branch_one, attn_squares_one, record_one, grad_rows, up_apart, down_apart = forward_one(
+    qkv_both, down_apart, own_grad_seq = settled
+    branch_one, attn_squares_one, record_one, grad_rows, up_apart = forward_one(
         out_zero, next_normed, own_grad_seq
     )
     grad_one, grad_one_low, sums_one, small_one, operands_one = backward_layer(

time: 580 us -> 564 us (0.972)
  Pallas kernels: 55.9 us -> 77.8 us
  matrix products: 65 us -> 44.8 us
  local copies, waits for them, and re-layouts: 62.8 us -> 46.5 us
  waiting for transfers between devices: 140 us -> 155 us
  other arithmetic: 29.3 us -> 18.5 us
    pallas_call x0 -> x4, Pallas kernels: none -> 21 us  [expert_call(): pl.pallas_call(kernel, out_shape=[pltpu.HBM(shape, dtype) for shape, dtyp...]
    unnamed x274 -> x208, local copies, waits for them, and re-layouts: 31.9 us -> 16.5 us
    dot_general x14 -> x8, matrix products: 20.8 us -> 9.44 us  [product_nt(): lax.dot_general(left_mat, right_mat, (((1,), (1,)), ((), ())), preferred_...]
    dot_general x16 -> x12, matrix products: 32.8 us -> 22.1 us  [product(): return jnp.dot(left_mat, right_mat, preferred_element_type=jnp.float32)]
    all_to_all x21, waiting for transfers between devices: 92.5 us -> 101 us  [exchange(): return lax.all_to_all(blocks, axes, split_axis=0, concat_axis=0, tiled=True)]
    select_n x3 -> x1, other arithmetic: 12.2 us -> 3.95 us  [by_layer(): jnp.where(on_first, of_other_layer, of_own_layer)]
  transfers between devices with their start and end apart: 81 -> 81, of which waited for: 40 -> 40; matrix products, arithmetic and copies ran while one was open for 17% -> 15% of each run, Pallas kernels for 9% -> 12%
where the time goes in v4:
time: 564 us; the launch traced here: 554 us
  waiting for transfers between devices  155 us (27%)
  starting transfers between devices  114 us (20%)
  blocking collectives  81.2 us (14%)
  Pallas kernels  77.8 us (14%)
  local copies, waits for them, and re-layouts  46.5 us (8%)
  matrix products  44.8 us (8%)
  other arithmetic  18.5 us (3%)
  between operations  16.2 us (3%)
    all_to_all x21, waiting for transfers between devices, exchange(): return lax.all_to_all(blocks, axes, split_axis=0, concat_axis=0, tiled=True)  101 us
    all_to_all x21, starting transfers between devices, exchange(): return lax.all_to_all(blocks, axes, split_axis=0, concat_axis=0, tiled=True)  83.1 us
    all_gather x4, blocking collectives, gather_rows(): return lax.all_gather(block, DP, axis=0, tiled=True)  63.5 us
    dot_general x12, matrix products, product(): return jnp.dot(left_mat, right_mat, preferred_element_type=jnp.float32)  22.1 us
    pallas_call x4, Pallas kernels, expert_call(): pl.pallas_call(kernel, out_shape=[pltpu.HBM(shape, dtype) for shape, dtyp...  21 us
    all_to_all x2, blocking collectives, exchange(): return lax.all_to_all(blocks, axes, split_axis=0, concat_axis=0, tiled=True)  17.7 us
    unnamed x208, local copies, waits for them, and re-layouts  16.5 us
    ppermute x9, starting transfers between devices, permute_copies(): blocks.append(lax.ppermute(block, axis, route))  15.2 us
  transfers between devices with their start and end apart: 81, of which 40 were waited for; matrix products, arithmetic and copies ran while one was open for 15% of the time, Pallas kernels for 12%

profile of v4, /device:TPU:0, one launch (start us, length us, event | category | flops | bytes accessed | tf_op | source)
XLA Modules:
  0.0 554.5 jit_solution(4690532805655973686)
XLA Ops:
  10.2 3.0 collective-permute-start
  17.1 2.9 all-to-all-start
  25.5 5.1 all-to-all-done
  32.9 3.5 all-to-all-start.1
  37.3 7.1 %dynamic-slice_bitcast_fusion = (bf16[1024,1024]{1,0:T(8,128)(2,1)}, bf16[1024,1024]{1,0:T(8,128)(2,1)}, bf16[1024,1024]{1,0:T(8,128)(2,1)}, bf16[1024,1024]{1,0:T(8,128)(2,1)}) fusion(bf16[2,1024,1024]{2,1,0:T(8,128)(2,1)} %bitcast.218, s32[]{:T(128)S(6)} %select_n.167, s32[]{:T(128)S(6)} %select_n.163, bf16[2,1024,1024]{2,1,0:T(8,128)(2,1)} %bitcast.219), kind=kLoop, calls=%fused_computation.8 | loop fusion | bytes 16777224 | tf_op jit(solution)/shard_map/jit(dynamic_index_in_dim)/squeeze | solution.py:732
  44.3 3.9 all-to-all-done.1
  49.6 4.4 all-to-all-start.2
  62.8 7.1 %collective-permute-done.4.refs_2_ = bf16[64,1024]{1,0:T(8,128)(2,1)S(1)} collective-permute-done((bf16[64,1024]{1,0:T(8,128)(2,1)S(1)}, bf16[64,1024]{1,0:T(8,128)(2,1)S(1)}, u32[]{:S(2)}, u32[]{:S(2)}) %collective-permute-start.4) | collective-permute-done | bytes 131104 | tf_op jit(solution)/shard_map/ppermute | solution.py:101
  70.7 6.6 %collective-permute-done.7.refs_2_ = bf16[64,1024]{1,0:T(8,128)(2,1)S(1)} collective-permute-done((bf16[64,1024]{1,0:T(8,128)(2,1)S(1)}, bf16[64,1024]{1,0:T(8,128)(2,1)S(1)}, u32[]{:S(2)}, u32[]{:S(2)}) %collective-permute-start.7) | collective-permute-done | bytes 131104 | tf_op jit(solution)/shard_map/ppermute | solution.py:117
  87.3 3.5 all-to-all-start.3
  90.8 5.9 %all-gather.5.cloned.1.call-done = bf16[2048,1024]{1,0:T(8,128)(2,1)} async-done(((bf16[256,1024]{1,0:T(8,128)(2,1)}), bf16[2048,1024]{1,0:T(8,128)(2,1)}) %all-gather.5.cloned.1.call-update) | async-done | bytes 4194320 | tf_op jit(solution)/shard_map/all_gather | solution.py:776
  99.4 15.7 %all_gather.23.refs_0_ = bf16[256,1024]{1,0:T(8,128)(2,1)S(1)} all-gather(bf16[64,1024]{1,0:T(8,128)(2,1)S(1)} %get-tuple-element.251), channel_id=1, replica_groups=mesh['section'=2,'expert'=4,'dp'=4] {'dp'}, dimensions={0}, use_global_device_ids=true | all-gather | bytes 655360 | tf_op jit(solution)/shard_map/all_gather | solution.py:63
  120.6 4.0 all-to-all-start.4
  128.1 13.8 %all-to-all-done.4 = bf16[8,40,1024]{2,1,0:T(8,128)(2,1)S(1)} async-done(((bf16[8,40,1024]{2,1,0:T(8,128)(2,1)}), bf16[8,40,1024]{2,1,0:T(8,128)(2,1)S(1)}, u32[]{:S(2)}, u32[]{:S(2)}) %all-to-all-start.4) | async-done | bytes 655392 | tf_op jit(solution)/shard_map/all_to_all | solution.py:54
  142.0 4.9 expert_forward.2
  146.9 4.2 all-to-all-start.5
  151.2 3.6 fusion.33
  156.5 5.4 all-to-all-done.5
  161.8 3.1 add_convert_fusion.1
  164.9 3.7 all-to-all-start.6
  169.8 4.7 slice_bitcast_fusion.2
  174.5 3.9 broadcast_select_fusion
  178.4 5.1 all-to-all-done.6.blocks_ref
  183.9 16.1 %all_gather.25.refs_4_ = bf16[256,1024]{1,0:T(8,128)(2,1)S(1)} all-gather(bf16[64,1024]{1,0:T(8,128)(2,1)S(1)} %get-tuple-element.277), channel_id=1, replica_groups=mesh['section'=2,'expert'=4,'dp'=4] {'dp'}, dimensions={0}, use_global_device_ids=true | all-gather | bytes 655360 | tf_op jit(solution)/shard_map/all_gather | solution.py:63
  205.1 3.3 all-to-all-start.7
  208.5 4.7 slice_bitcast_fusion
  218.0 3.5 all-to-all-start.8
  221.6 15.6 %all_gather.26.refs_0_ = bf16[256,1024]{1,0:T(8,128)(2,1)S(1)} all-gather(bf16[64,1024]{1,0:T(8,128)(2,1)S(1)} %get-tuple-element.286), channel_id=1, replica_groups=mesh['section'=2,'expert'=4,'dp'=4] {'dp'}, dimensions={0}, use_global_device_ids=true | all-gather | bytes 655360 | tf_op jit(solution)/shard_map/all_gather | solution.py:63
  239.9 4.0 all-to-all-start.9
  246.5 3.6 fusion.41
  250.1 4.4 all-to-all-done.9
  255.3 4.8 expert_forward.3
  260.1 4.2 all-to-all-start.11
  265.2 5.6 %expert_backward.2 = (bf16[320,1024]{1,0:T(8,128)(2,1)}, bf16[320,1024]{1,0:T(8,128)(2,1)}, bf16[320,1024]{1,0:T(8,128)(2,1)}) custom-call(s32[1]{0:T(128)} %bitcast.place, bf16[320,1024]{1,0:T(8,128)(2,1)S(1)} %bitcast.197, f32[320,1]{1,0:T(8,128)S(1)} %copy-done.41, bf16[1024,1024]{1,0:T(8,128)(2,1)} %get-tuple-element.258.refs_0_, ...), custom_call_target="tpu_custom_call" | custom-call | tf_op jit(solution)/shard_map/expert_backward/pallas_call | solution.py:316
  275.0 4.2 all-to-all-start.10
  279.3 3.1 fusion.44
  282.5 3.4 fusion.18.refs_2_
  289.9 2.8 fusion.7
  299.5 5.2 all-to-all-start.12
  305.5 14.1 %all-to-all-done.12.blocks_ref = bf16[4,64,1024]{2,1,0:T(8,128)(2,1)S(1)} async-done(((bf16[4,64,1024]{2,1,0:T(8,128)(2,1)}), bf16[4,64,1024]{2,1,0:T(8,128)(2,1)S(1)}, u32[]{:S(2)}, u32[]{:S(2)}) %all-to-all-start.12) | async-done | bytes 524320 | tf_op jit(solution)/shard_map/all_to_all | solution.py:54
  323.2 8.5 %all_to_all.115 = bf16[4,64,256]{2,1,0:T(8,128)(2,1)S(1)} all-to-all(bf16[4,64,256]{2,1,0:T(8,128)(2,1)S(1)} %get-tuple-element.331), channel_id=1, replica_groups=mesh['section'=2,'expert'=4,'dp'=4] {'dp'}, dimensions={0} | all-to-all | bytes 262144 | tf_op jit(solution)/shard_map/all_to_all | solution.py:54
  336.7 4.1 all-to-all-start.14
  341.0 3.8 pair_grads.5
  345.4 10.5 %all-to-all-done.14.blocks_ref = bf16[4,64,1024]{2,1,0:T(8,128)(2,1)} async-done(((bf16[4,64,1024]{2,1,0:T(8,128)(2,1)}), bf16[4,64,1024]{2,1,0:T(8,128)(2,1)}, u32[]{:S(2)}, u32[]{:S(2)}) %all-to-all-start.14) | async-done | bytes 524320 | tf_op jit(solution)/shard_map/all_to_all | solution.py:54
  359.6 16.1 %all_gather.27 = bf16[256,1024]{1,0:T(8,128)(2,1)S(1)} all-gather(bf16[64,1024]{1,0:T(8,128)(2,1)S(1)} %get-tuple-element.340.grad_ref), channel_id=1, replica_groups=mesh['section'=2,'expert'=4,'dp'=4] {'dp'}, dimensions={0}, use_global_device_ids=true | all-gather | bytes 655360 | tf_op jit(solution)/shard_map/all_gather | solution.py:63
  377.5 3.7 all-to-all-start.15
  393.0 5.7 %expert_backward.3 = (bf16[320,1024]{1,0:T(8,128)(2,1)}, bf16[320,1024]{1,0:T(8,128)(2,1)}, bf16[320,1024]{1,0:T(8,128)(2,1)}) custom-call(s32[1]{0:T(128)} %bitcast.place, bf16[320,1024]{1,0:T(8,128)(2,1)S(1)} %bitcast.196, f32[320,1]{1,0:T(8,128)S(1)} %copy-done.40, bf16[1024,1024]{1,0:T(8,128)(2,1)} %get-tuple-element.258.refs_0_, ...), custom_call_target="tpu_custom_call" | custom-call | tf_op jit(solution)/shard_map/expert_backward/pallas_call | solution.py:316
  401.1 4.2 all-to-all-start.16
  409.5 6.2 %owner_grads.2 = f32[2,1024,1024]{2,1,0:T(8,128)} custom-call(s32[1]{0:T(128)} %bitcast.place, bf16[320,1024]{1,0:T(8,128)(2,1)} %get-tuple-element.368.refs_0_, bf16[320,1024]{1,0:T(8,128)(2,1)} %collective-permute-done.25.refs_1_, bf16[320,1024]{1,0:T(8,128)(2,1)} %get-tuple-element.370.refs_2_, bf16[320,1024]{1,0:T(8,128)(2,1)} %collective-permute-done.26.refs_3_, ...), custom_call_target="tpu_custom_call" | custom-call | tf_op jit(solution)/shard_map/owner_grads/pallas_call | solution.py:507
  416.4 5.3 collective-permute-done.30.refs_2_
  425.8 5.2 all-to-all-start.17
  438.8 6.5 %all-to-all-done.17.blocks_ref = bf16[4,64,1024]{2,1,0:T(8,128)(2,1)} async-done(((bf16[4,64,1024]{2,1,0:T(8,128)(2,1)}), bf16[4,64,1024]{2,1,0:T(8,128)(2,1)}, u32[]{:S(2)}, u32[]{:S(2)}) %all-to-all-start.17) | async-done | bytes 524320 | tf_op jit(solution)/shard_map/all_to_all | solution.py:54
  445.4 3.8 mid_back.3
  449.2 9.2 %all_to_all.116 = bf16[4,64,256]{2,1,0:T(8,128)(2,1)S(1)} all-to-all(bf16[4,64,256]{2,1,0:T(8,128)(2,1)S(1)} %get-tuple-element.388), channel_id=1, replica_groups=mesh['section'=2,'expert'=4,'dp'=4] {'dp'}, dimensions={0} | all-to-all | bytes 262144 | tf_op jit(solution)/shard_map/all_to_all | solution.py:54
  467.8 3.6 all-to-all-start.19
  473.9 12.5 %all-to-all-done.19.blocks_ref = bf16[4,64,1024]{2,1,0:T(8,128)(2,1)S(1)} async-done(((bf16[4,64,1024]{2,1,0:T(8,128)(2,1)}), bf16[4,64,1024]{2,1,0:T(8,128)(2,1)S(1)}, u32[]{:S(2)}, u32[]{:S(2)}) %all-to-all-start.19) | async-done | bytes 524320 | tf_op jit(solution)/shard_map/all_to_all | solution.py:54
  490.5 3.6 all-to-all-start.20
  494.2 6.3 %owner_grads.3 = f32[2,1024,1024]{2,1,0:T(8,128)} custom-call(s32[1]{0:T(128)} %bitcast.place, bf16[320,1024]{1,0:T(8,128)(2,1)} %bitcast.192, bf16[320,1024]{1,0:T(8,128)(2,1)} %collective-permute-done.42.refs_1_, bf16[320,1024]{1,0:T(8,128)(2,1)} %bitcast.195, bf16[320,1024]{1,0:T(8,128)(2,1)} %collective-permute-done.43.refs_3_, ...), custom_call_target="tpu_custom_call" | custom-call | tf_op jit(solution)/shard_map/owner_grads/pallas_call | solution.py:507
  500.5 4.6 all-to-all-done.20
  507.6 3.4 all-to-all-start.21
  511.0 8.2 %reduce-scatter.14.cloned.1.call-done = bf16[256,896]{1,0:T(8,128)(2,1)} async-done(((bf16[1024,896]{1,0:T(8,128)(2,1)}), bf16[256,896]{1,0:T(8,128)(2,1)}) %reduce-scatter.14.cloned.1.call-update) | async-done | bytes 458768 | tf_op jit(solution)/shard_map/reduce_scatter | solution.py:982
  519.2 4.6 all-to-all-start.22
  527.1 9.8 %all-to-all-done.22.refs_4_ = bf16[4,64,896]{2,1,0:T(8,128)(2,1)S(1)} async-done(((bf16[4,64,896]{2,1,0:T(8,128)(2,1)}), bf16[4,64,896]{2,1,0:T(8,128)(2,1)S(1)}, u32[]{:S(2)}, u32[]{:S(2)}) %all-to-all-start.22) | async-done | bytes 458784 | tf_op jit(solution)/shard_map/all_to_all | solution.py:54
  544.2 3.0 finish_weights.1
  (469 shorter events, 158.0 us)
Async XLA Ops:
  7.2 71.2 %all-gather.9.cloned.1.call-start = ((), (), s32[]{:S(2)}) async-start(), calls=%async_computation.35 | async-start | bytes 4718592 | tf_op jit(solution)/shard_map/all_gather | solution.py:792
  10.2 12.2 %collective-permute-start = (bf16[64,1024]{1,0:T(8,128)(2,1)}, bf16[64,1024]{1,0:T(8,128)(2,1)S(1)}, u32[]{:S(2)}, u32[]{:S(2)}) collective-permute-start(bf16[64,1024]{1,0:T(8,128)(2,1)} %bitcast.205), channel_id=1, source_target_pairs={{3,0},{0,1},{1,2},{2,3},{7,4},{4,5},{5,6},{6,7},{11,8},{8,9},{9,10... | collective-permute-start | bytes 393224 | tf_op jit(solution)/shard_map/ppermute | solution.py:101
  13.2 11.4 %collective-permute-start.1 = (bf16[64,1024]{1,0:T(8,128)(2,1)}, bf16[64,1024]{1,0:T(8,128)(2,1)S(1)}, u32[]{:S(2)}, u32[]{:S(2)}) collective-permute-start(bf16[64,1024]{1,0:T(8,128)(2,1)} %bitcast.206), channel_id=1, source_target_pairs={{2,0},{3,1},{0,2},{1,3},{6,4},{7,5},{4,6},{5,7},{10,8},{11,9},{8,1... | collective-permute-start | bytes 393224 | tf_op jit(solution)/shard_map/ppermute | solution.py:101
  15.8 8.9 %collective-permute-start.2 = (bf16[64,1024]{1,0:T(8,128)(2,1)}, bf16[64,1024]{1,0:T(8,128)(2,1)S(1)}, u32[]{:S(2)}, u32[]{:S(2)}) collective-permute-start(bf16[64,1024]{1,0:T(8,128)(2,1)} %bitcast.207), channel_id=1, source_target_pairs={{1,0},{2,1},{3,2},{0,3},{5,4},{6,5},{7,6},{4,7},{9,8},{10,9},{11,1... | collective-permute-start | bytes 393224 | tf_op jit(solution)/shard_map/ppermute | solution.py:101
  17.1 13.4 %all-to-all-start = ((bf16[32,8,128]{2,1,0:T(8,128)(2,1)}), bf16[32,8,128]{2,1,0:T(8,128)(2,1)S(1)}, u32[]{:S(2)}, u32[]{:S(2)}) async-start(bf16[32,8,128]{2,1,0:T(8,128)(2,1)} %broadcast_in_dim.49), calls=%async_computation | async-start | bytes 131072 | tf_op jit(solution)/shard_map/all_to_all | solution.py:54
  20.1 76.6 %all-gather.5.cloned.1.call-start = ((), (), s32[]{:S(2)}) async-start(), calls=%async_computation.28 | async-start | bytes 4718592 | tf_op jit(solution)/shard_map/all_gather | solution.py:776
  32.9 15.4 %all-to-all-start.1 = ((bf16[4,64,768]{2,1,0:T(8,128)(2,1)}), bf16[4,64,768]{2,1,0:T(8,128)(2,1)S(1)}, u32[]{:S(2)}, u32[]{:S(2)}) async-start(bf16[4,64,768]{2,1,0:T(8,128)(2,1)} %reshape.440), calls=%async_computation.1 | async-start | bytes 786432 | tf_op jit(solution)/shard_map/all_to_all | solution.py:54
  49.6 28.8 %all-to-all-start.2 = ((bf16[4,4,64,768]{3,2,1,0:T(8,128)(2,1)}), bf16[4,4,64,768]{3,2,1,0:T(8,128)(2,1)}, u32[]{:S(2)}, u32[]{:S(2)}) async-start(bf16[4,4,64,768]{3,2,1,0:T(8,128)(2,1)} %broadcast_in_dim.51), calls=%async_computation.2 | async-start | bytes 3145728 | tf_op jit(solution)/shard_map/all_to_all | solution.py:54
  54.0 97.2 %all-gather.7.cloned.1.call-start = ((), (), s32[]{:S(2)}) async-start(), calls=%async_computation.29 | async-start | bytes 4718592 | tf_op jit(solution)/shard_map/all_gather | solution.py:809
  54.0 8.3 %collective-permute-start.3 = (bf16[64,1024]{1,0:T(8,128)(2,1)S(1)}, bf16[64,1024]{1,0:T(8,128)(2,1)S(1)}, u32[]{:S(2)}, u32[]{:S(2)}) collective-permute-start(bf16[64,1024]{1,0:T(8,128)(2,1)S(1)} %fusion.55.refs_0_), channel_id=1, source_target_pairs={{3,0},{0,1},{1,2},{2,3},{7,4},{4,5},{5,6},{6,7},{11,8},{8,9},{9,10... | collective-permute-start | bytes 393224 | tf_op jit(solution)/shard_map/ppermute | solution.py:101
  54.1 15.9 %collective-permute-start.4 = (bf16[64,1024]{1,0:T(8,128)(2,1)S(1)}, bf16[64,1024]{1,0:T(8,128)(2,1)S(1)}, u32[]{:S(2)}, u32[]{:S(2)}) collective-permute-start(bf16[64,1024]{1,0:T(8,128)(2,1)S(1)} %fusion.55.refs_0_), channel_id=1, source_target_pairs={{2,0},{3,1},{0,2},{1,3},{6,4},{7,5},{4,6},{5,7},{10,8},{11,9},{8,1... | collective-permute-start | bytes 393224 | tf_op jit(solution)/shard_map/ppermute | solution.py:101
  56.1 13.9 %collective-permute-start.5 = (bf16[64,1024]{1,0:T(8,128)(2,1)S(1)}, bf16[64,1024]{1,0:T(8,128)(2,1)S(1)}, u32[]{:S(2)}, u32[]{:S(2)}) collective-permute-start(bf16[64,1024]{1,0:T(8,128)(2,1)S(1)} %fusion.55.refs_0_), channel_id=1, source_target_pairs={{1,0},{2,1},{3,2},{0,3},{5,4},{6,5},{7,6},{4,7},{9,8},{10,9},{11,1... | collective-permute-start | bytes 393224 | tf_op jit(solution)/shard_map/ppermute | solution.py:101
  57.9 12.8 %collective-permute-start.6 = (bf16[64,1024]{1,0:T(8,128)(2,1)S(1)}, bf16[64,1024]{1,0:T(8,128)(2,1)S(1)}, u32[]{:S(2)}, u32[]{:S(2)}) collective-permute-start(bf16[64,1024]{1,0:T(8,128)(2,1)S(1)} %get-tuple-element.245), channel_id=1, source_target_pairs={{3,0},{0,1},{1,2},{2,3},{7,4},{4,5},{5,6},{6,7},{11,8},{8,9},{9,10... | collective-permute-start | bytes 393224 | tf_op jit(solution)/shard_map/ppermute | solution.py:117
  58.4 18.9 %collective-permute-start.7 = (bf16[64,1024]{1,0:T(8,128)(2,1)S(1)}, bf16[64,1024]{1,0:T(8,128)(2,1)S(1)}, u32[]{:S(2)}, u32[]{:S(2)}) collective-permute-start(bf16[64,1024]{1,0:T(8,128)(2,1)S(1)} %get-tuple-element.246), channel_id=1, source_target_pairs={{2,0},{3,1},{0,2},{1,3},{6,4},{7,5},{4,6},{5,7},{10,8},{11,9},{8,1... | collective-permute-start | bytes 393224 | tf_op jit(solution)/shard_map/ppermute | solution.py:117
  62.3 15.0 %collective-permute-start.8 = (bf16[64,1024]{1,0:T(8,128)(2,1)S(1)}, bf16[64,1024]{1,0:T(8,128)(2,1)S(1)}, u32[]{:S(2)}, u32[]{:S(2)}) collective-permute-start(bf16[64,1024]{1,0:T(8,128)(2,1)S(1)} %get-tuple-element.247), channel_id=1, source_target_pairs={{1,0},{2,1},{3,2},{0,3},{5,4},{6,5},{7,6},{4,7},{9,8},{10,9},{11,1... | collective-permute-start | bytes 393224 | tf_op jit(solution)/shard_map/ppermute | solution.py:117
  78.4 3.8 collective-permute-start.9
  80.1 61.9 %collective-permute-start.13 = (bf16[1024,1024]{1,0:T(8,128)(2,1)}, bf16[1024,1024]{1,0:T(8,128)(2,1)}, u32[]{:S(2)}, u32[]{:S(2)}) collective-permute-start(bf16[1024,1024]{1,0:T(8,128)(2,1)} %get-tuple-element.259), channel_id=1, source_target_pairs={{0,16},{16,0},{1,17},{17,1},{2,18},{18,2},{3,19},{19,3},{4,20},{20... | collective-permute-start | bytes 6291464 | tf_op jit(solution)/shard_map/ppermute | solution.py:683
  80.6 61.4 %collective-permute-start.14 = (bf16[1024,1024]{1,0:T(8,128)(2,1)}, bf16[1024,1024]{1,0:T(8,128)(2,1)}, u32[]{:S(2)}, u32[]{:S(2)}) collective-permute-start(bf16[1024,1024]{1,0:T(8,128)(2,1)} %get-tuple-element.261), channel_id=1, source_target_pairs={{0,16},{16,0},{1,17},{17,1},{2,18},{18,2},{3,19},{19,3},{4,20},{20... | collective-permute-start | bytes 6291464 | tf_op jit(solution)/shard_map/ppermute | solution.py:683
  87.3 9.8 %all-to-all-start.3 = ((bf16[4,64,256]{2,1,0:T(8,128)(2,1)}), bf16[4,64,256]{2,1,0:T(8,128)(2,1)S(1)}, u32[]{:S(2)}, u32[]{:S(2)}) async-start(bf16[4,64,256]{2,1,0:T(8,128)(2,1)} %bitcast.30), calls=%async_computation.3 | async-start | bytes 262144 | tf_op jit(solution)/shard_map/all_to_all | solution.py:54
  116.3 9.3 %collective-permute-start.10 = (bf16[64,1024]{1,0:T(8,128)(2,1)S(1)}, bf16[64,1024]{1,0:T(8,128)(2,1)S(1)}, u32[]{:S(2)}, u32[]{:S(2)}) collective-permute-start(bf16[64,1024]{1,0:T(8,128)(2,1)S(1)} %dynamic-slice_bitcast_fusion.4.refs_0_.grad_ref), channel_id=1, source_target_pairs={{3,0},{0,1},{1,2},{2,3},{7,4},{4,5},{5,6},{6,7},{11,8},{8,9},{9,10... | collective-permute-start | bytes 393224 | tf_op jit(solution)/shard_map/ppermute | solution.py:101
  118.1 10.0 %collective-permute-start.11 = (bf16[64,1024]{1,0:T(8,128)(2,1)S(1)}, bf16[64,1024]{1,0:T(8,128)(2,1)S(1)}, u32[]{:S(2)}, u32[]{:S(2)}) collective-permute-start(bf16[64,1024]{1,0:T(8,128)(2,1)S(1)} %dynamic-slice_bitcast_fusion.4.refs_0_.grad_ref), channel_id=1, source_target_pairs={{2,0},{3,1},{0,2},{1,3},{6,4},{7,5},{4,6},{5,7},{10,8},{11,9},{8,1... | collective-permute-start | bytes 393224 | tf_op jit(solution)/shard_map/ppermute | solution.py:101
  120.6 7.5 %collective-permute-start.12 = (bf16[64,1024]{1,0:T(8,128)(2,1)S(1)}, bf16[64,1024]{1,0:T(8,128)(2,1)S(1)}, u32[]{:S(2)}, u32[]{:S(2)}) collective-permute-start(bf16[64,1024]{1,0:T(8,128)(2,1)S(1)} %dynamic-slice_bitcast_fusion.4.refs_0_.grad_ref), channel_id=1, source_target_pairs={{1,0},{2,1},{3,2},{0,3},{5,4},{6,5},{7,6},{4,7},{9,8},{10,9},{11,1... | collective-permute-start | bytes 393224 | tf_op jit(solution)/shard_map/ppermute | solution.py:101
  120.6 21.4 %all-to-all-start.4 = ((bf16[8,40,1024]{2,1,0:T(8,128)(2,1)}), bf16[8,40,1024]{2,1,0:T(8,128)(2,1)S(1)}, u32[]{:S(2)}, u32[]{:S(2)}) async-start(bf16[8,40,1024]{2,1,0:T(8,128)(2,1)} %bitcast.222), calls=%async_computation.4 | async-start | bytes 1310720 | tf_op jit(solution)/shard_map/all_to_all | solution.py:54
  146.9 14.9 %all-to-all-start.5 = ((bf16[8,40,1024]{2,1,0:T(8,128)(2,1)}), bf16[8,40,1024]{2,1,0:T(8,128)(2,1)}, u32[]{:S(2)}, u32[]{:S(2)}) async-start(bf16[8,40,1024]{2,1,0:T(8,128)(2,1)} %bitcast.234), calls=%async_computation.5 | async-start | bytes 1310720 | tf_op jit(solution)/shard_map/all_to_all | solution.py:54
  164.9 18.7 %all-to-all-start.6 = ((bf16[4,64,1024]{2,1,0:T(8,128)(2,1)}), bf16[4,64,1024]{2,1,0:T(8,128)(2,1)S(1)}, u32[]{:S(2)}, u32[]{:S(2)}) async-start(bf16[4,64,1024]{2,1,0:T(8,128)(2,1)} %bitcast.45), calls=%async_computation.6 | async-start | bytes 1048576 | tf_op jit(solution)/shard_map/all_to_all | solution.py:54
  205.1 9.2 %all-to-all-start.7 = ((bf16[4,64,256]{2,1,0:T(8,128)(2,1)}), bf16[4,64,256]{2,1,0:T(8,128)(2,1)S(1)}, u32[]{:S(2)}, u32[]{:S(2)}) async-start(bf16[4,64,256]{2,1,0:T(8,128)(2,1)} %bitcast.49), calls=%async_computation.7 | async-start | bytes 262144 | tf_op jit(solution)/shard_map/all_to_all | solution.py:54
  218.0 19.2 %all-to-all-start.8 = ((bf16[8,40,1024]{2,1,0:T(8,128)(2,1)}), bf16[8,40,1024]{2,1,0:T(8,128)(2,1)S(1)}, u32[]{:S(2)}, u32[]{:S(2)}) async-start(bf16[8,40,1024]{2,1,0:T(8,128)(2,1)} %bitcast.221), calls=%async_computation.8 | async-start | bytes 1310720 | tf_op jit(solution)/shard_map/all_to_all | solution.py:54
  239.9 14.6 %all-to-all-start.9 = ((bf16[8,40,1024]{2,1,0:T(8,128)(2,1)}), bf16[8,40,1024]{2,1,0:T(8,128)(2,1)S(1)}, u32[]{:S(2)}, u32[]{:S(2)}) async-start(bf16[8,40,1024]{2,1,0:T(8,128)(2,1)} %bitcast.223), calls=%async_computation.9 | async-start | bytes 1310720 | tf_op jit(solution)/shard_map/all_to_all | solution.py:54
  260.1 14.9 %all-to-all-start.11 = ((bf16[8,40,1024]{2,1,0:T(8,128)(2,1)}), bf16[8,40,1024]{2,1,0:T(8,128)(2,1)}, u32[]{:S(2)}, u32[]{:S(2)}) async-start(bf16[8,40,1024]{2,1,0:T(8,128)(2,1)} %bitcast.235), calls=%async_computation.11 | async-start | bytes 1310720 | tf_op jit(solution)/shard_map/all_to_all | solution.py:54
  275.0 14.9 %all-to-all-start.10 = ((bf16[8,40,1024]{2,1,0:T(8,128)(2,1)}), bf16[8,40,1024]{2,1,0:T(8,128)(2,1)}, u32[]{:S(2)}, u32[]{:S(2)}) async-start(bf16[8,40,1024]{2,1,0:T(8,128)(2,1)} %bitcast.232), calls=%async_computation.10 | async-start | bytes 1310720 | tf_op jit(solution)/shard_map/all_to_all | solution.py:54
  279.2 66.2 %reduce-scatter.6.cloned.1.call-start = ((), (), s32[]{:S(2)}) async-start(), calls=%async_computation.30 | async-start | bytes 655360 | tf_op jit(solution)/shard_map/reduce_scatter | solution.py:955
  282.4 105.9 %reduce-scatter.8.cloned.1.call-start = ((), (), s32[]{:S(2)}) async-start(), calls=%async_computation.31 | async-start | bytes 2621440 | tf_op jit(solution)/shard_map/reduce_scatter | solution.py:982
  299.5 20.1 %all-to-all-start.12 = ((bf16[4,64,1024]{2,1,0:T(8,128)(2,1)}), bf16[4,64,1024]{2,1,0:T(8,128)(2,1)S(1)}, u32[]{:S(2)}, u32[]{:S(2)}) async-start(bf16[4,64,1024]{2,1,0:T(8,128)(2,1)} %bitcast.227), calls=%async_computation.12 | async-start | bytes 1048576 | tf_op jit(solution)/shard_map/all_to_all | solution.py:54
  335.7 5.3 collective-permute-start.22
  335.7 5.3 collective-permute-start.23
  336.2 4.7 collective-permute-start.20
  336.2 4.7 collective-permute-start.21
  336.7 19.2 %all-to-all-start.14 = ((bf16[4,64,1024]{2,1,0:T(8,128)(2,1)}), bf16[4,64,1024]{2,1,0:T(8,128)(2,1)}, u32[]{:S(2)}, u32[]{:S(2)}) async-start(bf16[4,64,1024]{2,1,0:T(8,128)(2,1)} %bitcast.224), calls=%async_computation.14 | async-start | bytes 1048576 | tf_op jit(solution)/shard_map/all_to_all | solution.py:54
  340.9 49.3 %reduce-scatter.10.cloned.1.call-start = ((), (), s32[]{:S(2)}) async-start(), calls=%async_computation.32 | async-start | bytes 2293760 | tf_op jit(solution)/shard_map/reduce_scatter | solution.py:982
  344.8 54.2 %collective-permute-start.25 = (bf16[320,1024]{1,0:T(8,128)(2,1)}, bf16[320,1024]{1,0:T(8,128)(2,1)}, u32[]{:S(2)}, u32[]{:S(2)}) collective-permute-start(bf16[320,1024]{1,0:T(8,128)(2,1)} %get-tuple-element.368.refs_0_), channel_id=1, source_target_pairs={{0,16},{16,0},{1,17},{17,1},{2,18},{18,2},{3,19},{19,3},{4,20},{20... | collective-permute-start | bytes 1966088 | tf_op jit(solution)/shard_map/ppermute | solution.py:683
  344.9 54.1 %collective-permute-start.28 = (bf16[320,1024]{1,0:T(8,128)(2,1)}, bf16[320,1024]{1,0:T(8,128)(2,1)}, u32[]{:S(2)}, u32[]{:S(2)}) collective-permute-start(bf16[320,1024]{1,0:T(8,128)(2,1)} %get-tuple-element.374.refs_6_), channel_id=1, source_target_pairs={{0,16},{16,0},{1,17},{17,1},{2,18},{18,2},{3,19},{19,3},{4,20},{20... | collective-permute-start | bytes 1966088 | tf_op jit(solution)/shard_map/ppermute | solution.py:683
  345.3 53.6 %collective-permute-start.26 = (bf16[320,1024]{1,0:T(8,128)(2,1)}, bf16[320,1024]{1,0:T(8,128)(2,1)}, u32[]{:S(2)}, u32[]{:S(2)}) collective-permute-start(bf16[320,1024]{1,0:T(8,128)(2,1)} %get-tuple-element.370.refs_2_), channel_id=1, source_target_pairs={{0,16},{16,0},{1,17},{17,1},{2,18},{18,2},{3,19},{19,3},{4,20},{20... | collective-permute-start | bytes 1966088 | tf_op jit(solution)/shard_map/ppermute | solution.py:683
  377.5 14.6 %all-to-all-start.15 = ((bf16[8,40,1024]{2,1,0:T(8,128)(2,1)}), bf16[8,40,1024]{2,1,0:T(8,128)(2,1)S(1)}, u32[]{:S(2)}, u32[]{:S(2)}) async-start(bf16[8,40,1024]{2,1,0:T(8,128)(2,1)} %bitcast.220), calls=%async_computation.16 | async-start | bytes 1310720 | tf_op jit(solution)/shard_map/all_to_all | solution.py:54
  401.1 22.0 %all-to-all-start.16 = ((bf16[8,40,1024]{2,1,0:T(8,128)(2,1)}), bf16[8,40,1024]{2,1,0:T(8,128)(2,1)}, u32[]{:S(2)}, u32[]{:S(2)}) async-start(bf16[8,40,1024]{2,1,0:T(8,128)(2,1)} %bitcast.233), calls=%async_computation.19 | async-start | bytes 1310720 | tf_op jit(solution)/shard_map/all_to_all | solution.py:54
  405.4 10.4 %collective-permute-start.29 = (bf16[64,1408]{1,0:T(8,128)(2,1)}, bf16[64,1408]{1,0:T(8,128)(2,1)S(1)}, u32[]{:S(2)}, u32[]{:S(2)}) collective-permute-start(bf16[64,1408]{1,0:T(8,128)(2,1)} %get-tuple-element.365), channel_id=1, source_target_pairs={{3,0},{0,1},{1,2},{2,3},{7,4},{4,5},{5,6},{6,7},{11,8},{8,9},{9,10... | collective-permute-start | bytes 540680 | tf_op jit(solution)/shard_map/ppermute | solution.py:117
  405.4 16.3 %collective-permute-start.30 = (bf16[64,1408]{1,0:T(8,128)(2,1)}, bf16[64,1408]{1,0:T(8,128)(2,1)S(1)}, u32[]{:S(2)}, u32[]{:S(2)}) collective-permute-start(bf16[64,1408]{1,0:T(8,128)(2,1)} %get-tuple-element.366), channel_id=1, source_target_pairs={{2,0},{3,1},{0,2},{1,3},{6,4},{7,5},{4,6},{5,7},{10,8},{11,9},{8,1... | collective-permute-start | bytes 540680 | tf_op jit(solution)/shard_map/ppermute | solution.py:117
  407.0 15.4 %collective-permute-start.31 = (bf16[64,1408]{1,0:T(8,128)(2,1)}, bf16[64,1408]{1,0:T(8,128)(2,1)S(1)}, u32[]{:S(2)}, u32[]{:S(2)}) collective-permute-start(bf16[64,1408]{1,0:T(8,128)(2,1)} %get-tuple-element.367), channel_id=1, source_target_pairs={{1,0},{2,1},{3,2},{0,3},{5,4},{6,5},{7,6},{4,7},{9,8},{10,9},{11,1... | collective-permute-start | bytes 540680 | tf_op jit(solution)/shard_map/ppermute | solution.py:117
  425.8 19.5 %all-to-all-start.17 = ((bf16[4,64,1024]{2,1,0:T(8,128)(2,1)}), bf16[4,64,1024]{2,1,0:T(8,128)(2,1)}, u32[]{:S(2)}, u32[]{:S(2)}) async-start(bf16[4,64,1024]{2,1,0:T(8,128)(2,1)} %bitcast.228), calls=%async_computation.20 | async-start | bytes 1048576 | tf_op jit(solution)/shard_map/all_to_all | solution.py:54
  431.0 74.8 %reduce-scatter.12.cloned.1.call-start = ((), (), s32[]{:S(2)}) async-start(), calls=%async_computation.33 | async-start | bytes 2621440 | tf_op jit(solution)/shard_map/reduce_scatter | solution.py:982
  445.3 73.9 %reduce-scatter.14.cloned.1.call-start = ((), (), s32[]{:S(2)}) async-start(), calls=%async_computation.34 | async-start | bytes 2293760 | tf_op jit(solution)/shard_map/reduce_scatter | solution.py:982
  467.8 18.7 %all-to-all-start.19 = ((bf16[4,64,1024]{2,1,0:T(8,128)(2,1)}), bf16[4,64,1024]{2,1,0:T(8,128)(2,1)S(1)}, u32[]{:S(2)}, u32[]{:S(2)}) async-start(bf16[4,64,1024]{2,1,0:T(8,128)(2,1)} %bitcast.90), calls=%async_computation.22 | async-start | bytes 1048576 | tf_op jit(solution)/shard_map/all_to_all | solution.py:54
  471.4 19.1 %collective-permute-start.42 = (bf16[320,1024]{1,0:T(8,128)(2,1)S(1)}, bf16[320,1024]{1,0:T(8,128)(2,1)}, u32[]{:S(2)}, u32[]{:S(2)}) collective-permute-start(bf16[320,1024]{1,0:T(8,128)(2,1)S(1)} %bitcast.191), channel_id=1, source_target_pairs={{0,16},{16,0},{1,17},{17,1},{2,18},{18,2},{3,19},{19,3},{4,20},{20... | collective-permute-start | bytes 1966088 | tf_op jit(solution)/shard_map/ppermute | solution.py:683
  471.6 18.9 %collective-permute-start.43 = (bf16[320,1024]{1,0:T(8,128)(2,1)S(1)}, bf16[320,1024]{1,0:T(8,128)(2,1)}, u32[]{:S(2)}, u32[]{:S(2)}) collective-permute-start(bf16[320,1024]{1,0:T(8,128)(2,1)S(1)} %bitcast.194), channel_id=1, source_target_pairs={{0,16},{16,0},{1,17},{17,1},{2,18},{18,2},{3,19},{19,3},{4,20},{20... | collective-permute-start | bytes 1966088 | tf_op jit(solution)/shard_map/ppermute | solution.py:683
  472.0 18.5 %collective-permute-start.45 = (bf16[320,1024]{1,0:T(8,128)(2,1)}, bf16[320,1024]{1,0:T(8,128)(2,1)}, u32[]{:S(2)}, u32[]{:S(2)}) collective-permute-start(bf16[320,1024]{1,0:T(8,128)(2,1)} %get-tuple-element.423.refs_6_), channel_id=1, source_target_pairs={{0,16},{16,0},{1,17},{17,1},{2,18},{18,2},{3,19},{19,3},{4,20},{20... | collective-permute-start | bytes 1966088 | tf_op jit(solution)/shard_map/ppermute | solution.py:683
  472.1 18.4 %collective-permute-start.44 = (bf16[320,1024]{1,0:T(8,128)(2,1)}, bf16[320,1024]{1,0:T(8,128)(2,1)}, u32[]{:S(2)}, u32[]{:S(2)}) collective-permute-start(bf16[320,1024]{1,0:T(8,128)(2,1)} %get-tuple-element.421.refs_4_), channel_id=1, source_target_pairs={{0,16},{16,0},{1,17},{17,1},{2,18},{18,2},{3,19},{19,3},{4,20},{20... | collective-permute-start | bytes 1966088 | tf_op jit(solution)/shard_map/ppermute | solution.py:683
  490.5 14.6 %all-to-all-start.20 = ((f32[32,16,128]{2,1,0:T(8,128)}), f32[32,16,128]{2,1,0:T(8,128)S(1)}, u32[]{:S(2)}, u32[]{:S(2)}) async-start(f32[32,16,128]{2,1,0:T(8,128)} %pack_small.1), calls=%async_computation.23 | async-start | bytes 524288 | tf_op jit(solution)/shard_map/all_to_all | solution.py:54
  507.6 11.6 %all-to-all-start.21 = ((bf16[4,64,512]{2,1,0:T(8,128)(2,1)}), bf16[4,64,512]{2,1,0:T(8,128)(2,1)S(1)}, u32[]{:S(2)}, u32[]{:S(2)}) async-start(bf16[4,64,512]{2,1,0:T(8,128)(2,1)} %bitcast.99), calls=%async_computation.25 | async-start | bytes 524288 | tf_op jit(solution)/shard_map/all_to_all | solution.py:54
  519.2 17.7 %all-to-all-start.22 = ((bf16[4,64,896]{2,1,0:T(8,128)(2,1)}), bf16[4,64,896]{2,1,0:T(8,128)(2,1)S(1)}, u32[]{:S(2)}, u32[]{:S(2)}) async-start(bf16[4,64,896]{2,1,0:T(8,128)(2,1)} %bitcast.237), calls=%async_computation.27 | async-start | bytes 917504 | tf_op jit(solution)/shard_map/all_to_all | solution.py:54
  523.8 13.1 %collective-permute-start.41 = (f32[64,1024]{1,0:T(8,128)}, f32[64,1024]{1,0:T(8,128)}, u32[]{:S(2)}, u32[]{:S(2)}) collective-permute-start(f32[64,1024]{1,0:T(8,128)} %get-tuple-element.398.refs_6_), channel_id=1, source_target_pairs={{0,16},{16,0},{1,17},{17,1},{2,18},{18,2},{3,19},{19,3},{4,20},{20... | collective-permute-start | bytes 786440 | tf_op jit(solution)/shard_map/ppermute | solution.py:683
  523.8 13.7 %collective-permute-start.40 = (f32[64,1024]{1,0:T(8,128)}, f32[64,1024]{1,0:T(8,128)}, u32[]{:S(2)}, u32[]{:S(2)}) collective-permute-start(f32[64,1024]{1,0:T(8,128)} %get-tuple-element.397.refs_4_), channel_id=1, source_target_pairs={{0,16},{16,0},{1,17},{17,1},{2,18},{18,2},{3,19},{19,3},{4,20},{20... | collective-permute-start | bytes 786440 | tf_op jit(solution)/shard_map/ppermute | solution.py:683
  524.3 18.0 %collective-permute-start.51 = (bf16[256,512]{1,0:T(8,128)(2,1)S(1)}, bf16[256,512]{1,0:T(8,128)(2,1)}, u32[]{:S(2)}, u32[]{:S(2)}) collective-permute-start(bf16[256,512]{1,0:T(8,128)(2,1)S(1)} %copy-done.25), channel_id=1, source_target_pairs={{0,16},{16,0},{1,17},{17,1},{2,18},{18,2},{3,19},{19,3},{4,20},{20... | collective-permute-start | bytes 786440 | tf_op jit(solution)/shard_map/ppermute | solution.py:683
  526.1 17.8 %collective-permute-start.49 = (bf16[4,64,896]{2,1,0:T(8,128)(2,1)S(1)}, bf16[4,64,896]{2,1,0:T(8,128)(2,1)S(1)}, u32[]{:S(2)}, u32[]{:S(2)}) collective-permute-start(bf16[4,64,896]{2,1,0:T(8,128)(2,1)S(1)} %slice.248.refs_6_), channel_id=1, source_target_pairs={{0,16},{16,0},{1,17},{17,1},{2,18},{18,2},{3,19},{19,3},{4,20},{20... | collective-permute-start | bytes 1376264 | tf_op jit(solution)/shard_map/ppermute | solution.py:683
  536.9 7.3 %collective-permute-start.48 = (bf16[4,64,896]{2,1,0:T(8,128)(2,1)S(1)}, bf16[4,64,896]{2,1,0:T(8,128)(2,1)}, u32[]{:S(2)}, u32[]{:S(2)}) collective-permute-start(bf16[4,64,896]{2,1,0:T(8,128)(2,1)S(1)} %all-to-all-done.22.refs_4_), channel_id=1, source_target_pairs={{0,16},{16,0},{1,17},{17,1},{2,18},{18,2},{3,19},{19,3},{4,20},{20... | collective-permute-start | bytes 1376264 | tf_op jit(solution)/shard_map/ppermute | solution.py:683
  537.0 7.0 %collective-permute-start.47 = (bf16[4,64,512]{2,1,0:T(8,128)(2,1)S(1)}, bf16[4,64,512]{2,1,0:T(8,128)(2,1)S(1)}, u32[]{:S(2)}, u32[]{:S(2)}) collective-permute-start(bf16[4,64,512]{2,1,0:T(8,128)(2,1)S(1)} %slice.247.refs_2_), channel_id=1, source_target_pairs={{0,16},{16,0},{1,17},{17,1},{2,18},{18,2},{3,19},{19,3},{4,20},{20... | collective-permute-start | bytes 786440 | tf_op jit(solution)/shard_map/ppermute | solution.py:683
  (122 other events, 2095.2 us)
Sparse Core Ops, SparseCore 0:
  9.9 39.9 all-gather.8
  52.4 44.2 all-gather.4
  99.2 43.1 all-gather.6
  282.5 23.3 reduce-scatter.5
  309.3 33.4 reduce-scatter.7
  346.0 33.0 reduce-scatter.9
  445.4 34.8 reduce-scatter.11
  483.4 35.8 reduce-scatter.13

commit v5 on v4

--- a/solution.py
+++ b/solution.py
@@ -855,14 +855,15 @@
         mid_seq = gather_rows(mid)
         small_weights = params_all[0, 4:]
 
+        expert_blocks = packed_rows(mid_seq, table)
         expert_rows, ((gate_probs, gate, coef), own_grad_seq) = beside(
             over_homes,
-            packed_rows(mid_seq, table),
-            lambda mid_seq, small_weights, grad: (
+            expert_blocks,
+            lambda blocks, mid_seq, small_weights, grad: (
                 coefficients(mid_seq, small_weights, hot),
-                in_order(permute_copies(grad, DP), DP).reshape(full_len, width),
+                in_order(permute_copies(started(grad, blocks), DP), DP).reshape(full_len, width),
             ),
-            (mid_seq, small_weights, own_grad),
+            (expert_blocks, mid_seq, small_weights, own_grad),
         )
         expert_rows = expert_rows.reshape(-1, width)
         scale, exp_hidden, exp_hidden_low, exp_out = expert_forward(
@@ -952,7 +953,7 @@
         )
         expert_part = product_tn(table, returned.reshape(-1, width))
         branch_part = coef[:, 0:1] * dense_part + coef[:, 1:2] * gate * expert_part
-        branch = lax.psum_scatter(low(branch_part), DP, scatter_dimension=0, tiled=True)
+        branch = low(branch_part)
         record = SimpleNamespace(
             params=params,
             small_weights=small_weights,
@@ -1047,12 +1048,22 @@
             return g_dense, product_tn(d_small, mid_seq)
 
         expert_back = expert_back.reshape(-1, slots, width)
+        parts_one, g_exp_down = (), None
         if layer == 0:
-            returned, (parts_one, g_exp_down) = beside(
+            d_dense, d_small, d_up, d_mid_part, early = dense_grad
+            returned, (parts_one, (g_dense, g_small)) = beside(
                 over_homes,
                 expert_back,
-                lambda early, *mats: (sent_parts(early, DP), owner_grads(section_id, *mats)),
-                (dense_grad[4], owner_mats(2), owner_mats(3)),
+                lambda early, *operands: (sent_parts(early, DP), dense_grads(*operands)),
+                (early, record.hidden_low, d_dense, record.mid_seq, d_up, d_small),
+            )
+            d_mid_part = d_mid_part + product_tn(table, returned.reshape(-1, width))
+            d_mid, (g_exp_down, settle) = beside(
+                over_dp,
+                row_blocks(d_mid_part),
+                lambda left, right, settle: (owner_grads(section_id, left, right), settle),
+                (owner_mats(2), owner_mats(3)),
+                (settle,),
             )
         else:
             returned, dense_grad = beside(
@@ -1061,22 +1072,15 @@
                 lambda blocks, *operands: dense_back(*started(operands, blocks)),
                 (expert_back, *dense_operands),
             )
-        d_dense, d_small, d_up, d_mid_part, _ = dense_grad
-        d_mid_part = d_mid_part + product_tn(table, returned.reshape(-1, width))
-        mid_blocks, operands = lax.optimization_barrier(
-            (
+            d_dense, d_small, d_up, d_mid_part, _ = dense_grad
+            d_mid_part = d_mid_part + product_tn(table, returned.reshape(-1, width))
+            d_mid, (g_dense, g_small) = beside(
+                over_dp,
                 row_blocks(d_mid_part),
+                dense_grads,
                 (record.hidden_low, d_dense, record.mid_seq, d_up, d_small),
             )
-        )
-        g_dense, g_small = dense_grads(*operands)
-        if layer == 1:
-            dense_sum = over_expert(g_dense)
-        d_mid, g_dense, g_small = lax.optimization_barrier(
-            (over_dp(mid_blocks), g_dense, g_small)
-        )
-        if layer == 0:
-            dense_sum = over_expert(g_dense)
+        dense_sum = over_expert(g_dense)
         d_resid, d_attn, d_mixed, d_gain_one, d_shift_one = mid_back(
             layer, d_mid, record.residual, params[1:2], grad_low, proj_both, dp_size
         )
@@ -1092,16 +1096,16 @@
         )
         g_attn = pair_grads(section_id, (record.mixed, d_attn), (normed_seq, d_qkv))
         attn_sum = over_expert(g_attn)
-        beside_it = (g_attn, settle)
+        beside_it = g_attn
         d_normed, beside_it = lax.optimization_barrier((over_dp(in_blocks), beside_it))
         d_input, d_input_low, d_gain_zero, d_shift_zero = input_back(
             d_normed, record.layer_in, params[0:1], d_resid
         )
         small_grads = (d_gain_zero, d_gain_one, d_shift_zero, d_shift_one, g_small)
         if layer == 0:
-            extra = (parts_one, owner_mats, g_exp_down)
+            extra = (parts_one, owner_mats, g_exp_down, settle)
         else:
-            extra = (expert_operands, swapped, beside_it[1])
+            extra = (expert_operands, swapped)
         return d_input, d_input_low, (dense_sum, attn_sum), small_grads, extra
 
     own_grad = lax.dynamic_index_in_dim(cotangent[:, 0], section_id, 0, keepdims=False)
@@ -1111,15 +1115,12 @@
         out_zero, next_normed, own_grad_seq
     )
     grad_one, grad_one_low, sums_one, small_one, operands_one = backward_layer(
-        1, own_grad, own_grad_seq, record_one, settle=branch_one, grad_rows=grad_rows
+        1, own_grad, own_grad_seq, record_one, grad_rows=grad_rows
     )
     dense_one, attn_one = sums_one
-    branch_one = operands_one[2].astype(jnp.float32)
-    out_one = record_one.residual + branch_one
-    squares_one = jnp.concatenate(
-        [attn_squares_one, column_sums(branch_one * branch_one), column_sums(out_one * out_one)]
-    )
-    out_one = low(out_one)
+    branch_one = lax.psum_scatter(
+        after(branch_one, grad_one_low), DP, scatter_dimension=0, tiled=True
+    )
     grad_zero, _, (dense_zero, attn_zero), small_zero, extra = backward_layer(
         0,
         grad_one_low,
@@ -1127,8 +1128,15 @@
         record_zero,
         (dense_one[:, :half_hidden], attn_one),
         operands_one,
-    )
-    parts_one, owner_mats, grad_exp_down = extra
+        branch_one,
+    )
+    parts_one, owner_mats, grad_exp_down, branch_one = extra
+    branch_one = branch_one.astype(jnp.float32)
+    out_one = record_one.residual + branch_one
+    squares_one = jnp.concatenate(
+        [attn_squares_one, column_sums(branch_one * branch_one), column_sums(out_one * out_one)]
+    )
+    out_one = low(out_one)
 
     moved_one = in_order(after(parts_one, grad_zero), DP)
     small_message = pack_small(
@@ -1141,12 +1149,21 @@
         (owner_mats(0), owner_mats(1)),
     )
     up_zero = over_dp(by_rows(after(dense_zero[:, :half_hidden], small_moved), dp_size))
-    attn_zero = over_dp(by_rows(after(attn_zero, up_zero), dp_size))
+
+    def of_both(of_zero, of_one):
+        return of_zero, other_core(of_zero), of_one, other_core(of_one)
+
+    def last_rows(small_moved, *rows):
+        return jnp.sum(small_moved, axis=0), finish_rows(section_id, *rows)
+
+    attn_zero, (small_sum, (activations, input_grads)) = beside(
+        over_dp,
+        by_rows(after(attn_zero, up_zero), dp_size),
+        last_rows,
+        (small_moved, of_both(out_zero, out_one), of_both(grad_zero, grad_one)),
+    )
     up_one, attn_one = moved_one[..., :half_hidden], moved_one[..., half_hidden:]
     down_zero, down_one = dense_zero[:, half_hidden:], dense_one[:, half_hidden:]
-
-    def of_both(of_zero, of_one):
-        return of_zero, other_core(of_zero), of_one, other_core(of_one)
 
     grad_qkv, grad_proj, grad_up, grad_down = finish_weights(
         section_id,
@@ -1155,10 +1172,6 @@
         of_both(down_zero, down_one),
         hidden_rows,
     )
-    activations, input_grads = finish_rows(
-        section_id, of_both(out_zero, out_one), of_both(grad_zero, grad_one)
-    )
-    small_sum = jnp.sum(small_moved, axis=0)
     place = expert_id * dp_size + lax.axis_index(DP)
     sums = lax.dynamic_slice_in_dim(
         small_sum[:small_count], place * weight_rows % LANES, weight_rows, axis=1

time: 564 us -> 558 us (0.989)
  waiting for transfers between devices: 155 us -> 134 us
  blocking collectives: 81.2 us -> 97.7 us
    all_to_all x2 -> x3, blocking collectives: 17.7 us -> 34.6 us  [exchange(): return lax.all_to_all(blocks, axes, split_axis=0, concat_axis=0, tiled=True)]
    all_to_all x21 -> x20, waiting for transfers between devices: 101 us -> 87.5 us  [exchange(): return lax.all_to_all(blocks, axes, split_axis=0, concat_axis=0, tiled=True)]
    reduce_scatter x4, waiting for transfers between devices: 8.22 us -> 1.82 us  [over_expert(): return lax.psum_scatter(grad_mat, EX, scatter_dimension=0, tiled=True)]
    all_to_all x21 -> x20, starting transfers between devices: 83.1 us -> 80.5 us  [exchange(): return lax.all_to_all(blocks, axes, split_axis=0, concat_axis=0, tiled=True)]
    unnamed x208 -> x228, local copies, waits for them, and re-layouts: 16.5 us -> 18.2 us
  transfers between devices with their start and end apart: 81 -> 80, of which waited for: 40 -> 35; matrix products, arithmetic and copies ran while one was open for 15% -> 15% of each run, Pallas kernels for 12% -> 12%
where the time goes in v5:
time: 558 us; the launch traced here: 548 us
  waiting for transfers between devices  134 us (24%)
  starting transfers between devices  113 us (20%)
  blocking collectives  97.7 us (18%)
  Pallas kernels  76.8 us (14%)
  local copies, waits for them, and re-layouts  48.2 us (9%)
  matrix products  45.2 us (8%)
  other arithmetic  16.4 us (3%)
  between operations  16.3 us (3%)
    all_to_all x20, waiting for transfers between devices, exchange(): return lax.all_to_all(blocks, axes, split_axis=0, concat_axis=0, tiled=True)  87.5 us
    all_to_all x20, starting transfers between devices, exchange(): return lax.all_to_all(blocks, axes, split_axis=0, concat_axis=0, tiled=True)  80.5 us
    all_gather x4, blocking collectives, gather_rows(): return lax.all_gather(block, DP, axis=0, tiled=True)  63.1 us
    all_to_all x3, blocking collectives, exchange(): return lax.all_to_all(blocks, axes, split_axis=0, concat_axis=0, tiled=True)  34.6 us
    dot_general x12, matrix products, product(): return jnp.dot(left_mat, right_mat, preferred_element_type=jnp.float32)  22.1 us
    pallas_call x4, Pallas kernels, expert_call(): pl.pallas_call(kernel, out_shape=[pltpu.HBM(shape, dtype) for shape, dtyp...  21.2 us
    unnamed x228, local copies, waits for them, and re-layouts  18.2 us
    ppermute x6, waiting for transfers between devices, sent_parts(): lax.ppermute(parts[step], axis, [((i - step) % count, i) for i in range(c...  16.6 us
  transfers between devices with their start and end apart: 80, of which 35 were waited for; matrix products, arithmetic and copies ran while one was open for 15% of the time, Pallas kernels for 12%

profile of v5, /device:TPU:0, one launch (start us, length us, event | category | flops | bytes accessed | tf_op | source)
XLA Modules:
  0.0 548.4 jit_solution(13322899844594072636)
XLA Ops:
  10.2 3.0 collective-permute-start
  17.1 2.9 all-to-all-start
  25.5 5.1 all-to-all-done
  32.9 3.5 all-to-all-start.1
  37.3 7.1 %dynamic-slice_bitcast_fusion = (bf16[1024,1024]{1,0:T(8,128)(2,1)}, bf16[1024,1024]{1,0:T(8,128)(2,1)}, bf16[1024,1024]{1,0:T(8,128)(2,1)}, bf16[1024,1024]{1,0:T(8,128)(2,1)}) fusion(bf16[2,1024,1024]{2,1,0:T(8,128)(2,1)} %bitcast.218, s32[]{:T(128)S(6)} %select_n.163, s32[]{:T(128)S(6)} %select_n.154, bf16[2,1024,1024]{2,1,0:T(8,128)(2,1)} %bitcast.219), kind=kLoop, calls=%fused_computation.8 | loop fusion | bytes 16777224 | tf_op jit(solution)/shard_map/jit(dynamic_index_in_dim)/squeeze | solution.py:732
  44.3 3.9 all-to-all-done.1
  49.6 4.4 all-to-all-start.2
  62.9 7.1 %collective-permute-done.4.refs_2_ = bf16[64,1024]{1,0:T(8,128)(2,1)S(1)} collective-permute-done((bf16[64,1024]{1,0:T(8,128)(2,1)S(1)}, bf16[64,1024]{1,0:T(8,128)(2,1)S(1)}, u32[]{:S(2)}, u32[]{:S(2)}) %collective-permute-start.4) | collective-permute-done | bytes 131104 | tf_op jit(solution)/shard_map/ppermute | solution.py:101
  70.7 6.6 %collective-permute-done.7.refs_2_ = bf16[64,1024]{1,0:T(8,128)(2,1)S(1)} collective-permute-done((bf16[64,1024]{1,0:T(8,128)(2,1)S(1)}, bf16[64,1024]{1,0:T(8,128)(2,1)S(1)}, u32[]{:S(2)}, u32[]{:S(2)}) %collective-permute-start.7) | collective-permute-done | bytes 131104 | tf_op jit(solution)/shard_map/ppermute | solution.py:117
  87.3 3.5 all-to-all-start.3
  90.8 6.0 %all-gather.5.cloned.1.call-done = bf16[2048,1024]{1,0:T(8,128)(2,1)} async-done(((bf16[256,1024]{1,0:T(8,128)(2,1)}), bf16[2048,1024]{1,0:T(8,128)(2,1)}) %all-gather.5.cloned.1.call-update) | async-done | bytes 4194320 | tf_op jit(solution)/shard_map/all_gather | solution.py:776
  99.4 15.7 %all_gather.23.refs_0_ = bf16[256,1024]{1,0:T(8,128)(2,1)S(1)} all-gather(bf16[64,1024]{1,0:T(8,128)(2,1)S(1)} %get-tuple-element.268), channel_id=1, replica_groups=mesh['section'=2,'expert'=4,'dp'=4] {'dp'}, dimensions={0}, use_global_device_ids=true | all-gather | bytes 655360 | tf_op jit(solution)/shard_map/all_gather | solution.py:63
  120.6 4.0 all-to-all-start.4
  128.2 13.8 %all-to-all-done.4 = bf16[8,40,1024]{2,1,0:T(8,128)(2,1)S(1)} async-done(((bf16[8,40,1024]{2,1,0:T(8,128)(2,1)}), bf16[8,40,1024]{2,1,0:T(8,128)(2,1)S(1)}, u32[]{:S(2)}, u32[]{:S(2)}) %all-to-all-start.4) | async-done | bytes 655392 | tf_op jit(solution)/shard_map/all_to_all | solution.py:54
  142.0 4.9 expert_forward.2
  146.9 4.2 all-to-all-start.5
  151.2 3.6 fusion.33
  157.3 4.6 all-to-all-done.5
  161.8 3.1 add_convert_fusion.1
  164.9 3.7 all-to-all-start.6
  169.8 4.7 slice_bitcast_fusion.2
  174.5 3.8 broadcast_select_fusion
  178.3 5.3 all-to-all-done.6.blocks_ref
  184.5 16.0 %all_gather.25.refs_4_ = bf16[256,1024]{1,0:T(8,128)(2,1)S(1)} all-gather(bf16[64,1024]{1,0:T(8,128)(2,1)S(1)} %get-tuple-element.293), channel_id=1, replica_groups=mesh['section'=2,'expert'=4,'dp'=4] {'dp'}, dimensions={0}, use_global_device_ids=true | all-gather | bytes 655360 | tf_op jit(solution)/shard_map/all_gather | solution.py:63
  205.7 3.3 all-to-all-start.7
  209.1 4.7 slice_bitcast_fusion
  217.3 3.7 all-to-all-start.8
  221.0 15.6 %all_gather.26.refs_0_ = bf16[256,1024]{1,0:T(8,128)(2,1)S(1)} all-gather(bf16[64,1024]{1,0:T(8,128)(2,1)S(1)} %get-tuple-element.302), channel_id=1, replica_groups=mesh['section'=2,'expert'=4,'dp'=4] {'dp'}, dimensions={0}, use_global_device_ids=true | all-gather | bytes 655360 | tf_op jit(solution)/shard_map/all_gather | solution.py:63
  239.3 4.0 all-to-all-start.9
  244.8 3.6 fusion.41
  248.4 5.6 %all-to-all-done.9 = bf16[8,40,1024]{2,1,0:T(8,128)(2,1)S(1)} async-done(((bf16[8,40,1024]{2,1,0:T(8,128)(2,1)}), bf16[8,40,1024]{2,1,0:T(8,128)(2,1)S(1)}, u32[]{:S(2)}, u32[]{:S(2)}) %all-to-all-start.9) | async-done | bytes 655392 | tf_op jit(solution)/shard_map/all_to_all | solution.py:54
  253.9 4.9 expert_forward.3
  258.9 4.2 all-to-all-start.11
  264.0 5.6 %expert_backward.2 = (bf16[320,1024]{1,0:T(8,128)(2,1)}, bf16[320,1024]{1,0:T(8,128)(2,1)}, bf16[320,1024]{1,0:T(8,128)(2,1)}) custom-call(s32[1]{0:T(128)} %bitcast.place, bf16[320,1024]{1,0:T(8,128)(2,1)S(1)} %bitcast.197, f32[320,1]{1,0:T(8,128)S(1)} %copy-done.50, bf16[1024,1024]{1,0:T(8,128)(2,1)} %get-tuple-element.275.refs_0_, ...), custom_call_target="tpu_custom_call" | custom-call | tf_op jit(solution)/shard_map/expert_backward/pallas_call | solution.py:316
  273.8 4.2 all-to-all-start.10
  278.1 3.0 fusion.44
  285.1 3.6 all-to-all-done.10
  291.4 5.0 all-to-all-start.12
  305.5 6.0 %all-to-all-done.12.blocks_ref = bf16[4,64,1024]{2,1,0:T(8,128)(2,1)} async-done(((bf16[4,64,1024]{2,1,0:T(8,128)(2,1)}), bf16[4,64,1024]{2,1,0:T(8,128)(2,1)}, u32[]{:S(2)}, u32[]{:S(2)}) %all-to-all-start.12) | async-done | bytes 524320 | tf_op jit(solution)/shard_map/all_to_all | solution.py:54
  311.8 3.8 mid_back.2
  315.6 8.6 %all_to_all.115 = bf16[4,64,256]{2,1,0:T(8,128)(2,1)S(1)} all-to-all(bf16[4,64,256]{2,1,0:T(8,128)(2,1)S(1)} %get-tuple-element.348), channel_id=1, replica_groups=mesh['section'=2,'expert'=4,'dp'=4] {'dp'}, dimensions={0} | all-to-all | bytes 262144 | tf_op jit(solution)/shard_map/all_to_all | solution.py:54
  332.8 17.6 %all_to_all.116.blocks_ref = bf16[4,64,1024]{2,1,0:T(8,128)(2,1)S(1)} all-to-all(bf16[4,64,1024]{2,1,0:T(8,128)(2,1)S(1)} %bitcast.224), channel_id=1, replica_groups=mesh['section'=2,'expert'=4,'dp'=4] {'dp'}, dimensions={0} | all-to-all | bytes 1048576 | tf_op jit(solution)/shard_map/all_to_all | solution.py:54
  351.5 15.7 %all_gather.27 = bf16[256,1024]{1,0:T(8,128)(2,1)S(1)} all-gather(bf16[64,1024]{1,0:T(8,128)(2,1)S(1)} %get-tuple-element.356.grad_ref), channel_id=1, replica_groups=mesh['section'=2,'expert'=4,'dp'=4] {'dp'}, dimensions={0}, use_global_device_ids=true | all-gather | bytes 655360 | tf_op jit(solution)/shard_map/all_gather | solution.py:63
  368.4 3.6 all-to-all-start.15
  374.2 4.0 fusion.25.refs_2_
  387.2 5.7 %expert_backward.3 = (bf16[320,1024]{1,0:T(8,128)(2,1)}, bf16[320,1024]{1,0:T(8,128)(2,1)}, bf16[320,1024]{1,0:T(8,128)(2,1)}) custom-call(s32[1]{0:T(128)} %bitcast.place, bf16[320,1024]{1,0:T(8,128)(2,1)S(1)} %bitcast.196, f32[320,1]{1,0:T(8,128)S(1)} %copy-done.49, bf16[1024,1024]{1,0:T(8,128)(2,1)} %get-tuple-element.275.refs_0_, ...), custom_call_target="tpu_custom_call" | custom-call | tf_op jit(solution)/shard_map/expert_backward/pallas_call | solution.py:316
  393.5 5.1 all-to-all-start.16
  404.9 4.1 pair_grads.6
  410.8 7.5 %collective-permute-done.25.refs_2_ = bf16[64,1408]{1,0:T(8,128)(2,1)} collective-permute-done((bf16[64,1408]{1,0:T(8,128)(2,1)}, bf16[64,1408]{1,0:T(8,128)(2,1)}, u32[]{:S(2)}, u32[]{:S(2)}) %collective-permute-start.25) | collective-permute-done | bytes 180256 | tf_op jit(solution)/shard_map/ppermute | solution.py:117
  425.2 7.0 %all-to-all-start.17 = ((bf16[4,64,1024]{2,1,0:T(8,128)(2,1)}), bf16[4,64,1024]{2,1,0:T(8,128)(2,1)S(1)}, u32[]{:S(2)}, u32[]{:S(2)}) async-start(bf16[4,64,1024]{2,1,0:T(8,128)(2,1)} %bitcast.86), calls=%async_computation.19 | async-start | bytes 1048576 | tf_op jit(solution)/shard_map/all_to_all | solution.py:54
  432.2 6.4 %owner_grads.2 = f32[2,1024,1024]{2,1,0:T(8,128)} custom-call(s32[1]{0:T(128)} %bitcast.place, bf16[320,1024]{1,0:T(8,128)(2,1)} %get-tuple-element.396.refs_0_, bf16[320,1024]{1,0:T(8,128)(2,1)} %copy-done.83, bf16[320,1024]{1,0:T(8,128)(2,1)} %get-tuple-element.398.refs_2_, bf16[320,1024]{1,0:T(8,128)(2,1)} %copy-done.85, ...), custom_call_target="tpu_custom_call" | custom-call | tf_op jit(solution)/shard_map/owner_grads/pallas_call | solution.py:507
  438.6 8.3 %all-to-all-done.17.blocks_ref = bf16[4,64,1024]{2,1,0:T(8,128)(2,1)S(1)} async-done(((bf16[4,64,1024]{2,1,0:T(8,128)(2,1)}), bf16[4,64,1024]{2,1,0:T(8,128)(2,1)S(1)}, u32[]{:S(2)}, u32[]{:S(2)}) %all-to-all-start.17) | async-done | bytes 524320 | tf_op jit(solution)/shard_map/all_to_all | solution.py:54
  446.9 3.1 mid_back.3
  450.0 8.4 %all_to_all.117 = bf16[4,64,256]{2,1,0:T(8,128)(2,1)S(1)} all-to-all(bf16[4,64,256]{2,1,0:T(8,128)(2,1)S(1)} %get-tuple-element.407), channel_id=1, replica_groups=mesh['section'=2,'expert'=4,'dp'=4] {'dp'}, dimensions={0} | all-to-all | bytes 262144 | tf_op jit(solution)/shard_map/all_to_all | solution.py:54
  467.9 3.6 all-to-all-start.19
  474.0 12.5 %all-to-all-done.19.blocks_ref = bf16[4,64,1024]{2,1,0:T(8,128)(2,1)S(1)} async-done(((bf16[4,64,1024]{2,1,0:T(8,128)(2,1)}), bf16[4,64,1024]{2,1,0:T(8,128)(2,1)S(1)}, u32[]{:S(2)}, u32[]{:S(2)}) %all-to-all-start.19) | async-done | bytes 524320 | tf_op jit(solution)/shard_map/all_to_all | solution.py:54
  490.6 3.6 all-to-all-start.20
  494.3 6.3 %owner_grads.3 = f32[2,1024,1024]{2,1,0:T(8,128)} custom-call(s32[1]{0:T(128)} %bitcast.place, bf16[320,1024]{1,0:T(8,128)(2,1)} %bitcast.192, bf16[320,1024]{1,0:T(8,128)(2,1)} %collective-permute-done.38.refs_1_, bf16[320,1024]{1,0:T(8,128)(2,1)} %bitcast.195, bf16[320,1024]{1,0:T(8,128)(2,1)} %collective-permute-done.39.refs_3_, ...), custom_call_target="tpu_custom_call" | custom-call | tf_op jit(solution)/shard_map/owner_grads/pallas_call | solution.py:507
  500.6 4.6 all-to-all-done.20
  507.7 3.4 all-to-all-start.21
  512.2 7.1 %all-to-all-done.21.refs_0_ = bf16[4,64,512]{2,1,0:T(8,128)(2,1)S(1)} async-done(((bf16[4,64,512]{2,1,0:T(8,128)(2,1)}), bf16[4,64,512]{2,1,0:T(8,128)(2,1)S(1)}, u32[]{:S(2)}, u32[]{:S(2)}) %all-to-all-start.21) | async-done | bytes 262176 | tf_op jit(solution)/shard_map/all_to_all | solution.py:54
  520.1 3.5 all-to-all-start.22
  532.0 3.1 all-to-all-done.22.refs_4_
  538.1 3.0 finish_weights.1
  (488 shorter events, 155.0 us)
Async XLA Ops:
  7.2 71.2 %all-gather.9.cloned.1.call-start = ((), (), s32[]{:S(2)}) async-start(), calls=%async_computation.35 | async-start | bytes 4718592 | tf_op jit(solution)/shard_map/all_gather | solution.py:792
  10.2 12.2 %collective-permute-start = (bf16[64,1024]{1,0:T(8,128)(2,1)}, bf16[64,1024]{1,0:T(8,128)(2,1)S(1)}, u32[]{:S(2)}, u32[]{:S(2)}) collective-permute-start(bf16[64,1024]{1,0:T(8,128)(2,1)} %bitcast.205), channel_id=1, source_target_pairs={{3,0},{0,1},{1,2},{2,3},{7,4},{4,5},{5,6},{6,7},{11,8},{8,9},{9,10... | collective-permute-start | bytes 393224 | tf_op jit(solution)/shard_map/ppermute | solution.py:101
  13.2 11.4 %collective-permute-start.1 = (bf16[64,1024]{1,0:T(8,128)(2,1)}, bf16[64,1024]{1,0:T(8,128)(2,1)S(1)}, u32[]{:S(2)}, u32[]{:S(2)}) collective-permute-start(bf16[64,1024]{1,0:T(8,128)(2,1)} %bitcast.206), channel_id=1, source_target_pairs={{2,0},{3,1},{0,2},{1,3},{6,4},{7,5},{4,6},{5,7},{10,8},{11,9},{8,1... | collective-permute-start | bytes 393224 | tf_op jit(solution)/shard_map/ppermute | solution.py:101
  15.8 8.9 %collective-permute-start.2 = (bf16[64,1024]{1,0:T(8,128)(2,1)}, bf16[64,1024]{1,0:T(8,128)(2,1)S(1)}, u32[]{:S(2)}, u32[]{:S(2)}) collective-permute-start(bf16[64,1024]{1,0:T(8,128)(2,1)} %bitcast.207), channel_id=1, source_target_pairs={{1,0},{2,1},{3,2},{0,3},{5,4},{6,5},{7,6},{4,7},{9,8},{10,9},{11,1... | collective-permute-start | bytes 393224 | tf_op jit(solution)/shard_map/ppermute | solution.py:101
  17.1 13.4 %all-to-all-start = ((bf16[32,8,128]{2,1,0:T(8,128)(2,1)}), bf16[32,8,128]{2,1,0:T(8,128)(2,1)S(1)}, u32[]{:S(2)}, u32[]{:S(2)}) async-start(bf16[32,8,128]{2,1,0:T(8,128)(2,1)} %broadcast_in_dim.50), calls=%async_computation | async-start | bytes 131072 | tf_op jit(solution)/shard_map/all_to_all | solution.py:54
  20.1 76.7 %all-gather.5.cloned.1.call-start = ((), (), s32[]{:S(2)}) async-start(), calls=%async_computation.28 | async-start | bytes 4718592 | tf_op jit(solution)/shard_map/all_gather | solution.py:776
  32.9 15.4 %all-to-all-start.1 = ((bf16[4,64,768]{2,1,0:T(8,128)(2,1)}), bf16[4,64,768]{2,1,0:T(8,128)(2,1)S(1)}, u32[]{:S(2)}, u32[]{:S(2)}) async-start(bf16[4,64,768]{2,1,0:T(8,128)(2,1)} %reshape.440), calls=%async_computation.1 | async-start | bytes 786432 | tf_op jit(solution)/shard_map/all_to_all | solution.py:54
  49.6 28.9 %all-to-all-start.2 = ((bf16[4,4,64,768]{3,2,1,0:T(8,128)(2,1)}), bf16[4,4,64,768]{3,2,1,0:T(8,128)(2,1)}, u32[]{:S(2)}, u32[]{:S(2)}) async-start(bf16[4,4,64,768]{3,2,1,0:T(8,128)(2,1)} %broadcast_in_dim.51), calls=%async_computation.2 | async-start | bytes 3145728 | tf_op jit(solution)/shard_map/all_to_all | solution.py:54
  54.0 97.2 %all-gather.7.cloned.1.call-start = ((), (), s32[]{:S(2)}) async-start(), calls=%async_computation.29 | async-start | bytes 4718592 | tf_op jit(solution)/shard_map/all_gather | solution.py:809
  54.0 8.3 %collective-permute-start.3 = (bf16[64,1024]{1,0:T(8,128)(2,1)S(1)}, bf16[64,1024]{1,0:T(8,128)(2,1)S(1)}, u32[]{:S(2)}, u32[]{:S(2)}) collective-permute-start(bf16[64,1024]{1,0:T(8,128)(2,1)S(1)} %fusion.55.refs_0_), channel_id=1, source_target_pairs={{3,0},{0,1},{1,2},{2,3},{7,4},{4,5},{5,6},{6,7},{11,8},{8,9},{9,10... | collective-permute-start | bytes 393224 | tf_op jit(solution)/shard_map/ppermute | solution.py:101
  54.1 15.9 %collective-permute-start.4 = (bf16[64,1024]{1,0:T(8,128)(2,1)S(1)}, bf16[64,1024]{1,0:T(8,128)(2,1)S(1)}, u32[]{:S(2)}, u32[]{:S(2)}) collective-permute-start(bf16[64,1024]{1,0:T(8,128)(2,1)S(1)} %fusion.55.refs_0_), channel_id=1, source_target_pairs={{2,0},{3,1},{0,2},{1,3},{6,4},{7,5},{4,6},{5,7},{10,8},{11,9},{8,1... | collective-permute-start | bytes 393224 | tf_op jit(solution)/shard_map/ppermute | solution.py:101
  56.1 13.9 %collective-permute-start.5 = (bf16[64,1024]{1,0:T(8,128)(2,1)S(1)}, bf16[64,1024]{1,0:T(8,128)(2,1)S(1)}, u32[]{:S(2)}, u32[]{:S(2)}) collective-permute-start(bf16[64,1024]{1,0:T(8,128)(2,1)S(1)} %fusion.55.refs_0_), channel_id=1, source_target_pairs={{1,0},{2,1},{3,2},{0,3},{5,4},{6,5},{7,6},{4,7},{9,8},{10,9},{11,1... | collective-permute-start | bytes 393224 | tf_op jit(solution)/shard_map/ppermute | solution.py:101
  57.9 12.8 %collective-permute-start.6 = (bf16[64,1024]{1,0:T(8,128)(2,1)S(1)}, bf16[64,1024]{1,0:T(8,128)(2,1)S(1)}, u32[]{:S(2)}, u32[]{:S(2)}) collective-permute-start(bf16[64,1024]{1,0:T(8,128)(2,1)S(1)} %get-tuple-element.261), channel_id=1, source_target_pairs={{3,0},{0,1},{1,2},{2,3},{7,4},{4,5},{5,6},{6,7},{11,8},{8,9},{9,10... | collective-permute-start | bytes 393224 | tf_op jit(solution)/shard_map/ppermute | solution.py:117
  58.5 18.9 %collective-permute-start.7 = (bf16[64,1024]{1,0:T(8,128)(2,1)S(1)}, bf16[64,1024]{1,0:T(8,128)(2,1)S(1)}, u32[]{:S(2)}, u32[]{:S(2)}) collective-permute-start(bf16[64,1024]{1,0:T(8,128)(2,1)S(1)} %get-tuple-element.262), channel_id=1, source_target_pairs={{2,0},{3,1},{0,2},{1,3},{6,4},{7,5},{4,6},{5,7},{10,8},{11,9},{8,1... | collective-permute-start | bytes 393224 | tf_op jit(solution)/shard_map/ppermute | solution.py:117
  62.4 15.0 %collective-permute-start.8 = (bf16[64,1024]{1,0:T(8,128)(2,1)S(1)}, bf16[64,1024]{1,0:T(8,128)(2,1)S(1)}, u32[]{:S(2)}, u32[]{:S(2)}) collective-permute-start(bf16[64,1024]{1,0:T(8,128)(2,1)S(1)} %get-tuple-element.263), channel_id=1, source_target_pairs={{1,0},{2,1},{3,2},{0,3},{5,4},{6,5},{7,6},{4,7},{9,8},{10,9},{11,1... | collective-permute-start | bytes 393224 | tf_op jit(solution)/shard_map/ppermute | solution.py:117
  78.5 3.8 collective-permute-start.9
  80.7 61.3 %collective-permute-start.14 = (bf16[1024,1024]{1,0:T(8,128)(2,1)}, bf16[1024,1024]{1,0:T(8,128)(2,1)}, u32[]{:S(2)}, u32[]{:S(2)}) collective-permute-start(bf16[1024,1024]{1,0:T(8,128)(2,1)} %get-tuple-element.276), channel_id=1, source_target_pairs={{0,16},{16,0},{1,17},{17,1},{2,18},{18,2},{3,19},{19,3},{4,20},{20... | collective-permute-start | bytes 6291464 | tf_op jit(solution)/shard_map/ppermute | solution.py:683
  81.2 60.8 %collective-permute-start.15 = (bf16[1024,1024]{1,0:T(8,128)(2,1)}, bf16[1024,1024]{1,0:T(8,128)(2,1)}, u32[]{:S(2)}, u32[]{:S(2)}) collective-permute-start(bf16[1024,1024]{1,0:T(8,128)(2,1)} %get-tuple-element.278), channel_id=1, source_target_pairs={{0,16},{16,0},{1,17},{17,1},{2,18},{18,2},{3,19},{19,3},{4,20},{20... | collective-permute-start | bytes 6291464 | tf_op jit(solution)/shard_map/ppermute | solution.py:683
  87.3 9.8 %all-to-all-start.3 = ((bf16[4,64,256]{2,1,0:T(8,128)(2,1)}), bf16[4,64,256]{2,1,0:T(8,128)(2,1)S(1)}, u32[]{:S(2)}, u32[]{:S(2)}) async-start(bf16[4,64,256]{2,1,0:T(8,128)(2,1)} %bitcast.30), calls=%async_computation.3 | async-start | bytes 262144 | tf_op jit(solution)/shard_map/all_to_all | solution.py:54
  116.3 9.3 %collective-permute-start.11 = (bf16[64,1024]{1,0:T(8,128)(2,1)S(1)}, bf16[64,1024]{1,0:T(8,128)(2,1)S(1)}, u32[]{:S(2)}, u32[]{:S(2)}) collective-permute-start(bf16[64,1024]{1,0:T(8,128)(2,1)S(1)} %dynamic-slice_bitcast_fusion.4.refs_0_.grad_ref), channel_id=1, source_target_pairs={{3,0},{0,1},{1,2},{2,3},{7,4},{4,5},{5,6},{6,7},{11,8},{8,9},{9,10... | collective-permute-start | bytes 393224 | tf_op jit(solution)/shard_map/ppermute | solution.py:101
  118.1 10.0 %collective-permute-start.12 = (bf16[64,1024]{1,0:T(8,128)(2,1)S(1)}, bf16[64,1024]{1,0:T(8,128)(2,1)S(1)}, u32[]{:S(2)}, u32[]{:S(2)}) collective-permute-start(bf16[64,1024]{1,0:T(8,128)(2,1)S(1)} %dynamic-slice_bitcast_fusion.4.refs_0_.grad_ref), channel_id=1, source_target_pairs={{2,0},{3,1},{0,2},{1,3},{6,4},{7,5},{4,6},{5,7},{10,8},{11,9},{8,1... | collective-permute-start | bytes 393224 | tf_op jit(solution)/shard_map/ppermute | solution.py:101
  120.6 7.5 %collective-permute-start.13 = (bf16[64,1024]{1,0:T(8,128)(2,1)S(1)}, bf16[64,1024]{1,0:T(8,128)(2,1)S(1)}, u32[]{:S(2)}, u32[]{:S(2)}) collective-permute-start(bf16[64,1024]{1,0:T(8,128)(2,1)S(1)} %dynamic-slice_bitcast_fusion.4.refs_0_.grad_ref), channel_id=1, source_target_pairs={{1,0},{2,1},{3,2},{0,3},{5,4},{6,5},{7,6},{4,7},{9,8},{10,9},{11,1... | collective-permute-start | bytes 393224 | tf_op jit(solution)/shard_map/ppermute | solution.py:101
  120.6 21.4 %all-to-all-start.4 = ((bf16[8,40,1024]{2,1,0:T(8,128)(2,1)}), bf16[8,40,1024]{2,1,0:T(8,128)(2,1)S(1)}, u32[]{:S(2)}, u32[]{:S(2)}) async-start(bf16[8,40,1024]{2,1,0:T(8,128)(2,1)} %bitcast.222), calls=%async_computation.4 | async-start | bytes 1310720 | tf_op jit(solution)/shard_map/all_to_all | solution.py:54
  146.9 14.9 %all-to-all-start.5 = ((bf16[8,40,1024]{2,1,0:T(8,128)(2,1)}), bf16[8,40,1024]{2,1,0:T(8,128)(2,1)}, u32[]{:S(2)}, u32[]{:S(2)}) async-start(bf16[8,40,1024]{2,1,0:T(8,128)(2,1)} %bitcast.233), calls=%async_computation.5 | async-start | bytes 1310720 | tf_op jit(solution)/shard_map/all_to_all | solution.py:54
  164.9 18.7 %all-to-all-start.6 = ((bf16[4,64,1024]{2,1,0:T(8,128)(2,1)}), bf16[4,64,1024]{2,1,0:T(8,128)(2,1)S(1)}, u32[]{:S(2)}, u32[]{:S(2)}) async-start(bf16[4,64,1024]{2,1,0:T(8,128)(2,1)} %bitcast.45), calls=%async_computation.6 | async-start | bytes 1048576 | tf_op jit(solution)/shard_map/all_to_all | solution.py:54
  205.7 9.2 %all-to-all-start.7 = ((bf16[4,64,256]{2,1,0:T(8,128)(2,1)}), bf16[4,64,256]{2,1,0:T(8,128)(2,1)S(1)}, u32[]{:S(2)}, u32[]{:S(2)}) async-start(bf16[4,64,256]{2,1,0:T(8,128)(2,1)} %bitcast.50), calls=%async_computation.7 | async-start | bytes 262144 | tf_op jit(solution)/shard_map/all_to_all | solution.py:54
  217.3 19.3 %all-to-all-start.8 = ((bf16[8,40,1024]{2,1,0:T(8,128)(2,1)}), bf16[8,40,1024]{2,1,0:T(8,128)(2,1)S(1)}, u32[]{:S(2)}, u32[]{:S(2)}) async-start(bf16[8,40,1024]{2,1,0:T(8,128)(2,1)} %bitcast.221), calls=%async_computation.8 | async-start | bytes 1310720 | tf_op jit(solution)/shard_map/all_to_all | solution.py:54
  239.3 14.6 %all-to-all-start.9 = ((bf16[8,40,1024]{2,1,0:T(8,128)(2,1)}), bf16[8,40,1024]{2,1,0:T(8,128)(2,1)S(1)}, u32[]{:S(2)}, u32[]{:S(2)}) async-start(bf16[8,40,1024]{2,1,0:T(8,128)(2,1)} %bitcast.223), calls=%async_computation.9 | async-start | bytes 1310720 | tf_op jit(solution)/shard_map/all_to_all | solution.py:54
  258.9 14.9 %all-to-all-start.11 = ((bf16[8,40,1024]{2,1,0:T(8,128)(2,1)}), bf16[8,40,1024]{2,1,0:T(8,128)(2,1)}, u32[]{:S(2)}, u32[]{:S(2)}) async-start(bf16[8,40,1024]{2,1,0:T(8,128)(2,1)} %bitcast.234), calls=%async_computation.11 | async-start | bytes 1310720 | tf_op jit(solution)/shard_map/all_to_all | solution.py:54
  273.8 14.9 %all-to-all-start.10 = ((bf16[8,40,1024]{2,1,0:T(8,128)(2,1)}), bf16[8,40,1024]{2,1,0:T(8,128)(2,1)}, u32[]{:S(2)}, u32[]{:S(2)}) async-start(bf16[8,40,1024]{2,1,0:T(8,128)(2,1)} %bitcast.232), calls=%async_computation.10 | async-start | bytes 1310720 | tf_op jit(solution)/shard_map/all_to_all | solution.py:54
  291.4 20.0 %all-to-all-start.12 = ((bf16[4,64,1024]{2,1,0:T(8,128)(2,1)}), bf16[4,64,1024]{2,1,0:T(8,128)(2,1)}, u32[]{:S(2)}, u32[]{:S(2)}) async-start(bf16[4,64,1024]{2,1,0:T(8,128)(2,1)} %bitcast.227), calls=%async_computation.12 | async-start | bytes 1048576 | tf_op jit(solution)/shard_map/all_to_all | solution.py:54
  296.4 85.1 %reduce-scatter.6.cloned.1.call-start = ((), (), s32[]{:S(2)}) async-start(), calls=%async_computation.30 | async-start | bytes 2621440 | tf_op jit(solution)/shard_map/reduce_scatter | solution.py:983
  297.0 3.8 collective-permute-start.19
  311.5 73.7 %reduce-scatter.8.cloned.1.call-start = ((), (), s32[]{:S(2)}) async-start(), calls=%async_computation.31 | async-start | bytes 2293760 | tf_op jit(solution)/shard_map/reduce_scatter | solution.py:983
  368.4 18.7 %all-to-all-start.15 = ((bf16[8,40,1024]{2,1,0:T(8,128)(2,1)}), bf16[8,40,1024]{2,1,0:T(8,128)(2,1)S(1)}, u32[]{:S(2)}, u32[]{:S(2)}) async-start(bf16[8,40,1024]{2,1,0:T(8,128)(2,1)} %bitcast.220), calls=%async_computation.15 | async-start | bytes 1310720 | tf_op jit(solution)/shard_map/all_to_all | solution.py:54
  372.0 66.6 %reduce-scatter.10.cloned.1.call-start = ((), (), s32[]{:S(2)}) async-start(), calls=%async_computation.32 | async-start | bytes 655360 | tf_op jit(solution)/shard_map/reduce_scatter | solution.py:1121
  392.9 7.2 %collective-permute-start.27 = (bf16[256,1024]{1,0:T(8,128)(2,1)S(1)}, bf16[256,1024]{1,0:T(8,128)(2,1)}, u32[]{:S(2)}, u32[]{:S(2)}) collective-permute-start(bf16[256,1024]{1,0:T(8,128)(2,1)S(1)} %all_gather.23.refs_0_), channel_id=1, source_target_pairs={{0,16},{16,0},{1,17},{17,1},{2,18},{18,2},{3,19},{19,3},{4,20},{20... | collective-permute-start | bytes 1572872 | tf_op jit(solution)/shard_map/ppermute | solution.py:683
  393.0 9.5 %collective-permute-start.28 = (bf16[256,1024]{1,0:T(8,128)(2,1)}, bf16[256,1024]{1,0:T(8,128)(2,1)}, u32[]{:S(2)}, u32[]{:S(2)}) collective-permute-start(bf16[256,1024]{1,0:T(8,128)(2,1)} %fusion.25.refs_2_), channel_id=1, source_target_pairs={{0,16},{16,0},{1,17},{17,1},{2,18},{18,2},{3,19},{19,3},{4,20},{20... | collective-permute-start | bytes 1572872 | tf_op jit(solution)/shard_map/ppermute | solution.py:683
  393.5 24.8 %all-to-all-start.16 = ((bf16[8,40,1024]{2,1,0:T(8,128)(2,1)}), bf16[8,40,1024]{2,1,0:T(8,128)(2,1)}, u32[]{:S(2)}, u32[]{:S(2)}) async-start(bf16[8,40,1024]{2,1,0:T(8,128)(2,1)} %bitcast.231), calls=%async_computation.18 | async-start | bytes 1310720 | tf_op jit(solution)/shard_map/all_to_all | solution.py:54
  398.6 107.3 %reduce-scatter.14.cloned.1.call-start = ((), (), s32[]{:S(2)}) async-start(), calls=%async_computation.34 | async-start | bytes 2621440 | tf_op jit(solution)/shard_map/reduce_scatter | solution.py:983
  398.6 6.3 %collective-permute-start.29 = (bf16[256,1024]{1,0:T(8,128)(2,1)}, bf16[256,1024]{1,0:T(8,128)(2,1)S(1)}, u32[]{:S(2)}, u32[]{:S(2)}) collective-permute-start(bf16[256,1024]{1,0:T(8,128)(2,1)} %copy-done.30), channel_id=1, source_target_pairs={{0,16},{16,0},{1,17},{17,1},{2,18},{18,2},{3,19},{19,3},{4,20},{20... | collective-permute-start | bytes 1572872 | tf_op jit(solution)/shard_map/ppermute | solution.py:683
  399.1 5.8 %collective-permute-start.30 = (bf16[256,1024]{1,0:T(8,128)(2,1)S(1)}, bf16[256,1024]{1,0:T(8,128)(2,1)S(1)}, u32[]{:S(2)}, u32[]{:S(2)}) collective-permute-start(bf16[256,1024]{1,0:T(8,128)(2,1)S(1)} %get-tuple-element.388.refs_6_), channel_id=1, source_target_pairs={{0,16},{16,0},{1,17},{17,1},{2,18},{18,2},{3,19},{19,3},{4,20},{20... | collective-permute-start | bytes 1572872 | tf_op jit(solution)/shard_map/ppermute | solution.py:683
  399.2 11.6 %collective-permute-start.24 = (bf16[64,1408]{1,0:T(8,128)(2,1)}, bf16[64,1408]{1,0:T(8,128)(2,1)S(1)}, u32[]{:S(2)}, u32[]{:S(2)}) collective-permute-start(bf16[64,1408]{1,0:T(8,128)(2,1)} %get-tuple-element.382), channel_id=1, source_target_pairs={{3,0},{0,1},{1,2},{2,3},{7,4},{4,5},{5,6},{6,7},{11,8},{8,9},{9,10... | collective-permute-start | bytes 540680 | tf_op jit(solution)/shard_map/ppermute | solution.py:117
  400.1 18.2 %collective-permute-start.25 = (bf16[64,1408]{1,0:T(8,128)(2,1)}, bf16[64,1408]{1,0:T(8,128)(2,1)}, u32[]{:S(2)}, u32[]{:S(2)}) collective-permute-start(bf16[64,1408]{1,0:T(8,128)(2,1)} %get-tuple-element.383), channel_id=1, source_target_pairs={{2,0},{3,1},{0,2},{1,3},{6,4},{7,5},{4,6},{5,7},{10,8},{11,9},{8,1... | collective-permute-start | bytes 540680 | tf_op jit(solution)/shard_map/ppermute | solution.py:117
  402.4 15.8 %collective-permute-start.26 = (bf16[64,1408]{1,0:T(8,128)(2,1)}, bf16[64,1408]{1,0:T(8,128)(2,1)}, u32[]{:S(2)}, u32[]{:S(2)}) collective-permute-start(bf16[64,1408]{1,0:T(8,128)(2,1)} %get-tuple-element.384), channel_id=1, source_target_pairs={{1,0},{2,1},{3,2},{0,3},{5,4},{6,5},{7,6},{4,7},{9,8},{10,9},{11,1... | collective-permute-start | bytes 540680 | tf_op jit(solution)/shard_map/ppermute | solution.py:117
  418.4 4.2 collective-permute-start.34
  418.9 4.6 collective-permute-start.32
  419.0 5.3 collective-permute-start.33
  425.2 21.7 %all-to-all-start.17 = ((bf16[4,64,1024]{2,1,0:T(8,128)(2,1)}), bf16[4,64,1024]{2,1,0:T(8,128)(2,1)S(1)}, u32[]{:S(2)}, u32[]{:S(2)}) async-start(bf16[4,64,1024]{2,1,0:T(8,128)(2,1)} %bitcast.86), calls=%async_computation.19 | async-start | bytes 1048576 | tf_op jit(solution)/shard_map/all_to_all | solution.py:54
  432.2 87.2 %reduce-scatter.12.cloned.1.call-start = ((), (), s32[]{:S(2)}) async-start(), calls=%async_computation.33 | async-start | bytes 2293760 | tf_op jit(solution)/shard_map/reduce_scatter | solution.py:983
  467.9 18.7 %all-to-all-start.19 = ((bf16[4,64,1024]{2,1,0:T(8,128)(2,1)}), bf16[4,64,1024]{2,1,0:T(8,128)(2,1)S(1)}, u32[]{:S(2)}, u32[]{:S(2)}) async-start(bf16[4,64,1024]{2,1,0:T(8,128)(2,1)} %bitcast.90), calls=%async_computation.24 | async-start | bytes 1048576 | tf_op jit(solution)/shard_map/all_to_all | solution.py:54
  471.5 19.1 %collective-permute-start.38 = (bf16[320,1024]{1,0:T(8,128)(2,1)S(1)}, bf16[320,1024]{1,0:T(8,128)(2,1)}, u32[]{:S(2)}, u32[]{:S(2)}) collective-permute-start(bf16[320,1024]{1,0:T(8,128)(2,1)S(1)} %bitcast.191), channel_id=1, source_target_pairs={{0,16},{16,0},{1,17},{17,1},{2,18},{18,2},{3,19},{19,3},{4,20},{20... | collective-permute-start | bytes 1966088 | tf_op jit(solution)/shard_map/ppermute | solution.py:683
  471.7 18.9 %collective-permute-start.39 = (bf16[320,1024]{1,0:T(8,128)(2,1)S(1)}, bf16[320,1024]{1,0:T(8,128)(2,1)}, u32[]{:S(2)}, u32[]{:S(2)}) collective-permute-start(bf16[320,1024]{1,0:T(8,128)(2,1)S(1)} %bitcast.194), channel_id=1, source_target_pairs={{0,16},{16,0},{1,17},{17,1},{2,18},{18,2},{3,19},{19,3},{4,20},{20... | collective-permute-start | bytes 1966088 | tf_op jit(solution)/shard_map/ppermute | solution.py:683
  472.1 18.5 %collective-permute-start.41 = (bf16[320,1024]{1,0:T(8,128)(2,1)}, bf16[320,1024]{1,0:T(8,128)(2,1)}, u32[]{:S(2)}, u32[]{:S(2)}) collective-permute-start(bf16[320,1024]{1,0:T(8,128)(2,1)} %get-tuple-element.438.refs_6_), channel_id=1, source_target_pairs={{0,16},{16,0},{1,17},{17,1},{2,18},{18,2},{3,19},{19,3},{4,20},{20... | collective-permute-start | bytes 1966088 | tf_op jit(solution)/shard_map/ppermute | solution.py:683
  472.2 18.4 %collective-permute-start.40 = (bf16[320,1024]{1,0:T(8,128)(2,1)}, bf16[320,1024]{1,0:T(8,128)(2,1)}, u32[]{:S(2)}, u32[]{:S(2)}) collective-permute-start(bf16[320,1024]{1,0:T(8,128)(2,1)} %get-tuple-element.436.refs_4_), channel_id=1, source_target_pairs={{0,16},{16,0},{1,17},{17,1},{2,18},{18,2},{3,19},{19,3},{4,20},{20... | collective-permute-start | bytes 1966088 | tf_op jit(solution)/shard_map/ppermute | solution.py:683
  490.6 14.6 %all-to-all-start.20 = ((f32[32,16,128]{2,1,0:T(8,128)}), f32[32,16,128]{2,1,0:T(8,128)S(1)}, u32[]{:S(2)}, u32[]{:S(2)}) async-start(f32[32,16,128]{2,1,0:T(8,128)} %pack_small.1), calls=%async_computation.25 | async-start | bytes 524288 | tf_op jit(solution)/shard_map/all_to_all | solution.py:54
  507.7 11.6 %all-to-all-start.21 = ((bf16[4,64,512]{2,1,0:T(8,128)(2,1)}), bf16[4,64,512]{2,1,0:T(8,128)(2,1)S(1)}, u32[]{:S(2)}, u32[]{:S(2)}) async-start(bf16[4,64,512]{2,1,0:T(8,128)(2,1)} %bitcast.93), calls=%async_computation.26 | async-start | bytes 524288 | tf_op jit(solution)/shard_map/all_to_all | solution.py:54
  511.1 8.2 %collective-permute-start.45 = (f32[64,1024]{1,0:T(8,128)S(1)}, f32[64,1024]{1,0:T(8,128)S(1)}, u32[]{:S(2)}, u32[]{:S(2)}) collective-permute-start(f32[64,1024]{1,0:T(8,128)S(1)} %copy-done.39), channel_id=1, source_target_pairs={{0,16},{16,0},{1,17},{17,1},{2,18},{18,2},{3,19},{19,3},{4,20},{20... | collective-permute-start | bytes 786440 | tf_op jit(solution)/shard_map/ppermute | solution.py:683
  511.2 8.8 %collective-permute-start.44 = (f32[64,1024]{1,0:T(8,128)S(1)}, f32[64,1024]{1,0:T(8,128)S(1)}, u32[]{:S(2)}, u32[]{:S(2)}) collective-permute-start(f32[64,1024]{1,0:T(8,128)S(1)} %get-tuple-element.451.refs_4_), channel_id=1, source_target_pairs={{0,16},{16,0},{1,17},{17,1},{2,18},{18,2},{3,19},{19,3},{4,20},{20... | collective-permute-start | bytes 786440 | tf_op jit(solution)/shard_map/ppermute | solution.py:683
  511.7 7.6 %collective-permute-start.42 = (bf16[64,1024]{1,0:T(8,128)(2,1)S(1)}, bf16[64,1024]{1,0:T(8,128)(2,1)S(1)}, u32[]{:S(2)}, u32[]{:S(2)}) collective-permute-start(bf16[64,1024]{1,0:T(8,128)(2,1)S(1)} %copy-done.20), channel_id=1, source_target_pairs={{0,16},{16,0},{1,17},{17,1},{2,18},{18,2},{3,19},{19,3},{4,20},{20... | collective-permute-start | bytes 393224 | tf_op jit(solution)/shard_map/ppermute | solution.py:683
  511.8 8.3 %collective-permute-start.43 = (bf16[64,1024]{1,0:T(8,128)(2,1)S(1)}, bf16[64,1024]{1,0:T(8,128)(2,1)S(1)}, u32[]{:S(2)}, u32[]{:S(2)}) collective-permute-start(bf16[64,1024]{1,0:T(8,128)(2,1)S(1)} %get-tuple-element.449.refs_2_), channel_id=1, source_target_pairs={{0,16},{16,0},{1,17},{17,1},{2,18},{18,2},{3,19},{19,3},{4,20},{20... | collective-permute-start | bytes 393224 | tf_op jit(solution)/shard_map/ppermute | solution.py:683
  520.1 15.0 %all-to-all-start.22 = ((bf16[4,64,896]{2,1,0:T(8,128)(2,1)}), bf16[4,64,896]{2,1,0:T(8,128)(2,1)S(1)}, u32[]{:S(2)}, u32[]{:S(2)}) async-start(bf16[4,64,896]{2,1,0:T(8,128)(2,1)} %bitcast.236), calls=%async_computation.27 | async-start | bytes 917504 | tf_op jit(solution)/shard_map/all_to_all | solution.py:54
  523.6 12.9 %collective-permute-start.51 = (bf16[256,512]{1,0:T(8,128)(2,1)S(1)}, bf16[256,512]{1,0:T(8,128)(2,1)}, u32[]{:S(2)}, u32[]{:S(2)}) collective-permute-start(bf16[256,512]{1,0:T(8,128)(2,1)S(1)} %copy-done.28), channel_id=1, source_target_pairs={{0,16},{16,0},{1,17},{17,1},{2,18},{18,2},{3,19},{19,3},{4,20},{20... | collective-permute-start | bytes 786440 | tf_op jit(solution)/shard_map/ppermute | solution.py:683
  524.8 13.2 %collective-permute-start.49 = (bf16[4,64,896]{2,1,0:T(8,128)(2,1)S(1)}, bf16[4,64,896]{2,1,0:T(8,128)(2,1)S(1)}, u32[]{:S(2)}, u32[]{:S(2)}) collective-permute-start(bf16[4,64,896]{2,1,0:T(8,128)(2,1)S(1)} %slice.248.refs_6_), channel_id=1, source_target_pairs={{0,16},{16,0},{1,17},{17,1},{2,18},{18,2},{3,19},{19,3},{4,20},{20... | collective-permute-start | bytes 1376264 | tf_op jit(solution)/shard_map/ppermute | solution.py:683
  (131 other events, 2094.5 us)
Sparse Core Ops, SparseCore 0:
  9.9 39.9 all-gather.8
  52.4 44.3 all-gather.4
  99.2 43.1 all-gather.6
  311.6 32.6 reduce-scatter.5
  347.5 37.6 reduce-scatter.7
  387.4 25.9 reduce-scatter.9
  418.4 38.5 reduce-scatter.13
  468.0 33.5 reduce-scatter.11

commit v6 on v5

--- a/solution.py
+++ b/solution.py
@@ -353,6 +353,28 @@
                     copy.start()
 
     return [copies(0, part) for part in range(2)]
+
+
+def combine(table, returned, base, weight=None):
+    def kernel(table_ref, returned_ref, base_ref, *refs):
+        expert_part = product_tn(table_ref[...], returned_ref[...])
+        if weight is None:
+            refs[-1][...] = low(base_ref[...] + expert_part)
+        else:
+            refs[-2][...] = expert_part
+            weights = refs[0][...]
+            refs[-1][...] = low(weights[:, 0:1] * base_ref[...] + weights[:, 1:2] * expert_part)
+
+    shape = (table.shape[1], returned.shape[1])
+    outs = [jax.ShapeDtypeStruct(shape, jnp.bfloat16)]
+    if weight is not None:
+        outs = [jax.ShapeDtypeStruct(shape, jnp.float32)] + outs
+    return pl.pallas_call(
+        kernel,
+        out_shape=outs,
+        compiler_params=pltpu.CompilerParams(vmem_limit_bytes=32 << 20),
+        name="combine",
+    )(table, returned, base, *(() if weight is None else (weight,)))
 
 
 def row_scales(logits, expert):
@@ -508,7 +530,7 @@
         kernel,
         out_shape=jax.ShapeDtypeStruct((2, left_width, right_width), jnp.float32),
         grid=(2, tiles),
-        in_specs=[SCALAR] + [IN_HBM] * 8,
+        in_specs=[SCALAR] + [IN_HBM, WHOLE] * 4,
         out_specs=pl.BlockSpec((1, OWNER_TILE, right_width), lambda expert, tile: (expert, tile, 0)),
         scratch_shapes=[
             pltpu.VMEM((2, rows, left_width), jnp.bfloat16),
@@ -517,7 +539,13 @@
         ],
         compiler_params=pltpu.CompilerParams(vmem_limit_bytes=40 << 20),
         name="owner_grads",
-    )(section_id.reshape(1), *[in_hbm(mat) for mat in (*left_mats, *right_mats)])
+    )(
+        section_id.reshape(1),
+        *[
+            mat if index % 2 else in_hbm(mat)
+            for index, mat in enumerate((*left_mats, *right_mats))
+        ],
+    )
 
 
 def statistics(value_rows):
@@ -1057,13 +1085,13 @@
                 lambda early, *operands: (sent_parts(early, DP), dense_grads(*operands)),
                 (early, record.hidden_low, d_dense, record.mid_seq, d_up, d_small),
             )
-            d_mid_part = d_mid_part + product_tn(table, returned.reshape(-1, width))
+            (d_mid_part,) = combine(table, returned.reshape(-1, width), d_mid_part)
             d_mid, (g_exp_down, settle) = beside(
                 over_dp,
                 row_blocks(d_mid_part),
                 lambda left, right, settle: (owner_grads(section_id, left, right), settle),
-                (owner_mats(2), owner_mats(3)),
-                (settle,),
+                (),
+                (owner_mats(2), owner_mats(3), settle),
             )
         else:
             returned, dense_grad = beside(
@@ -1095,9 +1123,11 @@
             (in_blocks, record.normed_seq, d_qkv)
         )
         g_attn = pair_grads(section_id, (record.mixed, d_attn), (normed_seq, d_qkv))
-        attn_sum = over_expert(g_attn)
-        beside_it = g_attn
-        d_normed, beside_it = lax.optimization_barrier((over_dp(in_blocks), beside_it))
+        if layer == 1:
+            attn_sum = over_expert(g_attn)
+        d_normed, g_attn = lax.optimization_barrier((over_dp(in_blocks), g_attn))
+        if layer == 0:
+            attn_sum = over_expert(g_attn)
         d_input, d_input_low, d_gain_zero, d_shift_zero = input_back(
             d_normed, record.layer_in, params[0:1], d_resid
         )

time: 558 us -> 550 us (0.986)
  waiting for transfers between devices: 134 us -> 126 us
    all_to_all x20, waiting for transfers between devices: 87.5 us -> 78.2 us  [exchange(): return lax.all_to_all(blocks, axes, split_axis=0, concat_axis=0, tiled=True)]
    dot_general x6 -> x5, matrix products: 12.8 us -> 11.9 us  [product_tn(): lax.dot_general(left_mat, right_mat, (((0,), (0,)), ((), ())), preferred_...]
    unnamed x228 -> x212, local copies, waits for them, and re-layouts: 18.2 us -> 17.4 us
  transfers between devices with their start and end apart: 80 -> 80, of which waited for: 35 -> 37; matrix products, arithmetic and copies ran while one was open for 15% -> 14% of each run, Pallas kernels for 12% -> 13%
where the time goes in v6:
time: 550 us; the launch traced here: 541 us
  waiting for transfers between devices  126 us (23%)
  starting transfers between devices  114 us (21%)
  blocking collectives  97.9 us (18%)
  Pallas kernels  81.4 us (15%)
  local copies, waits for them, and re-layouts  47 us (9%)
  matrix products  42.6 us (8%)
  between operations  16.2 us (3%)
  other arithmetic  15.3 us (3%)
    all_to_all x20, starting transfers between devices, exchange(): return lax.all_to_all(blocks, axes, split_axis=0, concat_axis=0, tiled=True)  81.3 us
    all_to_all x20, waiting for transfers between devices, exchange(): return lax.all_to_all(blocks, axes, split_axis=0, concat_axis=0, tiled=True)  78.2 us
    all_gather x4, blocking collectives, gather_rows(): return lax.all_gather(block, DP, axis=0, tiled=True)  63.2 us
    all_to_all x3, blocking collectives, exchange(): return lax.all_to_all(blocks, axes, split_axis=0, concat_axis=0, tiled=True)  34.6 us
    pallas_call x4, Pallas kernels, expert_call(): pl.pallas_call(kernel, out_shape=[pltpu.HBM(shape, dtype) for shape, dtyp...  22.2 us
    dot_general x12, matrix products, product(): return jnp.dot(left_mat, right_mat, preferred_element_type=jnp.float32)  20.3 us
    unnamed x212, local copies, waits for them, and re-layouts  17.4 us
    ppermute x9, starting transfers between devices, permute_copies(): blocks.append(lax.ppermute(block, axis, route))  15.1 us
  transfers between devices with their start and end apart: 80, of which 37 were waited for; matrix products, arithmetic and copies ran while one was open for 14% of the time, Pallas kernels for 13%

profile of v6, /device:TPU:0, one launch (start us, length us, event | category | flops | bytes accessed | tf_op | source)
XLA Modules:
  0.0 540.7 jit_solution(16652919902911226101)
XLA Ops:
  10.2 3.0 collective-permute-start
  17.1 2.9 all-to-all-start
  25.5 5.1 all-to-all-done
  32.9 3.5 all-to-all-start.1
  37.3 7.0 %dynamic-slice_bitcast_fusion = (bf16[1024,1024]{1,0:T(8,128)(2,1)}, bf16[1024,1024]{1,0:T(8,128)(2,1)}, bf16[1024,1024]{1,0:T(8,128)(2,1)}, bf16[1024,1024]{1,0:T(8,128)(2,1)}) fusion(bf16[2,1024,1024]{2,1,0:T(8,128)(2,1)} %bitcast.219, s32[]{:T(128)S(6)} %select_n.163, s32[]{:T(128)S(6)} %select_n.154, bf16[2,1024,1024]{2,1,0:T(8,128)(2,1)} %bitcast.220), kind=kLoop, calls=%fused_computation.8 | loop fusion | bytes 16777224 | tf_op jit(solution)/shard_map/jit(dynamic_index_in_dim)/squeeze | solution.py:760
  44.3 3.9 all-to-all-done.1
  49.6 3.6 all-to-all-start.2
  62.0 7.1 %collective-permute-done.4.refs_2_ = bf16[64,1024]{1,0:T(8,128)(2,1)S(1)} collective-permute-done((bf16[64,1024]{1,0:T(8,128)(2,1)S(1)}, bf16[64,1024]{1,0:T(8,128)(2,1)S(1)}, u32[]{:S(2)}, u32[]{:S(2)}) %collective-permute-start.4) | collective-permute-done | bytes 131104 | tf_op jit(solution)/shard_map/ppermute | solution.py:101
  69.9 6.6 %collective-permute-done.7.refs_2_ = bf16[64,1024]{1,0:T(8,128)(2,1)S(1)} collective-permute-done((bf16[64,1024]{1,0:T(8,128)(2,1)S(1)}, bf16[64,1024]{1,0:T(8,128)(2,1)S(1)}, u32[]{:S(2)}, u32[]{:S(2)}) %collective-permute-start.7) | collective-permute-done | bytes 131104 | tf_op jit(solution)/shard_map/ppermute | solution.py:117
  84.8 3.5 all-to-all-start.3
  88.3 7.5 %all-gather.5.cloned.1.call-done = bf16[2048,1024]{1,0:T(8,128)(2,1)} async-done(((bf16[256,1024]{1,0:T(8,128)(2,1)}), bf16[2048,1024]{1,0:T(8,128)(2,1)}) %all-gather.5.cloned.1.call-update) | async-done | bytes 4194320 | tf_op jit(solution)/shard_map/all_gather | solution.py:804
  98.8 16.0 %all_gather.23.refs_0_ = bf16[256,1024]{1,0:T(8,128)(2,1)S(1)} all-gather(bf16[64,1024]{1,0:T(8,128)(2,1)S(1)} %get-tuple-element.259), channel_id=1, replica_groups=mesh['section'=2,'expert'=4,'dp'=4] {'dp'}, dimensions={0}, use_global_device_ids=true | all-gather | bytes 655360 | tf_op jit(solution)/shard_map/all_gather | solution.py:63
  120.4 4.0 all-to-all-start.4
  127.9 13.2 %all-to-all-done.4 = bf16[8,40,1024]{2,1,0:T(8,128)(2,1)S(1)} async-done(((bf16[8,40,1024]{2,1,0:T(8,128)(2,1)}), bf16[8,40,1024]{2,1,0:T(8,128)(2,1)S(1)}, u32[]{:S(2)}, u32[]{:S(2)}) %all-to-all-start.4) | async-done | bytes 655392 | tf_op jit(solution)/shard_map/all_to_all | solution.py:54
  141.1 4.9 expert_forward.2
  146.1 4.2 all-to-all-start.5
  150.4 3.6 fusion.32
  155.6 5.4 all-to-all-done.5
  161.0 3.1 add_convert_fusion.1
  164.1 4.2 all-to-all-start.6
  169.5 4.8 slice_bitcast_fusion.2
  174.3 3.4 broadcast_select_fusion
  177.7 5.5 %all-to-all-done.6.blocks_ref = bf16[4,64,1024]{2,1,0:T(8,128)(2,1)S(1)} async-done(((bf16[4,64,1024]{2,1,0:T(8,128)(2,1)}), bf16[4,64,1024]{2,1,0:T(8,128)(2,1)S(1)}, u32[]{:S(2)}, u32[]{:S(2)}) %all-to-all-start.6) | async-done | bytes 524320 | tf_op jit(solution)/shard_map/all_to_all | solution.py:54
  183.6 16.1 %all_gather.25.refs_4_ = bf16[256,1024]{1,0:T(8,128)(2,1)S(1)} all-gather(bf16[64,1024]{1,0:T(8,128)(2,1)S(1)} %get-tuple-element.284), channel_id=1, replica_groups=mesh['section'=2,'expert'=4,'dp'=4] {'dp'}, dimensions={0}, use_global_device_ids=true | all-gather | bytes 655360 | tf_op jit(solution)/shard_map/all_gather | solution.py:63
  204.8 3.3 all-to-all-start.7
  208.2 4.7 slice_bitcast_fusion
  217.7 3.5 all-to-all-start.8
  221.2 15.6 %all_gather.26.refs_0_ = bf16[256,1024]{1,0:T(8,128)(2,1)S(1)} all-gather(bf16[64,1024]{1,0:T(8,128)(2,1)S(1)} %get-tuple-element.293), channel_id=1, replica_groups=mesh['section'=2,'expert'=4,'dp'=4] {'dp'}, dimensions={0}, use_global_device_ids=true | all-gather | bytes 655360 | tf_op jit(solution)/shard_map/all_gather | solution.py:63
  238.4 4.1 all-to-all-start.9
  242.5 3.6 fusion.40
  246.1 7.0 %all-to-all-done.9 = bf16[8,40,1024]{2,1,0:T(8,128)(2,1)S(1)} async-done(((bf16[8,40,1024]{2,1,0:T(8,128)(2,1)}), bf16[8,40,1024]{2,1,0:T(8,128)(2,1)S(1)}, u32[]{:S(2)}, u32[]{:S(2)}) %all-to-all-start.9) | async-done | bytes 655392 | tf_op jit(solution)/shard_map/all_to_all | solution.py:54
  253.1 4.9 expert_forward.3
  258.0 4.2 all-to-all-start.11
  263.2 5.6 %expert_backward.2 = (bf16[320,1024]{1,0:T(8,128)(2,1)}, bf16[320,1024]{1,0:T(8,128)(2,1)}, bf16[320,1024]{1,0:T(8,128)(2,1)}) custom-call(s32[1]{0:T(128)} %bitcast.29.place, bf16[320,1024]{1,0:T(8,128)(2,1)S(1)} %bitcast.195, f32[320,1]{1,0:T(8,128)S(1)} %copy-done.50, bf16[1024,1024]{1,0:T(8,128)(2,1)} %get-tuple-element.266.refs_0_, ...), custom_call_target="tpu_custom_call" | custom-call | tf_op jit(solution)/shard_map/expert_backward/pallas_call | solution.py:316
  272.9 4.2 all-to-all-start.10
  277.2 3.0 fusion.43
  284.7 3.1 all-to-all-done.10
  290.6 5.0 all-to-all-start.12
  303.4 7.2 %all-to-all-done.12.blocks_ref = bf16[4,64,1024]{2,1,0:T(8,128)(2,1)} async-done(((bf16[4,64,1024]{2,1,0:T(8,128)(2,1)}), bf16[4,64,1024]{2,1,0:T(8,128)(2,1)}, u32[]{:S(2)}, u32[]{:S(2)}) %all-to-all-start.12) | async-done | bytes 524320 | tf_op jit(solution)/shard_map/all_to_all | solution.py:54
  311.0 3.8 mid_back.2
  316.0 8.6 %all_to_all.115 = bf16[4,64,256]{2,1,0:T(8,128)(2,1)S(1)} all-to-all(bf16[4,64,256]{2,1,0:T(8,128)(2,1)S(1)} %get-tuple-element.339), channel_id=1, replica_groups=mesh['section'=2,'expert'=4,'dp'=4] {'dp'}, dimensions={0} | all-to-all | bytes 262144 | tf_op jit(solution)/shard_map/all_to_all | solution.py:54
  333.2 17.6 %all_to_all.116.blocks_ref = bf16[4,64,1024]{2,1,0:T(8,128)(2,1)S(1)} all-to-all(bf16[4,64,1024]{2,1,0:T(8,128)(2,1)S(1)} %bitcast.225), channel_id=1, replica_groups=mesh['section'=2,'expert'=4,'dp'=4] {'dp'}, dimensions={0} | all-to-all | bytes 1048576 | tf_op jit(solution)/shard_map/all_to_all | solution.py:54
  352.5 15.5 %all_gather.27 = bf16[256,1024]{1,0:T(8,128)(2,1)S(1)} all-gather(bf16[64,1024]{1,0:T(8,128)(2,1)S(1)} %get-tuple-element.347.grad_ref), channel_id=1, replica_groups=mesh['section'=2,'expert'=4,'dp'=4] {'dp'}, dimensions={0}, use_global_device_ids=true | all-gather | bytes 655360 | tf_op jit(solution)/shard_map/all_gather | solution.py:63
  369.9 4.3 all-to-all-start.15
  376.8 4.1 fusion.24.refs_2_
  388.5 6.8 %expert_backward.3 = (bf16[320,1024]{1,0:T(8,128)(2,1)}, bf16[320,1024]{1,0:T(8,128)(2,1)}, bf16[320,1024]{1,0:T(8,128)(2,1)}) custom-call(s32[1]{0:T(128)} %bitcast.29.place, bf16[320,1024]{1,0:T(8,128)(2,1)} %bitcast.83.rows_ref, f32[320,1]{1,0:T(8,128)S(1)} %copy-done.49, bf16[1024,1024]{1,0:T(8,128)(2,1)} %get-tuple-element.266.refs_0_, ...), custom_call_target="tpu_custom_call" | custom-call | tf_op jit(solution)/shard_map/expert_backward/pallas_call | solution.py:316
  395.9 4.2 all-to-all-start.16
  408.1 4.0 pair_grads.6
  412.3 6.7 %collective-permute-done.24.refs_2_ = bf16[64,1408]{1,0:T(8,128)(2,1)} collective-permute-done((bf16[64,1408]{1,0:T(8,128)(2,1)}, bf16[64,1408]{1,0:T(8,128)(2,1)}, u32[]{:S(2)}, u32[]{:S(2)}) %collective-permute-start.24) | collective-permute-done | bytes 180256 | tf_op jit(solution)/shard_map/ppermute | solution.py:117
  421.5 7.1 %all-to-all-start.17 = ((bf16[4,64,1024]{2,1,0:T(8,128)(2,1)}), bf16[4,64,1024]{2,1,0:T(8,128)(2,1)S(1)}, u32[]{:S(2)}, u32[]{:S(2)}) async-start(bf16[4,64,1024]{2,1,0:T(8,128)(2,1)} %bitcast.86), calls=%async_computation.19 | async-start | bytes 1048576 | tf_op jit(solution)/shard_map/all_to_all | solution.py:54
  433.7 6.3 %owner_grads.2 = f32[2,1024,1024]{2,1,0:T(8,128)} custom-call(s32[1]{0:T(128)} %bitcast.29.place, bf16[320,1024]{1,0:T(8,128)(2,1)} %get-tuple-element.382.refs_0_, bf16[320,1024]{1,0:T(8,128)(2,1)S(1)} %collective-permute-done.30.refs_1_, bf16[320,1024]{1,0:T(8,128)(2,1)} %get-tuple-element.383.refs_2_, ...), custom_call_target="tpu_custom_call" | custom-call | tf_op jit(solution)/shard_map/owner_grads/pallas_call | solution.py:529
  440.1 3.1 all-to-all-done.17.blocks_ref
  443.2 2.8 mid_back.3
  446.0 8.5 %all_to_all.117 = bf16[4,64,256]{2,1,0:T(8,128)(2,1)S(1)} all-to-all(bf16[4,64,256]{2,1,0:T(8,128)(2,1)S(1)} %get-tuple-element.388), channel_id=1, replica_groups=mesh['section'=2,'expert'=4,'dp'=4] {'dp'}, dimensions={0} | all-to-all | bytes 262144 | tf_op jit(solution)/shard_map/all_to_all | solution.py:54
  458.4 3.5 all-to-all-start.19
  467.4 7.2 %all-to-all-done.19.blocks_ref = bf16[4,64,1024]{2,1,0:T(8,128)(2,1)S(1)} async-done(((bf16[4,64,1024]{2,1,0:T(8,128)(2,1)}), bf16[4,64,1024]{2,1,0:T(8,128)(2,1)S(1)}, u32[]{:S(2)}, u32[]{:S(2)}) %all-to-all-start.19) | async-done | bytes 524320 | tf_op jit(solution)/shard_map/all_to_all | solution.py:54
  481.2 3.7 all-to-all-start.20
  485.0 7.9 %owner_grads.3 = f32[2,1024,1024]{2,1,0:T(8,128)} custom-call(s32[1]{0:T(128)} %bitcast.29.place, bf16[320,1024]{1,0:T(8,128)(2,1)} %bitcast.191, bf16[320,1024]{1,0:T(8,128)(2,1)S(1)} %collective-permute-done.38.refs_1_, bf16[320,1024]{1,0:T(8,128)(2,1)} %bitcast.194, bf16[320,1024]{1,0:T(8,128)(2,1)} %collective-permute-done.39.refs_3_, ...), custom_call_target="tpu_custom_call" | custom-call | tf_op jit(solution)/shard_map/owner_grads/pallas_call | solution.py:529
  492.9 3.0 all-to-all-done.20
  497.8 3.4 all-to-all-start.21
  502.3 7.1 %all-to-all-done.21.refs_0_ = bf16[4,64,512]{2,1,0:T(8,128)(2,1)S(1)} async-done(((bf16[4,64,512]{2,1,0:T(8,128)(2,1)}), bf16[4,64,512]{2,1,0:T(8,128)(2,1)S(1)}, u32[]{:S(2)}, u32[]{:S(2)}) %all-to-all-start.21) | async-done | bytes 262176 | tf_op jit(solution)/shard_map/all_to_all | solution.py:54
  509.8 4.6 all-to-all-start.22
  523.9 3.7 all-to-all-done.22.refs_4_
  530.5 3.0 finish_weights.1
  (474 shorter events, 152.6 us)
Async XLA Ops:
  7.2 70.3 %all-gather.9.cloned.1.call-start = ((), (), s32[]{:S(2)}) async-start(), calls=%async_computation.35 | async-start | bytes 4718592 | tf_op jit(solution)/shard_map/all_gather | solution.py:820
  10.2 12.2 %collective-permute-start = (bf16[64,1024]{1,0:T(8,128)(2,1)}, bf16[64,1024]{1,0:T(8,128)(2,1)S(1)}, u32[]{:S(2)}, u32[]{:S(2)}) collective-permute-start(bf16[64,1024]{1,0:T(8,128)(2,1)} %bitcast.203), channel_id=1, source_target_pairs={{3,0},{0,1},{1,2},{2,3},{7,4},{4,5},{5,6},{6,7},{11,8},{8,9},{9,10... | collective-permute-start | bytes 393224 | tf_op jit(solution)/shard_map/ppermute | solution.py:101
  13.2 11.4 %collective-permute-start.1 = (bf16[64,1024]{1,0:T(8,128)(2,1)}, bf16[64,1024]{1,0:T(8,128)(2,1)S(1)}, u32[]{:S(2)}, u32[]{:S(2)}) collective-permute-start(bf16[64,1024]{1,0:T(8,128)(2,1)} %bitcast.204), channel_id=1, source_target_pairs={{2,0},{3,1},{0,2},{1,3},{6,4},{7,5},{4,6},{5,7},{10,8},{11,9},{8,1... | collective-permute-start | bytes 393224 | tf_op jit(solution)/shard_map/ppermute | solution.py:101
  15.8 8.9 %collective-permute-start.2 = (bf16[64,1024]{1,0:T(8,128)(2,1)}, bf16[64,1024]{1,0:T(8,128)(2,1)S(1)}, u32[]{:S(2)}, u32[]{:S(2)}) collective-permute-start(bf16[64,1024]{1,0:T(8,128)(2,1)} %bitcast.205), channel_id=1, source_target_pairs={{1,0},{2,1},{3,2},{0,3},{5,4},{6,5},{7,6},{4,7},{9,8},{10,9},{11,1... | collective-permute-start | bytes 393224 | tf_op jit(solution)/shard_map/ppermute | solution.py:101
  17.1 13.4 %all-to-all-start = ((bf16[32,8,128]{2,1,0:T(8,128)(2,1)}), bf16[32,8,128]{2,1,0:T(8,128)(2,1)S(1)}, u32[]{:S(2)}, u32[]{:S(2)}) async-start(bf16[32,8,128]{2,1,0:T(8,128)(2,1)} %broadcast_in_dim.50), calls=%async_computation | async-start | bytes 131072 | tf_op jit(solution)/shard_map/all_to_all | solution.py:54
  20.1 75.8 %all-gather.5.cloned.1.call-start = ((), (), s32[]{:S(2)}) async-start(), calls=%async_computation.28 | async-start | bytes 4718592 | tf_op jit(solution)/shard_map/all_gather | solution.py:804
  32.9 15.4 %all-to-all-start.1 = ((bf16[4,64,768]{2,1,0:T(8,128)(2,1)}), bf16[4,64,768]{2,1,0:T(8,128)(2,1)S(1)}, u32[]{:S(2)}, u32[]{:S(2)}) async-start(bf16[4,64,768]{2,1,0:T(8,128)(2,1)} %reshape.439), calls=%async_computation.1 | async-start | bytes 786432 | tf_op jit(solution)/shard_map/all_to_all | solution.py:54
  49.6 27.9 %all-to-all-start.2 = ((bf16[4,4,64,768]{3,2,1,0:T(8,128)(2,1)}), bf16[4,4,64,768]{3,2,1,0:T(8,128)(2,1)S(1)}, u32[]{:S(2)}, u32[]{:S(2)}) async-start(bf16[4,4,64,768]{3,2,1,0:T(8,128)(2,1)} %broadcast_in_dim.51), calls=%async_computation.2 | async-start | bytes 3145728 | tf_op jit(solution)/shard_map/all_to_all | solution.py:54
  53.1 97.2 %all-gather.7.cloned.1.call-start = ((), (), s32[]{:S(2)}) async-start(), calls=%async_computation.29 | async-start | bytes 4718592 | tf_op jit(solution)/shard_map/all_gather | solution.py:837
  53.2 8.3 %collective-permute-start.3 = (bf16[64,1024]{1,0:T(8,128)(2,1)S(1)}, bf16[64,1024]{1,0:T(8,128)(2,1)S(1)}, u32[]{:S(2)}, u32[]{:S(2)}) collective-permute-start(bf16[64,1024]{1,0:T(8,128)(2,1)S(1)} %fusion.55.refs_0_), channel_id=1, source_target_pairs={{3,0},{0,1},{1,2},{2,3},{7,4},{4,5},{5,6},{6,7},{11,8},{8,9},{9,10... | collective-permute-start | bytes 393224 | tf_op jit(solution)/shard_map/ppermute | solution.py:101
  53.2 15.9 %collective-permute-start.4 = (bf16[64,1024]{1,0:T(8,128)(2,1)S(1)}, bf16[64,1024]{1,0:T(8,128)(2,1)S(1)}, u32[]{:S(2)}, u32[]{:S(2)}) collective-permute-start(bf16[64,1024]{1,0:T(8,128)(2,1)S(1)} %fusion.55.refs_0_), channel_id=1, source_target_pairs={{2,0},{3,1},{0,2},{1,3},{6,4},{7,5},{4,6},{5,7},{10,8},{11,9},{8,1... | collective-permute-start | bytes 393224 | tf_op jit(solution)/shard_map/ppermute | solution.py:101
  55.3 13.9 %collective-permute-start.5 = (bf16[64,1024]{1,0:T(8,128)(2,1)S(1)}, bf16[64,1024]{1,0:T(8,128)(2,1)S(1)}, u32[]{:S(2)}, u32[]{:S(2)}) collective-permute-start(bf16[64,1024]{1,0:T(8,128)(2,1)S(1)} %fusion.55.refs_0_), channel_id=1, source_target_pairs={{1,0},{2,1},{3,2},{0,3},{5,4},{6,5},{7,6},{4,7},{9,8},{10,9},{11,1... | collective-permute-start | bytes 393224 | tf_op jit(solution)/shard_map/ppermute | solution.py:101
  57.1 12.8 %collective-permute-start.6 = (bf16[64,1024]{1,0:T(8,128)(2,1)S(1)}, bf16[64,1024]{1,0:T(8,128)(2,1)S(1)}, u32[]{:S(2)}, u32[]{:S(2)}) collective-permute-start(bf16[64,1024]{1,0:T(8,128)(2,1)S(1)} %get-tuple-element.253), channel_id=1, source_target_pairs={{3,0},{0,1},{1,2},{2,3},{7,4},{4,5},{5,6},{6,7},{11,8},{8,9},{9,10... | collective-permute-start | bytes 393224 | tf_op jit(solution)/shard_map/ppermute | solution.py:117
  57.6 18.9 %collective-permute-start.7 = (bf16[64,1024]{1,0:T(8,128)(2,1)S(1)}, bf16[64,1024]{1,0:T(8,128)(2,1)S(1)}, u32[]{:S(2)}, u32[]{:S(2)}) collective-permute-start(bf16[64,1024]{1,0:T(8,128)(2,1)S(1)} %get-tuple-element.254), channel_id=1, source_target_pairs={{2,0},{3,1},{0,2},{1,3},{6,4},{7,5},{4,6},{5,7},{10,8},{11,9},{8,1... | collective-permute-start | bytes 393224 | tf_op jit(solution)/shard_map/ppermute | solution.py:117
  61.5 15.0 %collective-permute-start.8 = (bf16[64,1024]{1,0:T(8,128)(2,1)S(1)}, bf16[64,1024]{1,0:T(8,128)(2,1)S(1)}, u32[]{:S(2)}, u32[]{:S(2)}) collective-permute-start(bf16[64,1024]{1,0:T(8,128)(2,1)S(1)} %get-tuple-element.255), channel_id=1, source_target_pairs={{1,0},{2,1},{3,2},{0,3},{5,4},{6,5},{7,6},{4,7},{9,8},{10,9},{11,1... | collective-permute-start | bytes 393224 | tf_op jit(solution)/shard_map/ppermute | solution.py:117
  77.5 3.6 collective-permute-start.9
  79.1 62.0 %collective-permute-start.13 = (bf16[1024,1024]{1,0:T(8,128)(2,1)}, bf16[1024,1024]{1,0:T(8,128)(2,1)}, u32[]{:S(2)}, u32[]{:S(2)}) collective-permute-start(bf16[1024,1024]{1,0:T(8,128)(2,1)} %get-tuple-element.267), channel_id=1, source_target_pairs={{0,16},{16,0},{1,17},{17,1},{2,18},{18,2},{3,19},{19,3},{4,20},{20... | collective-permute-start | bytes 6291464 | tf_op jit(solution)/shard_map/ppermute | solution.py:711
  79.7 61.5 %collective-permute-start.14 = (bf16[1024,1024]{1,0:T(8,128)(2,1)}, bf16[1024,1024]{1,0:T(8,128)(2,1)}, u32[]{:S(2)}, u32[]{:S(2)}) collective-permute-start(bf16[1024,1024]{1,0:T(8,128)(2,1)} %get-tuple-element.269), channel_id=1, source_target_pairs={{0,16},{16,0},{1,17},{17,1},{2,18},{18,2},{3,19},{19,3},{4,20},{20... | collective-permute-start | bytes 6291464 | tf_op jit(solution)/shard_map/ppermute | solution.py:711
  84.8 11.1 %all-to-all-start.3 = ((bf16[4,64,256]{2,1,0:T(8,128)(2,1)}), bf16[4,64,256]{2,1,0:T(8,128)(2,1)S(1)}, u32[]{:S(2)}, u32[]{:S(2)}) async-start(bf16[4,64,256]{2,1,0:T(8,128)(2,1)} %bitcast.30), calls=%async_computation.3 | async-start | bytes 262144 | tf_op jit(solution)/shard_map/all_to_all | solution.py:54
  116.1 9.3 %collective-permute-start.10 = (bf16[64,1024]{1,0:T(8,128)(2,1)S(1)}, bf16[64,1024]{1,0:T(8,128)(2,1)S(1)}, u32[]{:S(2)}, u32[]{:S(2)}) collective-permute-start(bf16[64,1024]{1,0:T(8,128)(2,1)S(1)} %dynamic-slice_bitcast_fusion.4.refs_0_.grad_ref), channel_id=1, source_target_pairs={{3,0},{0,1},{1,2},{2,3},{7,4},{4,5},{5,6},{6,7},{11,8},{8,9},{9,10... | collective-permute-start | bytes 393224 | tf_op jit(solution)/shard_map/ppermute | solution.py:101
  117.8 10.0 %collective-permute-start.11 = (bf16[64,1024]{1,0:T(8,128)(2,1)S(1)}, bf16[64,1024]{1,0:T(8,128)(2,1)S(1)}, u32[]{:S(2)}, u32[]{:S(2)}) collective-permute-start(bf16[64,1024]{1,0:T(8,128)(2,1)S(1)} %dynamic-slice_bitcast_fusion.4.refs_0_.grad_ref), channel_id=1, source_target_pairs={{2,0},{3,1},{0,2},{1,3},{6,4},{7,5},{4,6},{5,7},{10,8},{11,9},{8,1... | collective-permute-start | bytes 393224 | tf_op jit(solution)/shard_map/ppermute | solution.py:101
  120.4 7.5 %collective-permute-start.12 = (bf16[64,1024]{1,0:T(8,128)(2,1)S(1)}, bf16[64,1024]{1,0:T(8,128)(2,1)S(1)}, u32[]{:S(2)}, u32[]{:S(2)}) collective-permute-start(bf16[64,1024]{1,0:T(8,128)(2,1)S(1)} %dynamic-slice_bitcast_fusion.4.refs_0_.grad_ref), channel_id=1, source_target_pairs={{1,0},{2,1},{3,2},{0,3},{5,4},{6,5},{7,6},{4,7},{9,8},{10,9},{11,1... | collective-permute-start | bytes 393224 | tf_op jit(solution)/shard_map/ppermute | solution.py:101
  120.4 20.8 %all-to-all-start.4 = ((bf16[8,40,1024]{2,1,0:T(8,128)(2,1)}), bf16[8,40,1024]{2,1,0:T(8,128)(2,1)S(1)}, u32[]{:S(2)}, u32[]{:S(2)}) async-start(bf16[8,40,1024]{2,1,0:T(8,128)(2,1)} %bitcast.223), calls=%async_computation.4 | async-start | bytes 1310720 | tf_op jit(solution)/shard_map/all_to_all | solution.py:54
  146.1 14.9 %all-to-all-start.5 = ((bf16[8,40,1024]{2,1,0:T(8,128)(2,1)}), bf16[8,40,1024]{2,1,0:T(8,128)(2,1)}, u32[]{:S(2)}, u32[]{:S(2)}) async-start(bf16[8,40,1024]{2,1,0:T(8,128)(2,1)} %bitcast.235), calls=%async_computation.5 | async-start | bytes 1310720 | tf_op jit(solution)/shard_map/all_to_all | solution.py:54
  164.1 19.2 %all-to-all-start.6 = ((bf16[4,64,1024]{2,1,0:T(8,128)(2,1)}), bf16[4,64,1024]{2,1,0:T(8,128)(2,1)S(1)}, u32[]{:S(2)}, u32[]{:S(2)}) async-start(bf16[4,64,1024]{2,1,0:T(8,128)(2,1)} %bitcast.45), calls=%async_computation.6 | async-start | bytes 1048576 | tf_op jit(solution)/shard_map/all_to_all | solution.py:54
  204.8 9.2 %all-to-all-start.7 = ((bf16[4,64,256]{2,1,0:T(8,128)(2,1)}), bf16[4,64,256]{2,1,0:T(8,128)(2,1)S(1)}, u32[]{:S(2)}, u32[]{:S(2)}) async-start(bf16[4,64,256]{2,1,0:T(8,128)(2,1)} %bitcast.50), calls=%async_computation.7 | async-start | bytes 262144 | tf_op jit(solution)/shard_map/all_to_all | solution.py:54
  217.7 19.1 %all-to-all-start.8 = ((bf16[8,40,1024]{2,1,0:T(8,128)(2,1)}), bf16[8,40,1024]{2,1,0:T(8,128)(2,1)S(1)}, u32[]{:S(2)}, u32[]{:S(2)}) async-start(bf16[8,40,1024]{2,1,0:T(8,128)(2,1)} %bitcast.222), calls=%async_computation.8 | async-start | bytes 1310720 | tf_op jit(solution)/shard_map/all_to_all | solution.py:54
  238.4 14.7 %all-to-all-start.9 = ((bf16[8,40,1024]{2,1,0:T(8,128)(2,1)}), bf16[8,40,1024]{2,1,0:T(8,128)(2,1)S(1)}, u32[]{:S(2)}, u32[]{:S(2)}) async-start(bf16[8,40,1024]{2,1,0:T(8,128)(2,1)} %bitcast.224), calls=%async_computation.9 | async-start | bytes 1310720 | tf_op jit(solution)/shard_map/all_to_all | solution.py:54
  258.0 14.9 %all-to-all-start.11 = ((bf16[8,40,1024]{2,1,0:T(8,128)(2,1)}), bf16[8,40,1024]{2,1,0:T(8,128)(2,1)}, u32[]{:S(2)}, u32[]{:S(2)}) async-start(bf16[8,40,1024]{2,1,0:T(8,128)(2,1)} %bitcast.236), calls=%async_computation.11 | async-start | bytes 1310720 | tf_op jit(solution)/shard_map/all_to_all | solution.py:54
  272.9 14.9 %all-to-all-start.10 = ((bf16[8,40,1024]{2,1,0:T(8,128)(2,1)}), bf16[8,40,1024]{2,1,0:T(8,128)(2,1)}, u32[]{:S(2)}, u32[]{:S(2)}) async-start(bf16[8,40,1024]{2,1,0:T(8,128)(2,1)} %bitcast.234), calls=%async_computation.10 | async-start | bytes 1310720 | tf_op jit(solution)/shard_map/all_to_all | solution.py:54
  290.6 20.0 %all-to-all-start.12 = ((bf16[4,64,1024]{2,1,0:T(8,128)(2,1)}), bf16[4,64,1024]{2,1,0:T(8,128)(2,1)}, u32[]{:S(2)}, u32[]{:S(2)}) async-start(bf16[4,64,1024]{2,1,0:T(8,128)(2,1)} %bitcast.229), calls=%async_computation.12 | async-start | bytes 1048576 | tf_op jit(solution)/shard_map/all_to_all | solution.py:54
  295.6 88.1 %reduce-scatter.6.cloned.1.call-start = ((), (), s32[]{:S(2)}) async-start(), calls=%async_computation.30 | async-start | bytes 2621440 | tf_op jit(solution)/shard_map/reduce_scatter | solution.py:1011
  296.1 3.6 collective-permute-start.17
  296.2 3.6 collective-permute-start.18
  310.7 74.9 %reduce-scatter.8.cloned.1.call-start = ((), (), s32[]{:S(2)}) async-start(), calls=%async_computation.31 | async-start | bytes 2293760 | tf_op jit(solution)/shard_map/reduce_scatter | solution.py:1011
  369.9 17.8 %all-to-all-start.15 = ((bf16[8,40,1024]{2,1,0:T(8,128)(2,1)}), bf16[8,40,1024]{2,1,0:T(8,128)(2,1)}, u32[]{:S(2)}, u32[]{:S(2)}) async-start(bf16[8,40,1024]{2,1,0:T(8,128)(2,1)} %bitcast.221), calls=%async_computation.15 | async-start | bytes 1310720 | tf_op jit(solution)/shard_map/all_to_all | solution.py:54
  374.2 65.9 %reduce-scatter.10.cloned.1.call-start = ((), (), s32[]{:S(2)}) async-start(), calls=%async_computation.32 | async-start | bytes 655360 | tf_op jit(solution)/shard_map/reduce_scatter | solution.py:1151
  395.3 6.6 %collective-permute-start.26 = (bf16[256,1024]{1,0:T(8,128)(2,1)S(1)}, bf16[256,1024]{1,0:T(8,128)(2,1)}, u32[]{:S(2)}, u32[]{:S(2)}) collective-permute-start(bf16[256,1024]{1,0:T(8,128)(2,1)S(1)} %all_gather.23.refs_0_), channel_id=1, source_target_pairs={{0,16},{16,0},{1,17},{17,1},{2,18},{18,2},{3,19},{19,3},{4,20},{20... | collective-permute-start | bytes 1572872 | tf_op jit(solution)/shard_map/ppermute | solution.py:711
  395.5 8.7 %collective-permute-start.27 = (bf16[256,1024]{1,0:T(8,128)(2,1)}, bf16[256,1024]{1,0:T(8,128)(2,1)}, u32[]{:S(2)}, u32[]{:S(2)}) collective-permute-start(bf16[256,1024]{1,0:T(8,128)(2,1)} %fusion.24.refs_2_), channel_id=1, source_target_pairs={{0,16},{16,0},{1,17},{17,1},{2,18},{18,2},{3,19},{19,3},{4,20},{20... | collective-permute-start | bytes 1572872 | tf_op jit(solution)/shard_map/ppermute | solution.py:711
  395.9 23.2 %all-to-all-start.16 = ((bf16[8,40,1024]{2,1,0:T(8,128)(2,1)}), bf16[8,40,1024]{2,1,0:T(8,128)(2,1)}, u32[]{:S(2)}, u32[]{:S(2)}) async-start(bf16[8,40,1024]{2,1,0:T(8,128)(2,1)} %bitcast.233), calls=%async_computation.18 | async-start | bytes 1310720 | tf_op jit(solution)/shard_map/all_to_all | solution.py:54
  400.1 95.8 %reduce-scatter.14.cloned.1.call-start = ((), (), s32[]{:S(2)}) async-start(), calls=%async_computation.34 | async-start | bytes 2621440 | tf_op jit(solution)/shard_map/reduce_scatter | solution.py:1011
  400.1 6.9 %collective-permute-start.28 = (bf16[256,1024]{1,0:T(8,128)(2,1)}, bf16[256,1024]{1,0:T(8,128)(2,1)S(1)}, u32[]{:S(2)}, u32[]{:S(2)}) collective-permute-start(bf16[256,1024]{1,0:T(8,128)(2,1)} %copy-done.30), channel_id=1, source_target_pairs={{0,16},{16,0},{1,17},{17,1},{2,18},{18,2},{3,19},{19,3},{4,20},{20... | collective-permute-start | bytes 1572872 | tf_op jit(solution)/shard_map/ppermute | solution.py:711
  400.5 6.6 %collective-permute-start.29 = (bf16[256,1024]{1,0:T(8,128)(2,1)S(1)}, bf16[256,1024]{1,0:T(8,128)(2,1)S(1)}, u32[]{:S(2)}, u32[]{:S(2)}) collective-permute-start(bf16[256,1024]{1,0:T(8,128)(2,1)S(1)} %get-tuple-element.378.refs_6_), channel_id=1, source_target_pairs={{0,16},{16,0},{1,17},{17,1},{2,18},{18,2},{3,19},{19,3},{4,20},{20... | collective-permute-start | bytes 1572872 | tf_op jit(solution)/shard_map/ppermute | solution.py:711
  400.7 11.6 %collective-permute-start.23 = (bf16[64,1408]{1,0:T(8,128)(2,1)}, bf16[64,1408]{1,0:T(8,128)(2,1)}, u32[]{:S(2)}, u32[]{:S(2)}) collective-permute-start(bf16[64,1408]{1,0:T(8,128)(2,1)} %get-tuple-element.372), channel_id=1, source_target_pairs={{3,0},{0,1},{1,2},{2,3},{7,4},{4,5},{5,6},{6,7},{11,8},{8,9},{9,10... | collective-permute-start | bytes 540680 | tf_op jit(solution)/shard_map/ppermute | solution.py:117
  401.9 17.2 %collective-permute-start.24 = (bf16[64,1408]{1,0:T(8,128)(2,1)}, bf16[64,1408]{1,0:T(8,128)(2,1)}, u32[]{:S(2)}, u32[]{:S(2)}) collective-permute-start(bf16[64,1408]{1,0:T(8,128)(2,1)} %get-tuple-element.373), channel_id=1, source_target_pairs={{2,0},{3,1},{0,2},{1,3},{6,4},{7,5},{4,6},{5,7},{10,8},{11,9},{8,1... | collective-permute-start | bytes 540680 | tf_op jit(solution)/shard_map/ppermute | solution.py:117
  404.2 14.9 %collective-permute-start.25 = (bf16[64,1408]{1,0:T(8,128)(2,1)}, bf16[64,1408]{1,0:T(8,128)(2,1)}, u32[]{:S(2)}, u32[]{:S(2)}) collective-permute-start(bf16[64,1408]{1,0:T(8,128)(2,1)} %get-tuple-element.374), channel_id=1, source_target_pairs={{1,0},{2,1},{3,2},{0,3},{5,4},{6,5},{7,6},{4,7},{9,8},{10,9},{11,1... | collective-permute-start | bytes 540680 | tf_op jit(solution)/shard_map/ppermute | solution.py:117
  421.5 21.7 %all-to-all-start.17 = ((bf16[4,64,1024]{2,1,0:T(8,128)(2,1)}), bf16[4,64,1024]{2,1,0:T(8,128)(2,1)S(1)}, u32[]{:S(2)}, u32[]{:S(2)}) async-start(bf16[4,64,1024]{2,1,0:T(8,128)(2,1)} %bitcast.86), calls=%async_computation.19 | async-start | bytes 1048576 | tf_op jit(solution)/shard_map/all_to_all | solution.py:54
  429.1 3.7 collective-permute-start.31
  429.1 4.6 collective-permute-start.32
  458.4 16.2 %all-to-all-start.19 = ((bf16[4,64,1024]{2,1,0:T(8,128)(2,1)}), bf16[4,64,1024]{2,1,0:T(8,128)(2,1)S(1)}, u32[]{:S(2)}, u32[]{:S(2)}) async-start(bf16[4,64,1024]{2,1,0:T(8,128)(2,1)} %bitcast.226), calls=%async_computation.22 | async-start | bytes 1048576 | tf_op jit(solution)/shard_map/all_to_all | solution.py:54
  461.9 47.8 %reduce-scatter.12.cloned.1.call-start = ((), (), s32[]{:S(2)}) async-start(), calls=%async_computation.33 | async-start | bytes 2293760 | tf_op jit(solution)/shard_map/reduce_scatter | solution.py:1011
  474.6 6.6 %collective-permute-start.38 = (bf16[320,1024]{1,0:T(8,128)(2,1)S(1)}, bf16[320,1024]{1,0:T(8,128)(2,1)S(1)}, u32[]{:S(2)}, u32[]{:S(2)}) collective-permute-start(bf16[320,1024]{1,0:T(8,128)(2,1)S(1)} %bitcast.190), channel_id=1, source_target_pairs={{0,16},{16,0},{1,17},{17,1},{2,18},{18,2},{3,19},{19,3},{4,20},{20... | collective-permute-start | bytes 1966088 | tf_op jit(solution)/shard_map/ppermute | solution.py:711
  474.7 6.5 %collective-permute-start.39 = (bf16[320,1024]{1,0:T(8,128)(2,1)S(1)}, bf16[320,1024]{1,0:T(8,128)(2,1)}, u32[]{:S(2)}, u32[]{:S(2)}) collective-permute-start(bf16[320,1024]{1,0:T(8,128)(2,1)S(1)} %bitcast.193), channel_id=1, source_target_pairs={{0,16},{16,0},{1,17},{17,1},{2,18},{18,2},{3,19},{19,3},{4,20},{20... | collective-permute-start | bytes 1966088 | tf_op jit(solution)/shard_map/ppermute | solution.py:711
  475.2 6.0 %collective-permute-start.41 = (bf16[320,1024]{1,0:T(8,128)(2,1)}, bf16[320,1024]{1,0:T(8,128)(2,1)}, u32[]{:S(2)}, u32[]{:S(2)}) collective-permute-start(bf16[320,1024]{1,0:T(8,128)(2,1)} %get-tuple-element.422.refs_6_), channel_id=1, source_target_pairs={{0,16},{16,0},{1,17},{17,1},{2,18},{18,2},{3,19},{19,3},{4,20},{20... | collective-permute-start | bytes 1966088 | tf_op jit(solution)/shard_map/ppermute | solution.py:711
  475.3 5.9 %collective-permute-start.40 = (bf16[320,1024]{1,0:T(8,128)(2,1)}, bf16[320,1024]{1,0:T(8,128)(2,1)}, u32[]{:S(2)}, u32[]{:S(2)}) collective-permute-start(bf16[320,1024]{1,0:T(8,128)(2,1)} %get-tuple-element.420.refs_4_), channel_id=1, source_target_pairs={{0,16},{16,0},{1,17},{17,1},{2,18},{18,2},{3,19},{19,3},{4,20},{20... | collective-permute-start | bytes 1966088 | tf_op jit(solution)/shard_map/ppermute | solution.py:711
  481.2 14.7 %all-to-all-start.20 = ((f32[32,16,128]{2,1,0:T(8,128)}), f32[32,16,128]{2,1,0:T(8,128)S(1)}, u32[]{:S(2)}, u32[]{:S(2)}) async-start(f32[32,16,128]{2,1,0:T(8,128)} %pack_small.1), calls=%async_computation.25 | async-start | bytes 524288 | tf_op jit(solution)/shard_map/all_to_all | solution.py:54
  497.8 11.6 %all-to-all-start.21 = ((bf16[4,64,512]{2,1,0:T(8,128)(2,1)}), bf16[4,64,512]{2,1,0:T(8,128)(2,1)S(1)}, u32[]{:S(2)}, u32[]{:S(2)}) async-start(bf16[4,64,512]{2,1,0:T(8,128)(2,1)} %bitcast.93), calls=%async_computation.26 | async-start | bytes 524288 | tf_op jit(solution)/shard_map/all_to_all | solution.py:54
  501.2 8.5 %collective-permute-start.45 = (f32[64,1024]{1,0:T(8,128)S(1)}, f32[64,1024]{1,0:T(8,128)S(1)}, u32[]{:S(2)}, u32[]{:S(2)}) collective-permute-start(f32[64,1024]{1,0:T(8,128)S(1)} %copy-done.41), channel_id=1, source_target_pairs={{0,16},{16,0},{1,17},{17,1},{2,18},{18,2},{3,19},{19,3},{4,20},{20... | collective-permute-start | bytes 786440 | tf_op jit(solution)/shard_map/ppermute | solution.py:711
  501.3 8.5 %collective-permute-start.44 = (f32[64,1024]{1,0:T(8,128)S(1)}, f32[64,1024]{1,0:T(8,128)S(1)}, u32[]{:S(2)}, u32[]{:S(2)}) collective-permute-start(f32[64,1024]{1,0:T(8,128)S(1)} %get-tuple-element.435.refs_4_), channel_id=1, source_target_pairs={{0,16},{16,0},{1,17},{17,1},{2,18},{18,2},{3,19},{19,3},{4,20},{20... | collective-permute-start | bytes 786440 | tf_op jit(solution)/shard_map/ppermute | solution.py:711
  501.8 8.0 %collective-permute-start.42 = (bf16[64,1024]{1,0:T(8,128)(2,1)S(1)}, bf16[64,1024]{1,0:T(8,128)(2,1)S(1)}, u32[]{:S(2)}, u32[]{:S(2)}) collective-permute-start(bf16[64,1024]{1,0:T(8,128)(2,1)S(1)} %copy-done.20), channel_id=1, source_target_pairs={{0,16},{16,0},{1,17},{17,1},{2,18},{18,2},{3,19},{19,3},{4,20},{20... | collective-permute-start | bytes 393224 | tf_op jit(solution)/shard_map/ppermute | solution.py:711
  501.9 7.9 %collective-permute-start.43 = (bf16[64,1024]{1,0:T(8,128)(2,1)S(1)}, bf16[64,1024]{1,0:T(8,128)(2,1)S(1)}, u32[]{:S(2)}, u32[]{:S(2)}) collective-permute-start(bf16[64,1024]{1,0:T(8,128)(2,1)S(1)} %get-tuple-element.433.refs_2_), channel_id=1, source_target_pairs={{0,16},{16,0},{1,17},{17,1},{2,18},{18,2},{3,19},{19,3},{4,20},{20... | collective-permute-start | bytes 393224 | tf_op jit(solution)/shard_map/ppermute | solution.py:711
  509.8 17.7 %all-to-all-start.22 = ((bf16[4,64,896]{2,1,0:T(8,128)(2,1)}), bf16[4,64,896]{2,1,0:T(8,128)(2,1)S(1)}, u32[]{:S(2)}, u32[]{:S(2)}) async-start(bf16[4,64,896]{2,1,0:T(8,128)(2,1)} %bitcast.238), calls=%async_computation.27 | async-start | bytes 917504 | tf_op jit(solution)/shard_map/all_to_all | solution.py:54
  514.5 14.4 %collective-permute-start.51 = (bf16[256,512]{1,0:T(8,128)(2,1)S(1)}, bf16[256,512]{1,0:T(8,128)(2,1)S(1)}, u32[]{:S(2)}, u32[]{:S(2)}) collective-permute-start(bf16[256,512]{1,0:T(8,128)(2,1)S(1)} %copy-done.28), channel_id=1, source_target_pairs={{0,16},{16,0},{1,17},{17,1},{2,18},{18,2},{3,19},{19,3},{4,20},{20... | collective-permute-start | bytes 786440 | tf_op jit(solution)/shard_map/ppermute | solution.py:711
  515.8 14.7 %collective-permute-start.49 = (bf16[4,64,896]{2,1,0:T(8,128)(2,1)S(1)}, bf16[4,64,896]{2,1,0:T(8,128)(2,1)S(1)}, u32[]{:S(2)}, u32[]{:S(2)}) collective-permute-start(bf16[4,64,896]{2,1,0:T(8,128)(2,1)S(1)} %slice.248.refs_6_), channel_id=1, source_target_pairs={{0,16},{16,0},{1,17},{17,1},{2,18},{18,2},{3,19},{19,3},{4,20},{20... | collective-permute-start | bytes 1376264 | tf_op jit(solution)/shard_map/ppermute | solution.py:711
  (124 other events, 2138.2 us)
Sparse Core Ops, SparseCore 0:
  9.9 39.9 all-gather.8
  52.4 43.4 all-gather.4
  98.3 42.4 all-gather.6
  310.8 32.6 reduce-scatter.5
  346.7 34.3 reduce-scatter.7
  383.3 30.2 reduce-scatter.9
  419.2 38.7 reduce-scatter.13
  474.7 34.9 reduce-scatter.11

commit v7 on v6

--- a/solution.py
+++ b/solution.py
@@ -74,11 +74,6 @@
 def beside(move, blocks, work, operands, late=()):
     blocks, operands = lax.optimization_barrier((blocks, operands))
     return lax.optimization_barrier((move(blocks), work(*operands, *late)))
-
-
-def started(operands, blocks):
-    tile = blocks[0, :16, :128]
-    return after(operands, other_core(tile))
 
 
 def over_dp(blocks):
@@ -887,11 +882,11 @@
         expert_rows, ((gate_probs, gate, coef), own_grad_seq) = beside(
             over_homes,
             expert_blocks,
-            lambda blocks, mid_seq, small_weights, grad: (
+            lambda mid_seq, small_weights, grad: (
                 coefficients(mid_seq, small_weights, hot),
-                in_order(permute_copies(started(grad, blocks), DP), DP).reshape(full_len, width),
+                in_order(permute_copies(grad, DP), DP).reshape(full_len, width),
             ),
-            (expert_blocks, mid_seq, small_weights, own_grad),
+            (mid_seq, small_weights, own_grad),
         )
         expert_rows = expert_rows.reshape(-1, width)
         scale, exp_hidden, exp_hidden_low, exp_out = expert_forward(
@@ -1097,8 +1092,8 @@
             returned, dense_grad = beside(
                 over_homes,
                 expert_back,
-                lambda blocks, *operands: dense_back(*started(operands, blocks)),
-                (expert_back, *dense_operands),
+                dense_back,
+                dense_operands,
             )
             d_dense, d_small, d_up, d_mid_part, _ = dense_grad
             d_mid_part = d_mid_part + product_tn(table, returned.reshape(-1, width))

time: 550 us -> 550 us (level)
    unnamed x212 -> x214, local copies, waits for them, and re-layouts: 17.4 us -> 16.7 us
  transfers between devices with their start and end apart: 80 -> 80, of which waited for: 37 -> 37; matrix products, arithmetic and copies ran while one was open for 14% -> 15% of each run, Pallas kernels for 13% -> 13%
where the time goes in v7:
time: 550 us; the launch traced here: 540 us
  waiting for transfers between devices  126 us (23%)
  starting transfers between devices  114 us (21%)
  blocking collectives  98.1 us (18%)
  Pallas kernels  81.4 us (15%)
  local copies, waits for them, and re-layouts  46.4 us (8%)
  matrix products  43.4 us (8%)
  between operations  16.2 us (3%)
  other arithmetic  15.4 us (3%)
    all_to_all x20, starting transfers between devices, exchange(): return lax.all_to_all(blocks, axes, split_axis=0, concat_axis=0, tiled=True)  80.9 us
    all_to_all x20, waiting for transfers between devices, exchange(): return lax.all_to_all(blocks, axes, split_axis=0, concat_axis=0, tiled=True)  78.1 us
    all_gather x4, blocking collectives, gather_rows(): return lax.all_gather(block, DP, axis=0, tiled=True)  63.4 us
    all_to_all x3, blocking collectives, exchange(): return lax.all_to_all(blocks, axes, split_axis=0, concat_axis=0, tiled=True)  34.7 us
    pallas_call x4, Pallas kernels, expert_call(): pl.pallas_call(kernel, out_shape=[pltpu.HBM(shape, dtype) for shape, dtyp...  22.2 us
    dot_general x12, matrix products, product(): return jnp.dot(left_mat, right_mat, preferred_element_type=jnp.float32)  20.9 us
    unnamed x214, local copies, waits for them, and re-layouts  16.7 us
    ppermute x9, starting transfers between devices, permute_copies(): blocks.append(lax.ppermute(block, axis, route))  15.1 us
  transfers between devices with their start and end apart: 80, of which 37 were waited for; matrix products, arithmetic and copies ran while one was open for 15% of the time, Pallas kernels for 13%

profile of v7, /device:TPU:0, one launch (start us, length us, event | category | flops | bytes accessed | tf_op | source)
XLA Modules:
  0.0 540.4 jit_solution(17692748482598835702)
XLA Ops:
  10.2 3.0 collective-permute-start
  17.1 2.9 all-to-all-start
  25.5 5.1 all-to-all-done
  32.7 3.5 all-to-all-start.1
  37.3 7.0 %dynamic-slice_bitcast_fusion = (bf16[1024,1024]{1,0:T(8,128)(2,1)}, bf16[1024,1024]{1,0:T(8,128)(2,1)}, bf16[1024,1024]{1,0:T(8,128)(2,1)}, bf16[1024,1024]{1,0:T(8,128)(2,1)}) fusion(bf16[2,1024,1024]{2,1,0:T(8,128)(2,1)} %bitcast.219, s32[]{:T(128)S(6)} %select_n.163, s32[]{:T(128)S(6)} %select_n.154, bf16[2,1024,1024]{2,1,0:T(8,128)(2,1)} %bitcast.220), kind=kLoop, calls=%fused_computation.8 | loop fusion | bytes 16777224 | tf_op jit(solution)/shard_map/jit(dynamic_index_in_dim)/squeeze | solution.py:755
  44.3 3.7 all-to-all-done.1
  49.3 3.6 all-to-all-start.2
  61.8 7.1 %collective-permute-done.4.refs_2_ = bf16[64,1024]{1,0:T(8,128)(2,1)S(1)} collective-permute-done((bf16[64,1024]{1,0:T(8,128)(2,1)S(1)}, bf16[64,1024]{1,0:T(8,128)(2,1)S(1)}, u32[]{:S(2)}, u32[]{:S(2)}) %collective-permute-start.4) | collective-permute-done | bytes 131104 | tf_op jit(solution)/shard_map/ppermute | solution.py:96
  69.7 6.6 %collective-permute-done.7.refs_2_ = bf16[64,1024]{1,0:T(8,128)(2,1)S(1)} collective-permute-done((bf16[64,1024]{1,0:T(8,128)(2,1)S(1)}, bf16[64,1024]{1,0:T(8,128)(2,1)S(1)}, u32[]{:S(2)}, u32[]{:S(2)}) %collective-permute-start.7) | collective-permute-done | bytes 131104 | tf_op jit(solution)/shard_map/ppermute | solution.py:112
  84.5 3.5 all-to-all-start.3
  88.1 7.6 %all-gather.5.cloned.1.call-done = bf16[2048,1024]{1,0:T(8,128)(2,1)} async-done(((bf16[256,1024]{1,0:T(8,128)(2,1)}), bf16[2048,1024]{1,0:T(8,128)(2,1)}) %all-gather.5.cloned.1.call-update) | async-done | bytes 4194320 | tf_op jit(solution)/shard_map/all_gather | solution.py:799
  98.6 16.0 %all_gather.23.refs_0_ = bf16[256,1024]{1,0:T(8,128)(2,1)S(1)} all-gather(bf16[64,1024]{1,0:T(8,128)(2,1)S(1)} %get-tuple-element.255), channel_id=1, replica_groups=mesh['section'=2,'expert'=4,'dp'=4] {'dp'}, dimensions={0}, use_global_device_ids=true | all-gather | bytes 655360 | tf_op jit(solution)/shard_map/all_gather | solution.py:63
  120.1 4.0 all-to-all-start.4
  127.7 13.2 %all-to-all-done.4 = bf16[8,40,1024]{2,1,0:T(8,128)(2,1)S(1)} async-done(((bf16[8,40,1024]{2,1,0:T(8,128)(2,1)}), bf16[8,40,1024]{2,1,0:T(8,128)(2,1)S(1)}, u32[]{:S(2)}, u32[]{:S(2)}) %all-to-all-start.4) | async-done | bytes 655392 | tf_op jit(solution)/shard_map/all_to_all | solution.py:54
  140.9 4.9 expert_forward.2
  145.8 4.2 all-to-all-start.5
  150.1 3.6 fusion.32
  155.4 5.4 all-to-all-done.5
  160.7 3.1 add_convert_fusion.1
  163.8 4.2 all-to-all-start.6
  169.2 4.8 slice_bitcast_fusion.2
  174.0 3.4 broadcast_select_fusion
  177.5 5.5 %all-to-all-done.6.blocks_ref = bf16[4,64,1024]{2,1,0:T(8,128)(2,1)S(1)} async-done(((bf16[4,64,1024]{2,1,0:T(8,128)(2,1)}), bf16[4,64,1024]{2,1,0:T(8,128)(2,1)S(1)}, u32[]{:S(2)}, u32[]{:S(2)}) %all-to-all-start.6) | async-done | bytes 524320 | tf_op jit(solution)/shard_map/all_to_all | solution.py:54
  183.3 16.1 %all_gather.25.refs_4_ = bf16[256,1024]{1,0:T(8,128)(2,1)S(1)} all-gather(bf16[64,1024]{1,0:T(8,128)(2,1)S(1)} %get-tuple-element.280), channel_id=1, replica_groups=mesh['section'=2,'expert'=4,'dp'=4] {'dp'}, dimensions={0}, use_global_device_ids=true | all-gather | bytes 655360 | tf_op jit(solution)/shard_map/all_gather | solution.py:63
  204.5 3.3 all-to-all-start.7
  207.9 4.7 slice_bitcast_fusion
  217.4 3.5 all-to-all-start.8
  220.9 15.6 %all_gather.26.refs_0_ = bf16[256,1024]{1,0:T(8,128)(2,1)S(1)} all-gather(bf16[64,1024]{1,0:T(8,128)(2,1)S(1)} %get-tuple-element.289), channel_id=1, replica_groups=mesh['section'=2,'expert'=4,'dp'=4] {'dp'}, dimensions={0}, use_global_device_ids=true | all-gather | bytes 655360 | tf_op jit(solution)/shard_map/all_gather | solution.py:63
  238.0 4.1 all-to-all-start.9
  242.2 3.6 fusion.40
  245.8 6.9 %all-to-all-done.9 = bf16[8,40,1024]{2,1,0:T(8,128)(2,1)S(1)} async-done(((bf16[8,40,1024]{2,1,0:T(8,128)(2,1)}), bf16[8,40,1024]{2,1,0:T(8,128)(2,1)S(1)}, u32[]{:S(2)}, u32[]{:S(2)}) %all-to-all-start.9) | async-done | bytes 655392 | tf_op jit(solution)/shard_map/all_to_all | solution.py:54
  252.8 4.9 expert_forward.3
  257.7 4.2 all-to-all-start.11
  262.9 5.6 %expert_backward.2 = (bf16[320,1024]{1,0:T(8,128)(2,1)}, bf16[320,1024]{1,0:T(8,128)(2,1)}, bf16[320,1024]{1,0:T(8,128)(2,1)}) custom-call(s32[1]{0:T(128)} %bitcast.29.place, bf16[320,1024]{1,0:T(8,128)(2,1)S(1)} %bitcast.195, f32[320,1]{1,0:T(8,128)S(1)} %copy-done.50, bf16[1024,1024]{1,0:T(8,128)(2,1)} %get-tuple-element.262.refs_0_, ...), custom_call_target="tpu_custom_call" | custom-call | tf_op jit(solution)/shard_map/expert_backward/pallas_call | solution.py:311
  272.6 4.2 all-to-all-start.10
  276.9 3.0 fusion.43
  284.4 3.1 all-to-all-done.10
  290.3 5.0 all-to-all-start.12
  303.1 7.2 %all-to-all-done.12.blocks_ref = bf16[4,64,1024]{2,1,0:T(8,128)(2,1)} async-done(((bf16[4,64,1024]{2,1,0:T(8,128)(2,1)}), bf16[4,64,1024]{2,1,0:T(8,128)(2,1)}, u32[]{:S(2)}, u32[]{:S(2)}) %all-to-all-start.12) | async-done | bytes 524320 | tf_op jit(solution)/shard_map/all_to_all | solution.py:54
  310.6 3.8 mid_back.2
  315.6 8.6 %all_to_all.115 = bf16[4,64,256]{2,1,0:T(8,128)(2,1)S(1)} all-to-all(bf16[4,64,256]{2,1,0:T(8,128)(2,1)S(1)} %get-tuple-element.331), channel_id=1, replica_groups=mesh['section'=2,'expert'=4,'dp'=4] {'dp'}, dimensions={0} | all-to-all | bytes 262144 | tf_op jit(solution)/shard_map/all_to_all | solution.py:54
  332.9 17.6 %all_to_all.116.blocks_ref = bf16[4,64,1024]{2,1,0:T(8,128)(2,1)S(1)} all-to-all(bf16[4,64,1024]{2,1,0:T(8,128)(2,1)S(1)} %bitcast.225), channel_id=1, replica_groups=mesh['section'=2,'expert'=4,'dp'=4] {'dp'}, dimensions={0} | all-to-all | bytes 1048576 | tf_op jit(solution)/shard_map/all_to_all | solution.py:54
  350.9 15.7 %all_gather.27 = bf16[256,1024]{1,0:T(8,128)(2,1)S(1)} all-gather(bf16[64,1024]{1,0:T(8,128)(2,1)S(1)} %get-tuple-element.339.grad_ref), channel_id=1, replica_groups=mesh['section'=2,'expert'=4,'dp'=4] {'dp'}, dimensions={0}, use_global_device_ids=true | all-gather | bytes 655360 | tf_op jit(solution)/shard_map/all_gather | solution.py:63
  368.4 4.4 all-to-all-start.15
  375.5 3.4 fusion.24.refs_2_
  378.9 2.8 fusion.99
  388.8 6.8 %expert_backward.3 = (bf16[320,1024]{1,0:T(8,128)(2,1)}, bf16[320,1024]{1,0:T(8,128)(2,1)}, bf16[320,1024]{1,0:T(8,128)(2,1)}) custom-call(s32[1]{0:T(128)} %bitcast.29.place, bf16[320,1024]{1,0:T(8,128)(2,1)} %bitcast.83.rows_ref, f32[320,1]{1,0:T(8,128)S(1)} %copy-done.49, bf16[1024,1024]{1,0:T(8,128)(2,1)} %get-tuple-element.262.refs_0_, ...), custom_call_target="tpu_custom_call" | custom-call | tf_op jit(solution)/shard_map/expert_backward/pallas_call | solution.py:311
  396.1 4.2 all-to-all-start.16
  408.2 4.0 pair_grads.6
  412.4 6.6 %collective-permute-done.24.refs_2_ = bf16[64,1408]{1,0:T(8,128)(2,1)} collective-permute-done((bf16[64,1408]{1,0:T(8,128)(2,1)}, bf16[64,1408]{1,0:T(8,128)(2,1)}, u32[]{:S(2)}, u32[]{:S(2)}) %collective-permute-start.24) | collective-permute-done | bytes 180256 | tf_op jit(solution)/shard_map/ppermute | solution.py:112
  421.4 7.1 %all-to-all-start.17 = ((bf16[4,64,1024]{2,1,0:T(8,128)(2,1)}), bf16[4,64,1024]{2,1,0:T(8,128)(2,1)S(1)}, u32[]{:S(2)}, u32[]{:S(2)}) async-start(bf16[4,64,1024]{2,1,0:T(8,128)(2,1)} %bitcast.86), calls=%async_computation.19 | async-start | bytes 1048576 | tf_op jit(solution)/shard_map/all_to_all | solution.py:54
  433.6 6.3 %owner_grads.2 = f32[2,1024,1024]{2,1,0:T(8,128)} custom-call(s32[1]{0:T(128)} %bitcast.29.place, bf16[320,1024]{1,0:T(8,128)(2,1)} %get-tuple-element.374.refs_0_, bf16[320,1024]{1,0:T(8,128)(2,1)S(1)} %collective-permute-done.30.refs_1_, bf16[320,1024]{1,0:T(8,128)(2,1)} %get-tuple-element.375.refs_2_, ...), custom_call_target="tpu_custom_call" | custom-call | tf_op jit(solution)/shard_map/owner_grads/pallas_call | solution.py:524
  440.0 3.2 all-to-all-done.17.blocks_ref
  446.0 8.5 %all_to_all.117 = bf16[4,64,256]{2,1,0:T(8,128)(2,1)S(1)} all-to-all(bf16[4,64,256]{2,1,0:T(8,128)(2,1)S(1)} %get-tuple-element.380), channel_id=1, replica_groups=mesh['section'=2,'expert'=4,'dp'=4] {'dp'}, dimensions={0} | all-to-all | bytes 262144 | tf_op jit(solution)/shard_map/all_to_all | solution.py:54
  458.4 3.5 all-to-all-start.19
  467.4 7.2 %all-to-all-done.19.blocks_ref = bf16[4,64,1024]{2,1,0:T(8,128)(2,1)S(1)} async-done(((bf16[4,64,1024]{2,1,0:T(8,128)(2,1)}), bf16[4,64,1024]{2,1,0:T(8,128)(2,1)S(1)}, u32[]{:S(2)}, u32[]{:S(2)}) %all-to-all-start.19) | async-done | bytes 524320 | tf_op jit(solution)/shard_map/all_to_all | solution.py:54
  481.3 3.3 all-to-all-start.20
  484.7 7.9 %owner_grads.3 = f32[2,1024,1024]{2,1,0:T(8,128)} custom-call(s32[1]{0:T(128)} %bitcast.29.place, bf16[320,1024]{1,0:T(8,128)(2,1)} %bitcast.191, bf16[320,1024]{1,0:T(8,128)(2,1)S(1)} %collective-permute-done.38.refs_1_, bf16[320,1024]{1,0:T(8,128)(2,1)} %bitcast.194, bf16[320,1024]{1,0:T(8,128)(2,1)} %collective-permute-done.39.refs_3_, ...), custom_call_target="tpu_custom_call" | custom-call | tf_op jit(solution)/shard_map/owner_grads/pallas_call | solution.py:524
  492.5 3.0 all-to-all-done.20
  497.5 3.4 all-to-all-start.21
  502.0 7.1 %all-to-all-done.21.refs_0_ = bf16[4,64,512]{2,1,0:T(8,128)(2,1)S(1)} async-done(((bf16[4,64,512]{2,1,0:T(8,128)(2,1)}), bf16[4,64,512]{2,1,0:T(8,128)(2,1)S(1)}, u32[]{:S(2)}, u32[]{:S(2)}) %all-to-all-start.21) | async-done | bytes 262176 | tf_op jit(solution)/shard_map/all_to_all | solution.py:54
  509.5 4.6 all-to-all-start.22
  523.5 3.7 all-to-all-done.22.refs_4_
  530.2 3.0 finish_weights.1
  (476 shorter events, 153.4 us)
Async XLA Ops:
  7.2 70.1 %all-gather.9.cloned.1.call-start = ((), (), s32[]{:S(2)}) async-start(), calls=%async_computation.35 | async-start | bytes 4718592 | tf_op jit(solution)/shard_map/all_gather | solution.py:815
  10.2 12.2 %collective-permute-start = (bf16[64,1024]{1,0:T(8,128)(2,1)}, bf16[64,1024]{1,0:T(8,128)(2,1)S(1)}, u32[]{:S(2)}, u32[]{:S(2)}) collective-permute-start(bf16[64,1024]{1,0:T(8,128)(2,1)} %bitcast.203), channel_id=1, source_target_pairs={{3,0},{0,1},{1,2},{2,3},{7,4},{4,5},{5,6},{6,7},{11,8},{8,9},{9,10... | collective-permute-start | bytes 393224 | tf_op jit(solution)/shard_map/ppermute | solution.py:96
  13.2 11.4 %collective-permute-start.1 = (bf16[64,1024]{1,0:T(8,128)(2,1)}, bf16[64,1024]{1,0:T(8,128)(2,1)S(1)}, u32[]{:S(2)}, u32[]{:S(2)}) collective-permute-start(bf16[64,1024]{1,0:T(8,128)(2,1)} %bitcast.204), channel_id=1, source_target_pairs={{2,0},{3,1},{0,2},{1,3},{6,4},{7,5},{4,6},{5,7},{10,8},{11,9},{8,1... | collective-permute-start | bytes 393224 | tf_op jit(solution)/shard_map/ppermute | solution.py:96
  15.8 8.9 %collective-permute-start.2 = (bf16[64,1024]{1,0:T(8,128)(2,1)}, bf16[64,1024]{1,0:T(8,128)(2,1)S(1)}, u32[]{:S(2)}, u32[]{:S(2)}) collective-permute-start(bf16[64,1024]{1,0:T(8,128)(2,1)} %bitcast.205), channel_id=1, source_target_pairs={{1,0},{2,1},{3,2},{0,3},{5,4},{6,5},{7,6},{4,7},{9,8},{10,9},{11,1... | collective-permute-start | bytes 393224 | tf_op jit(solution)/shard_map/ppermute | solution.py:96
  17.1 13.4 %all-to-all-start = ((bf16[32,8,128]{2,1,0:T(8,128)(2,1)}), bf16[32,8,128]{2,1,0:T(8,128)(2,1)S(1)}, u32[]{:S(2)}, u32[]{:S(2)}) async-start(bf16[32,8,128]{2,1,0:T(8,128)(2,1)} %broadcast_in_dim.50), calls=%async_computation | async-start | bytes 131072 | tf_op jit(solution)/shard_map/all_to_all | solution.py:54
  20.1 75.6 %all-gather.5.cloned.1.call-start = ((), (), s32[]{:S(2)}) async-start(), calls=%async_computation.28 | async-start | bytes 4718592 | tf_op jit(solution)/shard_map/all_gather | solution.py:799
  32.7 15.4 %all-to-all-start.1 = ((bf16[4,64,768]{2,1,0:T(8,128)(2,1)}), bf16[4,64,768]{2,1,0:T(8,128)(2,1)S(1)}, u32[]{:S(2)}, u32[]{:S(2)}) async-start(bf16[4,64,768]{2,1,0:T(8,128)(2,1)} %reshape.439), calls=%async_computation.1 | async-start | bytes 786432 | tf_op jit(solution)/shard_map/all_to_all | solution.py:54
  49.3 27.9 %all-to-all-start.2 = ((bf16[4,4,64,768]{3,2,1,0:T(8,128)(2,1)}), bf16[4,4,64,768]{3,2,1,0:T(8,128)(2,1)S(1)}, u32[]{:S(2)}, u32[]{:S(2)}) async-start(bf16[4,4,64,768]{3,2,1,0:T(8,128)(2,1)} %broadcast_in_dim.51), calls=%async_computation.2 | async-start | bytes 3145728 | tf_op jit(solution)/shard_map/all_to_all | solution.py:54
  52.9 97.2 %all-gather.7.cloned.1.call-start = ((), (), s32[]{:S(2)}) async-start(), calls=%async_computation.29 | async-start | bytes 4718592 | tf_op jit(solution)/shard_map/all_gather | solution.py:832
  53.0 8.3 %collective-permute-start.3 = (bf16[64,1024]{1,0:T(8,128)(2,1)S(1)}, bf16[64,1024]{1,0:T(8,128)(2,1)S(1)}, u32[]{:S(2)}, u32[]{:S(2)}) collective-permute-start(bf16[64,1024]{1,0:T(8,128)(2,1)S(1)} %fusion.55.refs_0_), channel_id=1, source_target_pairs={{3,0},{0,1},{1,2},{2,3},{7,4},{4,5},{5,6},{6,7},{11,8},{8,9},{9,10... | collective-permute-start | bytes 393224 | tf_op jit(solution)/shard_map/ppermute | solution.py:96
  53.0 15.9 %collective-permute-start.4 = (bf16[64,1024]{1,0:T(8,128)(2,1)S(1)}, bf16[64,1024]{1,0:T(8,128)(2,1)S(1)}, u32[]{:S(2)}, u32[]{:S(2)}) collective-permute-start(bf16[64,1024]{1,0:T(8,128)(2,1)S(1)} %fusion.55.refs_0_), channel_id=1, source_target_pairs={{2,0},{3,1},{0,2},{1,3},{6,4},{7,5},{4,6},{5,7},{10,8},{11,9},{8,1... | collective-permute-start | bytes 393224 | tf_op jit(solution)/shard_map/ppermute | solution.py:96
  55.0 13.9 %collective-permute-start.5 = (bf16[64,1024]{1,0:T(8,128)(2,1)S(1)}, bf16[64,1024]{1,0:T(8,128)(2,1)S(1)}, u32[]{:S(2)}, u32[]{:S(2)}) collective-permute-start(bf16[64,1024]{1,0:T(8,128)(2,1)S(1)} %fusion.55.refs_0_), channel_id=1, source_target_pairs={{1,0},{2,1},{3,2},{0,3},{5,4},{6,5},{7,6},{4,7},{9,8},{10,9},{11,1... | collective-permute-start | bytes 393224 | tf_op jit(solution)/shard_map/ppermute | solution.py:96
  56.8 12.8 %collective-permute-start.6 = (bf16[64,1024]{1,0:T(8,128)(2,1)S(1)}, bf16[64,1024]{1,0:T(8,128)(2,1)S(1)}, u32[]{:S(2)}, u32[]{:S(2)}) collective-permute-start(bf16[64,1024]{1,0:T(8,128)(2,1)S(1)} %get-tuple-element.249), channel_id=1, source_target_pairs={{3,0},{0,1},{1,2},{2,3},{7,4},{4,5},{5,6},{6,7},{11,8},{8,9},{9,10... | collective-permute-start | bytes 393224 | tf_op jit(solution)/shard_map/ppermute | solution.py:112
  57.4 18.9 %collective-permute-start.7 = (bf16[64,1024]{1,0:T(8,128)(2,1)S(1)}, bf16[64,1024]{1,0:T(8,128)(2,1)S(1)}, u32[]{:S(2)}, u32[]{:S(2)}) collective-permute-start(bf16[64,1024]{1,0:T(8,128)(2,1)S(1)} %get-tuple-element.250), channel_id=1, source_target_pairs={{2,0},{3,1},{0,2},{1,3},{6,4},{7,5},{4,6},{5,7},{10,8},{11,9},{8,1... | collective-permute-start | bytes 393224 | tf_op jit(solution)/shard_map/ppermute | solution.py:112
  61.3 15.0 %collective-permute-start.8 = (bf16[64,1024]{1,0:T(8,128)(2,1)S(1)}, bf16[64,1024]{1,0:T(8,128)(2,1)S(1)}, u32[]{:S(2)}, u32[]{:S(2)}) collective-permute-start(bf16[64,1024]{1,0:T(8,128)(2,1)S(1)} %get-tuple-element.251), channel_id=1, source_target_pairs={{1,0},{2,1},{3,2},{0,3},{5,4},{6,5},{7,6},{4,7},{9,8},{10,9},{11,1... | collective-permute-start | bytes 393224 | tf_op jit(solution)/shard_map/ppermute | solution.py:112
  77.3 3.6 collective-permute-start.9
  78.9 62.0 %collective-permute-start.13 = (bf16[1024,1024]{1,0:T(8,128)(2,1)}, bf16[1024,1024]{1,0:T(8,128)(2,1)}, u32[]{:S(2)}, u32[]{:S(2)}) collective-permute-start(bf16[1024,1024]{1,0:T(8,128)(2,1)} %get-tuple-element.263), channel_id=1, source_target_pairs={{0,16},{16,0},{1,17},{17,1},{2,18},{18,2},{3,19},{19,3},{4,20},{20... | collective-permute-start | bytes 6291464 | tf_op jit(solution)/shard_map/ppermute | solution.py:706
  79.5 61.4 %collective-permute-start.14 = (bf16[1024,1024]{1,0:T(8,128)(2,1)}, bf16[1024,1024]{1,0:T(8,128)(2,1)}, u32[]{:S(2)}, u32[]{:S(2)}) collective-permute-start(bf16[1024,1024]{1,0:T(8,128)(2,1)} %get-tuple-element.265), channel_id=1, source_target_pairs={{0,16},{16,0},{1,17},{17,1},{2,18},{18,2},{3,19},{19,3},{4,20},{20... | collective-permute-start | bytes 6291464 | tf_op jit(solution)/shard_map/ppermute | solution.py:706
  84.5 11.1 %all-to-all-start.3 = ((bf16[4,64,256]{2,1,0:T(8,128)(2,1)}), bf16[4,64,256]{2,1,0:T(8,128)(2,1)S(1)}, u32[]{:S(2)}, u32[]{:S(2)}) async-start(bf16[4,64,256]{2,1,0:T(8,128)(2,1)} %bitcast.30), calls=%async_computation.3 | async-start | bytes 262144 | tf_op jit(solution)/shard_map/all_to_all | solution.py:54
  115.8 9.3 %collective-permute-start.10 = (bf16[64,1024]{1,0:T(8,128)(2,1)S(1)}, bf16[64,1024]{1,0:T(8,128)(2,1)S(1)}, u32[]{:S(2)}, u32[]{:S(2)}) collective-permute-start(bf16[64,1024]{1,0:T(8,128)(2,1)S(1)} %dynamic-slice_bitcast_fusion.4.refs_0_.grad_ref), channel_id=1, source_target_pairs={{3,0},{0,1},{1,2},{2,3},{7,4},{4,5},{5,6},{6,7},{11,8},{8,9},{9,10... | collective-permute-start | bytes 393224 | tf_op jit(solution)/shard_map/ppermute | solution.py:96
  117.6 10.0 %collective-permute-start.11 = (bf16[64,1024]{1,0:T(8,128)(2,1)S(1)}, bf16[64,1024]{1,0:T(8,128)(2,1)S(1)}, u32[]{:S(2)}, u32[]{:S(2)}) collective-permute-start(bf16[64,1024]{1,0:T(8,128)(2,1)S(1)} %dynamic-slice_bitcast_fusion.4.refs_0_.grad_ref), channel_id=1, source_target_pairs={{2,0},{3,1},{0,2},{1,3},{6,4},{7,5},{4,6},{5,7},{10,8},{11,9},{8,1... | collective-permute-start | bytes 393224 | tf_op jit(solution)/shard_map/ppermute | solution.py:96
  120.1 7.5 %collective-permute-start.12 = (bf16[64,1024]{1,0:T(8,128)(2,1)S(1)}, bf16[64,1024]{1,0:T(8,128)(2,1)S(1)}, u32[]{:S(2)}, u32[]{:S(2)}) collective-permute-start(bf16[64,1024]{1,0:T(8,128)(2,1)S(1)} %dynamic-slice_bitcast_fusion.4.refs_0_.grad_ref), channel_id=1, source_target_pairs={{1,0},{2,1},{3,2},{0,3},{5,4},{6,5},{7,6},{4,7},{9,8},{10,9},{11,1... | collective-permute-start | bytes 393224 | tf_op jit(solution)/shard_map/ppermute | solution.py:96
  120.1 20.8 %all-to-all-start.4 = ((bf16[8,40,1024]{2,1,0:T(8,128)(2,1)}), bf16[8,40,1024]{2,1,0:T(8,128)(2,1)S(1)}, u32[]{:S(2)}, u32[]{:S(2)}) async-start(bf16[8,40,1024]{2,1,0:T(8,128)(2,1)} %bitcast.223), calls=%async_computation.4 | async-start | bytes 1310720 | tf_op jit(solution)/shard_map/all_to_all | solution.py:54
  145.8 14.9 %all-to-all-start.5 = ((bf16[8,40,1024]{2,1,0:T(8,128)(2,1)}), bf16[8,40,1024]{2,1,0:T(8,128)(2,1)}, u32[]{:S(2)}, u32[]{:S(2)}) async-start(bf16[8,40,1024]{2,1,0:T(8,128)(2,1)} %bitcast.235), calls=%async_computation.5 | async-start | bytes 1310720 | tf_op jit(solution)/shard_map/all_to_all | solution.py:54
  163.8 19.2 %all-to-all-start.6 = ((bf16[4,64,1024]{2,1,0:T(8,128)(2,1)}), bf16[4,64,1024]{2,1,0:T(8,128)(2,1)S(1)}, u32[]{:S(2)}, u32[]{:S(2)}) async-start(bf16[4,64,1024]{2,1,0:T(8,128)(2,1)} %bitcast.45), calls=%async_computation.6 | async-start | bytes 1048576 | tf_op jit(solution)/shard_map/all_to_all | solution.py:54
  204.5 9.2 %all-to-all-start.7 = ((bf16[4,64,256]{2,1,0:T(8,128)(2,1)}), bf16[4,64,256]{2,1,0:T(8,128)(2,1)S(1)}, u32[]{:S(2)}, u32[]{:S(2)}) async-start(bf16[4,64,256]{2,1,0:T(8,128)(2,1)} %bitcast.50), calls=%async_computation.7 | async-start | bytes 262144 | tf_op jit(solution)/shard_map/all_to_all | solution.py:54
  217.4 19.1 %all-to-all-start.8 = ((bf16[8,40,1024]{2,1,0:T(8,128)(2,1)}), bf16[8,40,1024]{2,1,0:T(8,128)(2,1)S(1)}, u32[]{:S(2)}, u32[]{:S(2)}) async-start(bf16[8,40,1024]{2,1,0:T(8,128)(2,1)} %bitcast.222), calls=%async_computation.8 | async-start | bytes 1310720 | tf_op jit(solution)/shard_map/all_to_all | solution.py:54
  238.0 14.7 %all-to-all-start.9 = ((bf16[8,40,1024]{2,1,0:T(8,128)(2,1)}), bf16[8,40,1024]{2,1,0:T(8,128)(2,1)S(1)}, u32[]{:S(2)}, u32[]{:S(2)}) async-start(bf16[8,40,1024]{2,1,0:T(8,128)(2,1)} %bitcast.224), calls=%async_computation.9 | async-start | bytes 1310720 | tf_op jit(solution)/shard_map/all_to_all | solution.py:54
  257.7 14.9 %all-to-all-start.11 = ((bf16[8,40,1024]{2,1,0:T(8,128)(2,1)}), bf16[8,40,1024]{2,1,0:T(8,128)(2,1)}, u32[]{:S(2)}, u32[]{:S(2)}) async-start(bf16[8,40,1024]{2,1,0:T(8,128)(2,1)} %bitcast.236), calls=%async_computation.11 | async-start | bytes 1310720 | tf_op jit(solution)/shard_map/all_to_all | solution.py:54
  272.6 14.9 %all-to-all-start.10 = ((bf16[8,40,1024]{2,1,0:T(8,128)(2,1)}), bf16[8,40,1024]{2,1,0:T(8,128)(2,1)}, u32[]{:S(2)}, u32[]{:S(2)}) async-start(bf16[8,40,1024]{2,1,0:T(8,128)(2,1)} %bitcast.234), calls=%async_computation.10 | async-start | bytes 1310720 | tf_op jit(solution)/shard_map/all_to_all | solution.py:54
  290.3 20.1 %all-to-all-start.12 = ((bf16[4,64,1024]{2,1,0:T(8,128)(2,1)}), bf16[4,64,1024]{2,1,0:T(8,128)(2,1)}, u32[]{:S(2)}, u32[]{:S(2)}) async-start(bf16[4,64,1024]{2,1,0:T(8,128)(2,1)} %bitcast.229), calls=%async_computation.12 | async-start | bytes 1048576 | tf_op jit(solution)/shard_map/all_to_all | solution.py:54
  295.3 88.7 %reduce-scatter.6.cloned.1.call-start = ((), (), s32[]{:S(2)}) async-start(), calls=%async_computation.30 | async-start | bytes 2621440 | tf_op jit(solution)/shard_map/reduce_scatter | solution.py:1006
  295.8 3.6 collective-permute-start.17
  295.8 3.6 collective-permute-start.18
  310.3 75.5 %reduce-scatter.8.cloned.1.call-start = ((), (), s32[]{:S(2)}) async-start(), calls=%async_computation.31 | async-start | bytes 2293760 | tf_op jit(solution)/shard_map/reduce_scatter | solution.py:1006
  368.4 19.4 %all-to-all-start.15 = ((bf16[8,40,1024]{2,1,0:T(8,128)(2,1)}), bf16[8,40,1024]{2,1,0:T(8,128)(2,1)}, u32[]{:S(2)}, u32[]{:S(2)}) async-start(bf16[8,40,1024]{2,1,0:T(8,128)(2,1)} %bitcast.221), calls=%async_computation.15 | async-start | bytes 1310720 | tf_op jit(solution)/shard_map/all_to_all | solution.py:54
  372.8 67.2 %reduce-scatter.10.cloned.1.call-start = ((), (), s32[]{:S(2)}) async-start(), calls=%async_computation.32 | async-start | bytes 655360 | tf_op jit(solution)/shard_map/reduce_scatter | solution.py:1146
  395.6 6.0 %collective-permute-start.26 = (bf16[256,1024]{1,0:T(8,128)(2,1)S(1)}, bf16[256,1024]{1,0:T(8,128)(2,1)}, u32[]{:S(2)}, u32[]{:S(2)}) collective-permute-start(bf16[256,1024]{1,0:T(8,128)(2,1)S(1)} %all_gather.23.refs_0_), channel_id=1, source_target_pairs={{0,16},{16,0},{1,17},{17,1},{2,18},{18,2},{3,19},{19,3},{4,20},{20... | collective-permute-start | bytes 1572872 | tf_op jit(solution)/shard_map/ppermute | solution.py:706
  395.7 8.2 %collective-permute-start.27 = (bf16[256,1024]{1,0:T(8,128)(2,1)}, bf16[256,1024]{1,0:T(8,128)(2,1)}, u32[]{:S(2)}, u32[]{:S(2)}) collective-permute-start(bf16[256,1024]{1,0:T(8,128)(2,1)} %fusion.24.refs_2_), channel_id=1, source_target_pairs={{0,16},{16,0},{1,17},{17,1},{2,18},{18,2},{3,19},{19,3},{4,20},{20... | collective-permute-start | bytes 1572872 | tf_op jit(solution)/shard_map/ppermute | solution.py:706
  396.1 22.9 %all-to-all-start.16 = ((bf16[8,40,1024]{2,1,0:T(8,128)(2,1)}), bf16[8,40,1024]{2,1,0:T(8,128)(2,1)}, u32[]{:S(2)}, u32[]{:S(2)}) async-start(bf16[8,40,1024]{2,1,0:T(8,128)(2,1)} %bitcast.233), calls=%async_computation.18 | async-start | bytes 1310720 | tf_op jit(solution)/shard_map/all_to_all | solution.py:54
  400.4 95.2 %reduce-scatter.14.cloned.1.call-start = ((), (), s32[]{:S(2)}) async-start(), calls=%async_computation.34 | async-start | bytes 2621440 | tf_op jit(solution)/shard_map/reduce_scatter | solution.py:1006
  400.4 6.7 %collective-permute-start.28 = (bf16[256,1024]{1,0:T(8,128)(2,1)}, bf16[256,1024]{1,0:T(8,128)(2,1)S(1)}, u32[]{:S(2)}, u32[]{:S(2)}) collective-permute-start(bf16[256,1024]{1,0:T(8,128)(2,1)} %copy-done.30), channel_id=1, source_target_pairs={{0,16},{16,0},{1,17},{17,1},{2,18},{18,2},{3,19},{19,3},{4,20},{20... | collective-permute-start | bytes 1572872 | tf_op jit(solution)/shard_map/ppermute | solution.py:706
  400.8 6.4 %collective-permute-start.29 = (bf16[256,1024]{1,0:T(8,128)(2,1)S(1)}, bf16[256,1024]{1,0:T(8,128)(2,1)S(1)}, u32[]{:S(2)}, u32[]{:S(2)}) collective-permute-start(bf16[256,1024]{1,0:T(8,128)(2,1)S(1)} %get-tuple-element.370.refs_6_), channel_id=1, source_target_pairs={{0,16},{16,0},{1,17},{17,1},{2,18},{18,2},{3,19},{19,3},{4,20},{20... | collective-permute-start | bytes 1572872 | tf_op jit(solution)/shard_map/ppermute | solution.py:706
  401.0 11.4 %collective-permute-start.23 = (bf16[64,1408]{1,0:T(8,128)(2,1)}, bf16[64,1408]{1,0:T(8,128)(2,1)}, u32[]{:S(2)}, u32[]{:S(2)}) collective-permute-start(bf16[64,1408]{1,0:T(8,128)(2,1)} %get-tuple-element.364), channel_id=1, source_target_pairs={{3,0},{0,1},{1,2},{2,3},{7,4},{4,5},{5,6},{6,7},{11,8},{8,9},{9,10... | collective-permute-start | bytes 540680 | tf_op jit(solution)/shard_map/ppermute | solution.py:112
  401.6 17.5 %collective-permute-start.24 = (bf16[64,1408]{1,0:T(8,128)(2,1)}, bf16[64,1408]{1,0:T(8,128)(2,1)}, u32[]{:S(2)}, u32[]{:S(2)}) collective-permute-start(bf16[64,1408]{1,0:T(8,128)(2,1)} %get-tuple-element.365), channel_id=1, source_target_pairs={{2,0},{3,1},{0,2},{1,3},{6,4},{7,5},{4,6},{5,7},{10,8},{11,9},{8,1... | collective-permute-start | bytes 540680 | tf_op jit(solution)/shard_map/ppermute | solution.py:112
  403.9 15.1 %collective-permute-start.25 = (bf16[64,1408]{1,0:T(8,128)(2,1)}, bf16[64,1408]{1,0:T(8,128)(2,1)}, u32[]{:S(2)}, u32[]{:S(2)}) collective-permute-start(bf16[64,1408]{1,0:T(8,128)(2,1)} %get-tuple-element.366), channel_id=1, source_target_pairs={{1,0},{2,1},{3,2},{0,3},{5,4},{6,5},{7,6},{4,7},{9,8},{10,9},{11,1... | collective-permute-start | bytes 540680 | tf_op jit(solution)/shard_map/ppermute | solution.py:112
  421.4 21.7 %all-to-all-start.17 = ((bf16[4,64,1024]{2,1,0:T(8,128)(2,1)}), bf16[4,64,1024]{2,1,0:T(8,128)(2,1)S(1)}, u32[]{:S(2)}, u32[]{:S(2)}) async-start(bf16[4,64,1024]{2,1,0:T(8,128)(2,1)} %bitcast.86), calls=%async_computation.19 | async-start | bytes 1048576 | tf_op jit(solution)/shard_map/all_to_all | solution.py:54
  429.0 3.7 collective-permute-start.33
  429.0 4.6 collective-permute-start.32
  458.4 16.1 %all-to-all-start.19 = ((bf16[4,64,1024]{2,1,0:T(8,128)(2,1)}), bf16[4,64,1024]{2,1,0:T(8,128)(2,1)S(1)}, u32[]{:S(2)}, u32[]{:S(2)}) async-start(bf16[4,64,1024]{2,1,0:T(8,128)(2,1)} %bitcast.226), calls=%async_computation.22 | async-start | bytes 1048576 | tf_op jit(solution)/shard_map/all_to_all | solution.py:54
  461.9 47.5 %reduce-scatter.12.cloned.1.call-start = ((), (), s32[]{:S(2)}) async-start(), calls=%async_computation.33 | async-start | bytes 2293760 | tf_op jit(solution)/shard_map/reduce_scatter | solution.py:1006
  474.6 6.7 %collective-permute-start.38 = (bf16[320,1024]{1,0:T(8,128)(2,1)S(1)}, bf16[320,1024]{1,0:T(8,128)(2,1)S(1)}, u32[]{:S(2)}, u32[]{:S(2)}) collective-permute-start(bf16[320,1024]{1,0:T(8,128)(2,1)S(1)} %bitcast.190), channel_id=1, source_target_pairs={{0,16},{16,0},{1,17},{17,1},{2,18},{18,2},{3,19},{19,3},{4,20},{20... | collective-permute-start | bytes 1966088 | tf_op jit(solution)/shard_map/ppermute | solution.py:706
  474.7 6.6 %collective-permute-start.39 = (bf16[320,1024]{1,0:T(8,128)(2,1)S(1)}, bf16[320,1024]{1,0:T(8,128)(2,1)}, u32[]{:S(2)}, u32[]{:S(2)}) collective-permute-start(bf16[320,1024]{1,0:T(8,128)(2,1)S(1)} %bitcast.193), channel_id=1, source_target_pairs={{0,16},{16,0},{1,17},{17,1},{2,18},{18,2},{3,19},{19,3},{4,20},{20... | collective-permute-start | bytes 1966088 | tf_op jit(solution)/shard_map/ppermute | solution.py:706
  475.2 6.1 %collective-permute-start.41 = (bf16[320,1024]{1,0:T(8,128)(2,1)}, bf16[320,1024]{1,0:T(8,128)(2,1)}, u32[]{:S(2)}, u32[]{:S(2)}) collective-permute-start(bf16[320,1024]{1,0:T(8,128)(2,1)} %get-tuple-element.414.refs_6_), channel_id=1, source_target_pairs={{0,16},{16,0},{1,17},{17,1},{2,18},{18,2},{3,19},{19,3},{4,20},{20... | collective-permute-start | bytes 1966088 | tf_op jit(solution)/shard_map/ppermute | solution.py:706
  475.3 6.0 %collective-permute-start.40 = (bf16[320,1024]{1,0:T(8,128)(2,1)}, bf16[320,1024]{1,0:T(8,128)(2,1)}, u32[]{:S(2)}, u32[]{:S(2)}) collective-permute-start(bf16[320,1024]{1,0:T(8,128)(2,1)} %get-tuple-element.412.refs_4_), channel_id=1, source_target_pairs={{0,16},{16,0},{1,17},{17,1},{2,18},{18,2},{3,19},{19,3},{4,20},{20... | collective-permute-start | bytes 1966088 | tf_op jit(solution)/shard_map/ppermute | solution.py:706
  481.3 14.3 %all-to-all-start.20 = ((f32[32,16,128]{2,1,0:T(8,128)}), f32[32,16,128]{2,1,0:T(8,128)S(1)}, u32[]{:S(2)}, u32[]{:S(2)}) async-start(f32[32,16,128]{2,1,0:T(8,128)} %pack_small.1), calls=%async_computation.25 | async-start | bytes 524288 | tf_op jit(solution)/shard_map/all_to_all | solution.py:54
  497.5 11.6 %all-to-all-start.21 = ((bf16[4,64,512]{2,1,0:T(8,128)(2,1)}), bf16[4,64,512]{2,1,0:T(8,128)(2,1)S(1)}, u32[]{:S(2)}, u32[]{:S(2)}) async-start(bf16[4,64,512]{2,1,0:T(8,128)(2,1)} %bitcast.93), calls=%async_computation.26 | async-start | bytes 524288 | tf_op jit(solution)/shard_map/all_to_all | solution.py:54
  500.9 8.5 %collective-permute-start.45 = (f32[64,1024]{1,0:T(8,128)S(1)}, f32[64,1024]{1,0:T(8,128)S(1)}, u32[]{:S(2)}, u32[]{:S(2)}) collective-permute-start(f32[64,1024]{1,0:T(8,128)S(1)} %copy-done.41), channel_id=1, source_target_pairs={{0,16},{16,0},{1,17},{17,1},{2,18},{18,2},{3,19},{19,3},{4,20},{20... | collective-permute-start | bytes 786440 | tf_op jit(solution)/shard_map/ppermute | solution.py:706
  501.0 8.5 %collective-permute-start.44 = (f32[64,1024]{1,0:T(8,128)S(1)}, f32[64,1024]{1,0:T(8,128)S(1)}, u32[]{:S(2)}, u32[]{:S(2)}) collective-permute-start(f32[64,1024]{1,0:T(8,128)S(1)} %get-tuple-element.427.refs_4_), channel_id=1, source_target_pairs={{0,16},{16,0},{1,17},{17,1},{2,18},{18,2},{3,19},{19,3},{4,20},{20... | collective-permute-start | bytes 786440 | tf_op jit(solution)/shard_map/ppermute | solution.py:706
  501.5 7.9 %collective-permute-start.42 = (bf16[64,1024]{1,0:T(8,128)(2,1)S(1)}, bf16[64,1024]{1,0:T(8,128)(2,1)S(1)}, u32[]{:S(2)}, u32[]{:S(2)}) collective-permute-start(bf16[64,1024]{1,0:T(8,128)(2,1)S(1)} %copy-done.20), channel_id=1, source_target_pairs={{0,16},{16,0},{1,17},{17,1},{2,18},{18,2},{3,19},{19,3},{4,20},{20... | collective-permute-start | bytes 393224 | tf_op jit(solution)/shard_map/ppermute | solution.py:706
  501.6 7.9 %collective-permute-start.43 = (bf16[64,1024]{1,0:T(8,128)(2,1)S(1)}, bf16[64,1024]{1,0:T(8,128)(2,1)S(1)}, u32[]{:S(2)}, u32[]{:S(2)}) collective-permute-start(bf16[64,1024]{1,0:T(8,128)(2,1)S(1)} %get-tuple-element.425.refs_2_), channel_id=1, source_target_pairs={{0,16},{16,0},{1,17},{17,1},{2,18},{18,2},{3,19},{19,3},{4,20},{20... | collective-permute-start | bytes 393224 | tf_op jit(solution)/shard_map/ppermute | solution.py:706
  509.5 17.7 %all-to-all-start.22 = ((bf16[4,64,896]{2,1,0:T(8,128)(2,1)}), bf16[4,64,896]{2,1,0:T(8,128)(2,1)S(1)}, u32[]{:S(2)}, u32[]{:S(2)}) async-start(bf16[4,64,896]{2,1,0:T(8,128)(2,1)} %bitcast.238), calls=%async_computation.27 | async-start | bytes 917504 | tf_op jit(solution)/shard_map/all_to_all | solution.py:54
  514.1 14.4 %collective-permute-start.51 = (bf16[256,512]{1,0:T(8,128)(2,1)S(1)}, bf16[256,512]{1,0:T(8,128)(2,1)S(1)}, u32[]{:S(2)}, u32[]{:S(2)}) collective-permute-start(bf16[256,512]{1,0:T(8,128)(2,1)S(1)} %copy-done.28), channel_id=1, source_target_pairs={{0,16},{16,0},{1,17},{17,1},{2,18},{18,2},{3,19},{19,3},{4,20},{20... | collective-permute-start | bytes 786440 | tf_op jit(solution)/shard_map/ppermute | solution.py:706
  515.4 14.7 %collective-permute-start.49 = (bf16[4,64,896]{2,1,0:T(8,128)(2,1)S(1)}, bf16[4,64,896]{2,1,0:T(8,128)(2,1)S(1)}, u32[]{:S(2)}, u32[]{:S(2)}) collective-permute-start(bf16[4,64,896]{2,1,0:T(8,128)(2,1)S(1)} %slice.246.refs_6_), channel_id=1, source_target_pairs={{0,16},{16,0},{1,17},{17,1},{2,18},{18,2},{3,19},{19,3},{4,20},{20... | collective-permute-start | bytes 1376264 | tf_op jit(solution)/shard_map/ppermute | solution.py:706
  (125 other events, 2180.3 us)
Sparse Core Ops, SparseCore 0:
  9.9 39.9 all-gather.8
  52.4 43.2 all-gather.4
  98.1 42.4 all-gather.6
  310.5 32.6 reduce-scatter.5
  346.3 35.3 reduce-scatter.7
  384.0 29.4 reduce-scatter.9
  419.2 38.5 reduce-scatter.13
  474.7 34.6 reduce-scatter.11
